TPU v7x, 8 devices: a whole 2x2x1 slice. The times are simulated.
8 devices in a mesh: dp: 2 (over z, y), tp: 4 (over x, core).
Axes of the slice: x: 2, y: 2, z: 1, core: 2. Of those that a mesh axis runs over, the one named last changes fastest.
Arguments:
- ids: int32 [4, 256], P('dp'), parts along dimension 0
- emb: bfloat16 [32768, 2304], P('tp')
- g: bfloat16 [2304], replicated
- w: bfloat16 [2304, 4096], P(None, 'tp')
- du: bfloat16 [4, 256, 4096], P('dp', None, 'tp'), parts along dimension 0
- dres: bfloat16 [4, 256, 2304], P('dp', 'tp'), parts along dimension 0
Outputs:
- output 1: bfloat16 [4, 256, 4096], P('dp', None, 'tp'), parts along dimension 0
- output 2: bfloat16 [4, 256, 2304], P('dp', 'tp'), parts along dimension 0
- output 3: float32 [65536, 2304], P(('dp', 'tp')), parts along dimension 0
- output 4: float32 [2304, 8192], P(None, ('dp', 'tp')), parts along dimension 1
- output 5: float32 [4608], P('dp'), parts along dimension 0
There are 2 independent parts. A program takes and returns all parts, laid end to end along the dimension named above; an argument that names none is the same for every part.
All inputs are finite; a program needn't handle non-finite values.
Results may differ from a plain program's by a relative error of at most 0.001.
Values are sent between devices in bfloat16 or wider.
A program may use at most 1 GiB of HBM per device.

v0:
```python
import jax
import jax.numpy as jnp
from jax import lax
from jax.sharding import PartitionSpec as P

EPS = 1e-6


def solution(mesh):
    groups = mesh.shape["tp"]

    def local(ids, emb, g, w, du, dres):
        r = lax.axis_index("tp")
        t = ids.shape[1]
        vl, d = emb.shape
        tl = t // groups
        lo = r * vl
        start = r * tl
        gf = g.astype(jnp.float32)
        cols = lax.broadcasted_iota(jnp.int32, (1, vl), 1)

        def micro(dg, inp):
            idm, dum, drm = inp
            oh = ((idm - lo)[:, None] == cols).astype(jnp.bfloat16)
            xp = jnp.dot(oh, emb, preferred_element_type=jnp.float32).astype(jnp.bfloat16)
            x = lax.psum(xp, "tp")
            xf = x.astype(jnp.float32)
            rs = lax.rsqrt(jnp.mean(xf * xf, axis=-1, keepdims=True) + EPS)
            nh = xf * rs
            n = (nh * gf).astype(jnp.bfloat16)
            u = jnp.dot(n, w, preferred_element_type=jnp.float32).astype(jnp.bfloat16)
            pdn = jnp.einsum("tf,df->td", dum, w, preferred_element_type=jnp.float32).astype(jnp.bfloat16)
            recv = lax.all_to_all(pdn, "tp", 0, 0, tiled=True).reshape(groups, tl, d)
            dn = jnp.sum(recv.astype(jnp.float32), axis=0)
            nhs = lax.dynamic_slice_in_dim(nh, start, tl, 0)
            rss = lax.dynamic_slice_in_dim(rs, start, tl, 0)
            gdn = gf * dn
            dxn = rss * (gdn - nhs * jnp.mean(nhs * gdn, axis=-1, keepdims=True))
            dx = (drm.astype(jnp.float32) + dxn).astype(jnp.bfloat16)
            dxa = lax.all_gather(dx, "tp", axis=0, tiled=True)
            dg = dg + jnp.sum(dn * nhs, axis=0)
            return dg, (u, lax.dynamic_slice_in_dim(x, start, tl, 0), n, dxa)

        dg, (u, xo, ns, dxs) = lax.scan(micro, jnp.zeros((d,), jnp.float32), (ids, du, dres))
        loc = (ids - lo).reshape(-1)
        oh = (lax.broadcasted_iota(jnp.int32, (vl, loc.shape[0]), 0) == loc[None, :]).astype(jnp.bfloat16)
        de = jnp.dot(oh, dxs.reshape(-1, d), preferred_element_type=jnp.float32)
        dw = jnp.einsum("ktd,ktf->df", ns, du, preferred_element_type=jnp.float32)
        dg = lax.psum(dg, "tp")
        return u, xo, de, dw, dg

    return jax.shard_map(
        local,
        mesh=mesh,
        in_specs=(P("dp", None), P("tp", None), P(None), P(None, "tp"), P("dp", None, "tp"), P("dp", "tp", None)),
        out_specs=(P("dp", None, "tp"), P("dp", "tp", None), P(("dp", "tp"), None), P(None, ("dp", "tp")), P("dp")),
        check_vma=False,
    )
```

profile of v0, /device:TPU:0, one launch (start us, length us, event | category | flops | bytes accessed | tf_op | source)
XLA Modules:
  0.0 223.6 jit_solution(1090461056515435112)
XLA Ops:
  7.2 0.7 convert_element_type.48
  7.9 160.5 %while.21 = (s32[]{:T(128)}, f32[2304]{0:T(1024)}, bf16[2,256,1024]{2,1,0:T(8,128)(2,1)}, bf16[2,64,2304]{2,1,0:T(8,128)(2,1)}, bf16[2,256,2304]{2,1,0:T(8,128)(...) while((s32[]{:T(128)}, f32[2304]{0:T(1024)}, ...), condition=%wide.region_6.7_spmd.clone, body=%wide.region_0.6_spmd.clone.sunk | while | flops 12094195712 | bytes 111906632 | solution.py:44
  7.9 0.0 all-reduce.2.cloned.1.call-start
  7.9 0.7 fusion.34
  8.6 16.9 %fusion.35 = bf16[256,2304]{1,0:T(8,128)(2,1)} fusion(bf16[8192,2304]{1,0:T(8,128)(2,1)} %get-tuple-element.395, s32[256]{0:T(256)S(1)} %bitcast.52), kind=kOutput, calls=%fused_computation.5.clone.1 | convolution fusion | flops 9666363392 | bytes 38929408 | tf_op jit(solution)/shard_map/while/body/eval_jaxpr/dot_general | solution.py:25
  25.5 0.0 all-reduce.2.cloned.1.call-update
  25.6 0.0 copy-done.10
  25.6 4.8 %convolution_convert_fusion.3 = bf16[256,2304]{1,0:T(8,128)(2,1)} fusion(bf16[2304,1024]{1,0:T(8,128)(2,1)} %get-tuple-element.392, bf16[2,256,1024]{2,1,0:T(8,128)(2,1)S(1)} %copy-done.10, s32[]{:T(128)S(6)} %copy.25), kind=kOutput, calls=%fused_computation.4.clone.1 | convolution fusion | flops 1208549376 | bytes 6422532 | tf_op jit(solution)/shard_map/while/body/eval_jaxpr/tf,df->td/dot_general | solution.py:32
  30.4 4.6 %all-to-all-start = ((bf16[4,64,2304]{2,1,0:T(8,128)(2,1)}), bf16[4,64,2304]{2,1,0:T(8,128)(2,1)}, u32[]{:S(2)}, u32[]{:S(2)}) async-start(bf16[4,64,2304]{2,1,0:T(8,128)(2,1)} %bitcast.50), calls=%async_computation | async-start | bytes 2359296 | tf_op jit(solution)/shard_map/while/body/eval_jaxpr/all_to_all | solution.py:33
  35.0 0.0 all-gather.2.cloned.1.call-start
  35.0 30.3 %all-reduce.2.cloned.1.call-done = bf16[256,2304]{1,0:T(8,128)(2,1)} async-done(((bf16[256,2304]{1,0:T(8,128)(2,1)}), bf16[256,2304]{1,0:T(8,128)(2,1)}) %all-reduce.2.cloned.1.call-update) | async-done | bytes 1179664 | tf_op jit(solution)/shard_map/while/body/eval_jaxpr/psum | solution.py:26
  65.2 1.6 fusion.36
  66.8 0.6 dynamic-slice.5
  67.5 1.5 convert_multiply_fusion.4
  68.9 0.0 copy-start
  69.0 0.0 all-to-all-done
  69.0 0.0 copy-start.1
  69.0 0.0 copy-start.6
  69.0 1.6 convert_reduce_fusion.2
  70.6 0.7 multiply_reduce_fusion.3
  71.4 0.9 fusion.38
  72.3 0.0 all-gather.2.cloned.1.call-update
  72.3 0.0 copy-done
  72.3 0.7 bitcast_dynamic-update-slice_fusion.6
  73.0 4.7 %fusion.37 = bf16[2,256,1024]{2,1,0:T(8,128)(2,1)} fusion(bf16[2,256,1024]{2,1,0:T(8,128)(2,1)} %get-tuple-element.371, s32[]{:T(128)S(6)} %copy.25, bf16[2304,1024]{1,0:T(8,128)(2,1)} %get-tuple-element.392, f32[2304]{0:T(1024)S(1)} %get-tuple-element.397, bf16[256,2304]{1,0:T(8,128)(2,1)S(1)} %copy-done, f32[256]{0:T(256)S(1)} %add_rsqrt_fusion.2), kind=kOutput, calls=%fused_computation.13.clone.1 | convolution fusion | flops 1210580992 | bytes 6432772 | tf_op jit(solution)/shard_map/while/body/eval_jaxpr/dot_general | solution.py:31
  77.8 0.3 bitcast_dynamic-update-slice_fusion.7
  78.1 0.0 copy-start.8
  78.1 1.4 copy-done.8
  79.5 0.0 copy-start.4
  79.5 7.7 %all-gather.2.cloned.1.call-done = bf16[256,2304]{1,0:T(8,128)(2,1)} async-done(((bf16[64,2304]{1,0:T(8,128)(2,1)}), bf16[256,2304]{1,0:T(8,128)(2,1)}) %all-gather.2.cloned.1.call-update) | async-done | bytes 1179664 | tf_op jit(solution)/shard_map/while/body/eval_jaxpr/all_gather | solution.py:40
  87.2 2.4 %bitcast_dynamic-update-slice_fusion.8 = bf16[2,256,2304]{2,1,0:T(8,128)(2,1)} fusion(bf16[2,256,2304]{2,1,0:T(8,128)(2,1)} %get-tuple-element.374, s32[]{:T(128)S(6)} %copy.25, bf16[256,2304]{1,0:T(8,128)(2,1)} %all-gather.2.cloned.1.call-done), kind=kLoop, calls=%fused_computation.14.clone.1 | loop fusion | bytes 2359300 | tf_op jit(solution)/shard_map/while/body/jit(dynamic_update_index_in_dim)/dynamic_update_slice | solution.py:44
  89.6 0.7 fusion.34
  90.3 16.9 %fusion.35 = bf16[256,2304]{1,0:T(8,128)(2,1)} fusion(bf16[8192,2304]{1,0:T(8,128)(2,1)} %get-tuple-element.395, s32[256]{0:T(256)S(1)} %bitcast.52), kind=kOutput, calls=%fused_computation.5.clone.1 | convolution fusion | flops 9666363392 | bytes 38929408 | tf_op jit(solution)/shard_map/while/body/eval_jaxpr/dot_general | solution.py:25
  107.2 0.0 all-reduce.2.cloned.1.call-update
  107.2 4.8 %convolution_convert_fusion.3 = bf16[256,2304]{1,0:T(8,128)(2,1)} fusion(bf16[2304,1024]{1,0:T(8,128)(2,1)} %get-tuple-element.392, bf16[2,256,1024]{2,1,0:T(8,128)(2,1)S(1)} %copy-done.10, s32[]{:T(128)S(6)} %copy.25), kind=kOutput, calls=%fused_computation.4.clone.1 | convolution fusion | flops 1208549376 | bytes 6422532 | tf_op jit(solution)/shard_map/while/body/eval_jaxpr/tf,df->td/dot_general | solution.py:32
  112.0 4.3 %all-to-all-start = ((bf16[4,64,2304]{2,1,0:T(8,128)(2,1)}), bf16[4,64,2304]{2,1,0:T(8,128)(2,1)}, u32[]{:S(2)}, u32[]{:S(2)}) async-start(bf16[4,64,2304]{2,1,0:T(8,128)(2,1)} %bitcast.50), calls=%async_computation | async-start | bytes 2359296 | tf_op jit(solution)/shard_map/while/body/eval_jaxpr/all_to_all | solution.py:33
  116.3 0.0 all-gather.2.cloned.1.call-start
  116.4 27.7 %all-reduce.2.cloned.1.call-done = bf16[256,2304]{1,0:T(8,128)(2,1)} async-done(((bf16[256,2304]{1,0:T(8,128)(2,1)}), bf16[256,2304]{1,0:T(8,128)(2,1)}) %all-reduce.2.cloned.1.call-update) | async-done | bytes 1179664 | tf_op jit(solution)/shard_map/while/body/eval_jaxpr/psum | solution.py:26
  144.1 1.6 fusion.36
  145.7 0.6 dynamic-slice.5
  146.3 1.5 convert_multiply_fusion.4
  147.8 0.0 all-to-all-done
  147.8 0.0 copy-start.1
  147.8 1.6 convert_reduce_fusion.2
  149.5 0.7 multiply_reduce_fusion.3
  150.2 0.0 copy-done.6
  150.2 0.9 fusion.38
  151.1 0.0 all-gather.2.cloned.1.call-update
  151.1 0.0 copy-done
  151.2 0.7 bitcast_dynamic-update-slice_fusion.6
  151.9 4.7 %fusion.37 = bf16[2,256,1024]{2,1,0:T(8,128)(2,1)} fusion(bf16[2,256,1024]{2,1,0:T(8,128)(2,1)} %get-tuple-element.371, s32[]{:T(128)S(6)} %copy.25, bf16[2304,1024]{1,0:T(8,128)(2,1)} %get-tuple-element.392, f32[2304]{0:T(1024)S(1)} %get-tuple-element.397, bf16[256,2304]{1,0:T(8,128)(2,1)S(1)} %copy-done, f32[256]{0:T(256)S(1)} %add_rsqrt_fusion.2), kind=kOutput, calls=%fused_computation.13.clone.1 | convolution fusion | flops 1210580992 | bytes 6432772 | tf_op jit(solution)/shard_map/while/body/eval_jaxpr/dot_general | solution.py:31
  156.6 0.3 bitcast_dynamic-update-slice_fusion.7
  156.9 0.0 copy-start.8
  157.0 1.4 copy-done.8
  158.4 0.0 copy-done.2
  158.4 0.0 copy-start.4
  158.4 7.6 %all-gather.2.cloned.1.call-done = bf16[256,2304]{1,0:T(8,128)(2,1)} async-done(((bf16[64,2304]{1,0:T(8,128)(2,1)}), bf16[256,2304]{1,0:T(8,128)(2,1)}) %all-gather.2.cloned.1.call-update) | async-done | bytes 1179664 | tf_op jit(solution)/shard_map/while/body/eval_jaxpr/all_gather | solution.py:40
  166.0 2.4 %bitcast_dynamic-update-slice_fusion.8 = bf16[2,256,2304]{2,1,0:T(8,128)(2,1)} fusion(bf16[2,256,2304]{2,1,0:T(8,128)(2,1)} %get-tuple-element.374, s32[]{:T(128)S(6)} %copy.25, bf16[256,2304]{1,0:T(8,128)(2,1)} %all-gather.2.cloned.1.call-done), kind=kLoop, calls=%fused_computation.14.clone.1 | loop fusion | bytes 2359300 | tf_op jit(solution)/shard_map/while/body/jit(dynamic_update_index_in_dim)/dynamic_update_slice | solution.py:44
  168.4 0.7 subtract_bitcast_fusion
  169.1 32.1 %fusion.13 = f32[8192,2304]{1,0:T(8,128)} fusion(bf16[512,2304]{1,0:T(8,128)(2,1)} %bitcast.54, s32[512]{0:T(512)S(1)} %bitcast.53), kind=kOutput, calls=%fused_computation.30 | convolution fusion | flops 19331547136 | bytes 77858816 | tf_op jit(solution)/shard_map/dot_general | solution.py:47
  201.2 0.0 copy-done.9
  201.2 5.2 %convolution_bitcast_fusion = f32[2304,1024]{1,0:T(8,128)} fusion(bf16[2,256,2304]{2,1,0:T(8,128)(2,1)S(1)} %copy-done.9, bf16[2,256,1024]{2,1,0:T(8,128)(2,1)S(1)} %copy-done.11), kind=kOutput, calls=%fused_computation.32 | convolution fusion | flops 2415919104 | bytes 12845056 | tf_op jit(solution)/shard_map/ktd,ktf->df/dot_general | solution.py:48
  206.4 0.0 copy-done.5
  206.4 10.7 %psum.16 = f32[2304]{0:T(1024)} all-reduce(f32[2304]{0:T(1024)S(1)} %copy-done.5), channel_id=1, replica_groups=mesh['dp'=2,'tp'=4] {'tp'}, use_global_device_ids=true, to_apply=%region_7.8 | all-reduce | flops 2304 | bytes 18432 | tf_op jit(solution)/shard_map/psum | solution.py:49
  (38 shorter events, 0.1 us)
Async XLA Ops:
  7.9 57.3 %all-reduce.2.cloned.1.call-start = ((), (), s32[]{:S(2)}) async-start(), calls=%async_computation.1 | async-start | bytes 2359296 | tf_op jit(solution)/shard_map/while/body/eval_jaxpr/psum | solution.py:26
  8.6 17.0 %copy-start.10 = (bf16[2,256,1024]{2,1,0:T(8,128)(2,1)S(1)}, bf16[2,256,1024]{2,1,0:T(8,128)(2,1)}, u32[]{:S(2)}) copy-start(bf16[2,256,1024]{2,1,0:T(8,128)(2,1)} %get-tuple-element.391) | copy-start | bytes 3145732 | tf_op jit(solution)/shard_map/while
  30.4 38.6 %all-to-all-start = ((bf16[4,64,2304]{2,1,0:T(8,128)(2,1)}), bf16[4,64,2304]{2,1,0:T(8,128)(2,1)}, u32[]{:S(2)}, u32[]{:S(2)}) async-start(bf16[4,64,2304]{2,1,0:T(8,128)(2,1)} %bitcast.50), calls=%async_computation | async-start | bytes 2359296 | tf_op jit(solution)/shard_map/while/body/eval_jaxpr/all_to_all | solution.py:33
  35.0 52.2 %all-gather.2.cloned.1.call-start = ((), (), s32[]{:S(2)}) async-start(), calls=%async_computation.2 | async-start | bytes 1474560 | tf_op jit(solution)/shard_map/while/body/eval_jaxpr/all_gather | solution.py:40
  68.9 3.4 %copy-start = (bf16[256,2304]{1,0:T(8,128)(2,1)S(1)}, bf16[256,2304]{1,0:T(8,128)(2,1)}, u32[]{:S(2)}) copy-start(bf16[256,2304]{1,0:T(8,128)(2,1)} %all-reduce.2.cloned.1.call-done) | copy-start | bytes 3538948 | tf_op jit(solution)/shard_map/while
  69.0 2.4 %copy-start.1 = (bf16[2,64,2304]{2,1,0:T(8,128)(2,1)S(1)}, bf16[2,64,2304]{2,1,0:T(8,128)(2,1)}, u32[]{:S(2)}) copy-start(bf16[2,64,2304]{2,1,0:T(8,128)(2,1)} %get-tuple-element.398) | copy-start | bytes 1769476 | tf_op jit(solution)/shard_map/while
  69.0 2.4 %copy-start.6 = (f32[64]{0:T(128)S(1)}, f32[64]{0:T(128)}, u32[]{:S(2)}) copy-start(f32[64]{0:T(128)} %dynamic-slice.5) | copy-start | bytes 772 | tf_op jit(solution)/shard_map/while
  73.0 4.7 %copy-start.7 = (bf16[2,256,2304]{2,1,0:T(8,128)(2,1)S(1)}, bf16[2,256,2304]{2,1,0:T(8,128)(2,1)}, u32[]{:S(2)}) copy-start(bf16[2,256,2304]{2,1,0:T(8,128)(2,1)} %get-tuple-element.373) | copy-start | bytes 7077892 | tf_op jit(solution)/shard_map/while
  77.8 1.8 copy-start.2
  77.8 1.8 copy-start.3
  78.1 1.4 copy-start.8
  79.5 10.0 %copy-start.4 = (f32[2304]{0:T(1024)}, f32[2304]{0:T(1024)S(1)}, u32[]{:S(2)}) copy-start(f32[2304]{0:T(1024)S(1)} %select_add_fusion.2) | copy-start | bytes 27652 | tf_op jit(solution)/shard_map/while
  89.6 54.5 %all-reduce.2.cloned.1.call-start = ((), (), s32[]{:S(2)}) async-start(), calls=%async_computation.1 | async-start | bytes 2359296 | tf_op jit(solution)/shard_map/while/body/eval_jaxpr/psum | solution.py:26
  90.3 17.0 %copy-start.10 = (bf16[2,256,1024]{2,1,0:T(8,128)(2,1)S(1)}, bf16[2,256,1024]{2,1,0:T(8,128)(2,1)}, u32[]{:S(2)}) copy-start(bf16[2,256,1024]{2,1,0:T(8,128)(2,1)} %get-tuple-element.391) | copy-start | bytes 3145732 | tf_op jit(solution)/shard_map/while
  112.0 35.8 %all-to-all-start = ((bf16[4,64,2304]{2,1,0:T(8,128)(2,1)}), bf16[4,64,2304]{2,1,0:T(8,128)(2,1)}, u32[]{:S(2)}, u32[]{:S(2)}) async-start(bf16[4,64,2304]{2,1,0:T(8,128)(2,1)} %bitcast.50), calls=%async_computation | async-start | bytes 2359296 | tf_op jit(solution)/shard_map/while/body/eval_jaxpr/all_to_all | solution.py:33
  116.3 49.7 %all-gather.2.cloned.1.call-start = ((), (), s32[]{:S(2)}) async-start(), calls=%async_computation.2 | async-start | bytes 1474560 | tf_op jit(solution)/shard_map/while/body/eval_jaxpr/all_gather | solution.py:40
  147.8 3.4 %copy-start = (bf16[256,2304]{1,0:T(8,128)(2,1)S(1)}, bf16[256,2304]{1,0:T(8,128)(2,1)}, u32[]{:S(2)}) copy-start(bf16[256,2304]{1,0:T(8,128)(2,1)} %all-reduce.2.cloned.1.call-done) | copy-start | bytes 3538948 | tf_op jit(solution)/shard_map/while
  147.8 2.4 %copy-start.1 = (bf16[2,64,2304]{2,1,0:T(8,128)(2,1)S(1)}, bf16[2,64,2304]{2,1,0:T(8,128)(2,1)}, u32[]{:S(2)}) copy-start(bf16[2,64,2304]{2,1,0:T(8,128)(2,1)} %get-tuple-element.398) | copy-start | bytes 1769476 | tf_op jit(solution)/shard_map/while
  147.8 2.4 %copy-start.6 = (f32[64]{0:T(128)S(1)}, f32[64]{0:T(128)}, u32[]{:S(2)}) copy-start(f32[64]{0:T(128)} %dynamic-slice.5) | copy-start | bytes 772 | tf_op jit(solution)/shard_map/while
  151.9 4.7 %copy-start.7 = (bf16[2,256,2304]{2,1,0:T(8,128)(2,1)S(1)}, bf16[2,256,2304]{2,1,0:T(8,128)(2,1)}, u32[]{:S(2)}) copy-start(bf16[2,256,2304]{2,1,0:T(8,128)(2,1)} %get-tuple-element.373) | copy-start | bytes 7077892 | tf_op jit(solution)/shard_map/while
  156.6 1.8 copy-start.2
  156.6 1.8 copy-start.3
  156.9 1.4 copy-start.8
  158.4 10.0 %copy-start.4 = (f32[2304]{0:T(1024)}, f32[2304]{0:T(1024)S(1)}, u32[]{:S(2)}) copy-start(f32[2304]{0:T(1024)S(1)} %select_add_fusion.2) | copy-start | bytes 27652 | tf_op jit(solution)/shard_map/while
  169.1 32.1 %copy-start.9 = (bf16[2,256,2304]{2,1,0:T(8,128)(2,1)S(1)}, bf16[2,256,2304]{2,1,0:T(8,128)(2,1)}, u32[]{:S(2)}) copy-start(bf16[2,256,2304]{2,1,0:T(8,128)(2,1)} %get-tuple-element.185) | copy-start | bytes 7077892
  169.1 32.1 %copy-start.11 = (bf16[2,256,1024]{2,1,0:T(8,128)(2,1)S(1)}, bf16[2,256,1024]{2,1,0:T(8,128)(2,1)}, u32[]{:S(2)}) copy-start(bf16[2,256,1024]{2,1,0:T(8,128)(2,1)} %get-tuple-element.410) | copy-start | bytes 3145732
  201.2 5.2 %copy-start.5 = (f32[2304]{0:T(1024)S(1)}, f32[2304]{0:T(1024)}, u32[]{:S(2)}) copy-start(f32[2304]{0:T(1024)} %get-tuple-element.186) | copy-start | bytes 27652
Sparse Core Ops, SparseCore 0:
  25.7 39.5 all-reduce.1
  72.4 14.7 all-gather.1
  107.3 36.6 all-reduce.1
  151.3 14.7 all-gather.1
where the time goes:
time: 224 us
  matrix products  90.1 us (40%)
  waiting for transfers between devices  73.4 us (33%)
  other arithmetic  16.2 us (7%)
  between operations  13.7 us (6%)
  blocking collectives  10.7 us (5%)
  local copies, waits for them, and re-layouts  10.3 us (5%)
  starting transfers between devices  8.92 us (4%)
    psum x2, waiting for transfers between devices, micro(): x = lax.psum(xp, 'tp')  58 us
    dot_general x2, matrix products, micro(): jnp.dot(oh, emb, preferred_element_type=jnp.float32).astype(jnp.bfloat16)  33.9 us
    dot_general x1, matrix products, local(): de = jnp.dot(oh, dxs.reshape(-1, d), preferred_element_type=jnp.float32)  32.1 us
    all_gather x2, waiting for transfers between devices, micro(): dxa = lax.all_gather(dx, 'tp', axis=0, tiled=True)  15.3 us
    psum x1, blocking collectives, local(): dg = lax.psum(dg, 'tp')  10.7 us
    dot_general x2, matrix products, micro(): jnp.einsum('tf,df->td', dum, w, preferred_element_type=jnp.float32)  9.57 us
    dot_general x2, matrix products, micro(): u = jnp.dot(n, w, preferred_element_type=jnp.float32).astype(jnp.bfloat16)  9.41 us
    all_to_all x2, starting transfers between devices, micro(): recv = lax.all_to_all(pdn, 'tp', 0, 0, tiled=True).reshape(groups, tl, d)  8.88 us
  transfers between devices with their start and end apart: 6, of which 4 were waited for; matrix products, arithmetic and copies ran while one was open for 13% of the time, Pallas kernels for 0%

commit v1 on v0

v1 whole, which is shorter than its diff:
```python
import functools

import jax
import jax.numpy as jnp
from jax import lax
from jax.experimental import pallas as pl
from jax.experimental.pallas import tpu as pltpu
from jax.sharding import PartitionSpec as P

EPS = 1e-6
F32 = jnp.float32
BF16 = jnp.bfloat16
ANY = pl.BlockSpec(memory_space=pl.ANY)
VMEM = pl.BlockSpec(memory_space=pltpu.VMEM)
SMEM = pl.BlockSpec(memory_space=pltpu.SMEM)
VLIM = 60 * 1024 * 1024


def call(body, name, outs, ins, out_specs, scratch, flops, nbytes, aliases=None):
    return pl.pallas_call(
        body,
        name=name,
        out_shape=outs,
        in_specs=ins,
        out_specs=out_specs,
        scratch_shapes=scratch,
        input_output_aliases=aliases or {},
        cost_estimate=pl.CostEstimate(flops=flops, bytes_accessed=nbytes, transcendentals=0),
        compiler_params=pltpu.CompilerParams(vmem_limit_bytes=VLIM),
    )


def pdn_kernel(du_ref, w_ref, *refs):
    outs, dup = refs[:4], refs[4]
    r = lax.axis_index("tp")
    k, tl = du_ref.shape[0], du_ref.shape[1] // 4
    d = w_ref.shape[0]
    n = k * tl
    for j in range(4):
        q = r ^ j
        for m in range(k):
            dup[pl.ds(j * n + m * tl, tl), :] = du_ref[m, pl.ds(q * tl, tl), :]
    blk = 256

    def step(i, c):
        wt = w_ref[pl.ds(pl.multiple_of(i * blk, blk), blk), :]
        p = lax.dot_general(dup[...], wt, (((1,), (1,)), ((), ())), preferred_element_type=F32)
        for j in range(4):
            outs[j][:, pl.ds(pl.multiple_of(i * blk, blk), blk)] = p[j * n:(j + 1) * n].astype(BF16)
        return c

    lax.fori_loop(0, d // blk, step, 0)


def gather_kernel(loc_ref, nxt_ref, emb_ref, keep_ref, send_ref, last_ref, dup_ref, cnt_ref, buf, tmp, xf, lst, sem):
    t = loc_ref.shape[0]
    vl = emb_ref.shape[0]
    h = keep_ref.shape[0]

    def scan(i, c):
        n, nl, nd = c
        v = loc_ref[i]
        own = jnp.logical_and(v >= 0, v < vl)
        lst[n] = i
        has = nxt_ref[i] < t
        last_ref[nl] = i
        dup_ref[nd] = i
        o = own.astype(jnp.int32)
        hi = has.astype(jnp.int32)
        return n + o, nl + o * (1 - hi), nd + o * hi

    n, nl, nd = lax.fori_loop(0, t, scan, (0, 0, 0), unroll=4)
    cnt_ref[0] = nl
    cnt_ref[1] = nd
    lst[n] = 0
    for a in range(1, 8):
        lst[n + a] = 0

    def start(i, c):
        v = loc_ref[lst[i]]
        b = pl.multiple_of((v >> 3) << 3, 8)
        pltpu.make_async_copy(emb_ref.at[pl.ds(b, 8), :], buf.at[i], sem).start()
        return c

    lax.fori_loop(0, n, start, 0)
    xf[...] = jnp.zeros_like(xf)

    def wait(i, c):
        pltpu.make_async_copy(emb_ref.at[pl.ds(0, 8), :], buf.at[0], sem).wait()
        return c

    lax.fori_loop(0, n, wait, 0)

    def take(g, c):
        for a in range(8):
            i = g * 8 + a
            tmp[a] = buf[i].astype(F32)
        for a in range(8):
            i = g * 8 + a
            dst = jnp.where(i < n, lst[i], t)
            sub = loc_ref[lst[i]] & 7
            xf[pl.ds(dst, 1), :] = tmp[a, pl.ds(sub, 1), :]
        return c

    lax.fori_loop(0, (n + 7) // 8, take, 0)
    keep_ref[...] = xf[0:h, :].astype(BF16)
    send_ref[...] = xf[h:2 * h, :].astype(BF16)


def zero_kernel(tok_ref, de_ref, z, sem):
    rows = z.shape[0]
    z[...] = jnp.zeros_like(z)
    n = de_ref.shape[0] // rows
    for i in range(n):
        pltpu.make_async_copy(z, de_ref.at[pl.ds(i * rows, rows), :], sem).start()
    for i in range(n):
        pltpu.make_async_copy(z, de_ref.at[pl.ds(0, rows), :], sem).wait()


def dx_kernel(x_ref, p0, p1, p2, p3, dres_ref, g_ref, de_ref, dx_ref, dg_ref):
    x = x_ref[...].astype(F32)
    g = g_ref[...].astype(F32)
    rs = lax.rsqrt(jnp.mean(x * x, axis=-1, keepdims=True) + EPS)
    nh = x * rs
    dn = (p0[...].astype(F32) + p1[...].astype(F32)) + (p2[...].astype(F32) + p3[...].astype(F32))
    gdn = g * dn
    mean = jnp.mean(nh * gdn, axis=-1, keepdims=True)
    dxn = rs * (gdn - nh * mean)
    dx_ref[...] = (dres_ref[...].astype(F32) + dxn).astype(BF16)
    dg_ref[...] = jnp.sum(dn * nh, axis=0, keepdims=True)


def proj_kernel(xm_ref, xo_ref, g_ref, w_ref, du_ref, u_ref, dw_ref, n_ref, du2, ub, dwb, usem, wsem):
    r = lax.axis_index("tp")
    k, t = du_ref.shape[0], du_ref.shape[1]
    tl = t // 4
    d, fc = w_ref.shape
    g = g_ref[...].astype(F32)
    par = r & 1
    for side, ref in ((0, xm_ref), (1, xo_ref)):
        for c in range(2):
            q = 2 * c + (par ^ side)
            for m in range(k):
                x = ref[(c * k + m) * tl:(c * k + m + 1) * tl, :].astype(F32)
                rs = lax.rsqrt(jnp.mean(x * x, axis=-1, keepdims=True) + EPS)
                n_ref[pl.ds(pl.multiple_of(m * t + q * tl, tl), tl), :] = ((x * rs) * g).astype(BF16)
    for m in range(k):
        du2[m * t:(m + 1) * t, :] = du_ref[m]
    ublk = 256
    ucopies = []
    for i in range(fc // ublk):
        ub[:, i * ublk:(i + 1) * ublk] = jnp.dot(
            n_ref[...], w_ref[:, i * ublk:(i + 1) * ublk], preferred_element_type=F32).astype(BF16)
    for m in range(k):
        c = pltpu.make_async_copy(ub.at[pl.ds(m * t, t), :], u_ref.at[m], usem)
        c.start()
        ucopies.append(c)
    blk = 256
    nb = d // blk
    copies = []
    for i in range(nb):
        dwb[i] = lax.dot_general(n_ref[:, i * blk:(i + 1) * blk], du2[...], (((0,), (0,)), ((), ())),
                                 preferred_element_type=F32)
        c = pltpu.make_async_copy(dwb.at[i], dw_ref.at[pl.ds(i * blk, blk), :], wsem)
        c.start()
        copies.append(c)
    for c in ucopies + copies:
        c.wait()


def scatter_kernel(loc_ref, nxt_ref, last_ref, dup_ref, cnt_ref, d0, d1, de_in, de_ref, xf, sem):
    h = d0.shape[0]
    xf[0:h, :] = d0[...].astype(F32)
    xf[h:2 * h, :] = d1[...].astype(F32)
    nl = cnt_ref[0]

    def add(i, c):
        a = dup_ref[i]
        b = nxt_ref[a]
        xf[pl.ds(b, 1), :] = xf[pl.ds(b, 1), :] + xf[pl.ds(a, 1), :]
        return c

    lax.fori_loop(0, cnt_ref[1], add, 0)

    def put(i, c):
        a = last_ref[i]
        pltpu.make_async_copy(xf.at[pl.ds(a, 1), :], de_ref.at[pl.ds(loc_ref[a], 1), :], sem).start()
        return c

    lax.fori_loop(0, nl, put, 0)

    def wait(i, c):
        pltpu.make_async_copy(xf.at[pl.ds(0, 1), :], de_ref.at[pl.ds(0, 1), :], sem).wait()
        return c

    lax.fori_loop(0, nl, wait, 0)


def solution(mesh):
    groups = mesh.shape["tp"]
    sib = [(i, i ^ 1) for i in range(groups)]
    cross = [(i, i ^ 2) for i in range(groups)]
    diag = [(i, i ^ 3) for i in range(groups)]

    def local(ids, emb, g, w, du, dres):
        r = lax.axis_index("tp")
        par = r & 1
        k, t = ids.shape
        vl, d = emb.shape
        fc = w.shape[1]
        tl = t // groups
        n = k * tl
        h = 2 * n
        g2 = g.reshape(1, d)
        S = jax.ShapeDtypeStruct
        o = ids.reshape(k, 2, 2, tl).transpose(2, 1, 0, 3).reshape(2, h)
        o = jnp.where(par == 0, o, o[::-1]).reshape(-1)
        loc = o - r * vl
        pos = jnp.arange(2 * h, dtype=jnp.int32)
        nxt = jnp.min(jnp.where((o[:, None] == o[None, :]) & (pos[None, :] > pos[:, None]), pos[None, :], 2 * h), axis=1)

        p0, p1, p2, p3 = call(
            pdn_kernel, "pdn", [S((n, d), BF16)] * 4, [VMEM, VMEM], [VMEM] * 4,
            [pltpu.VMEM((4 * n, fc), BF16)], 2 * 4 * n * fc * d, 2 * d * fc + 8 * n * (fc + d))(du, w)
        q2 = lax.ppermute(p2, "tp", cross)
        q3 = lax.ppermute(p3, "tp", diag)
        q1 = lax.ppermute(p1, "tp", sib)

        keep, send, last, dup, cnt = call(
            gather_kernel, "gather",
            [S((h, d), BF16), S((h, d), BF16), S((2 * h,), jnp.int32), S((2 * h,), jnp.int32), S((8,), jnp.int32)],
            [SMEM, SMEM, ANY], [VMEM, VMEM, SMEM, SMEM, SMEM],
            [pltpu.VMEM((2 * h, 8, d), BF16), pltpu.VMEM((8, 8, d), F32), pltpu.VMEM((2 * h + 8, d), F32),
             pltpu.SMEM((2 * h + 8,), jnp.int32), pltpu.SemaphoreType.DMA],
            8 * h * d * 8, 16 * h * d)(loc, nxt, emb)
        xh = keep + lax.ppermute(send, "tp", sib)
        xm = xh + lax.ppermute(xh, "tp", cross)
        xo = lax.ppermute(xm, "tp", sib)

        de = call(zero_kernel, "zero", S((vl, d), F32), [SMEM], ANY,
                  [pltpu.VMEM((256, d), F32), pltpu.SemaphoreType.DMA], 10_000_000_000, 4 * vl * d)(cnt)

        xown = lax.dynamic_slice_in_dim(xm, (r >> 1) * n, n, 0)
        dx, dgp = call(dx_kernel, "dx", [S((n, d), BF16), S((1, d), F32)], [VMEM] * 7 + [ANY], [VMEM] * 2, [],
                       30 * n * d, 16 * n * d)(xown, p0, q1, q2, q3, dres.reshape(n, d), g2, de)
        dxc = lax.ppermute(dx, "tp", cross)
        dxm = jnp.where(r < 2, jnp.concatenate([dx, dxc]), jnp.concatenate([dxc, dx]))
        dxo = lax.ppermute(dxm, "tp", sib)
        dgp = dgp + lax.ppermute(dgp, "tp", sib)
        dgp = dgp + lax.ppermute(dgp, "tp", cross)

        u, dw = call(
            proj_kernel, "proj", [S((k, t, fc), BF16), S((d, fc), F32)], [VMEM] * 5, [ANY, ANY],
            [pltpu.VMEM((k * t, d), BF16), pltpu.VMEM((k * t, fc), BF16), pltpu.VMEM((k * t, fc), BF16),
             pltpu.VMEM((d // 256, 256, fc), F32), pltpu.SemaphoreType.DMA, pltpu.SemaphoreType.DMA],
            4 * k * t * d * fc, 6 * d * fc)(xm, xo, g2, w, du)

        de = call(scatter_kernel, "scatter", S((vl, d), F32), [SMEM] * 5 + [VMEM, VMEM, ANY], ANY,
                  [pltpu.VMEM((2 * h, d), F32), pltpu.SemaphoreType.DMA], 8 * h * d, 8 * h * d,
                  {7: 0})(loc, nxt, last, dup, cnt, dxm, dxo, de)
        return u, xown.reshape(k, tl, d), de, dw, dgp.reshape(d)

    return jax.shard_map(
        local,
        mesh=mesh,
        in_specs=(P("dp", None), P("tp", None), P(None), P(None, "tp"), P("dp", None, "tp"), P("dp", "tp", None)),
        out_specs=(P("dp", None, "tp"), P("dp", "tp", None), P(("dp", "tp"), None), P(None, ("dp", "tp")), P("dp")),
        check_vma=False,
    )
```

time: 224 us -> 117 us (0.52)
  matrix products: 90.1 us -> 0 us
  Pallas kernels: 0 us -> 64.1 us
  waiting for transfers between devices: 73.4 us -> 37 us
  between operations: 13.7 us -> 0.79 us
  other arithmetic: 16.2 us -> 5.47 us
  blocking collectives: 10.7 us -> 0 us
  local copies, waits for them, and re-layouts: 10.3 us -> 3.46 us
  starting transfers between devices: 8.92 us -> 6.16 us
    dot_general x8 -> x0, matrix products: 90.1 us -> none  [the longest x2 33.9 us: micro(): jnp.dot(oh, emb, preferred_element_type=jnp.float32).astype(jnp.bfloat16)]
    pallas_call x0 -> x6, Pallas kernels: none -> 64.1 us  [the longest x1 24.5 us: local(): call(zero_kernel, 'zero', S((vl, d), F32), [SMEM], ANY, [pltpu.VMEM((256,...]
    psum x2 -> x0, waiting for transfers between devices: 58 us -> none  [micro(): x = lax.psum(xp, 'tp')]
    ppermute x0 -> x10, waiting for transfers between devices: none -> 37 us  [the longest x1 14.4 us: local(): dxc = lax.ppermute(dx, 'tp', cross)]
    all_gather x2 -> x0, waiting for transfers between devices: 15.3 us -> none  [micro(): dxa = lax.all_gather(dx, 'tp', axis=0, tiled=True)]
    psum x1 -> x0, blocking collectives: 10.7 us -> none  [local(): dg = lax.psum(dg, 'tp')]
    all_to_all x2 -> x0, starting transfers between devices: 8.88 us -> none  [micro(): recv = lax.all_to_all(pdn, 'tp', 0, 0, tiled=True).reshape(groups, tl, d)]
    reduce_sum x6 -> x0, other arithmetic: 7.89 us -> none  [the longest x2 3.25 us: micro(): dn = jnp.sum(recv.astype(jnp.float32), axis=0)]
  transfers between devices with their start and end apart: 6 -> 10, of which waited for: 4 -> 6; matrix products, arithmetic and copies ran while one was open for 13% -> 3% of each run, Pallas kernels for 0% -> 38%
where the time goes in v1:
time: 117 us
  Pallas kernels  64.1 us (55%)
  waiting for transfers between devices  37 us (32%)
  starting transfers between devices  6.16 us (5%)
  other arithmetic  5.47 us (5%)
  local copies, waits for them, and re-layouts  3.46 us (3%)
    pallas_call x1, Pallas kernels, local(): call(zero_kernel, 'zero', S((vl, d), F32), [SMEM], ANY, [pltpu.VMEM((256,...  24.5 us
    ppermute x1, waiting for transfers between devices, local(): dxc = lax.ppermute(dx, 'tp', cross)  14.4 us
    pallas_call x1, Pallas kernels, local(): call(proj_kernel, 'proj', [S((k, t, fc), BF16), S((d, fc), F32)], [VMEM]...  11.1 us
    pallas_call x1, Pallas kernels, local(): call(gather_kernel, 'gather', [S((h, d), BF16), S((h, d), BF16), S((2 * h...  11.1 us
    ppermute x1, waiting for transfers between devices, local(): q3 = lax.ppermute(p3, 'tp', diag)  11 us
    pallas_call x1, Pallas kernels, local(): call(pdn_kernel, 'pdn', [S((n, d), BF16)] * 4, [VMEM, VMEM], [VMEM] * 4,...  8.33 us
    pallas_call x1, Pallas kernels, local(): call(scatter_kernel, 'scatter', S((vl, d), F32), [SMEM] * 5 + [VMEM, VMEM...  5.3 us
    ppermute x1, waiting for transfers between devices, local(): q2 = lax.ppermute(p2, 'tp', cross)  3.85 us
  transfers between devices with their start and end apart: 10, of which 6 were waited for; matrix products, arithmetic and copies ran while one was open for 3% of the time, Pallas kernels for 38%

profile of v1, /device:TPU:0, one launch (start us, length us, event | category | flops | bytes accessed | tf_op | source)
XLA Modules:
  0.0 116.9 jit_solution(12459651604560184764)
XLA Ops:
  0.6 0.8 reshape.33
  1.4 0.1 reshape.34
  1.5 0.1 rev.3
  1.6 0.9 select_reduce_fusion.nxt_ref
  2.5 0.6 broadcast_subtract_fusion.loc_ref
  3.1 11.1 %gather.1 = (bf16[256,2304]{1,0:T(8,128)(2,1)}, bf16[256,2304]{1,0:T(8,128)(2,1)}, s32[512]{0:T(512)}, s32[512]{0:T(512)}, s32[8]{0:T(128)}) custom-call(s32[512]{0:T(512)} %broadcast_subtract_fusion.loc_ref, s32[512]{0:T(512)} %select_reduce_fusion.nxt_ref, bf16[8192,2304]{1,0:T(8,128)(2,1)} %emb_ref.1), custom_call_target="tpu_custom_call" | custom-call | flops 37748736 | bytes 9437184 | tf_op jit(solution)/shard_map/gather/pallas_call | solution.py:229
  14.1 0.0 collective-permute-start
  14.2 2.8 %collective-permute-done = bf16[256,2304]{1,0:T(8,128)(2,1)S(1)} collective-permute-done((bf16[256,2304]{1,0:T(8,128)(2,1)}, bf16[256,2304]{1,0:T(8,128)(2,1)S(1)}, u32[]{:S(2)}, u32[]{:S(2)}) %collective-permute-start) | collective-permute-done | bytes 1179680 | tf_op jit(solution)/shard_map/ppermute | solution.py:236
  17.0 1.6 %add.15 = bf16[256,2304]{1,0:T(8,128)(2,1)S(1)} add(bf16[256,2304]{1,0:T(8,128)(2,1)} %get-tuple-element.18, bf16[256,2304]{1,0:T(8,128)(2,1)S(1)} %collective-permute-done) | non-fusion elementwise | flops 589824 | bytes 3538944 | tf_op jit(solution)/shard_map/add | solution.py:236
  18.6 1.1 collective-permute-start.1
  19.7 8.3 %pdn.1 = (bf16[128,2304]{1,0:T(8,128)(2,1)}, bf16[128,2304]{1,0:T(8,128)(2,1)}, bf16[128,2304]{1,0:T(8,128)(2,1)}, bf16[128,2304]{1,0:T(8,128)(2,1)}) custom-call(bf16[2,256,1024]{2,1,0:T(8,128)(2,1)} %du_ref.3, bf16[2304,1024]{1,0:T(8,128)(2,1)} %w_ref.3), custom_call_target="tpu_custom_call" | custom-call | flops 2415919104 | bytes 8126464 | tf_op jit(solution)/shard_map/pdn/pallas_call | solution.py:222
  28.0 0.0 collective-permute-start.3
  28.0 0.9 collective-permute-start.4
  28.9 0.9 collective-permute-start.5
  29.9 0.0 copy-start.4
  29.9 24.5 %zero.1.de_ref.de_in = f32[8192,2304]{1,0:T(8,128)} custom-call(s32[8]{0:T(128)} %get-tuple-element.23.tok_ref.cnt_ref), custom_call_target="tpu_custom_call" | custom-call | flops 10000000000 | bytes 75497472 | tf_op jit(solution)/shard_map/zero/pallas_call | solution.py:240
  54.4 0.0 copy-done.4
  54.4 0.6 reshape.36.g_ref
  55.0 0.0 collective-permute-done.1
  55.0 0.3 add.16.xm_ref
  55.3 0.0 copy-start.1
  55.3 0.9 constant_dynamic-slice_fusion.x_ref
  56.2 0.0 collective-permute-done.3.p1
  56.2 3.8 %collective-permute-done.4.p2 = bf16[128,2304]{1,0:T(8,128)(2,1)} collective-permute-done((bf16[128,2304]{1,0:T(8,128)(2,1)}, bf16[128,2304]{1,0:T(8,128)(2,1)}, u32[]{:S(2)}, u32[]{:S(2)}) %collective-permute-start.4) | collective-permute-done | bytes 589856 | tf_op jit(solution)/shard_map/ppermute | solution.py:225
  60.1 11.0 %collective-permute-done.5.p3 = bf16[128,2304]{1,0:T(8,128)(2,1)} collective-permute-done((bf16[128,2304]{1,0:T(8,128)(2,1)}, bf16[128,2304]{1,0:T(8,128)(2,1)}, u32[]{:S(2)}, u32[]{:S(2)}) %collective-permute-start.5) | collective-permute-done | bytes 589856 | tf_op jit(solution)/shard_map/ppermute | solution.py:226
  71.0 3.8 %dx.1 = (bf16[128,2304]{1,0:T(8,128)(2,1)}, f32[1,2304]{1,0:T(1,128)}) custom-call(bf16[128,2304]{1,0:T(8,128)(2,1)} %constant_dynamic-slice_fusion.x_ref, bf16[128,2304]{1,0:T(8,128)(2,1)} %get-tuple-element.24.p0, bf16[128,2304]{1,0:T(8,128)(2,1)} %collective-permute-done.3.p1, bf16[128,2304]{1,0:T(8,128)(2,1)} %collective-permute-done.4.p2, ...), custom_call_target="tpu_custom_call" | custom-call | flops 8847360 | bytes 4718592 | tf_op jit(solution)/shard_map/dx/pallas_call | solution.py:244
  74.8 1.1 collective-permute-start.6
  75.9 0.0 copy-done.1
  75.9 0.4 collective-permute-start.2
  76.3 0.0 copy-start.3
  76.3 14.4 %collective-permute-done.6 = bf16[128,2304]{1,0:T(8,128)(2,1)S(1)} collective-permute-done((bf16[128,2304]{1,0:T(8,128)(2,1)}, bf16[128,2304]{1,0:T(8,128)(2,1)S(1)}, u32[]{:S(2)}, u32[]{:S(2)}) %collective-permute-start.6) | collective-permute-done | bytes 589856 | tf_op jit(solution)/shard_map/ppermute | solution.py:246
  90.7 1.5 %maximum_select_fusion.d0 = bf16[256,2304]{1,0:T(8,128)(2,1)S(1)} fusion(bf16[128,2304]{1,0:T(8,128)(2,1)S(1)} %collective-permute-done.6, bf16[128,2304]{1,0:T(8,128)(2,1)} %get-tuple-element.28, pred[]{:T(512)S(6)} %lt.7), kind=kLoop, calls=%fused_computation | loop fusion | flops 5308416 | bytes 2359297 | tf_op jit(solution)/shard_map/jit(_where)/select_n | solution.py:247
  92.2 0.0 copy-start
  92.2 0.0 collective-permute-start.7
  92.2 0.0 copy-done.3
  92.2 0.5 collective-permute-start.8
  92.7 2.3 %collective-permute-done.8 = f32[1,2304]{1,0:T(1,128)S(1)} collective-permute-done((f32[1,2304]{1,0:T(1,128)S(1)}, f32[1,2304]{1,0:T(1,128)S(1)}, u32[]{:S(2)}, u32[]{:S(2)}) %collective-permute-start.8) | collective-permute-done | bytes 9248 | tf_op jit(solution)/shard_map/ppermute | solution.py:249
  95.1 1.1 collective-permute-start.9
  96.2 2.5 %collective-permute-done.9 = f32[1,2304]{1,0:T(1,128)S(1)} collective-permute-done((f32[1,2304]{1,0:T(1,128)S(1)}, f32[1,2304]{1,0:T(1,128)S(1)}, u32[]{:S(2)}, u32[]{:S(2)}) %collective-permute-start.9) | collective-permute-done | bytes 9248 | tf_op jit(solution)/shard_map/ppermute | solution.py:250
  98.8 0.6 add_reduce_fusion
  99.4 0.0 collective-permute-done.2.xo_ref
  99.4 11.1 %proj.1 = (bf16[2,256,1024]{2,1,0:T(8,128)(2,1)}, f32[2304,1024]{1,0:T(8,128)}) custom-call(bf16[256,2304]{1,0:T(8,128)(2,1)} %copy-done.1, bf16[256,2304]{1,0:T(8,128)(2,1)} %collective-permute-done.2.xo_ref, bf16[1,2304]{1,0:T(2,128)(2,1)} %reshape.36.g_ref, bf16[2304,1024]{1,0:T(8,128)(2,1)} %w_ref.3, bf16[2,256,1024]{2,1,0:T(8,128)(2,1)} %du_ref.3), custom_call_target="tpu_custom_call" | custom-call | flops 4831838208 | bytes 14155776 | tf_op jit(solution)/shard_map/proj/pallas_call | solution.py:252
  110.5 0.0 copy-done
  110.6 0.0 collective-permute-done.7.d1
  110.6 0.0 copy-start.2
  110.6 1.0 copy-done.2
  111.6 5.3 %scatter.1 = f32[8192,2304]{1,0:T(8,128)} custom-call(s32[512]{0:T(512)} %broadcast_subtract_fusion.loc_ref, s32[512]{0:T(512)} %select_reduce_fusion.nxt_ref, s32[512]{0:T(512)} %get-tuple-element.21.last_ref, s32[512]{0:T(512)} %get-tuple-element.22.dup_ref, s32[8]{0:T(128)} %get-tuple-element.23.tok_ref.cnt_ref, ...), custom_call_target="tpu_custom_call", output_to_operand_aliasing={{}: (7, {})} | custom-call | flops 4718592 | bytes 4718592 | tf_op jit(solution)/shard_map/scatter/pallas_call | solution.py:258
  (4 shorter events, 0.0 us)
Async XLA Ops:
  14.1 2.9 %collective-permute-start = (bf16[256,2304]{1,0:T(8,128)(2,1)}, bf16[256,2304]{1,0:T(8,128)(2,1)S(1)}, u32[]{:S(2)}, u32[]{:S(2)}) collective-permute-start(bf16[256,2304]{1,0:T(8,128)(2,1)} %get-tuple-element.19), channel_id=1, source_target_pairs={{0,1},{1,0},{2,3},{3,2},{4,5},{5,4},{6,7},{7,6}} | collective-permute-start | bytes 3538952 | tf_op jit(solution)/shard_map/ppermute | solution.py:236
  18.6 36.4 %collective-permute-start.1 = (bf16[256,2304]{1,0:T(8,128)(2,1)S(1)}, bf16[256,2304]{1,0:T(8,128)(2,1)S(1)}, u32[]{:S(2)}, u32[]{:S(2)}) collective-permute-start(bf16[256,2304]{1,0:T(8,128)(2,1)S(1)} %add.15), channel_id=1, source_target_pairs={{0,2},{1,3},{2,0},{3,1},{4,6},{5,7},{6,4},{7,5}} | collective-permute-start | bytes 3538952 | tf_op jit(solution)/shard_map/ppermute | solution.py:237
  28.0 28.2 %collective-permute-start.3 = (bf16[128,2304]{1,0:T(8,128)(2,1)}, bf16[128,2304]{1,0:T(8,128)(2,1)}, u32[]{:S(2)}, u32[]{:S(2)}) collective-permute-start(bf16[128,2304]{1,0:T(8,128)(2,1)} %get-tuple-element.25), channel_id=1, source_target_pairs={{0,1},{1,0},{2,3},{3,2},{4,5},{5,4},{6,7},{7,6}} | collective-permute-start | bytes 1769480 | tf_op jit(solution)/shard_map/ppermute | solution.py:227
  28.0 32.0 %collective-permute-start.4 = (bf16[128,2304]{1,0:T(8,128)(2,1)}, bf16[128,2304]{1,0:T(8,128)(2,1)}, u32[]{:S(2)}, u32[]{:S(2)}) collective-permute-start(bf16[128,2304]{1,0:T(8,128)(2,1)} %get-tuple-element.26), channel_id=1, source_target_pairs={{0,2},{1,3},{2,0},{3,1},{4,6},{5,7},{6,4},{7,5}} | collective-permute-start | bytes 1769480 | tf_op jit(solution)/shard_map/ppermute | solution.py:225
  28.9 42.1 %collective-permute-start.5 = (bf16[128,2304]{1,0:T(8,128)(2,1)}, bf16[128,2304]{1,0:T(8,128)(2,1)}, u32[]{:S(2)}, u32[]{:S(2)}) collective-permute-start(bf16[128,2304]{1,0:T(8,128)(2,1)} %get-tuple-element.27), channel_id=1, source_target_pairs={{0,3},{1,2},{2,1},{3,0},{4,7},{5,6},{6,5},{7,4}} | collective-permute-start | bytes 1769480 | tf_op jit(solution)/shard_map/ppermute | solution.py:226
  29.9 24.5 %copy-start.4 = (bf16[2304]{0:T(1024)(128)(2,1)S(1)}, bf16[2304]{0:T(1024)(128)(2,1)}, u32[]{:S(2)}) copy-start(bf16[2304]{0:T(1024)(128)(2,1)} %param.8) | copy-start | bytes 13828
  55.3 20.6 %copy-start.1 = (bf16[256,2304]{1,0:T(8,128)(2,1)}, bf16[256,2304]{1,0:T(8,128)(2,1)S(1)}, u32[]{:S(2)}) copy-start(bf16[256,2304]{1,0:T(8,128)(2,1)S(1)} %add.16.xm_ref) | copy-start | bytes 3538948
  74.8 15.9 %collective-permute-start.6 = (bf16[128,2304]{1,0:T(8,128)(2,1)}, bf16[128,2304]{1,0:T(8,128)(2,1)S(1)}, u32[]{:S(2)}, u32[]{:S(2)}) collective-permute-start(bf16[128,2304]{1,0:T(8,128)(2,1)} %get-tuple-element.28), channel_id=1, source_target_pairs={{0,2},{1,3},{2,0},{3,1},{4,6},{5,7},{6,4},{7,5}} | collective-permute-start | bytes 1769480 | tf_op jit(solution)/shard_map/ppermute | solution.py:246
  75.9 23.5 %collective-permute-start.2 = (bf16[256,2304]{1,0:T(8,128)(2,1)S(1)}, bf16[256,2304]{1,0:T(8,128)(2,1)}, u32[]{:S(2)}, u32[]{:S(2)}) collective-permute-start(bf16[256,2304]{1,0:T(8,128)(2,1)S(1)} %add.16.xm_ref), channel_id=1, source_target_pairs={{0,1},{1,0},{2,3},{3,2},{4,5},{5,4},{6,7},{7,6}} | collective-permute-start | bytes 3538952 | tf_op jit(solution)/shard_map/ppermute | solution.py:238
  76.3 16.0 %copy-start.3 = (f32[1,2304]{1,0:T(1,128)S(1)}, f32[1,2304]{1,0:T(1,128)}, u32[]{:S(2)}) copy-start(f32[1,2304]{1,0:T(1,128)} %get-tuple-element.30) | copy-start | bytes 27652
  92.2 18.4 %copy-start = (bf16[256,2304]{1,0:T(8,128)(2,1)}, bf16[256,2304]{1,0:T(8,128)(2,1)S(1)}, u32[]{:S(2)}) copy-start(bf16[256,2304]{1,0:T(8,128)(2,1)S(1)} %maximum_select_fusion.d0) | copy-start | bytes 3538948
  92.2 18.4 %collective-permute-start.7 = (bf16[256,2304]{1,0:T(8,128)(2,1)S(1)}, bf16[256,2304]{1,0:T(8,128)(2,1)S(1)}, u32[]{:S(2)}, u32[]{:S(2)}) collective-permute-start(bf16[256,2304]{1,0:T(8,128)(2,1)S(1)} %maximum_select_fusion.d0), channel_id=1, source_target_pairs={{0,1},{1,0},{2,3},{3,2},{4,5},{5,4},{6,7},{7,6}} | collective-permute-start | bytes 3538952 | tf_op jit(solution)/shard_map/ppermute | solution.py:248
  92.2 2.8 %collective-permute-start.8 = (f32[1,2304]{1,0:T(1,128)S(1)}, f32[1,2304]{1,0:T(1,128)S(1)}, u32[]{:S(2)}, u32[]{:S(2)}) collective-permute-start(f32[1,2304]{1,0:T(1,128)S(1)} %copy-done.3), channel_id=1, source_target_pairs={{0,1},{1,0},{2,3},{3,2},{4,5},{5,4},{6,7},{7,6}} | collective-permute-start | bytes 27656 | tf_op jit(solution)/shard_map/ppermute | solution.py:249
  95.1 3.7 %collective-permute-start.9 = (f32[1,2304]{1,0:T(1,128)S(1)}, f32[1,2304]{1,0:T(1,128)S(1)}, u32[]{:S(2)}, u32[]{:S(2)}) collective-permute-start(f32[1,2304]{1,0:T(1,128)S(1)} %add.18), channel_id=1, source_target_pairs={{0,2},{1,3},{2,0},{3,1},{4,6},{5,7},{6,4},{7,5}} | collective-permute-start | bytes 27656 | tf_op jit(solution)/shard_map/ppermute | solution.py:250
  110.6 1.0 copy-start.2

commit v2 on v1

v2 whole, which is shorter than its diff:
```python
import functools

import jax
import jax.numpy as jnp
from jax import lax
from jax.experimental import pallas as pl
from jax.experimental.pallas import tpu as pltpu
from jax.sharding import PartitionSpec as P


EPS = 1e-6
F32 = jnp.float32
BF16 = jnp.bfloat16
ANY = pl.BlockSpec(memory_space=pl.ANY)
VMEM = pl.BlockSpec(memory_space=pltpu.VMEM)
SMEM = pl.BlockSpec(memory_space=pltpu.SMEM)
VLIM = 60 * 1024 * 1024


def call(body, outs, ins, out_specs, scratch, flops, nbytes, aliases=None):
    return pl.pallas_call(
        body,
        out_shape=outs,
        in_specs=ins,
        out_specs=out_specs,
        scratch_shapes=scratch,
        input_output_aliases=aliases or {},
        cost_estimate=pl.CostEstimate(flops=flops, bytes_accessed=nbytes, transcendentals=0),
        compiler_params=pltpu.CompilerParams(vmem_limit_bytes=VLIM),
    )


def pdn_kernel(js, zrows, tok_ref, du_ref, w_ref, *refs):
    nj = len(js)
    outs = refs[:nj]
    refs = refs[nj:]
    if zrows:
        de_ref, z, zsem = refs[0], refs[-2], refs[-1]
        refs = refs[1:-2]
        z[...] = jnp.zeros_like(z)
        zero_start(z, de_ref, 0, zrows, zsem)
    else:
        for a in range(8):
            refs[0][a] = 0
        refs = refs[1:]
    dub, dup, wb, dsem, wsem = refs
    r = lax.axis_index("tp")
    k, tl = dub.shape[0], dub.shape[1] // 4
    d = wb.shape[0]
    n = k * tl
    blk = 256
    nb = d // blk
    dc = pltpu.make_async_copy(du_ref, dub, dsem)
    dc.start()
    for i in range(nb):
        pltpu.make_async_copy(w_ref.at[pl.ds(i * blk, blk), :], wb.at[pl.ds(i * blk, blk), :], wsem.at[i]).start()
    dc.wait()
    for a, j in enumerate(js):
        q = r ^ j
        for m in range(k):
            dup[pl.ds(a * n + m * tl, tl), :] = dub[m, pl.ds(q * tl, tl), :]
    for i in range(nb):
        pltpu.make_async_copy(w_ref.at[pl.ds(i * blk, blk), :], wb.at[pl.ds(i * blk, blk), :], wsem.at[i]).wait()
        p = lax.dot_general(dup[...], wb[i * blk:(i + 1) * blk, :], (((1,), (1,)), ((), ())), preferred_element_type=F32)
        for a in range(nj):
            outs[a][:, i * blk:(i + 1) * blk] = p[a * n:(a + 1) * n].astype(BF16)
    if zrows:
        zero_wait(z, de_ref, zrows, zsem)


def zero_start(z, de_ref, lo, rows, sem):
    step = z.shape[0]
    for i in range(rows // step):
        pltpu.make_async_copy(z, de_ref.at[pl.ds(lo + i * step, step), :], sem).start()


def zero_wait(z, de_ref, rows, sem):
    step = z.shape[0]
    for _ in range(rows // step):
        pltpu.make_async_copy(z, de_ref.at[pl.ds(0, step), :], sem).wait()


def zero_kernel(tok_ref, de_in, de_ref, z, sem):
    z[...] = jnp.zeros_like(z)
    half = de_ref.shape[0] // 2
    zero_start(z, de_ref, half, half, sem)
    zero_wait(z, de_ref, half, sem)


def gather_kernel(loc_ref, nxt_ref, emb_ref, k0, s0, k1, s1, last_ref, dup_ref, cnt_ref, buf, tmp, xf, lst, sem):
    t = loc_ref.shape[0]
    vl = emb_ref.shape[0]
    h = k0.shape[0]

    def scan(i, c):
        n, nl, nd = c
        v = loc_ref[i]
        own = jnp.logical_and(v >= 0, v < vl)
        lst[n] = i
        has = nxt_ref[i] < t
        last_ref[nl] = i
        dup_ref[nd] = i
        o = own.astype(jnp.int32)
        hi = has.astype(jnp.int32)
        return n + o, nl + o * (1 - hi), nd + o * hi

    n, nl, nd = lax.fori_loop(0, t, scan, (0, 0, 0), unroll=4)
    cnt_ref[0] = nl
    cnt_ref[1] = nd

    def first(i, c):
        return c + (last_ref[i] < t // 2).astype(jnp.int32)

    cnt_ref[2] = lax.fori_loop(0, nl, first, 0)
    lst[n] = 0
    for a in range(1, 8):
        lst[n + a] = 0

    def start(i, c):
        v = loc_ref[lst[i]]
        b = pl.multiple_of((v >> 3) << 3, 8)
        pltpu.make_async_copy(emb_ref.at[pl.ds(b, 8), :], buf.at[i], sem).start()
        return c

    lax.fori_loop(0, n, start, 0)
    xf[...] = jnp.zeros_like(xf)

    def wait(i, c):
        pltpu.make_async_copy(emb_ref.at[pl.ds(0, 8), :], buf.at[0], sem).wait()
        return c

    lax.fori_loop(0, n, wait, 0)

    def take(g, c):
        for a in range(8):
            i = g * 8 + a
            tmp[a] = buf[i].astype(F32)
        for a in range(8):
            i = g * 8 + a
            dst = jnp.where(i < n, lst[i], t)
            sub = loc_ref[lst[i]] & 7
            xf[pl.ds(dst, 1), :] = tmp[a, pl.ds(sub, 1), :]
        return c

    lax.fori_loop(0, (n + 7) // 8, take, 0)
    for a, ref in enumerate((k0, s0, k1, s1)):
        ref[...] = xf[a * h:(a + 1) * h, :].astype(BF16)


def dx_kernel(m, xh_ref, z_ref, p0, p1, p2, p3, dres_ref, g_ref, tok_ref, *refs):
    if m == 1:
        xm0_ref, dg0_ref, xm_ref, dx_ref, dg_ref, x_ref = refs
    else:
        xm_ref, dx_ref, dg_ref = refs
    tl = dx_ref.shape[0]
    chip = lax.axis_index("tp") >> 1
    mine = pl.ds(pl.multiple_of(chip * tl, tl), tl)
    xm_ref[...] = xh_ref[...] + z_ref[...]
    if m == 1:
        x_ref[0] = xm0_ref[mine, :]
        x_ref[1] = xm_ref[mine, :]
    x = xm_ref[mine, :].astype(F32)
    g = g_ref[...].astype(F32)
    rs = lax.rsqrt(jnp.mean(x * x, axis=-1, keepdims=True) + EPS)
    nh = x * rs
    s = slice(m * tl, (m + 1) * tl)
    dn = (p0[s, :].astype(F32) + p1[s, :].astype(F32)) + (p2[s, :].astype(F32) + p3[s, :].astype(F32))
    gdn = g * dn
    mean = jnp.mean(nh * gdn, axis=-1, keepdims=True)
    dxn = rs * (gdn - nh * mean)
    dx_ref[...] = (dres_ref[m].astype(F32) + dxn).astype(BF16)
    dg = jnp.sum(dn * nh, axis=0, keepdims=True)
    dg_ref[...] = dg if m == 0 else dg + dg0_ref[...]


def fill_n(xm_ref, xo_ref, g_ref, n_ref, off):
    r = lax.axis_index("tp")
    par = r & 1
    tl = xm_ref.shape[0] // 2
    g = g_ref[...].astype(F32)
    for side, ref in ((0, xm_ref), (1, xo_ref)):
        for c in range(2):
            q = 2 * c + (par ^ side)
            x = ref[c * tl:(c + 1) * tl, :].astype(F32)
            rs = lax.rsqrt(jnp.mean(x * x, axis=-1, keepdims=True) + EPS)
            n_ref[pl.ds(pl.multiple_of(off + q * tl, tl), tl), :] = ((x * rs) * g).astype(BF16)


def umat(n_ref, w_ref, u_ref, lo):
    t = u_ref.shape[0]
    blk = 256
    for i in range(u_ref.shape[1] // blk):
        u_ref[:, i * blk:(i + 1) * blk] = jnp.dot(
            n_ref[lo:lo + t, :], w_ref[:, i * blk:(i + 1) * blk], preferred_element_type=F32).astype(BF16)


def u_kernel(xm_ref, xo_ref, g_ref, w_ref, tok_ref, u_ref, n_ref):
    fill_n(xm_ref, xo_ref, g_ref, n_ref, 0)
    umat(n_ref, w_ref, u_ref, 0)


def proj_kernel(n0_ref, xm_ref, xo_ref, g_ref, w_ref, du_ref, u0_ref, tok_ref, u_ref, dw_ref, n_ref, du2, ub, dwb, usem, wsem):
    k, t = du_ref.shape[0], du_ref.shape[1]
    d, _ = w_ref.shape
    copies = [pltpu.make_async_copy(u0_ref, u_ref.at[0], usem.at[0])]
    copies[0].start()
    n_ref[0:t, :] = n0_ref[...]
    fill_n(xm_ref, xo_ref, g_ref, n_ref, t)
    for m in range(k):
        du2[m * t:(m + 1) * t, :] = du_ref[m]
    umat(n_ref, w_ref, ub, t)
    c = pltpu.make_async_copy(ub, u_ref.at[1], usem.at[1])
    c.start()
    copies.append(c)
    blk = 256
    for i in range(d // blk):
        dwb[i] = lax.dot_general(n_ref[:, i * blk:(i + 1) * blk], du2[...], (((0,), (0,)), ((), ())),
                                 preferred_element_type=F32)
        c = pltpu.make_async_copy(dwb.at[i], dw_ref.at[pl.ds(i * blk, blk), :], wsem)
        c.start()
        copies.append(c)
    for c in copies:
        c.wait()


def scatter_kernel(m, loc_ref, nxt_ref, last_ref, dup_ref, cnt_ref, *refs):
    nd = 4 * (m + 1)
    ds, de_ref, xf, sem = refs[:nd], refs[-3], refs[-2], refs[-1]
    tl = ds[0].shape[0]
    chip = lax.axis_index("tp") >> 1
    for a, ref in enumerate(ds):
        c = chip if a % 2 == 0 else 1 - chip
        xf[pl.ds(pl.multiple_of((a // 2) * 2 * tl + c * tl, tl), tl), :] = ref[...].astype(F32)

    def add(i, c):
        a = dup_ref[i]
        b = nxt_ref[a]

        @pl.when(b < 4 * tl * (m + 1))
        def _():
            xf[pl.ds(b, 1), :] = xf[pl.ds(b, 1), :] + xf[pl.ds(a, 1), :]

        return c

    lax.fori_loop(0, cnt_ref[1], add, 0)

    def put(i, c):
        a = last_ref[i]
        pltpu.make_async_copy(xf.at[pl.ds(a, 1), :], de_ref.at[pl.ds(loc_ref[a], 1), :], sem).start()
        return c

    def wait(i, c):
        pltpu.make_async_copy(xf.at[pl.ds(0, 1), :], de_ref.at[pl.ds(0, 1), :], sem).wait()
        return c

    n0, n1 = (0, cnt_ref[2]) if m == 0 else (cnt_ref[2], cnt_ref[0])
    lax.fori_loop(n0, n1, put, 0)
    lax.fori_loop(n0, n1, wait, 0)


def solution(mesh):
    groups = mesh.shape["tp"]
    sib = [(i, i ^ 1) for i in range(groups)]
    cross = [(i, i ^ 2) for i in range(groups)]
    diag = [(i, i ^ 3) for i in range(groups)]

    def local(ids, emb, g, w, du, dres):
        r = lax.axis_index("tp")
        par = r & 1
        k, t = ids.shape
        vl, d = emb.shape
        fc = w.shape[1]
        tl = t // groups
        n = k * tl
        h = 2 * n
        g2 = g.reshape(1, d)
        S = jax.ShapeDtypeStruct
        D = pltpu.SemaphoreType.DMA

        def perm(v, p):
            return lax.ppermute(v, "tp", p)

        def pdn(js, zrows, tok):
            de = [S((vl, d), F32)] if zrows else [S((8,), jnp.int32)]
            return call(
                functools.partial(pdn_kernel, js, zrows), [S((n, d), BF16)] * len(js) + de,
                [ANY] * 3, [VMEM] * len(js) + [ANY if zrows else SMEM],
                [pltpu.VMEM((k, t, fc), BF16), pltpu.VMEM((len(js) * n, fc), BF16), pltpu.VMEM((d, fc), BF16), D, D((d // 256,))]
                + ([pltpu.VMEM((256, d), F32), D] if zrows else []),
                2 * len(js) * n * fc * d + (5_000_000_000 if zrows else 0), 2 * d * fc + 4 * n * (fc + d))(tok, du, w)

        p2, p3, zi = pdn((2, 3), 0, g2)
        q2 = perm(p2, cross)
        q3 = perm(p3, diag)

        o = ids.reshape(k, 2, 2, tl).transpose(0, 2, 1, 3) + zi[0]
        o = jnp.where(par == 0, o, o[:, ::-1]).reshape(-1)
        loc = o - r * vl
        pos = jnp.arange(2 * h, dtype=jnp.int32)
        nxt = jnp.min(jnp.where((o[:, None] == o[None, :]) & (pos[None, :] > pos[:, None]), pos[None, :], 2 * h), axis=1)
        k0, s0, k1, s1, last, dup, cnt = call(
            gather_kernel,
            [S((n, d), BF16)] * 4 + [S((2 * h,), jnp.int32), S((2 * h,), jnp.int32), S((8,), jnp.int32)],
            [SMEM, SMEM, ANY], [VMEM] * 4 + [SMEM] * 3,
            [pltpu.VMEM((2 * h, 8, d), BF16), pltpu.VMEM((8, 8, d), F32), pltpu.VMEM((2 * h + 8, d), F32),
             pltpu.SMEM((2 * h + 8,), jnp.int32), D],
            8 * h * d * 8, 16 * h * d)(loc, nxt, emb)
        y0 = perm(s0, sib)
        y1 = perm(s1, sib)
        p0, p1, de = pdn((0, 1), vl // 2, cnt)
        q1 = perm(p1, sib)
        xh0 = k0 + y0
        xh1 = k1 + y1
        z0 = perm(xh0, cross)
        z1 = perm(xh1, cross)
        de = call(zero_kernel, S((vl, d), F32), [ANY, ANY], ANY,
                  [pltpu.VMEM((256, d), F32), D], 5_000_000_000, 2 * vl * d, {1: 0})(xh1, de)

        def dxk(m, xh, z, tok, more):
            outs = [S((n, d), BF16), S((tl, d), BF16), S((1, d), F32)] + ([S((k, tl, d), BF16)] if m else [])
            return call(functools.partial(dx_kernel, m), outs, [VMEM] * 8 + [ANY] + [VMEM] * len(more),
                        [VMEM] * len(outs), [], 30 * n * d, 16 * n * d)(xh, z, p0, q1, q2, q3, dres, g2, tok, *more)

        xm0, dx0, dg0 = dxk(0, xh0, z0, de, ())
        c0 = perm(dx0, cross)
        xo0 = perm(xm0, sib)
        a0 = perm(dx0, sib)
        u0, n0 = call(u_kernel, [S((t, fc), BF16), S((t, d), BF16)], [VMEM] * 4 + [ANY], [VMEM] * 2, [],
                      2 * t * d * fc, 2 * d * fc)(xm0, xo0, g2, w, dg0)
        xm1, dx1, dg, x = dxk(1, xh1, z1, n0, (xm0, dg0))
        c1 = perm(dx1, cross)
        xo1 = perm(xm1, sib)
        a1 = perm(dx1, sib)
        b0 = perm(c0, sib)
        b1 = perm(c1, sib)
        dgs = dg + perm(dg, sib)
        dgs = dgs + perm(dgs, cross)

        u, dw = call(
            proj_kernel, [S((k, t, fc), BF16), S((d, fc), F32)], [VMEM] * 7 + [ANY], [ANY, ANY],
            [pltpu.VMEM((k * t, d), BF16), pltpu.VMEM((k * t, fc), BF16), pltpu.VMEM((t, fc), BF16),
             pltpu.VMEM((d // 256, 256, fc), F32), D((2,)), D],
            3 * k * t * d * fc, 6 * d * fc)(n0, xm1, xo1, g2, w, du, u0, dg)

        def scatter(m, parts, de, tok):
            return call(functools.partial(scatter_kernel, m), S((vl, d), F32),
                        [SMEM] * 5 + [VMEM] * len(parts) + [ANY, ANY], ANY,
                        [pltpu.VMEM((h * (m + 1), d), F32), D], 8 * h * d, 8 * h * d,
                        {6 + len(parts): 0})(loc, nxt, last, dup, cnt, *parts, tok, de)

        de = scatter(0, (dx0, c0, a0, b0), de, dw)
        de = scatter(1, (dx0, c0, a0, b0, dx1, c1, a1, b1), de, dw)
        return u, x, de, dw, dgs.reshape(d)

    return jax.shard_map(
        local,
        mesh=mesh,
        in_specs=(P("dp", None), P("tp", None), P(None), P(None, "tp"), P("dp", None, "tp"), P("dp", "tp", None)),
        out_specs=(P("dp", None, "tp"), P("dp", "tp", None), P(("dp", "tp"), None), P(None, ("dp", "tp")), P("dp")),
        check_vma=False,
    )
```

time: 117 us -> 143 us (1.22)
  Pallas kernels: 64.1 us -> 74.9 us
  waiting for transfers between devices: 37 us -> 41.3 us
  starting transfers between devices: 6.16 us -> 10.3 us
  local copies, waits for them, and re-layouts: 3.46 us -> 7.6 us
    pallas_call x6 -> x10, Pallas kernels: 64.1 us -> 74.9 us  [the longest x2 22.3 us: pdn(): call(functools.partial(pdn_kernel, js, zrows), [S((n, d), BF16)] * len(js...]
    unnamed x11 -> x30, local copies, waits for them, and re-layouts: 1.03 us -> 5.45 us
    ppermute x10 -> x17, waiting for transfers between devices: 37 us -> 41.3 us  [perm(): return lax.ppermute(v, 'tp', p)]
    ppermute x10 -> x17, starting transfers between devices: 6.16 us -> 10.3 us  [perm(): return lax.ppermute(v, 'tp', p)]
    add x4, other arithmetic: 2.46 us -> 4.55 us  [the longest x1 2.02 us: local(): xh1 = k1 + y1]
  transfers between devices with their start and end apart: 10 -> 17, of which waited for: 6 -> 7; matrix products, arithmetic and copies ran while one was open for 3% -> 3% of each run, Pallas kernels for 38% -> 32%
where the time goes in v2:
time: 143 us; the launch traced here: 142 us
  Pallas kernels  74.9 us (52%)
  waiting for transfers between devices  41.3 us (29%)
  starting transfers between devices  10.3 us (7%)
  local copies, waits for them, and re-layouts  7.6 us (5%)
  other arithmetic  6.69 us (5%)
    ppermute x17, waiting for transfers between devices, perm(): return lax.ppermute(v, 'tp', p)  41.3 us
    pallas_call x2, Pallas kernels, pdn(): call(functools.partial(pdn_kernel, js, zrows), [S((n, d), BF16)] * len(js...  22.3 us
    pallas_call x1, Pallas kernels, local(): call(zero_kernel, S((vl, d), F32), [ANY, ANY], ANY, [pltpu.VMEM((256, d),...  12.3 us
    pallas_call x1, Pallas kernels, local(): call(gather_kernel, [S((n, d), BF16)] * 4 + [S((2 * h,), jnp.int32), S((2...  11.6 us
    ppermute x17, starting transfers between devices, perm(): return lax.ppermute(v, 'tp', p)  10.3 us
    pallas_call x1, Pallas kernels, local(): call(proj_kernel, [S((k, t, fc), BF16), S((d, fc), F32)], [VMEM] * 7 + [A...  9.43 us
    pallas_call x2, Pallas kernels, dxk(): call(functools.partial(dx_kernel, m), outs, [VMEM] * 8 + [ANY] + [VMEM] *...  7.32 us
    pallas_call x2, Pallas kernels, scatter(): call(functools.partial(scatter_kernel, m), S((vl, d), F32), [SMEM] * 5 +...  6.49 us
  transfers between devices with their start and end apart: 17, of which 7 were waited for; matrix products, arithmetic and copies ran while one was open for 3% of the time, Pallas kernels for 32%

profile of v2, /device:TPU:0, one launch (start us, length us, event | category | flops | bytes accessed | tf_op | source)
XLA Modules:
  0.0 141.8 jit_solution(797164968681458948)
XLA Ops:
  0.6 0.8 reshape.24
  1.4 1.3 reshape.25.tok_ref.g_ref
  2.7 7.6 %shard_map.101 = (bf16[128,2304]{1,0:T(8,128)(2,1)}, bf16[128,2304]{1,0:T(8,128)(2,1)}, s32[8]{0:T(128)}) custom-call(bf16[1,2304]{1,0:T(2,128)(2,1)} %reshape.25.tok_ref.g_ref, bf16[2,256,1024]{2,1,0:T(8,128)(2,1)} %du_ref.5, bf16[2304,1024]{1,0:T(8,128)(2,1)} %w_ref.7), custom_call_target="tpu_custom_call" | custom-call | flops 1207959552 | bytes 6422528 | tf_op jit(solution)/shard_map/pallas_call | solution.py:285
  10.3 0.7 add_select_fusion
  10.9 0.1 reshape.26
  11.0 0.9 select_reduce_fusion.nxt_ref
  11.9 0.6 broadcast_subtract_fusion.loc_ref
  12.5 11.6 %shard_map.102 = (bf16[128,2304]{1,0:T(8,128)(2,1)}, bf16[128,2304]{1,0:T(8,128)(2,1)}, bf16[128,2304]{1,0:T(8,128)(2,1)}, bf16[128,2304]{1,0:T(8,128)(2,1)}, s32[512]{0:T(512)}, /*index=5*/s32[512]{0:T(512)}, s32[8]{0:T(128)}) custom-call(s32[512]{0:T(512)} %broadcast_subtract_fusion.loc_ref, s32[512]{0:T(512)} %select_reduce_fusion.nxt_ref, ...), custom_call_target="tpu_custom_call" | custom-call | flops 37748736 | bytes 9437184 | tf_op jit(solution)/shard_map/pallas_call | solution.py:301
  24.1 0.3 collective-permute-start
  24.4 0.2 collective-permute-start.5
  24.7 14.7 %shard_map.103 = (bf16[128,2304]{1,0:T(8,128)(2,1)}, bf16[128,2304]{1,0:T(8,128)(2,1)}, f32[8192,2304]{1,0:T(8,128)}) custom-call(s32[8]{0:T(128)} %get-tuple-element.32.tok_ref.cnt_ref, bf16[2,256,1024]{2,1,0:T(8,128)(2,1)} %du_ref.5, bf16[2304,1024]{1,0:T(8,128)(2,1)} %w_ref.7), custom_call_target="tpu_custom_call" | custom-call | flops 6207959552 | bytes 6422528 | tf_op jit(solution)/shard_map/pallas_call | solution.py:285
  39.4 0.3 collective-permute-start.2
  39.7 1.5 %collective-permute-start.3 = (bf16[128,2304]{1,0:T(8,128)(2,1)}, bf16[128,2304]{1,0:T(8,128)(2,1)S(1)}, u32[]{:S(2)}, u32[]{:S(2)}) collective-permute-start(bf16[128,2304]{1,0:T(8,128)(2,1)} %get-tuple-element.35), channel_id=1, source_target_pairs={{0,2},{1,3},{2,0},{3,1},{4,6},{5,7},{6,4},{7,5}} | collective-permute-start | bytes 1769480 | tf_op jit(solution)/shard_map/ppermute | solution.py:281
  41.2 0.1 collective-permute-start.4
  41.3 0.0 collective-permute-done
  41.3 1.2 add.21.xh_ref
  42.5 0.0 copy-start.1
  42.5 1.8 %collective-permute-start.1 = (bf16[128,2304]{1,0:T(8,128)(2,1)S(1)}, bf16[128,2304]{1,0:T(8,128)(2,1)S(1)}, u32[]{:S(2)}, u32[]{:S(2)}) collective-permute-start(bf16[128,2304]{1,0:T(8,128)(2,1)S(1)} %add.21.xh_ref), channel_id=1, source_target_pairs={{0,2},{1,3},{2,0},{3,1},{4,6},{5,7},{6,4},{7,5}} | collective-permute-start | bytes 1769480 | tf_op jit(solution)/shard_map/ppermute | solution.py:281
  44.2 0.0 collective-permute-done.5
  44.2 2.0 %add.22.tok_ref.xh_ref = bf16[128,2304]{1,0:T(8,128)(2,1)} add(bf16[128,2304]{1,0:T(8,128)(2,1)} %get-tuple-element.37, bf16[128,2304]{1,0:T(8,128)(2,1)S(1)} %collective-permute-done.5) | non-fusion elementwise | flops 294912 | bytes 1769472 | tf_op jit(solution)/shard_map/add | solution.py:313
  46.3 12.3 %shard_map.104.tok_ref.refs_5_ = f32[8192,2304]{1,0:T(8,128)} custom-call(bf16[128,2304]{1,0:T(8,128)(2,1)} %add.22.tok_ref.xh_ref, f32[8192,2304]{1,0:T(8,128)} %get-tuple-element.39.de_in), custom_call_target="tpu_custom_call", output_to_operand_aliasing={{}: (1, {})} | custom-call | flops 5000000000 | bytes 37748736 | tf_op jit(solution)/shard_map/pallas_call | solution.py:316
  58.6 0.0 copy-done.1
  58.6 0.0 collective-permute-done.2.p1
  58.7 0.0 collective-permute-done.3.p2
  58.7 9.2 %collective-permute-done.4.p3 = bf16[128,2304]{1,0:T(8,128)(2,1)S(1)} collective-permute-done((bf16[128,2304]{1,0:T(8,128)(2,1)}, bf16[128,2304]{1,0:T(8,128)(2,1)S(1)}, u32[]{:S(2)}, u32[]{:S(2)}) %collective-permute-start.4) | collective-permute-done | bytes 589856 | tf_op jit(solution)/shard_map/ppermute | solution.py:281
  67.9 12.8 %collective-permute-done.1.z_ref = bf16[128,2304]{1,0:T(8,128)(2,1)S(1)} collective-permute-done((bf16[128,2304]{1,0:T(8,128)(2,1)S(1)}, bf16[128,2304]{1,0:T(8,128)(2,1)S(1)}, u32[]{:S(2)}, u32[]{:S(2)}) %collective-permute-start.1) | collective-permute-done | bytes 589856 | tf_op jit(solution)/shard_map/ppermute | solution.py:281
  80.6 0.8 copy-done.8
  81.4 3.5 %shard_map.105 = (bf16[128,2304]{1,0:T(8,128)(2,1)}, bf16[64,2304]{1,0:T(8,128)(2,1)}, f32[1,2304]{1,0:T(1,128)}) custom-call(bf16[128,2304]{1,0:T(8,128)(2,1)} %copy-done.1, bf16[128,2304]{1,0:T(8,128)(2,1)} %copy-done.8, bf16[128,2304]{1,0:T(8,128)(2,1)} %get-tuple-element.33.p0, bf16[128,2304]{1,0:T(8,128)(2,1)} %copy-done.2, ...), custom_call_target="tpu_custom_call" | custom-call | flops 8847360 | bytes 4718592 | tf_op jit(solution)/shard_map/pallas_call | solution.py:321
  84.9 0.0 collective-permute-start.6
  84.9 1.8 %collective-permute-start.7 = (bf16[128,2304]{1,0:T(8,128)(2,1)S(1)}, bf16[128,2304]{1,0:T(8,128)(2,1)S(1)}, u32[]{:S(2)}, u32[]{:S(2)}) collective-permute-start(bf16[128,2304]{1,0:T(8,128)(2,1)S(1)} %copy-done), channel_id=1, source_target_pairs={{0,2},{1,3},{2,0},{3,1},{4,6},{5,7},{6,4},{7,5}} | collective-permute-start | bytes 1769480 | tf_op jit(solution)/shard_map/ppermute | solution.py:281
  86.7 0.4 collective-permute-done.6.xo_ref
  87.2 0.8 copy-done.10
  88.0 5.4 %shard_map.106 = (bf16[256,1024]{1,0:T(8,128)(2,1)}, bf16[256,2304]{1,0:T(8,128)(2,1)}) custom-call(bf16[128,2304]{1,0:T(8,128)(2,1)} %get-tuple-element.40.xm_ref.refs_0_, bf16[128,2304]{1,0:T(8,128)(2,1)} %copy-done.10, bf16[1,2304]{1,0:T(2,128)(2,1)} %reshape.25.tok_ref.g_ref, bf16[2304,1024]{1,0:T(8,128)(2,1)} %w_ref.7, ...), custom_call_target="tpu_custom_call" | custom-call | flops 1207959552 | bytes 4718592 | tf_op jit(solution)/shard_map/pallas_call | solution.py:328
  93.4 7.3 %collective-permute-done.7.z_ref = bf16[128,2304]{1,0:T(8,128)(2,1)S(1)} collective-permute-done((bf16[128,2304]{1,0:T(8,128)(2,1)S(1)}, bf16[128,2304]{1,0:T(8,128)(2,1)S(1)}, u32[]{:S(2)}, u32[]{:S(2)}) %collective-permute-start.7) | collective-permute-done | bytes 589856 | tf_op jit(solution)/shard_map/ppermute | solution.py:281
  100.7 0.8 copy-done.9
  101.5 3.8 %shard_map.107 = (bf16[128,2304]{1,0:T(8,128)(2,1)}, bf16[64,2304]{1,0:T(8,128)(2,1)}, f32[1,2304]{1,0:T(1,128)}, bf16[2,64,2304]{2,1,0:T(8,128)(2,1)}) custom-call(bf16[128,2304]{1,0:T(8,128)(2,1)} %add.22.tok_ref.xh_ref, bf16[128,2304]{1,0:T(8,128)(2,1)} %copy-done.9, bf16[128,2304]{1,0:T(8,128)(2,1)} %get-tuple-element.33.p0, ...), custom_call_target="tpu_custom_call" | custom-call | flops 8847360 | bytes 4718592 | tf_op jit(solution)/shard_map/pallas_call | solution.py:321
  105.3 0.0 collective-permute-start.8
  105.3 1.8 %collective-permute-start.9 = (bf16[64,2304]{1,0:T(8,128)(2,1)}, bf16[64,2304]{1,0:T(8,128)(2,1)S(1)}, u32[]{:S(2)}, u32[]{:S(2)}) collective-permute-start(bf16[64,2304]{1,0:T(8,128)(2,1)} %get-tuple-element.50.refs_0_), channel_id=1, source_target_pairs={{0,2},{1,3},{2,0},{3,1},{4,6},{5,7},{6,4},{7,5}} | collective-permute-start | bytes 884744 | tf_op jit(solution)/shard_map/ppermute | solution.py:281
  107.1 0.3 collective-permute-start.12
  107.4 0.0 collective-permute-start.15
  107.4 1.4 collective-permute-done.15
  108.8 0.7 add.23
  109.5 1.8 %collective-permute-start.16 = (f32[1,2304]{1,0:T(1,128)S(1)}, f32[1,2304]{1,0:T(1,128)S(1)}, u32[]{:S(2)}, u32[]{:S(2)}) collective-permute-start(f32[1,2304]{1,0:T(1,128)S(1)} %add.23), channel_id=1, source_target_pairs={{0,2},{1,3},{2,0},{3,1},{4,6},{5,7},{6,4},{7,5}} | collective-permute-start | bytes 27656 | tf_op jit(solution)/shard_map/ppermute | solution.py:281
  111.3 0.0 collective-permute-start.10
  111.3 4.2 %collective-permute-done.9.refs_1_ = bf16[64,2304]{1,0:T(8,128)(2,1)S(1)} collective-permute-done((bf16[64,2304]{1,0:T(8,128)(2,1)}, bf16[64,2304]{1,0:T(8,128)(2,1)S(1)}, u32[]{:S(2)}, u32[]{:S(2)}) %collective-permute-start.9) | collective-permute-done | bytes 294944 | tf_op jit(solution)/shard_map/ppermute | solution.py:281
  115.5 0.0 collective-permute-start.11
  115.5 6.0 %collective-permute-done.16 = f32[1,2304]{1,0:T(1,128)S(1)} collective-permute-done((f32[1,2304]{1,0:T(1,128)S(1)}, f32[1,2304]{1,0:T(1,128)S(1)}, u32[]{:S(2)}, u32[]{:S(2)}) %collective-permute-start.16) | collective-permute-done | bytes 9248 | tf_op jit(solution)/shard_map/ppermute | solution.py:281
  121.5 0.0 collective-permute-start.13
  121.5 0.6 add_reduce_fusion
  122.1 0.0 collective-permute-done.12.refs_5_
  122.1 0.5 collective-permute-start.14
  122.6 0.0 collective-permute-done.8.xo_ref
  122.6 0.8 copy-done.14
  123.5 9.4 %shard_map.108 = (bf16[2,256,1024]{2,1,0:T(8,128)(2,1)}, f32[2304,1024]{1,0:T(8,128)}) custom-call(bf16[256,2304]{1,0:T(8,128)(2,1)} %get-tuple-element.42.tok_ref.n0_ref, bf16[128,2304]{1,0:T(8,128)(2,1)} %get-tuple-element.43.xm_ref, bf16[128,2304]{1,0:T(8,128)(2,1)} %copy-done.14, bf16[1,2304]{1,0:T(2,128)(2,1)} %reshape.25.tok_ref.g_ref, ...), custom_call_target="tpu_custom_call" | custom-call | flops 3623878656 | bytes 14155776 | tf_op jit(solution)/shard_map/pallas_call | solution.py:339
  132.9 0.0 collective-permute-done.10.refs_2_
  132.9 0.0 collective-permute-done.11.refs_3_
  132.9 0.7 copy-done.6
  133.6 0.1 copy-done.7
  133.7 3.0 %shard_map.109.refs_9_ = f32[8192,2304]{1,0:T(8,128)} custom-call(s32[512]{0:T(512)} %broadcast_subtract_fusion.loc_ref, s32[512]{0:T(512)} %select_reduce_fusion.nxt_ref, s32[512]{0:T(512)} %get-tuple-element.48.last_ref, s32[512]{0:T(512)} %get-tuple-element.49.dup_ref, s32[8]{0:T(128)} %get-tuple-element.32.tok_ref.cnt_ref, ...), custom_call_target="tpu_custom_call", output_to_operand_aliasing={{}: (10, {})} | custom-call | flops 4718592 | bytes 4718592 | tf_op jit(solution)/shard_map/pallas_call | solution.py:346
  136.7 0.0 collective-permute-done.13.refs_6_
  136.7 0.0 collective-permute-done.14.refs_7_
  136.7 0.7 copy-done.12
  137.4 0.7 copy-done.13
  138.1 3.5 %shard_map.110 = f32[8192,2304]{1,0:T(8,128)} custom-call(s32[512]{0:T(512)} %broadcast_subtract_fusion.loc_ref, s32[512]{0:T(512)} %select_reduce_fusion.nxt_ref, s32[512]{0:T(512)} %get-tuple-element.48.last_ref, s32[512]{0:T(512)} %get-tuple-element.49.dup_ref, s32[8]{0:T(128)} %get-tuple-element.32.tok_ref.cnt_ref, ...), custom_call_target="tpu_custom_call", output_to_operand_aliasing={{}: (14, {})} | custom-call | flops 4718592 | bytes 4718592 | tf_op jit(solution)/shard_map/pallas_call | solution.py:346
  (21 shorter events, 0.0 us)
Async XLA Ops:
  24.1 17.1 %collective-permute-start = (bf16[128,2304]{1,0:T(8,128)(2,1)}, bf16[128,2304]{1,0:T(8,128)(2,1)S(1)}, u32[]{:S(2)}, u32[]{:S(2)}) collective-permute-start(bf16[128,2304]{1,0:T(8,128)(2,1)} %get-tuple-element.31), channel_id=1, source_target_pairs={{0,1},{1,0},{2,3},{3,2},{4,5},{5,4},{6,7},{7,6}} | collective-permute-start | bytes 1769480 | tf_op jit(solution)/shard_map/ppermute | solution.py:281
  24.4 19.8 %collective-permute-start.5 = (bf16[128,2304]{1,0:T(8,128)(2,1)}, bf16[128,2304]{1,0:T(8,128)(2,1)S(1)}, u32[]{:S(2)}, u32[]{:S(2)}) collective-permute-start(bf16[128,2304]{1,0:T(8,128)(2,1)} %get-tuple-element.38), channel_id=1, source_target_pairs={{0,1},{1,0},{2,3},{3,2},{4,5},{5,4},{6,7},{7,6}} | collective-permute-start | bytes 1769480 | tf_op jit(solution)/shard_map/ppermute | solution.py:281
  39.4 19.3 %collective-permute-start.2 = (bf16[128,2304]{1,0:T(8,128)(2,1)}, bf16[128,2304]{1,0:T(8,128)(2,1)S(1)}, u32[]{:S(2)}, u32[]{:S(2)}) collective-permute-start(bf16[128,2304]{1,0:T(8,128)(2,1)} %get-tuple-element.34), channel_id=1, source_target_pairs={{0,1},{1,0},{2,3},{3,2},{4,5},{5,4},{6,7},{7,6}} | collective-permute-start | bytes 1769480 | tf_op jit(solution)/shard_map/ppermute | solution.py:281
  39.7 19.0 %collective-permute-start.3 = (bf16[128,2304]{1,0:T(8,128)(2,1)}, bf16[128,2304]{1,0:T(8,128)(2,1)S(1)}, u32[]{:S(2)}, u32[]{:S(2)}) collective-permute-start(bf16[128,2304]{1,0:T(8,128)(2,1)} %get-tuple-element.35), channel_id=1, source_target_pairs={{0,2},{1,3},{2,0},{3,1},{4,6},{5,7},{6,4},{7,5}} | collective-permute-start | bytes 1769480 | tf_op jit(solution)/shard_map/ppermute | solution.py:281
  41.2 26.7 %collective-permute-start.4 = (bf16[128,2304]{1,0:T(8,128)(2,1)}, bf16[128,2304]{1,0:T(8,128)(2,1)S(1)}, u32[]{:S(2)}, u32[]{:S(2)}) collective-permute-start(bf16[128,2304]{1,0:T(8,128)(2,1)} %get-tuple-element.36), channel_id=1, source_target_pairs={{0,3},{1,2},{2,1},{3,0},{4,7},{5,6},{6,5},{7,4}} | collective-permute-start | bytes 1769480 | tf_op jit(solution)/shard_map/ppermute | solution.py:281
  42.5 16.1 %copy-start.1 = (bf16[128,2304]{1,0:T(8,128)(2,1)}, bf16[128,2304]{1,0:T(8,128)(2,1)S(1)}, u32[]{:S(2)}) copy-start(bf16[128,2304]{1,0:T(8,128)(2,1)S(1)} %add.21.xh_ref) | copy-start | bytes 1769476
  42.5 38.2 %collective-permute-start.1 = (bf16[128,2304]{1,0:T(8,128)(2,1)S(1)}, bf16[128,2304]{1,0:T(8,128)(2,1)S(1)}, u32[]{:S(2)}, u32[]{:S(2)}) collective-permute-start(bf16[128,2304]{1,0:T(8,128)(2,1)S(1)} %add.21.xh_ref), channel_id=1, source_target_pairs={{0,2},{1,3},{2,0},{3,1},{4,6},{5,7},{6,4},{7,5}} | collective-permute-start | bytes 1769480 | tf_op jit(solution)/shard_map/ppermute | solution.py:281
  58.6 26.3 %copy-start = (bf16[128,2304]{1,0:T(8,128)(2,1)S(1)}, bf16[128,2304]{1,0:T(8,128)(2,1)}, u32[]{:S(2)}) copy-start(bf16[128,2304]{1,0:T(8,128)(2,1)} %add.22.tok_ref.xh_ref) | copy-start | bytes 1769476
  58.6 22.0 %copy-start.2 = (bf16[128,2304]{1,0:T(8,128)(2,1)}, bf16[128,2304]{1,0:T(8,128)(2,1)S(1)}, u32[]{:S(2)}) copy-start(bf16[128,2304]{1,0:T(8,128)(2,1)S(1)} %collective-permute-done.2.p1) | copy-start | bytes 1769476
  58.7 22.0 %copy-start.3 = (bf16[128,2304]{1,0:T(8,128)(2,1)}, bf16[128,2304]{1,0:T(8,128)(2,1)S(1)}, u32[]{:S(2)}) copy-start(bf16[128,2304]{1,0:T(8,128)(2,1)S(1)} %collective-permute-done.3.p2) | copy-start | bytes 1769476
  67.8 12.8 %copy-start.4 = (bf16[128,2304]{1,0:T(8,128)(2,1)}, bf16[128,2304]{1,0:T(8,128)(2,1)S(1)}, u32[]{:S(2)}) copy-start(bf16[128,2304]{1,0:T(8,128)(2,1)S(1)} %collective-permute-done.4.p3) | copy-start | bytes 1769476
  80.6 0.8 copy-start.8
  84.9 2.2 %collective-permute-start.6 = (bf16[128,2304]{1,0:T(8,128)(2,1)}, bf16[128,2304]{1,0:T(8,128)(2,1)S(1)}, u32[]{:S(2)}, u32[]{:S(2)}) collective-permute-start(bf16[128,2304]{1,0:T(8,128)(2,1)} %get-tuple-element.40.xm_ref.refs_0_), channel_id=1, source_target_pairs={{0,1},{1,0},{2,3},{3,2},{4,5},{5,4},{6,7},{7,6}} | collective-permute-start | bytes 1769480 | tf_op jit(solution)/shard_map/ppermute | solution.py:281
  84.9 15.7 %collective-permute-start.7 = (bf16[128,2304]{1,0:T(8,128)(2,1)S(1)}, bf16[128,2304]{1,0:T(8,128)(2,1)S(1)}, u32[]{:S(2)}, u32[]{:S(2)}) collective-permute-start(bf16[128,2304]{1,0:T(8,128)(2,1)S(1)} %copy-done), channel_id=1, source_target_pairs={{0,2},{1,3},{2,0},{3,1},{4,6},{5,7},{6,4},{7,5}} | collective-permute-start | bytes 1769480 | tf_op jit(solution)/shard_map/ppermute | solution.py:281
  87.2 0.8 copy-start.10
  100.7 0.8 copy-start.9
  105.3 17.3 %collective-permute-start.8 = (bf16[128,2304]{1,0:T(8,128)(2,1)}, bf16[128,2304]{1,0:T(8,128)(2,1)S(1)}, u32[]{:S(2)}, u32[]{:S(2)}) collective-permute-start(bf16[128,2304]{1,0:T(8,128)(2,1)} %get-tuple-element.43.xm_ref), channel_id=1, source_target_pairs={{0,1},{1,0},{2,3},{3,2},{4,5},{5,4},{6,7},{7,6}} | collective-permute-start | bytes 1769480 | tf_op jit(solution)/shard_map/ppermute | solution.py:281
  105.3 10.1 %collective-permute-start.9 = (bf16[64,2304]{1,0:T(8,128)(2,1)}, bf16[64,2304]{1,0:T(8,128)(2,1)S(1)}, u32[]{:S(2)}, u32[]{:S(2)}) collective-permute-start(bf16[64,2304]{1,0:T(8,128)(2,1)} %get-tuple-element.50.refs_0_), channel_id=1, source_target_pairs={{0,2},{1,3},{2,0},{3,1},{4,6},{5,7},{6,4},{7,5}} | collective-permute-start | bytes 884744 | tf_op jit(solution)/shard_map/ppermute | solution.py:281
  107.1 15.0 %collective-permute-start.12 = (bf16[64,2304]{1,0:T(8,128)(2,1)}, bf16[64,2304]{1,0:T(8,128)(2,1)S(1)}, u32[]{:S(2)}, u32[]{:S(2)}) collective-permute-start(bf16[64,2304]{1,0:T(8,128)(2,1)} %get-tuple-element.51.refs_4_), channel_id=1, source_target_pairs={{0,2},{1,3},{2,0},{3,1},{4,6},{5,7},{6,4},{7,5}} | collective-permute-start | bytes 884744 | tf_op jit(solution)/shard_map/ppermute | solution.py:281
  107.4 1.4 collective-permute-start.15
  109.5 12.0 %collective-permute-start.16 = (f32[1,2304]{1,0:T(1,128)S(1)}, f32[1,2304]{1,0:T(1,128)S(1)}, u32[]{:S(2)}, u32[]{:S(2)}) collective-permute-start(f32[1,2304]{1,0:T(1,128)S(1)} %add.23), channel_id=1, source_target_pairs={{0,2},{1,3},{2,0},{3,1},{4,6},{5,7},{6,4},{7,5}} | collective-permute-start | bytes 27656 | tf_op jit(solution)/shard_map/ppermute | solution.py:281
  111.3 21.6 %collective-permute-start.10 = (bf16[64,2304]{1,0:T(8,128)(2,1)}, bf16[64,2304]{1,0:T(8,128)(2,1)S(1)}, u32[]{:S(2)}, u32[]{:S(2)}) collective-permute-start(bf16[64,2304]{1,0:T(8,128)(2,1)} %get-tuple-element.50.refs_0_), channel_id=1, source_target_pairs={{0,1},{1,0},{2,3},{3,2},{4,5},{5,4},{6,7},{7,6}} | collective-permute-start | bytes 884744 | tf_op jit(solution)/shard_map/ppermute | solution.py:281
  115.5 17.5 %copy-start.5 = (bf16[64,2304]{1,0:T(8,128)(2,1)}, bf16[64,2304]{1,0:T(8,128)(2,1)S(1)}, u32[]{:S(2)}) copy-start(bf16[64,2304]{1,0:T(8,128)(2,1)S(1)} %collective-permute-done.9.refs_1_) | copy-start | bytes 884740
  115.5 17.5 %collective-permute-start.11 = (bf16[64,2304]{1,0:T(8,128)(2,1)S(1)}, bf16[64,2304]{1,0:T(8,128)(2,1)S(1)}, u32[]{:S(2)}, u32[]{:S(2)}) collective-permute-start(bf16[64,2304]{1,0:T(8,128)(2,1)S(1)} %collective-permute-done.9.refs_1_), channel_id=1, source_target_pairs={{0,1},{1,0},{2,3},{3,2},{4,5},{5,4},{6,7},{7,6}} | collective-permute-start | bytes 884744 | tf_op jit(solution)/shard_map/ppermute | solution.py:281
  121.5 15.2 %collective-permute-start.13 = (bf16[64,2304]{1,0:T(8,128)(2,1)}, bf16[64,2304]{1,0:T(8,128)(2,1)S(1)}, u32[]{:S(2)}, u32[]{:S(2)}) collective-permute-start(bf16[64,2304]{1,0:T(8,128)(2,1)} %get-tuple-element.51.refs_4_), channel_id=1, source_target_pairs={{0,1},{1,0},{2,3},{3,2},{4,5},{5,4},{6,7},{7,6}} | collective-permute-start | bytes 884744 | tf_op jit(solution)/shard_map/ppermute | solution.py:281
  122.1 14.6 %copy-start.11 = (bf16[64,2304]{1,0:T(8,128)(2,1)}, bf16[64,2304]{1,0:T(8,128)(2,1)S(1)}, u32[]{:S(2)}) copy-start(bf16[64,2304]{1,0:T(8,128)(2,1)S(1)} %collective-permute-done.12.refs_5_) | copy-start | bytes 884740
  122.1 14.6 %collective-permute-start.14 = (bf16[64,2304]{1,0:T(8,128)(2,1)S(1)}, bf16[64,2304]{1,0:T(8,128)(2,1)S(1)}, u32[]{:S(2)}, u32[]{:S(2)}) collective-permute-start(bf16[64,2304]{1,0:T(8,128)(2,1)S(1)} %collective-permute-done.12.refs_5_), channel_id=1, source_target_pairs={{0,1},{1,0},{2,3},{3,2},{4,5},{5,4},{6,7},{7,6}} | collective-permute-start | bytes 884744 | tf_op jit(solution)/shard_map/ppermute | solution.py:281
  122.6 0.8 copy-start.14
  132.9 0.7 copy-start.6
  132.9 0.8 copy-start.7
  136.7 0.7 copy-start.12
  137.4 0.7 copy-start.13

commit v3 on v2

--- a/solution.py
+++ b/solution.py
@@ -30,20 +30,12 @@
     )
 
 
-def pdn_kernel(js, zrows, tok_ref, du_ref, w_ref, *refs):
+def pdn_kernel(js, du_ref, w_ref, *refs):
     nj = len(js)
     outs = refs[:nj]
-    refs = refs[nj:]
-    if zrows:
-        de_ref, z, zsem = refs[0], refs[-2], refs[-1]
-        refs = refs[1:-2]
-        z[...] = jnp.zeros_like(z)
-        zero_start(z, de_ref, 0, zrows, zsem)
-    else:
-        for a in range(8):
-            refs[0][a] = 0
-        refs = refs[1:]
-    dub, dup, wb, dsem, wsem = refs
+    flag_ref, dub, dup, wb, dsem, wsem = refs[nj:]
+    for a in range(8):
+        flag_ref[a] = 0
     r = lax.axis_index("tp")
     k, tl = dub.shape[0], dub.shape[1] // 4
     d = wb.shape[0]
@@ -64,8 +56,6 @@
         p = lax.dot_general(dup[...], wb[i * blk:(i + 1) * blk, :], (((1,), (1,)), ((), ())), preferred_element_type=F32)
         for a in range(nj):
             outs[a][:, i * blk:(i + 1) * blk] = p[a * n:(a + 1) * n].astype(BF16)
-    if zrows:
-        zero_wait(z, de_ref, zrows, zsem)
 
 
 def zero_start(z, de_ref, lo, rows, sem):
@@ -87,7 +77,7 @@
     zero_wait(z, de_ref, half, sem)
 
 
-def gather_kernel(loc_ref, nxt_ref, emb_ref, k0, s0, k1, s1, last_ref, dup_ref, cnt_ref, buf, tmp, xf, lst, sem):
+def gather_kernel(loc_ref, nxt_ref, emb_ref, k0, s0, k1, s1, last_ref, dup_ref, cnt_ref, de_ref, buf, tmp, xf, lst, z, sem, zsem):
     t = loc_ref.shape[0]
     vl = emb_ref.shape[0]
     h = k0.shape[0]
@@ -123,6 +113,8 @@
         return c
 
     lax.fori_loop(0, n, start, 0)
+    z[...] = jnp.zeros_like(z)
+    zero_start(z, de_ref, 0, vl // 2, zsem)
     xf[...] = jnp.zeros_like(xf)
 
     def wait(i, c):
@@ -145,6 +137,7 @@
     lax.fori_loop(0, (n + 7) // 8, take, 0)
     for a, ref in enumerate((k0, s0, k1, s1)):
         ref[...] = xf[a * h:(a + 1) * h, :].astype(BF16)
+    zero_wait(z, de_ref, vl // 2, zsem)
 
 
 def dx_kernel(m, xh_ref, z_ref, p0, p1, p2, p3, dres_ref, g_ref, tok_ref, *refs):
@@ -280,35 +273,29 @@
         def perm(v, p):
             return lax.ppermute(v, "tp", p)
 
-        def pdn(js, zrows, tok):
-            de = [S((vl, d), F32)] if zrows else [S((8,), jnp.int32)]
-            return call(
-                functools.partial(pdn_kernel, js, zrows), [S((n, d), BF16)] * len(js) + de,
-                [ANY] * 3, [VMEM] * len(js) + [ANY if zrows else SMEM],
-                [pltpu.VMEM((k, t, fc), BF16), pltpu.VMEM((len(js) * n, fc), BF16), pltpu.VMEM((d, fc), BF16), D, D((d // 256,))]
-                + ([pltpu.VMEM((256, d), F32), D] if zrows else []),
-                2 * len(js) * n * fc * d + (5_000_000_000 if zrows else 0), 2 * d * fc + 4 * n * (fc + d))(tok, du, w)
-
-        p2, p3, zi = pdn((2, 3), 0, g2)
+        p2, p3, p1, p0, zi = call(
+            functools.partial(pdn_kernel, (2, 3, 1, 0)), [S((n, d), BF16)] * 4 + [S((8,), jnp.int32)],
+            [ANY] * 2, [VMEM] * 4 + [SMEM],
+            [pltpu.VMEM((k, t, fc), BF16), pltpu.VMEM((4 * n, fc), BF16), pltpu.VMEM((d, fc), BF16), D, D((d // 256,))],
+            8 * n * fc * d, 2 * d * fc + 8 * n * (fc + d))(du, w)
         q2 = perm(p2, cross)
         q3 = perm(p3, diag)
+        q1 = perm(p1, sib)
 
         o = ids.reshape(k, 2, 2, tl).transpose(0, 2, 1, 3) + zi[0]
         o = jnp.where(par == 0, o, o[:, ::-1]).reshape(-1)
         loc = o - r * vl
         pos = jnp.arange(2 * h, dtype=jnp.int32)
         nxt = jnp.min(jnp.where((o[:, None] == o[None, :]) & (pos[None, :] > pos[:, None]), pos[None, :], 2 * h), axis=1)
-        k0, s0, k1, s1, last, dup, cnt = call(
+        k0, s0, k1, s1, last, dup, cnt, de = call(
             gather_kernel,
-            [S((n, d), BF16)] * 4 + [S((2 * h,), jnp.int32), S((2 * h,), jnp.int32), S((8,), jnp.int32)],
-            [SMEM, SMEM, ANY], [VMEM] * 4 + [SMEM] * 3,
+            [S((n, d), BF16)] * 4 + [S((2 * h,), jnp.int32), S((2 * h,), jnp.int32), S((8,), jnp.int32), S((vl, d), F32)],
+            [SMEM, SMEM, ANY], [VMEM] * 4 + [SMEM] * 3 + [ANY],
             [pltpu.VMEM((2 * h, 8, d), BF16), pltpu.VMEM((8, 8, d), F32), pltpu.VMEM((2 * h + 8, d), F32),
-             pltpu.SMEM((2 * h + 8,), jnp.int32), D],
-            8 * h * d * 8, 16 * h * d)(loc, nxt, emb)
+             pltpu.SMEM((2 * h + 8,), jnp.int32), pltpu.VMEM((256, d), F32), D, D],
+            5_000_000_000, 16 * h * d)(loc, nxt, emb)
         y0 = perm(s0, sib)
         y1 = perm(s1, sib)
-        p0, p1, de = pdn((0, 1), vl // 2, cnt)
-        q1 = perm(p1, sib)
         xh0 = k0 + y0
         xh1 = k1 + y1
         z0 = perm(xh0, cross)

time: 143 us -> 140 us (0.979)
  Pallas kernels: 74.9 us -> 73.2 us
    pallas_call x2 -> x1, Pallas kernels: 22.3 us -> 10.2 us  [local(): call(functools.partial(pdn_kernel, (2, 3, 1, 0)), [S((n, d), BF16)] * 4 +...]
    pallas_call x1, Pallas kernels: 11.6 us -> 21.9 us  [local(): call(gather_kernel, [S((n, d), BF16)] * 4 + [S((2 * h,), jnp.int32), S((2...]
  transfers between devices with their start and end apart: 17 -> 17, of which waited for: 7 -> 7; matrix products, arithmetic and copies ran while one was open for 3% -> 4% of each run, Pallas kernels for 32% -> 22%
where the time goes in v3:
time: 140 us; the launch traced here: 139 us
  Pallas kernels  73.2 us (52%)
  waiting for transfers between devices  40.1 us (29%)
  starting transfers between devices  10.5 us (8%)
  local copies, waits for them, and re-layouts  7.64 us (5%)
  other arithmetic  6.65 us (5%)
    ppermute x17, waiting for transfers between devices, perm(): return lax.ppermute(v, 'tp', p)  40.1 us
    pallas_call x1, Pallas kernels, local(): call(gather_kernel, [S((n, d), BF16)] * 4 + [S((2 * h,), jnp.int32), S((2...  21.9 us
    pallas_call x1, Pallas kernels, local(): call(zero_kernel, S((vl, d), F32), [ANY, ANY], ANY, [pltpu.VMEM((256, d),...  12.3 us
    ppermute x17, starting transfers between devices, perm(): return lax.ppermute(v, 'tp', p)  10.5 us
    pallas_call x1, Pallas kernels, local(): call(functools.partial(pdn_kernel, (2, 3, 1, 0)), [S((n, d), BF16)] * 4 +...  10.2 us
    pallas_call x1, Pallas kernels, local(): call(proj_kernel, [S((k, t, fc), BF16), S((d, fc), F32)], [VMEM] * 7 + [A...  9.43 us
    pallas_call x2, Pallas kernels, dxk(): call(functools.partial(dx_kernel, m), outs, [VMEM] * 8 + [ANY] + [VMEM] *...  7.33 us
    pallas_call x2, Pallas kernels, scatter(): call(functools.partial(scatter_kernel, m), S((vl, d), F32), [SMEM] * 5 +...  6.49 us
  transfers between devices with their start and end apart: 17, of which 7 were waited for; matrix products, arithmetic and copies ran while one was open for 4% of the time, Pallas kernels for 22%

profile of v3, /device:TPU:0, one launch (start us, length us, event | category | flops | bytes accessed | tf_op | source)
XLA Modules:
  0.0 139.0 jit_solution(18024916347971450019)
XLA Ops:
  0.6 0.8 reshape.24
  1.4 10.2 %shard_map.101 = (bf16[128,2304]{1,0:T(8,128)(2,1)}, bf16[128,2304]{1,0:T(8,128)(2,1)}, bf16[128,2304]{1,0:T(8,128)(2,1)}, bf16[128,2304]{1,0:T(8,128)(2,1)}, s32[8]{0:T(128)}) custom-call(bf16[2,256,1024]{2,1,0:T(8,128)(2,1)} %du_ref.3, bf16[2304,1024]{1,0:T(8,128)(2,1)} %w_ref.5), custom_call_target="tpu_custom_call" | custom-call | flops 2415919104 | bytes 8126464 | tf_op jit(solution)/shard_map/pallas_call | solution.py:276
  11.7 0.7 add_select_fusion
  12.3 0.1 reshape.25
  12.4 0.9 select_reduce_fusion.nxt_ref
  13.3 0.5 broadcast_subtract_fusion.loc_ref
  13.8 21.9 %shard_map.102 = (bf16[128,2304]{1,0:T(8,128)(2,1)}, bf16[128,2304]{1,0:T(8,128)(2,1)}, bf16[128,2304]{1,0:T(8,128)(2,1)}, bf16[128,2304]{1,0:T(8,128)(2,1)}, s3...) custom-call(s32[512]{0:T(512)} %broadcast_subtract_fusion.loc_ref, s32[512]{0:T(512)} %select_reduce_fusion.nxt_ref, ...), custom_call_target="tpu_custom_call" | custom-call | flops 5000000000 | bytes 9437184 | tf_op jit(solution)/shard_map/pallas_call | solution.py:290
  35.8 0.6 collective-permute-start
  36.3 0.0 collective-permute-start.5
  36.4 0.5 collective-permute-start.2
  36.9 1.5 %collective-permute-start.3 = (bf16[128,2304]{1,0:T(8,128)(2,1)}, bf16[128,2304]{1,0:T(8,128)(2,1)S(1)}, u32[]{:S(2)}, u32[]{:S(2)}) collective-permute-start(bf16[128,2304]{1,0:T(8,128)(2,1)} %get-tuple-element.34), channel_id=1, source_target_pairs={{0,2},{1,3},{2,0},{3,1},{4,6},{5,7},{6,4},{7,5}} | collective-permute-start | bytes 1769480 | tf_op jit(solution)/shard_map/ppermute | solution.py:274
  38.3 0.1 collective-permute-start.4
  38.4 0.0 collective-permute-done
  38.4 1.2 add.21.xh_ref
  39.6 0.0 copy-start.1
  39.6 1.8 %collective-permute-start.1 = (bf16[128,2304]{1,0:T(8,128)(2,1)S(1)}, bf16[128,2304]{1,0:T(8,128)(2,1)S(1)}, u32[]{:S(2)}, u32[]{:S(2)}) collective-permute-start(bf16[128,2304]{1,0:T(8,128)(2,1)S(1)} %add.21.xh_ref), channel_id=1, source_target_pairs={{0,2},{1,3},{2,0},{3,1},{4,6},{5,7},{6,4},{7,5}} | collective-permute-start | bytes 1769480 | tf_op jit(solution)/shard_map/ppermute | solution.py:274
  41.4 1.3 reshape.26.g_ref
  42.7 0.0 collective-permute-done.5
  42.7 2.0 %add.22.tok_ref.xh_ref = bf16[128,2304]{1,0:T(8,128)(2,1)} add(bf16[128,2304]{1,0:T(8,128)(2,1)} %get-tuple-element.36, bf16[128,2304]{1,0:T(8,128)(2,1)S(1)} %collective-permute-done.5) | non-fusion elementwise | flops 294912 | bytes 1769472 | tf_op jit(solution)/shard_map/add | solution.py:300
  44.7 12.3 %shard_map.103.tok_ref.refs_5_ = f32[8192,2304]{1,0:T(8,128)} custom-call(bf16[128,2304]{1,0:T(8,128)(2,1)} %add.22.tok_ref.xh_ref, f32[8192,2304]{1,0:T(8,128)} %get-tuple-element.38.de_in), custom_call_target="tpu_custom_call", output_to_operand_aliasing={{}: (1, {})} | custom-call | flops 5000000000 | bytes 37748736 | tf_op jit(solution)/shard_map/pallas_call | solution.py:303
  57.1 0.0 collective-permute-done.2.p1
  57.1 0.0 copy-start.2
  57.1 0.0 collective-permute-done.3.p2
  57.1 7.9 %collective-permute-done.4.p3 = bf16[128,2304]{1,0:T(8,128)(2,1)S(1)} collective-permute-done((bf16[128,2304]{1,0:T(8,128)(2,1)}, bf16[128,2304]{1,0:T(8,128)(2,1)S(1)}, u32[]{:S(2)}, u32[]{:S(2)}) %collective-permute-start.4) | collective-permute-done | bytes 589856 | tf_op jit(solution)/shard_map/ppermute | solution.py:274
  65.0 12.8 %collective-permute-done.1.z_ref = bf16[128,2304]{1,0:T(8,128)(2,1)S(1)} collective-permute-done((bf16[128,2304]{1,0:T(8,128)(2,1)S(1)}, bf16[128,2304]{1,0:T(8,128)(2,1)S(1)}, u32[]{:S(2)}, u32[]{:S(2)}) %collective-permute-start.1) | collective-permute-done | bytes 589856 | tf_op jit(solution)/shard_map/ppermute | solution.py:274
  77.8 0.8 copy-done.8
  78.6 3.5 %shard_map.104 = (bf16[128,2304]{1,0:T(8,128)(2,1)}, bf16[64,2304]{1,0:T(8,128)(2,1)}, f32[1,2304]{1,0:T(1,128)}) custom-call(bf16[128,2304]{1,0:T(8,128)(2,1)} %copy-done.1, bf16[128,2304]{1,0:T(8,128)(2,1)} %copy-done.8, bf16[128,2304]{1,0:T(8,128)(2,1)} %get-tuple-element.32.p0, bf16[128,2304]{1,0:T(8,128)(2,1)} %copy-done.2, ...), custom_call_target="tpu_custom_call" | custom-call | flops 8847360 | bytes 4718592 | tf_op jit(solution)/shard_map/pallas_call | solution.py:308
  82.1 0.0 collective-permute-start.6
  82.1 1.8 %collective-permute-start.7 = (bf16[128,2304]{1,0:T(8,128)(2,1)S(1)}, bf16[128,2304]{1,0:T(8,128)(2,1)S(1)}, u32[]{:S(2)}, u32[]{:S(2)}) collective-permute-start(bf16[128,2304]{1,0:T(8,128)(2,1)S(1)} %copy-done), channel_id=1, source_target_pairs={{0,2},{1,3},{2,0},{3,1},{4,6},{5,7},{6,4},{7,5}} | collective-permute-start | bytes 1769480 | tf_op jit(solution)/shard_map/ppermute | solution.py:274
  83.9 0.4 collective-permute-done.6.xo_ref
  84.3 0.8 copy-done.10
  85.1 5.4 %shard_map.105 = (bf16[256,1024]{1,0:T(8,128)(2,1)}, bf16[256,2304]{1,0:T(8,128)(2,1)}) custom-call(bf16[128,2304]{1,0:T(8,128)(2,1)} %get-tuple-element.39.xm_ref.refs_0_, bf16[128,2304]{1,0:T(8,128)(2,1)} %copy-done.10, bf16[1,2304]{1,0:T(2,128)(2,1)} %reshape.26.g_ref, bf16[2304,1024]{1,0:T(8,128)(2,1)} %w_ref.5, f32[1,2304]{1,0:T(1,128)} %get-tuple-element.40.tok_ref.refs_1_), custom_call_target="tpu_custom_call" | custom-call | flops 1207959552 | bytes 4718592 | tf_op jit(solution)/shard_map/pallas_call | solution.py:315
  90.5 7.3 %collective-permute-done.7.z_ref = bf16[128,2304]{1,0:T(8,128)(2,1)S(1)} collective-permute-done((bf16[128,2304]{1,0:T(8,128)(2,1)S(1)}, bf16[128,2304]{1,0:T(8,128)(2,1)S(1)}, u32[]{:S(2)}, u32[]{:S(2)}) %collective-permute-start.7) | collective-permute-done | bytes 589856 | tf_op jit(solution)/shard_map/ppermute | solution.py:274
  97.8 0.8 copy-done.9
  98.7 3.8 %shard_map.106 = (bf16[128,2304]{1,0:T(8,128)(2,1)}, bf16[64,2304]{1,0:T(8,128)(2,1)}, f32[1,2304]{1,0:T(1,128)}, bf16[2,64,2304]{2,1,0:T(8,128)(2,1)}) custom-call(bf16[128,2304]{1,0:T(8,128)(2,1)} %add.22.tok_ref.xh_ref, bf16[128,2304]{1,0:T(8,128)(2,1)} %copy-done.9, bf16[128,2304]{1,0:T(8,128)(2,1)} %get-tuple-element.32.p0, ...), custom_call_target="tpu_custom_call" | custom-call | flops 8847360 | bytes 4718592 | tf_op jit(solution)/shard_map/pallas_call | solution.py:308
  102.5 0.0 collective-permute-start.8
  102.5 1.8 %collective-permute-start.9 = (bf16[64,2304]{1,0:T(8,128)(2,1)}, bf16[64,2304]{1,0:T(8,128)(2,1)S(1)}, u32[]{:S(2)}, u32[]{:S(2)}) collective-permute-start(bf16[64,2304]{1,0:T(8,128)(2,1)} %get-tuple-element.50.refs_0_), channel_id=1, source_target_pairs={{0,2},{1,3},{2,0},{3,1},{4,6},{5,7},{6,4},{7,5}} | collective-permute-start | bytes 884744 | tf_op jit(solution)/shard_map/ppermute | solution.py:274
  104.3 0.3 collective-permute-start.12
  104.6 0.0 collective-permute-start.15
  104.6 1.4 collective-permute-done.15
  106.0 0.7 add.23
  106.7 1.8 %collective-permute-start.16 = (f32[1,2304]{1,0:T(1,128)S(1)}, f32[1,2304]{1,0:T(1,128)S(1)}, u32[]{:S(2)}, u32[]{:S(2)}) collective-permute-start(f32[1,2304]{1,0:T(1,128)S(1)} %add.23), channel_id=1, source_target_pairs={{0,2},{1,3},{2,0},{3,1},{4,6},{5,7},{6,4},{7,5}} | collective-permute-start | bytes 27656 | tf_op jit(solution)/shard_map/ppermute | solution.py:274
  108.4 0.0 collective-permute-start.10
  108.4 4.2 %collective-permute-done.9.refs_1_ = bf16[64,2304]{1,0:T(8,128)(2,1)S(1)} collective-permute-done((bf16[64,2304]{1,0:T(8,128)(2,1)}, bf16[64,2304]{1,0:T(8,128)(2,1)S(1)}, u32[]{:S(2)}, u32[]{:S(2)}) %collective-permute-start.9) | collective-permute-done | bytes 294944 | tf_op jit(solution)/shard_map/ppermute | solution.py:274
  112.6 0.0 collective-permute-start.11
  112.6 6.0 %collective-permute-done.16 = f32[1,2304]{1,0:T(1,128)S(1)} collective-permute-done((f32[1,2304]{1,0:T(1,128)S(1)}, f32[1,2304]{1,0:T(1,128)S(1)}, u32[]{:S(2)}, u32[]{:S(2)}) %collective-permute-start.16) | collective-permute-done | bytes 9248 | tf_op jit(solution)/shard_map/ppermute | solution.py:274
  118.7 0.0 collective-permute-start.13
  118.7 0.6 add_reduce_fusion
  119.3 0.0 collective-permute-done.12.refs_5_
  119.3 0.5 collective-permute-start.14
  119.8 0.0 collective-permute-done.8.xo_ref
  119.8 0.8 copy-done.14
  120.7 9.4 %shard_map.107 = (bf16[2,256,1024]{2,1,0:T(8,128)(2,1)}, f32[2304,1024]{1,0:T(8,128)}) custom-call(bf16[256,2304]{1,0:T(8,128)(2,1)} %get-tuple-element.41.tok_ref.n0_ref, bf16[128,2304]{1,0:T(8,128)(2,1)} %get-tuple-element.42.xm_ref, bf16[128,2304]{1,0:T(8,128)(2,1)} %copy-done.14, bf16[1,2304]{1,0:T(2,128)(2,1)} %reshape.26.g_ref, ...), custom_call_target="tpu_custom_call" | custom-call | flops 3623878656 | bytes 14155776 | tf_op jit(solution)/shard_map/pallas_call | solution.py:326
  130.1 0.0 collective-permute-done.10.refs_2_
  130.1 0.0 copy-start.6
  130.1 0.0 collective-permute-done.11.refs_3_
  130.1 0.7 copy-done.6
  130.8 0.1 copy-done.7
  130.9 3.0 %shard_map.108.refs_9_ = f32[8192,2304]{1,0:T(8,128)} custom-call(s32[512]{0:T(512)} %broadcast_subtract_fusion.loc_ref, s32[512]{0:T(512)} %select_reduce_fusion.nxt_ref, s32[512]{0:T(512)} %get-tuple-element.47.last_ref, s32[512]{0:T(512)} %get-tuple-element.48.dup_ref, s32[8]{0:T(128)} %get-tuple-element.49.cnt_ref, ...), custom_call_target="tpu_custom_call", output_to_operand_aliasing={{}: (10, {})} | custom-call | flops 4718592 | bytes 4718592 | tf_op jit(solution)/shard_map/pallas_call | solution.py:333
  133.9 0.0 collective-permute-done.13.refs_6_
  133.9 0.0 collective-permute-done.14.refs_7_
  133.9 0.7 copy-done.12
  134.6 0.7 copy-done.13
  135.3 3.5 %shard_map.109 = f32[8192,2304]{1,0:T(8,128)} custom-call(s32[512]{0:T(512)} %broadcast_subtract_fusion.loc_ref, s32[512]{0:T(512)} %select_reduce_fusion.nxt_ref, s32[512]{0:T(512)} %get-tuple-element.47.last_ref, s32[512]{0:T(512)} %get-tuple-element.48.dup_ref, s32[8]{0:T(128)} %get-tuple-element.49.cnt_ref, ...), custom_call_target="tpu_custom_call", output_to_operand_aliasing={{}: (14, {})} | custom-call | flops 4718592 | bytes 4718592 | tf_op jit(solution)/shard_map/pallas_call | solution.py:333
  (20 shorter events, 0.0 us)
Async XLA Ops:
  35.8 2.6 %collective-permute-start = (bf16[128,2304]{1,0:T(8,128)(2,1)}, bf16[128,2304]{1,0:T(8,128)(2,1)S(1)}, u32[]{:S(2)}, u32[]{:S(2)}) collective-permute-start(bf16[128,2304]{1,0:T(8,128)(2,1)} %get-tuple-element.31), channel_id=1, source_target_pairs={{0,1},{1,0},{2,3},{3,2},{4,5},{5,4},{6,7},{7,6}} | collective-permute-start | bytes 1769480 | tf_op jit(solution)/shard_map/ppermute | solution.py:274
  36.3 6.4 %collective-permute-start.5 = (bf16[128,2304]{1,0:T(8,128)(2,1)}, bf16[128,2304]{1,0:T(8,128)(2,1)S(1)}, u32[]{:S(2)}, u32[]{:S(2)}) collective-permute-start(bf16[128,2304]{1,0:T(8,128)(2,1)} %get-tuple-element.37), channel_id=1, source_target_pairs={{0,1},{1,0},{2,3},{3,2},{4,5},{5,4},{6,7},{7,6}} | collective-permute-start | bytes 1769480 | tf_op jit(solution)/shard_map/ppermute | solution.py:274
  36.4 20.7 %collective-permute-start.2 = (bf16[128,2304]{1,0:T(8,128)(2,1)}, bf16[128,2304]{1,0:T(8,128)(2,1)S(1)}, u32[]{:S(2)}, u32[]{:S(2)}) collective-permute-start(bf16[128,2304]{1,0:T(8,128)(2,1)} %get-tuple-element.33), channel_id=1, source_target_pairs={{0,1},{1,0},{2,3},{3,2},{4,5},{5,4},{6,7},{7,6}} | collective-permute-start | bytes 1769480 | tf_op jit(solution)/shard_map/ppermute | solution.py:274
  36.9 20.3 %collective-permute-start.3 = (bf16[128,2304]{1,0:T(8,128)(2,1)}, bf16[128,2304]{1,0:T(8,128)(2,1)S(1)}, u32[]{:S(2)}, u32[]{:S(2)}) collective-permute-start(bf16[128,2304]{1,0:T(8,128)(2,1)} %get-tuple-element.34), channel_id=1, source_target_pairs={{0,2},{1,3},{2,0},{3,1},{4,6},{5,7},{6,4},{7,5}} | collective-permute-start | bytes 1769480 | tf_op jit(solution)/shard_map/ppermute | solution.py:274
  38.3 26.7 %collective-permute-start.4 = (bf16[128,2304]{1,0:T(8,128)(2,1)}, bf16[128,2304]{1,0:T(8,128)(2,1)S(1)}, u32[]{:S(2)}, u32[]{:S(2)}) collective-permute-start(bf16[128,2304]{1,0:T(8,128)(2,1)} %get-tuple-element.35), channel_id=1, source_target_pairs={{0,3},{1,2},{2,1},{3,0},{4,7},{5,6},{6,5},{7,4}} | collective-permute-start | bytes 1769480 | tf_op jit(solution)/shard_map/ppermute | solution.py:274
  39.6 17.4 %copy-start.1 = (bf16[128,2304]{1,0:T(8,128)(2,1)}, bf16[128,2304]{1,0:T(8,128)(2,1)S(1)}, u32[]{:S(2)}) copy-start(bf16[128,2304]{1,0:T(8,128)(2,1)S(1)} %add.21.xh_ref) | copy-start | bytes 1769476
  39.6 38.2 %collective-permute-start.1 = (bf16[128,2304]{1,0:T(8,128)(2,1)S(1)}, bf16[128,2304]{1,0:T(8,128)(2,1)S(1)}, u32[]{:S(2)}, u32[]{:S(2)}) collective-permute-start(bf16[128,2304]{1,0:T(8,128)(2,1)S(1)} %add.21.xh_ref), channel_id=1, source_target_pairs={{0,2},{1,3},{2,0},{3,1},{4,6},{5,7},{6,4},{7,5}} | collective-permute-start | bytes 1769480 | tf_op jit(solution)/shard_map/ppermute | solution.py:274
  57.1 25.0 %copy-start = (bf16[128,2304]{1,0:T(8,128)(2,1)S(1)}, bf16[128,2304]{1,0:T(8,128)(2,1)}, u32[]{:S(2)}) copy-start(bf16[128,2304]{1,0:T(8,128)(2,1)} %add.22.tok_ref.xh_ref) | copy-start | bytes 1769476
  57.1 20.7 %copy-start.2 = (bf16[128,2304]{1,0:T(8,128)(2,1)}, bf16[128,2304]{1,0:T(8,128)(2,1)S(1)}, u32[]{:S(2)}) copy-start(bf16[128,2304]{1,0:T(8,128)(2,1)S(1)} %collective-permute-done.2.p1) | copy-start | bytes 1769476
  57.1 20.7 %copy-start.3 = (bf16[128,2304]{1,0:T(8,128)(2,1)}, bf16[128,2304]{1,0:T(8,128)(2,1)S(1)}, u32[]{:S(2)}) copy-start(bf16[128,2304]{1,0:T(8,128)(2,1)S(1)} %collective-permute-done.3.p2) | copy-start | bytes 1769476
  65.0 12.8 %copy-start.4 = (bf16[128,2304]{1,0:T(8,128)(2,1)}, bf16[128,2304]{1,0:T(8,128)(2,1)S(1)}, u32[]{:S(2)}) copy-start(bf16[128,2304]{1,0:T(8,128)(2,1)S(1)} %collective-permute-done.4.p3) | copy-start | bytes 1769476
  77.8 0.8 copy-start.8
  82.1 2.2 %collective-permute-start.6 = (bf16[128,2304]{1,0:T(8,128)(2,1)}, bf16[128,2304]{1,0:T(8,128)(2,1)S(1)}, u32[]{:S(2)}, u32[]{:S(2)}) collective-permute-start(bf16[128,2304]{1,0:T(8,128)(2,1)} %get-tuple-element.39.xm_ref.refs_0_), channel_id=1, source_target_pairs={{0,1},{1,0},{2,3},{3,2},{4,5},{5,4},{6,7},{7,6}} | collective-permute-start | bytes 1769480 | tf_op jit(solution)/shard_map/ppermute | solution.py:274
  82.1 15.7 %collective-permute-start.7 = (bf16[128,2304]{1,0:T(8,128)(2,1)S(1)}, bf16[128,2304]{1,0:T(8,128)(2,1)S(1)}, u32[]{:S(2)}, u32[]{:S(2)}) collective-permute-start(bf16[128,2304]{1,0:T(8,128)(2,1)S(1)} %copy-done), channel_id=1, source_target_pairs={{0,2},{1,3},{2,0},{3,1},{4,6},{5,7},{6,4},{7,5}} | collective-permute-start | bytes 1769480 | tf_op jit(solution)/shard_map/ppermute | solution.py:274
  84.3 0.8 copy-start.10
  97.8 0.8 copy-start.9
  102.5 17.3 %collective-permute-start.8 = (bf16[128,2304]{1,0:T(8,128)(2,1)}, bf16[128,2304]{1,0:T(8,128)(2,1)S(1)}, u32[]{:S(2)}, u32[]{:S(2)}) collective-permute-start(bf16[128,2304]{1,0:T(8,128)(2,1)} %get-tuple-element.42.xm_ref), channel_id=1, source_target_pairs={{0,1},{1,0},{2,3},{3,2},{4,5},{5,4},{6,7},{7,6}} | collective-permute-start | bytes 1769480 | tf_op jit(solution)/shard_map/ppermute | solution.py:274
  102.5 10.1 %collective-permute-start.9 = (bf16[64,2304]{1,0:T(8,128)(2,1)}, bf16[64,2304]{1,0:T(8,128)(2,1)S(1)}, u32[]{:S(2)}, u32[]{:S(2)}) collective-permute-start(bf16[64,2304]{1,0:T(8,128)(2,1)} %get-tuple-element.50.refs_0_), channel_id=1, source_target_pairs={{0,2},{1,3},{2,0},{3,1},{4,6},{5,7},{6,4},{7,5}} | collective-permute-start | bytes 884744 | tf_op jit(solution)/shard_map/ppermute | solution.py:274
  104.3 15.0 %collective-permute-start.12 = (bf16[64,2304]{1,0:T(8,128)(2,1)}, bf16[64,2304]{1,0:T(8,128)(2,1)S(1)}, u32[]{:S(2)}, u32[]{:S(2)}) collective-permute-start(bf16[64,2304]{1,0:T(8,128)(2,1)} %get-tuple-element.51.refs_4_), channel_id=1, source_target_pairs={{0,2},{1,3},{2,0},{3,1},{4,6},{5,7},{6,4},{7,5}} | collective-permute-start | bytes 884744 | tf_op jit(solution)/shard_map/ppermute | solution.py:274
  104.6 1.4 collective-permute-start.15
  106.7 12.0 %collective-permute-start.16 = (f32[1,2304]{1,0:T(1,128)S(1)}, f32[1,2304]{1,0:T(1,128)S(1)}, u32[]{:S(2)}, u32[]{:S(2)}) collective-permute-start(f32[1,2304]{1,0:T(1,128)S(1)} %add.23), channel_id=1, source_target_pairs={{0,2},{1,3},{2,0},{3,1},{4,6},{5,7},{6,4},{7,5}} | collective-permute-start | bytes 27656 | tf_op jit(solution)/shard_map/ppermute | solution.py:274
  108.4 21.7 %collective-permute-start.10 = (bf16[64,2304]{1,0:T(8,128)(2,1)}, bf16[64,2304]{1,0:T(8,128)(2,1)S(1)}, u32[]{:S(2)}, u32[]{:S(2)}) collective-permute-start(bf16[64,2304]{1,0:T(8,128)(2,1)} %get-tuple-element.50.refs_0_), channel_id=1, source_target_pairs={{0,1},{1,0},{2,3},{3,2},{4,5},{5,4},{6,7},{7,6}} | collective-permute-start | bytes 884744 | tf_op jit(solution)/shard_map/ppermute | solution.py:274
  112.6 17.5 %copy-start.5 = (bf16[64,2304]{1,0:T(8,128)(2,1)}, bf16[64,2304]{1,0:T(8,128)(2,1)S(1)}, u32[]{:S(2)}) copy-start(bf16[64,2304]{1,0:T(8,128)(2,1)S(1)} %collective-permute-done.9.refs_1_) | copy-start | bytes 884740
  112.6 17.5 %collective-permute-start.11 = (bf16[64,2304]{1,0:T(8,128)(2,1)S(1)}, bf16[64,2304]{1,0:T(8,128)(2,1)S(1)}, u32[]{:S(2)}, u32[]{:S(2)}) collective-permute-start(bf16[64,2304]{1,0:T(8,128)(2,1)S(1)} %collective-permute-done.9.refs_1_), channel_id=1, source_target_pairs={{0,1},{1,0},{2,3},{3,2},{4,5},{5,4},{6,7},{7,6}} | collective-permute-start | bytes 884744 | tf_op jit(solution)/shard_map/ppermute | solution.py:274
  118.7 15.2 %collective-permute-start.13 = (bf16[64,2304]{1,0:T(8,128)(2,1)}, bf16[64,2304]{1,0:T(8,128)(2,1)S(1)}, u32[]{:S(2)}, u32[]{:S(2)}) collective-permute-start(bf16[64,2304]{1,0:T(8,128)(2,1)} %get-tuple-element.51.refs_4_), channel_id=1, source_target_pairs={{0,1},{1,0},{2,3},{3,2},{4,5},{5,4},{6,7},{7,6}} | collective-permute-start | bytes 884744 | tf_op jit(solution)/shard_map/ppermute | solution.py:274
  119.3 14.6 %copy-start.11 = (bf16[64,2304]{1,0:T(8,128)(2,1)}, bf16[64,2304]{1,0:T(8,128)(2,1)S(1)}, u32[]{:S(2)}) copy-start(bf16[64,2304]{1,0:T(8,128)(2,1)S(1)} %collective-permute-done.12.refs_5_) | copy-start | bytes 884740
  119.3 14.6 %collective-permute-start.14 = (bf16[64,2304]{1,0:T(8,128)(2,1)S(1)}, bf16[64,2304]{1,0:T(8,128)(2,1)S(1)}, u32[]{:S(2)}, u32[]{:S(2)}) collective-permute-start(bf16[64,2304]{1,0:T(8,128)(2,1)S(1)} %collective-permute-done.12.refs_5_), channel_id=1, source_target_pairs={{0,1},{1,0},{2,3},{3,2},{4,5},{5,4},{6,7},{7,6}} | collective-permute-start | bytes 884744 | tf_op jit(solution)/shard_map/ppermute | solution.py:274
  119.8 0.8 copy-start.14
  130.1 0.7 copy-start.6
  130.1 0.8 copy-start.7
  133.9 0.7 copy-start.12
  134.6 0.7 copy-start.13

commit v4 on v3

v4 whole, which is shorter than its diff:
```python
import functools

import jax
import jax.numpy as jnp
from jax import lax
from jax.experimental import pallas as pl
from jax.experimental.pallas import tpu as pltpu
from jax.sharding import PartitionSpec as P


EPS = 1e-6
F32 = jnp.float32
BF16 = jnp.bfloat16
HBM = pl.BlockSpec(memory_space=pltpu.HBM)
VMEM = pl.BlockSpec(memory_space=pltpu.VMEM)
SMEM = pl.BlockSpec(memory_space=pltpu.SMEM)


def call(body, mib, outs, ins, out_specs, scratch, flops, nbytes, aliases=None):
    return pl.pallas_call(
        body,
        out_shape=outs,
        in_specs=ins,
        out_specs=out_specs,
        scratch_shapes=scratch,
        input_output_aliases=aliases or {},
        cost_estimate=pl.CostEstimate(flops=flops, bytes_accessed=nbytes, transcendentals=0),
        compiler_params=pltpu.CompilerParams(vmem_limit_bytes=mib << 20),
    )


def pdn_kernel(lo, first, *refs):
    if first:
        du_ref, w_ref, *outs, dup_ref, dub, wb, dsem, wsem = refs
    else:
        dup_ref, w_ref, *outs, wb, wsem = refs
    width = outs[0].shape[1]
    n = outs[0].shape[0]
    blk = 256
    nb = width // blk
    for i in range(nb):
        pltpu.make_async_copy(w_ref.at[pl.ds(lo + i * blk, blk), :], wb.at[pl.ds(i * blk, blk), :], wsem.at[i]).start()
    if first:
        k, tl = dub.shape[0], dub.shape[1] // 4
        dc = pltpu.make_async_copy(du_ref, dub, dsem)
        dc.start()
        r = lax.axis_index("tp")
        dc.wait()
        for a, j in enumerate((2, 3, 1, 0)):
            q = r ^ j
            for m in range(k):
                dup_ref[pl.ds(a * n + m * tl, tl), :] = dub[m, pl.ds(pl.multiple_of(q * tl, tl), tl), :]
    for i in range(nb):
        pltpu.make_async_copy(w_ref.at[pl.ds(lo + i * blk, blk), :], wb.at[pl.ds(i * blk, blk), :], wsem.at[i]).wait()
        p = lax.dot_general(dup_ref[...], wb[i * blk:(i + 1) * blk, :], (((1,), (1,)), ((), ())), preferred_element_type=F32)
        for a in range(4):
            outs[a][:, i * blk:(i + 1) * blk] = p[a * n:(a + 1) * n].astype(BF16)


def zero_start(z, de_ref, lo, rows, sem):
    step = z.shape[0]
    for i in range(rows // step):
        pltpu.make_async_copy(z, de_ref.at[pl.ds(lo + i * step, step), :], sem).start()


def zero_wait(z, de_ref, rows, sem):
    step = z.shape[0]
    for _ in range(rows // step):
        pltpu.make_async_copy(z, de_ref.at[pl.ds(0, step), :], sem).wait()


def zero_kernel(tok_ref, de_in, de_ref, z, sem):
    z[...] = jnp.zeros_like(z)
    half = de_ref.shape[0] // 2
    zero_start(z, de_ref, half, half, sem)
    zero_wait(z, de_ref, half, sem)


def gather_kernel(tok_ref, ids_ref, emb_ref, k0, s0, k1, s1, last_ref, dup_ref, cnt_ref, de_ref,
                  buf, tmp, xf, z, lpos, lrow, lnxt, tab, sem, zsem):
    k, t = ids_ref.shape
    vl = emb_ref.shape[0]
    h = k0.shape[0]
    tl = t // 4
    r = lax.axis_index("tp")
    z[...] = jnp.zeros_like(z)
    zero_start(z, de_ref, 0, vl // 2, zsem)
    n = 0
    for m in range(k):
        def scan(i, n):
            v = ids_ref[m, i] - r * vl
            q = i // tl
            lpos[n] = m * t + ((q ^ r) & 1) * h + (q >> 1) * tl + (i & (tl - 1))
            lrow[n] = v
            return n + jnp.logical_and(v >= 0, v < vl).astype(jnp.int32)

        n = lax.fori_loop(0, t, scan, n, unroll=8)

    def start(i, c):
        v = lrow[i]
        b = pl.multiple_of((v >> 3) << 3, 8)
        pltpu.make_async_copy(emb_ref.at[pl.ds(b, 8), :], buf.at[i], sem).start()
        lnxt[i] = -1
        return c

    lax.fori_loop(0, n, start, 0)
    for a in range(8):
        lpos[n + a] = k * t
        lrow[n + a] = 0
    xf[...] = jnp.zeros_like(xf)

    def link(i, c):
        v = lrow[i]
        p = tab[v]
        ok = jnp.logical_and(p >= 0, p < i)
        p = jnp.where(ok, p, 0)
        ok = jnp.logical_and(ok, lrow[p] == v)
        lnxt[jnp.where(ok, p, k * t)] = i
        tab[v] = i
        return c

    lax.fori_loop(0, n, link, 0)

    def lists(i, c):
        nl, nd, n0 = c
        x = lnxt[i]
        end = (x < 0).astype(jnp.int32)
        last_ref[0, nl] = lpos[i]
        last_ref[1, nl] = lrow[i]
        dup_ref[0, nd] = lpos[i]
        dup_ref[1, nd] = lpos[jnp.maximum(x, 0)]
        return nl + end, nd + 1 - end, n0 + end * (lpos[i] < t).astype(jnp.int32)

    nl, nd, n0 = lax.fori_loop(0, n, lists, (0, 0, 0))
    cnt_ref[0] = nl
    cnt_ref[1] = nd
    cnt_ref[2] = n0

    def wait(i, c):
        pltpu.make_async_copy(emb_ref.at[pl.ds(0, 8), :], buf.at[0], sem).wait()
        return c

    lax.fori_loop(0, n, wait, 0)

    def take(g, c):
        for a in range(8):
            tmp[a] = buf[g * 8 + a].astype(F32)
        for a in range(8):
            i = g * 8 + a
            xf[pl.ds(lpos[i], 1), :] = tmp[a, pl.ds(lrow[i] & 7, 1), :]
        return c

    lax.fori_loop(0, (n + 7) // 8, take, 0)
    for a, ref in enumerate((k0, s0, k1, s1)):
        ref[...] = xf[a * h:(a + 1) * h, :].astype(BF16)
    zero_wait(z, de_ref, vl // 2, zsem)


def dx_kernel(m, xh_ref, z_ref, p0, p1, p2, p3, r0, r1, r2, r3, dres_ref, g_ref, tok_ref, *refs):
    if m == 1:
        xm0_ref, dg0_ref, xm_ref, dx_ref, dg_ref, x_ref = refs
    else:
        xm_ref, dx_ref, dg_ref = refs
    tl = dx_ref.shape[0]
    chip = lax.axis_index("tp") >> 1
    mine = pl.ds(pl.multiple_of(chip * tl, tl), tl)
    xm_ref[...] = xh_ref[...] + z_ref[...]
    if m == 1:
        x_ref[0] = xm0_ref[mine, :]
        x_ref[1] = xm_ref[mine, :]
    x = xm_ref[mine, :].astype(F32)
    g = g_ref[...].astype(F32)
    rs = lax.rsqrt(jnp.mean(x * x, axis=-1, keepdims=True) + EPS)
    nh = x * rs
    s = slice(m * tl, (m + 1) * tl)
    dn = jnp.concatenate([
        (a[s, :].astype(F32) + b[s, :].astype(F32)) + (c[s, :].astype(F32) + e[s, :].astype(F32))
        for a, b, c, e in ((p0, p1, p2, p3), (r0, r1, r2, r3))], axis=1)
    gdn = g * dn
    mean = jnp.mean(nh * gdn, axis=-1, keepdims=True)
    dxn = rs * (gdn - nh * mean)
    dx_ref[...] = (dres_ref[m].astype(F32) + dxn).astype(BF16)
    dg = jnp.sum(dn * nh, axis=0, keepdims=True)
    dg_ref[...] = dg if m == 0 else dg + dg0_ref[...]


def fill_n(xm_ref, xo_ref, g_ref, n_ref, off):
    r = lax.axis_index("tp")
    par = r & 1
    tl = xm_ref.shape[0] // 2
    g = g_ref[...].astype(F32)
    for side, ref in ((0, xm_ref), (1, xo_ref)):
        for c in range(2):
            q = 2 * c + (par ^ side)
            x = ref[c * tl:(c + 1) * tl, :].astype(F32)
            rs = lax.rsqrt(jnp.mean(x * x, axis=-1, keepdims=True) + EPS)
            n_ref[pl.ds(pl.multiple_of(off + q * tl, tl), tl), :] = ((x * rs) * g).astype(BF16)


def umat(n_ref, w_ref, u_ref, lo):
    t = u_ref.shape[0]
    blk = 256
    for i in range(u_ref.shape[1] // blk):
        u_ref[:, i * blk:(i + 1) * blk] = jnp.dot(
            n_ref[lo:lo + t, :], w_ref[:, i * blk:(i + 1) * blk], preferred_element_type=F32).astype(BF16)


def u_kernel(xm_ref, xo_ref, g_ref, w_ref, tok_ref, u_ref, n_ref, flag_ref, ub, usem):
    flag_ref[0] = 0
    fill_n(xm_ref, xo_ref, g_ref, n_ref, 0)
    umat(n_ref, w_ref, ub, 0)
    c = pltpu.make_async_copy(ub, u_ref.at[0], usem)
    c.start()
    c.wait()


def proj_kernel(n0_ref, xm_ref, xo_ref, g_ref, w_ref, du_ref, u_in, tok_ref, u_ref, dw_ref, flag_ref, n_ref, du2, ub, dwb, usem, wsem):
    flag_ref[0] = 0
    k, t = du_ref.shape[0], du_ref.shape[1]
    d, _ = w_ref.shape
    copies = []
    n_ref[0:t, :] = n0_ref[...]
    fill_n(xm_ref, xo_ref, g_ref, n_ref, t)
    for m in range(k):
        du2[m * t:(m + 1) * t, :] = du_ref[m]
    umat(n_ref, w_ref, ub, t)
    c = pltpu.make_async_copy(ub, u_ref.at[1], usem)
    c.start()
    copies.append(c)
    blk = 256
    for i in range(d // blk):
        dwb[i] = lax.dot_general(n_ref[:, i * blk:(i + 1) * blk], du2[...], (((0,), (0,)), ((), ())),
                                 preferred_element_type=F32)
        c = pltpu.make_async_copy(dwb.at[i], dw_ref.at[pl.ds(i * blk, blk), :], wsem)
        c.start()
        copies.append(c)
    for c in copies:
        c.wait()


def scatter_kernel(m, last_ref, dup_ref, cnt_ref, *refs):
    nd = 4 * (m + 1)
    ds, de_ref, xf, sem = refs[:nd], refs[-3], refs[-2], refs[-1]
    tl = ds[0].shape[0]
    chip = lax.axis_index("tp") >> 1
    for a, ref in enumerate(ds):
        c = chip if a % 2 == 0 else 1 - chip
        xf[pl.ds(pl.multiple_of((a // 2) * 2 * tl + c * tl, tl), tl), :] = ref[...].astype(F32)

    def add(i, c):
        a = dup_ref[0, i]
        b = dup_ref[1, i]

        @pl.when(b < 4 * tl * (m + 1))
        def _():
            xf[pl.ds(b, 1), :] = xf[pl.ds(b, 1), :] + xf[pl.ds(a, 1), :]

        return c

    lax.fori_loop(0, cnt_ref[1], add, 0)

    def put(i, c):
        pltpu.make_async_copy(xf.at[pl.ds(last_ref[0, i], 1), :], de_ref.at[pl.ds(last_ref[1, i], 1), :], sem).start()
        return c

    def wait(i, c):
        pltpu.make_async_copy(xf.at[pl.ds(0, 1), :], de_ref.at[pl.ds(0, 1), :], sem).wait()
        return c

    n0, n1 = (0, cnt_ref[2]) if m == 0 else (cnt_ref[2], cnt_ref[0])
    lax.fori_loop(n0, n1, put, 0)
    lax.fori_loop(n0, n1, wait, 0)


def solution(mesh):
    groups = mesh.shape["tp"]
    sib = [(i, i ^ 1) for i in range(groups)]
    cross = [(i, i ^ 2) for i in range(groups)]
    diag = [(i, i ^ 3) for i in range(groups)]

    def local(ids, emb, g, w, du, dres):
        k, t = ids.shape
        vl, d = emb.shape
        fc = w.shape[1]
        tl = t // groups
        n = k * tl
        h = 2 * n
        g2 = g.reshape(1, d)
        S = jax.ShapeDtypeStruct
        D = pltpu.SemaphoreType.DMA

        def perm(v, p):
            return lax.ppermute(v, "tp", p)

        d1 = 5 * 256
        d2 = d - d1
        p2, p3, p1, p0, dup4 = call(
            functools.partial(pdn_kernel, 0, True), 60, [S((n, d1), BF16)] * 4 + [S((4 * n, fc), BF16)],
            [HBM] * 2, [VMEM] * 5, [pltpu.VMEM((k, t, fc), BF16), pltpu.VMEM((d1, fc), BF16), D, D((d1 // 256,))],
            8 * n * fc * d1, 2 * d1 * fc + 8 * n * (fc + d1))(du, w)
        r2, r3, r1, r0 = call(
            functools.partial(pdn_kernel, d1, False), 60, [S((n, d2), BF16)] * 4,
            [VMEM, HBM], [VMEM] * 4, [pltpu.VMEM((d2, fc), BF16), D((d2 // 256,))],
            8 * n * fc * d2, 2 * d2 * fc + 8 * n * (fc + d2))(dup4, w)
        q2 = perm(p2, cross)
        q3 = perm(p3, diag)
        v2 = perm(r2, cross)
        v3 = perm(r3, diag)
        q1 = perm(p1, sib)
        v1 = perm(r1, sib)

        k0, s0, k1, s1, last, dup, cnt, de = call(
            gather_kernel, 60,
            [S((n, d), BF16)] * 4 + [S((2, 2 * h + 8), jnp.int32)] * 2 + [S((8,), jnp.int32), S((vl, d), F32)],
            [HBM, SMEM, HBM], [VMEM] * 4 + [SMEM] * 3 + [HBM],
            [pltpu.VMEM((2 * h, 8, d), BF16), pltpu.VMEM((8, 8, d), F32), pltpu.VMEM((2 * h + 8, d), F32), pltpu.VMEM((256, d), F32)]
            + [pltpu.SMEM((2 * h + 8,), jnp.int32)] * 3 + [pltpu.SMEM((vl,), jnp.int32), D, D],
            5_000_000_000, 16 * h * d)(r2, ids, emb)
        y0 = perm(s0, sib)
        y1 = perm(s1, sib)
        xh0 = k0 + y0
        xh1 = k1 + y1
        z0 = perm(xh0, cross)
        z1 = perm(xh1, cross)
        de = call(zero_kernel, 8, S((vl, d), F32), [HBM, HBM], HBM,
                  [pltpu.VMEM((256, d), F32), D], 5_000_000_000, 2 * vl * d, {1: 0})(xh1, de)

        def dxk(m, xh, z, tok, more):
            outs = [S((n, d), BF16), S((tl, d), BF16), S((1, d), F32)] + ([S((k, tl, d), BF16)] if m else [])
            return call(functools.partial(dx_kernel, m), 16, outs, [VMEM] * 12 + [SMEM if m else HBM] + [VMEM] * len(more),
                        [VMEM] * len(outs), [], 30 * n * d, 16 * n * d)(xh, z, p0, q1, q2, q3, r0, v1, v2, v3, dres, g2, tok, *more)

        xm0, dx0, dg0 = dxk(0, xh0, z0, de, ())
        c0 = perm(dx0, cross)
        xo0 = perm(xm0, sib)
        a0 = perm(dx0, sib)
        u, n0, done0 = call(
            u_kernel, 24, [S((k, t, fc), BF16), S((t, d), BF16), S((8,), jnp.int32)], [VMEM] * 5, [HBM, VMEM, SMEM],
            [pltpu.VMEM((t, fc), BF16), D], 2 * t * d * fc, 2 * d * fc)(xm0, xo0, g2, w, dg0)
        xm1, dx1, dg, x = dxk(1, xh1, z1, done0, (xm0, dg0))
        c1 = perm(dx1, cross)
        xo1 = perm(xm1, sib)
        a1 = perm(dx1, sib)
        b0 = perm(c0, sib)
        b1 = perm(c1, sib)
        dgs = dg + perm(dg, sib)
        dgs = dgs + perm(dgs, cross)

        u, dw, done1 = call(
            proj_kernel, 36, [S((k, t, fc), BF16), S((d, fc), F32), S((8,), jnp.int32)],
            [VMEM] * 6 + [HBM, VMEM], [HBM, HBM, SMEM],
            [pltpu.VMEM((k * t, d), BF16), pltpu.VMEM((k * t, fc), BF16), pltpu.VMEM((t, fc), BF16),
             pltpu.VMEM((d // 256, 256, fc), F32), D, D],
            3 * k * t * d * fc, 6 * d * fc, {6: 0})(n0, xm1, xo1, g2, w, du, u, dg)

        def scatter(m, parts, de, tok):
            return call(functools.partial(scatter_kernel, m), 16, S((vl, d), F32),
                        [SMEM] * 3 + [VMEM] * len(parts) + [SMEM, HBM], HBM,
                        [pltpu.VMEM((h * (m + 1), d), F32), D], 8 * h * d, 8 * h * d,
                        {4 + len(parts): 0})(last, dup, cnt, *parts, tok, de)

        de = scatter(0, (dx0, c0, a0, b0), de, done1)
        de = scatter(1, (dx0, c0, a0, b0, dx1, c1, a1, b1), de, done1)
        return u, x, de, dw, dgs.reshape(d)

    return jax.shard_map(
        local,
        mesh=mesh,
        in_specs=(P("dp", None), P("tp", None), P(None), P(None, "tp"), P("dp", None, "tp"), P("dp", "tp", None)),
        out_specs=(P("dp", None, "tp"), P("dp", "tp", None), P(("dp", "tp"), None), P(None, ("dp", "tp")), P("dp")),
        check_vma=False,
    )
```

time: 140 us -> 122 us (0.87)
  Pallas kernels: 73.2 us -> 61.2 us
  waiting for transfers between devices: 40.1 us -> 47.6 us
  local copies, waits for them, and re-layouts: 7.64 us -> 0.74 us
  other arithmetic: 6.65 us -> 3.04 us
  starting transfers between devices: 10.5 us -> 7.06 us
    pallas_call x9 -> x10, Pallas kernels: 73.2 us -> 61.2 us  [the longest x1 18.4 us: local(): call(gather_kernel, 60, [S((n, d), BF16)] * 4 + [S((2, 2 * h + 8), jnp.in...]
    ppermute x17 -> x20, waiting for transfers between devices: 40.1 us -> 47.6 us  [perm(): return lax.ppermute(v, 'tp', p)]
    unnamed x30 -> x18, local copies, waits for them, and re-layouts: 5.49 us -> 0.04 us
    ppermute x17 -> x20, starting transfers between devices: 10.5 us -> 7.06 us  [perm(): return lax.ppermute(v, 'tp', p)]
  transfers between devices with their start and end apart: 17 -> 20, of which waited for: 7 -> 8; matrix products, arithmetic and copies ran while one was open for 4% -> 3% of each run, Pallas kernels for 22% -> 20%
where the time goes in v4:
time: 122 us; the launch traced here: 121 us
  Pallas kernels  61.2 us (50%)
  waiting for transfers between devices  47.6 us (39%)
  starting transfers between devices  7.06 us (6%)
  other arithmetic  3.04 us (2%)
    ppermute x20, waiting for transfers between devices, perm(): return lax.ppermute(v, 'tp', p)  47.6 us
    pallas_call x1, Pallas kernels, local(): call(gather_kernel, 60, [S((n, d), BF16)] * 4 + [S((2, 2 * h + 8), jnp.in...  18.4 us
    pallas_call x1, Pallas kernels, local(): call(zero_kernel, 8, S((vl, d), F32), [HBM, HBM], HBM, [pltpu.VMEM((256,...  12.3 us
    ppermute x20, starting transfers between devices, perm(): return lax.ppermute(v, 'tp', p)  7.06 us
    pallas_call x1, Pallas kernels, local(): call(functools.partial(pdn_kernel, 0, True), 60, [S((n, d1), BF16)] * 4 +...  6.82 us
    pallas_call x1, Pallas kernels, local(): call(proj_kernel, 36, [S((k, t, fc), BF16), S((d, fc), F32), S((8,), jnp....  6.66 us
    pallas_call x1, Pallas kernels, local(): call(functools.partial(pdn_kernel, d1, False), 60, [S((n, d2), BF16)] * 4...  6.07 us
    pallas_call x2, Pallas kernels, scatter(): call(functools.partial(scatter_kernel, m), 16, S((vl, d), F32), [SMEM] *...  5 us
  transfers between devices with their start and end apart: 20, of which 8 were waited for; matrix products, arithmetic and copies ran while one was open for 3% of the time, Pallas kernels for 20%

profile of v4, /device:TPU:0, one launch (start us, length us, event | category | flops | bytes accessed | tf_op | source)
XLA Modules:
  0.0 120.6 jit_solution(16116371800551109716)
XLA Ops:
  0.6 6.8 %shard_map.101 = (bf16[128,1280]{1,0:T(8,128)(2,1)}, bf16[128,1280]{1,0:T(8,128)(2,1)}, bf16[128,1280]{1,0:T(8,128)(2,1)}, bf16[128,1280]{1,0:T(8,128)(2,1)}, bf16[512,1024]{1,0:T(8,128)(2,1)}) custom-call(bf16[2,256,1024]{2,1,0:T(8,128)(2,1)} %du_ref.1, bf16[2304,1024]{1,0:T(8,128)(2,1)} %w_ref.3), custom_call_target="tpu_custom_call" | custom-call | flops 1342177280 | bytes 4980736 | tf_op jit(solution)/shard_map/pallas_call | solution.py:297
  7.5 6.1 %shard_map.102 = (bf16[128,1024]{1,0:T(8,128)(2,1)}, bf16[128,1024]{1,0:T(8,128)(2,1)}, bf16[128,1024]{1,0:T(8,128)(2,1)}, bf16[128,1024]{1,0:T(8,128)(2,1)}) custom-call(bf16[512,1024]{1,0:T(8,128)(2,1)} %get-tuple-element.35.refs_0_, bf16[2304,1024]{1,0:T(8,128)(2,1)} %w_ref.3), custom_call_target="tpu_custom_call" | custom-call | flops 1073741824 | bytes 4194304 | tf_op jit(solution)/shard_map/pallas_call | solution.py:301
  13.5 18.4 %shard_map.103 = (bf16[128,2304]{1,0:T(8,128)(2,1)}, bf16[128,2304]{1,0:T(8,128)(2,1)}, bf16[128,2304]{1,0:T(8,128)(2,1)}, bf16[128,2304]{1,0:T(8,128)(2,1)}, s3...) custom-call(bf16[128,1024]{1,0:T(8,128)(2,1)} %get-tuple-element.36.tok_ref, ...), custom_call_target="tpu_custom_call" | custom-call | flops 5000000000 | bytes 9437184 | tf_op jit(solution)/shard_map/pallas_call | solution.py:312
  31.9 0.0 collective-permute-start
  32.0 0.5 collective-permute-start.8
  32.5 0.0 collective-permute-start.5
  32.5 0.4 collective-permute-start.6
  32.9 1.2 %collective-permute-done = bf16[128,2304]{1,0:T(8,128)(2,1)S(1)} collective-permute-done((bf16[128,2304]{1,0:T(8,128)(2,1)}, bf16[128,2304]{1,0:T(8,128)(2,1)S(1)}, u32[]{:S(2)}, u32[]{:S(2)}) %collective-permute-start) | collective-permute-done | bytes 589856 | tf_op jit(solution)/shard_map/ppermute | solution.py:293
  34.2 1.2 add.12.xh_ref
  35.4 0.4 collective-permute-start.1
  35.8 0.0 collective-permute-start.2
  35.8 0.7 reshape.16.g_ref
  36.5 0.0 collective-permute-done.8
  36.5 1.6 %collective-permute-start.3 = (bf16[128,1280]{1,0:T(8,128)(2,1)}, bf16[128,1280]{1,0:T(8,128)(2,1)S(1)}, u32[]{:S(2)}, u32[]{:S(2)}) collective-permute-start(bf16[128,1280]{1,0:T(8,128)(2,1)} %get-tuple-element.41), channel_id=1, source_target_pairs={{0,2},{1,3},{2,0},{3,1},{4,6},{5,7},{6,4},{7,5}} | collective-permute-start | bytes 983048 | tf_op jit(solution)/shard_map/ppermute | solution.py:293
  38.1 1.2 add.13.tok_ref.xh_ref
  39.3 0.0 collective-permute-done.5.r1
  39.3 0.3 collective-permute-start.4
  39.6 2.3 %collective-permute-done.6.r2 = bf16[128,1024]{1,0:T(8,128)(2,1)S(1)} collective-permute-done((bf16[128,1024]{1,0:T(8,128)(2,1)}, bf16[128,1024]{1,0:T(8,128)(2,1)S(1)}, u32[]{:S(2)}, u32[]{:S(2)}) %collective-permute-start.6) | collective-permute-done | bytes 262176 | tf_op jit(solution)/shard_map/ppermute | solution.py:293
  41.9 0.0 collective-permute-start.7
  41.9 12.3 %shard_map.104.tok_ref.refs_5_ = f32[8192,2304]{1,0:T(8,128)} custom-call(bf16[128,2304]{1,0:T(8,128)(2,1)S(1)} %add.13.tok_ref.xh_ref, f32[8192,2304]{1,0:T(8,128)} %get-tuple-element.48.de_in), custom_call_target="tpu_custom_call", output_to_operand_aliasing={{}: (1, {})} | custom-call | flops 5000000000 | bytes 37748736 | tf_op jit(solution)/shard_map/pallas_call | solution.py:325
  54.2 0.0 slice-start
  54.2 0.0 copy-start.3
  54.3 0.0 copy-start.4
  54.3 0.0 copy-start.5
  54.3 0.0 copy-start.6
  54.3 18.9 %collective-permute-done.7.r3 = bf16[128,1024]{1,0:T(8,128)(2,1)S(1)} collective-permute-done((bf16[128,1024]{1,0:T(8,128)(2,1)}, bf16[128,1024]{1,0:T(8,128)(2,1)S(1)}, u32[]{:S(2)}, u32[]{:S(2)}) %collective-permute-start.7) | collective-permute-done | bytes 262176 | tf_op jit(solution)/shard_map/ppermute | solution.py:293
  73.2 0.0 collective-permute-done.2.p1
  73.2 0.0 collective-permute-done.3.p2
  73.2 0.0 collective-permute-done.4.p3
  73.2 0.0 collective-permute-done.1.z_ref
  73.2 0.0 copy-done
  73.2 0.0 copy-done.1
  73.2 0.0 copy-done.2
  73.2 0.0 slice-start.1
  73.3 0.7 shard_map.105
  73.9 0.3 collective-permute-start.9
  74.3 0.4 collective-permute-start.10
  74.7 1.3 %collective-permute-done.9.xo_ref = bf16[128,2304]{1,0:T(8,128)(2,1)S(1)} collective-permute-done((bf16[128,2304]{1,0:T(8,128)(2,1)S(1)}, bf16[128,2304]{1,0:T(8,128)(2,1)S(1)}, u32[]{:S(2)}, u32[]{:S(2)}) %collective-permute-start.9) | collective-permute-done | bytes 589856 | tf_op jit(solution)/shard_map/ppermute | solution.py:293
  76.0 0.0 slice-done
  76.0 3.3 %shard_map.106 = (bf16[2,256,1024]{2,1,0:T(8,128)(2,1)}, bf16[256,2304]{1,0:T(8,128)(2,1)S(1)}, s32[8]{0:T(128)S(1)}) custom-call(bf16[128,2304]{1,0:T(8,128)(2,1)S(1)} %get-tuple-element.49.xm_ref.refs_0_, bf16[128,2304]{1,0:T(8,128)(2,1)S(1)} %collective-permute-done.9.xo_ref, bf16[1,2304]{1,0:T(2,128)(2,1)S(1)} %reshape.16.g_ref, ...), custom_call_target="tpu_custom_call" | custom-call | flops 1207959552 | bytes 4718592 | tf_op jit(solution)/shard_map/pallas_call | solution.py:337
  79.3 10.4 %collective-permute-done.10.z_ref = bf16[128,2304]{1,0:T(8,128)(2,1)S(1)} collective-permute-done((bf16[128,2304]{1,0:T(8,128)(2,1)S(1)}, bf16[128,2304]{1,0:T(8,128)(2,1)S(1)}, u32[]{:S(2)}, u32[]{:S(2)}) %collective-permute-start.10) | collective-permute-done | bytes 589856 | tf_op jit(solution)/shard_map/ppermute | solution.py:293
  89.7 1.9 %shard_map.107 = (bf16[128,2304]{1,0:T(8,128)(2,1)S(1)}, bf16[64,2304]{1,0:T(8,128)(2,1)S(1)}, f32[1,2304]{1,0:T(1,128)S(1)}, bf16[2,64,2304]{2,1,0:T(8,128)(2,1)}) custom-call(bf16[128,2304]{1,0:T(8,128)(2,1)S(1)} %add.13.tok_ref.xh_ref, bf16[128,2304]{1,0:T(8,128)(2,1)S(1)} %collective-permute-done.10.z_ref, bf16[128,1280]{1,0:T(8,128)(2,1)S(1)} %copy-done.1, ...), custom_call_target="tpu_custom_call" | custom-call | flops 8847360 | bytes 4718592 | tf_op jit(solution)/shard_map/pallas_call | solution.py:330
  91.6 0.0 collective-permute-start.11
  91.6 0.4 collective-permute-start.12
  92.1 1.6 %collective-permute-start.15 = (bf16[64,2304]{1,0:T(8,128)(2,1)S(1)}, bf16[64,2304]{1,0:T(8,128)(2,1)S(1)}, u32[]{:S(2)}, u32[]{:S(2)}) collective-permute-start(bf16[64,2304]{1,0:T(8,128)(2,1)S(1)} %get-tuple-element.62.refs_4_), channel_id=1, source_target_pairs={{0,2},{1,3},{2,0},{3,1},{4,6},{5,7},{6,4},{7,5}} | collective-permute-start | bytes 884744 | tf_op jit(solution)/shard_map/ppermute | solution.py:293
  93.7 0.0 collective-permute-start.18
  93.7 1.2 collective-permute-done.18
  94.9 0.4 collective-permute-start.19
  95.3 0.0 collective-permute-start.13
  95.3 6.2 %collective-permute-done.12.refs_1_ = bf16[64,2304]{1,0:T(8,128)(2,1)S(1)} collective-permute-done((bf16[64,2304]{1,0:T(8,128)(2,1)S(1)}, bf16[64,2304]{1,0:T(8,128)(2,1)S(1)}, u32[]{:S(2)}, u32[]{:S(2)}) %collective-permute-start.12) | collective-permute-done | bytes 294944 | tf_op jit(solution)/shard_map/ppermute | solution.py:293
  101.5 0.0 collective-permute-start.14
  101.5 6.1 %collective-permute-done.19 = f32[1,2304]{1,0:T(1,128)S(1)} collective-permute-done((f32[1,2304]{1,0:T(1,128)S(1)}, f32[1,2304]{1,0:T(1,128)S(1)}, u32[]{:S(2)}, u32[]{:S(2)}) %collective-permute-start.19) | collective-permute-done | bytes 9248 | tf_op jit(solution)/shard_map/ppermute | solution.py:293
  107.6 0.0 collective-permute-start.16
  107.6 0.6 add_reduce_fusion
  108.2 0.0 collective-permute-done.15.refs_5_
  108.2 0.5 collective-permute-start.17
  108.7 0.0 collective-permute-done.11.xo_ref
  108.7 6.7 %shard_map.108 = (bf16[2,256,1024]{2,1,0:T(8,128)(2,1)}, f32[2304,1024]{1,0:T(8,128)}, s32[8]{0:T(128)S(1)}) custom-call(bf16[256,2304]{1,0:T(8,128)(2,1)S(1)} %get-tuple-element.51.n0_ref, bf16[128,2304]{1,0:T(8,128)(2,1)S(1)} %get-tuple-element.53.xm_ref, bf16[128,2304]{1,0:T(8,128)(2,1)S(1)} %collective-permute-done.11.xo_ref, ...), custom_call_target="tpu_custom_call", output_to_operand_aliasing={{0}: (6, {})} | custom-call | flops 3623878656 | bytes 14155776 | tf_op jit(solution)/shard_map/pallas_call | solution.py:349
  115.4 0.0 collective-permute-done.13.refs_2_
  115.4 0.0 collective-permute-done.14.refs_3_
  115.5 2.4 %shard_map.109.refs_9_ = f32[8192,2304]{1,0:T(8,128)} custom-call(s32[2,520]{1,0:T(2,128)S(1)} %copy-done.4, s32[2,520]{1,0:T(2,128)S(1)} %copy-done.5, s32[8]{0:T(128)S(1)} %copy-done.6, bf16[64,2304]{1,0:T(8,128)(2,1)S(1)} %get-tuple-element.61.refs_0_, bf16[64,2304]{1,0:T(8,128)(2,1)S(1)} %collective-permute-done.12.refs_1_, ...), custom_call_target="tpu_custom_call", output_to_operand_aliasing={{}: (8, {})} | custom-call | flops 4718592 | bytes 4718592 | tf_op jit(solution)/shard_map/pallas_call | solution.py:357
  117.9 0.0 collective-permute-done.16.refs_6_
  117.9 0.0 collective-permute-done.17.refs_7_
  117.9 2.6 %shard_map.110 = f32[8192,2304]{1,0:T(8,128)} custom-call(s32[2,520]{1,0:T(2,128)S(1)} %copy-done.4, s32[2,520]{1,0:T(2,128)S(1)} %copy-done.5, s32[8]{0:T(128)S(1)} %copy-done.6, bf16[64,2304]{1,0:T(8,128)(2,1)S(1)} %get-tuple-element.61.refs_0_, bf16[64,2304]{1,0:T(8,128)(2,1)S(1)} %collective-permute-done.12.refs_1_, ...), custom_call_target="tpu_custom_call", output_to_operand_aliasing={{}: (12, {})} | custom-call | flops 4718592 | bytes 4718592 | tf_op jit(solution)/shard_map/pallas_call | solution.py:357
  (10 shorter events, 0.0 us)
Async XLA Ops:
  31.9 2.2 %collective-permute-start = (bf16[128,2304]{1,0:T(8,128)(2,1)}, bf16[128,2304]{1,0:T(8,128)(2,1)S(1)}, u32[]{:S(2)}, u32[]{:S(2)}) collective-permute-start(bf16[128,2304]{1,0:T(8,128)(2,1)} %get-tuple-element.38), channel_id=1, source_target_pairs={{0,1},{1,0},{2,3},{3,2},{4,5},{5,4},{6,7},{7,6}} | collective-permute-start | bytes 1769480 | tf_op jit(solution)/shard_map/ppermute | solution.py:293
  32.0 4.6 %collective-permute-start.8 = (bf16[128,2304]{1,0:T(8,128)(2,1)}, bf16[128,2304]{1,0:T(8,128)(2,1)S(1)}, u32[]{:S(2)}, u32[]{:S(2)}) collective-permute-start(bf16[128,2304]{1,0:T(8,128)(2,1)} %get-tuple-element.47), channel_id=1, source_target_pairs={{0,1},{1,0},{2,3},{3,2},{4,5},{5,4},{6,7},{7,6}} | collective-permute-start | bytes 1769480 | tf_op jit(solution)/shard_map/ppermute | solution.py:293
  32.5 6.9 %collective-permute-start.5 = (bf16[128,1024]{1,0:T(8,128)(2,1)}, bf16[128,1024]{1,0:T(8,128)(2,1)S(1)}, u32[]{:S(2)}, u32[]{:S(2)}) collective-permute-start(bf16[128,1024]{1,0:T(8,128)(2,1)} %get-tuple-element.44), channel_id=1, source_target_pairs={{0,1},{1,0},{2,3},{3,2},{4,5},{5,4},{6,7},{7,6}} | collective-permute-start | bytes 786440 | tf_op jit(solution)/shard_map/ppermute | solution.py:293
  32.5 9.4 %collective-permute-start.6 = (bf16[128,1024]{1,0:T(8,128)(2,1)}, bf16[128,1024]{1,0:T(8,128)(2,1)S(1)}, u32[]{:S(2)}, u32[]{:S(2)}) collective-permute-start(bf16[128,1024]{1,0:T(8,128)(2,1)} %get-tuple-element.36.tok_ref), channel_id=1, source_target_pairs={{0,2},{1,3},{2,0},{3,1},{4,6},{5,7},{6,4},{7,5}} | collective-permute-start | bytes 786440 | tf_op jit(solution)/shard_map/ppermute | solution.py:293
  35.4 37.8 %collective-permute-start.1 = (bf16[128,2304]{1,0:T(8,128)(2,1)S(1)}, bf16[128,2304]{1,0:T(8,128)(2,1)S(1)}, u32[]{:S(2)}, u32[]{:S(2)}) collective-permute-start(bf16[128,2304]{1,0:T(8,128)(2,1)S(1)} %add.12.xh_ref), channel_id=1, source_target_pairs={{0,2},{1,3},{2,0},{3,1},{4,6},{5,7},{6,4},{7,5}} | collective-permute-start | bytes 1769480 | tf_op jit(solution)/shard_map/ppermute | solution.py:293
  35.8 37.4 %collective-permute-start.2 = (bf16[128,1280]{1,0:T(8,128)(2,1)}, bf16[128,1280]{1,0:T(8,128)(2,1)S(1)}, u32[]{:S(2)}, u32[]{:S(2)}) collective-permute-start(bf16[128,1280]{1,0:T(8,128)(2,1)} %get-tuple-element.40), channel_id=1, source_target_pairs={{0,1},{1,0},{2,3},{3,2},{4,5},{5,4},{6,7},{7,6}} | collective-permute-start | bytes 983048 | tf_op jit(solution)/shard_map/ppermute | solution.py:293
  36.5 36.7 %collective-permute-start.3 = (bf16[128,1280]{1,0:T(8,128)(2,1)}, bf16[128,1280]{1,0:T(8,128)(2,1)S(1)}, u32[]{:S(2)}, u32[]{:S(2)}) collective-permute-start(bf16[128,1280]{1,0:T(8,128)(2,1)} %get-tuple-element.41), channel_id=1, source_target_pairs={{0,2},{1,3},{2,0},{3,1},{4,6},{5,7},{6,4},{7,5}} | collective-permute-start | bytes 983048 | tf_op jit(solution)/shard_map/ppermute | solution.py:293
  39.3 33.9 %collective-permute-start.4 = (bf16[128,1280]{1,0:T(8,128)(2,1)}, bf16[128,1280]{1,0:T(8,128)(2,1)S(1)}, u32[]{:S(2)}, u32[]{:S(2)}) collective-permute-start(bf16[128,1280]{1,0:T(8,128)(2,1)} %get-tuple-element.42), channel_id=1, source_target_pairs={{0,3},{1,2},{2,1},{3,0},{4,7},{5,6},{6,5},{7,4}} | collective-permute-start | bytes 983048 | tf_op jit(solution)/shard_map/ppermute | solution.py:293
  41.9 31.3 %collective-permute-start.7 = (bf16[128,1024]{1,0:T(8,128)(2,1)}, bf16[128,1024]{1,0:T(8,128)(2,1)S(1)}, u32[]{:S(2)}, u32[]{:S(2)}) collective-permute-start(bf16[128,1024]{1,0:T(8,128)(2,1)} %get-tuple-element.45), channel_id=1, source_target_pairs={{0,3},{1,2},{2,1},{3,0},{4,7},{5,6},{6,5},{7,4}} | collective-permute-start | bytes 786440 | tf_op jit(solution)/shard_map/ppermute | solution.py:293
  41.9 31.3 %copy-start = (bf16[2,64,2304]{2,1,0:T(8,128)(2,1)S(1)}, bf16[2,64,2304]{2,1,0:T(8,128)(2,1)}, u32[]{:S(2)}) copy-start(bf16[2,64,2304]{2,1,0:T(8,128)(2,1)} %dres_ref.3) | copy-start | bytes 1769476
  41.9 31.3 %copy-start.1 = (bf16[128,1280]{1,0:T(8,128)(2,1)S(1)}, bf16[128,1280]{1,0:T(8,128)(2,1)}, u32[]{:S(2)}) copy-start(bf16[128,1280]{1,0:T(8,128)(2,1)} %get-tuple-element.39.p0) | copy-start | bytes 983044
  41.9 31.4 %copy-start.2 = (bf16[128,1024]{1,0:T(8,128)(2,1)S(1)}, bf16[128,1024]{1,0:T(8,128)(2,1)}, u32[]{:S(2)}) copy-start(bf16[128,1024]{1,0:T(8,128)(2,1)} %get-tuple-element.43.r0) | copy-start | bytes 786436
  54.2 21.7 %slice-start = ((s8[4718592]{0:T(1024)(128)(4,1)}), s8[4194304]{0:T(1024)(128)(4,1)S(1)}, s32[]{:S(2)}) async-start(s8[4718592]{0:T(1024)(128)(4,1)} %bitcast), calls=%async_computation | async-start | bytes 8388608
  54.2 54.5 %copy-start.3 = (bf16[2,256,1024]{2,1,0:T(8,128)(2,1)S(1)}, bf16[2,256,1024]{2,1,0:T(8,128)(2,1)}, u32[]{:S(2)}) copy-start(bf16[2,256,1024]{2,1,0:T(8,128)(2,1)} %du_ref.1) | copy-start | bytes 3145732
  54.3 61.2 %copy-start.4 = (s32[2,520]{1,0:T(2,128)S(1)}, s32[2,520]{1,0:T(2,128)}, u32[]{:S(2)}) copy-start(s32[2,520]{1,0:T(2,128)} %get-tuple-element.58.last_ref) | copy-start | bytes 12484
  54.3 61.2 %copy-start.5 = (s32[2,520]{1,0:T(2,128)S(1)}, s32[2,520]{1,0:T(2,128)}, u32[]{:S(2)}) copy-start(s32[2,520]{1,0:T(2,128)} %get-tuple-element.59.dup_ref) | copy-start | bytes 12484
  54.3 61.2 %copy-start.6 = (s32[8]{0:T(128)S(1)}, s32[8]{0:T(128)}, u32[]{:S(2)}) copy-start(s32[8]{0:T(128)} %get-tuple-element.60.cnt_ref) | copy-start | bytes 100
  73.2 2.7 %slice-start.1 = ((s8[4718592]{0:T(1024)(128)(4,1)}), s8[524288]{0:T(1024)(128)(4,1)S(1)}, s32[]{:S(2)}) async-start(s8[4718592]{0:T(1024)(128)(4,1)} %bitcast), calls=%async_computation.1 | async-start | bytes 1048576
  73.9 2.0 %collective-permute-start.9 = (bf16[128,2304]{1,0:T(8,128)(2,1)S(1)}, bf16[128,2304]{1,0:T(8,128)(2,1)S(1)}, u32[]{:S(2)}, u32[]{:S(2)}) collective-permute-start(bf16[128,2304]{1,0:T(8,128)(2,1)S(1)} %get-tuple-element.49.xm_ref.refs_0_), channel_id=1, source_target_pairs={{0,1},{1,0},{2,3},{3,2},{4,5},{5,4},{6,7},{7,6}} | collective-permute-start | bytes 1769480 | tf_op jit(solution)/shard_map/ppermute | solution.py:293
  74.3 15.4 %collective-permute-start.10 = (bf16[128,2304]{1,0:T(8,128)(2,1)S(1)}, bf16[128,2304]{1,0:T(8,128)(2,1)S(1)}, u32[]{:S(2)}, u32[]{:S(2)}) collective-permute-start(bf16[128,2304]{1,0:T(8,128)(2,1)S(1)} %add.13.tok_ref.xh_ref), channel_id=1, source_target_pairs={{0,2},{1,3},{2,0},{3,1},{4,6},{5,7},{6,4},{7,5}} | collective-permute-start | bytes 1769480 | tf_op jit(solution)/shard_map/ppermute | solution.py:293
  91.6 17.1 %collective-permute-start.11 = (bf16[128,2304]{1,0:T(8,128)(2,1)S(1)}, bf16[128,2304]{1,0:T(8,128)(2,1)S(1)}, u32[]{:S(2)}, u32[]{:S(2)}) collective-permute-start(bf16[128,2304]{1,0:T(8,128)(2,1)S(1)} %get-tuple-element.53.xm_ref), channel_id=1, source_target_pairs={{0,1},{1,0},{2,3},{3,2},{4,5},{5,4},{6,7},{7,6}} | collective-permute-start | bytes 1769480 | tf_op jit(solution)/shard_map/ppermute | solution.py:293
  91.6 9.9 %collective-permute-start.12 = (bf16[64,2304]{1,0:T(8,128)(2,1)S(1)}, bf16[64,2304]{1,0:T(8,128)(2,1)S(1)}, u32[]{:S(2)}, u32[]{:S(2)}) collective-permute-start(bf16[64,2304]{1,0:T(8,128)(2,1)S(1)} %get-tuple-element.61.refs_0_), channel_id=1, source_target_pairs={{0,2},{1,3},{2,0},{3,1},{4,6},{5,7},{6,4},{7,5}} | collective-permute-start | bytes 884744 | tf_op jit(solution)/shard_map/ppermute | solution.py:293
  92.1 16.2 %collective-permute-start.15 = (bf16[64,2304]{1,0:T(8,128)(2,1)S(1)}, bf16[64,2304]{1,0:T(8,128)(2,1)S(1)}, u32[]{:S(2)}, u32[]{:S(2)}) collective-permute-start(bf16[64,2304]{1,0:T(8,128)(2,1)S(1)} %get-tuple-element.62.refs_4_), channel_id=1, source_target_pairs={{0,2},{1,3},{2,0},{3,1},{4,6},{5,7},{6,4},{7,5}} | collective-permute-start | bytes 884744 | tf_op jit(solution)/shard_map/ppermute | solution.py:293
  93.7 1.2 collective-permute-start.18
  94.9 12.7 %collective-permute-start.19 = (f32[1,2304]{1,0:T(1,128)S(1)}, f32[1,2304]{1,0:T(1,128)S(1)}, u32[]{:S(2)}, u32[]{:S(2)}) collective-permute-start(f32[1,2304]{1,0:T(1,128)S(1)} %add.14), channel_id=1, source_target_pairs={{0,2},{1,3},{2,0},{3,1},{4,6},{5,7},{6,4},{7,5}} | collective-permute-start | bytes 27656 | tf_op jit(solution)/shard_map/ppermute | solution.py:293
  95.3 20.1 %collective-permute-start.13 = (bf16[64,2304]{1,0:T(8,128)(2,1)S(1)}, bf16[64,2304]{1,0:T(8,128)(2,1)S(1)}, u32[]{:S(2)}, u32[]{:S(2)}) collective-permute-start(bf16[64,2304]{1,0:T(8,128)(2,1)S(1)} %get-tuple-element.61.refs_0_), channel_id=1, source_target_pairs={{0,1},{1,0},{2,3},{3,2},{4,5},{5,4},{6,7},{7,6}} | collective-permute-start | bytes 884744 | tf_op jit(solution)/shard_map/ppermute | solution.py:293
  101.5 13.9 %collective-permute-start.14 = (bf16[64,2304]{1,0:T(8,128)(2,1)S(1)}, bf16[64,2304]{1,0:T(8,128)(2,1)S(1)}, u32[]{:S(2)}, u32[]{:S(2)}) collective-permute-start(bf16[64,2304]{1,0:T(8,128)(2,1)S(1)} %collective-permute-done.12.refs_1_), channel_id=1, source_target_pairs={{0,1},{1,0},{2,3},{3,2},{4,5},{5,4},{6,7},{7,6}} | collective-permute-start | bytes 884744 | tf_op jit(solution)/shard_map/ppermute | solution.py:293
  107.6 10.3 %collective-permute-start.16 = (bf16[64,2304]{1,0:T(8,128)(2,1)S(1)}, bf16[64,2304]{1,0:T(8,128)(2,1)S(1)}, u32[]{:S(2)}, u32[]{:S(2)}) collective-permute-start(bf16[64,2304]{1,0:T(8,128)(2,1)S(1)} %get-tuple-element.62.refs_4_), channel_id=1, source_target_pairs={{0,1},{1,0},{2,3},{3,2},{4,5},{5,4},{6,7},{7,6}} | collective-permute-start | bytes 884744 | tf_op jit(solution)/shard_map/ppermute | solution.py:293
  108.2 9.7 %collective-permute-start.17 = (bf16[64,2304]{1,0:T(8,128)(2,1)S(1)}, bf16[64,2304]{1,0:T(8,128)(2,1)S(1)}, u32[]{:S(2)}, u32[]{:S(2)}) collective-permute-start(bf16[64,2304]{1,0:T(8,128)(2,1)S(1)} %collective-permute-done.15.refs_5_), channel_id=1, source_target_pairs={{0,1},{1,0},{2,3},{3,2},{4,5},{5,4},{6,7},{7,6}} | collective-permute-start | bytes 884744 | tf_op jit(solution)/shard_map/ppermute | solution.py:293

commit v5 on v4

--- a/solution.py
+++ b/solution.py
@@ -69,22 +69,19 @@
         pltpu.make_async_copy(z, de_ref.at[pl.ds(0, step), :], sem).wait()
 
 
-def zero_kernel(tok_ref, de_in, de_ref, z, sem):
+def zero_kernel(tok_ref, de_ref, z, sem):
     z[...] = jnp.zeros_like(z)
-    half = de_ref.shape[0] // 2
-    zero_start(z, de_ref, half, half, sem)
-    zero_wait(z, de_ref, half, sem)
-
-
-def gather_kernel(tok_ref, ids_ref, emb_ref, k0, s0, k1, s1, last_ref, dup_ref, cnt_ref, de_ref,
-                  buf, tmp, xf, z, lpos, lrow, lnxt, tab, sem, zsem):
+    zero_start(z, de_ref, 0, de_ref.shape[0], sem)
+    zero_wait(z, de_ref, de_ref.shape[0], sem)
+
+
+def gather_kernel(tok_ref, ids_ref, emb_ref, k0, s0, k1, s1, last_ref, dup_ref, cnt_ref,
+                  buf, tmp, xf, lpos, lrow, lnxt, tab, sem):
     k, t = ids_ref.shape
     vl = emb_ref.shape[0]
     h = k0.shape[0]
     tl = t // 4
     r = lax.axis_index("tp")
-    z[...] = jnp.zeros_like(z)
-    zero_start(z, de_ref, 0, vl // 2, zsem)
     n = 0
     for m in range(k):
         def scan(i, n):
@@ -153,7 +150,6 @@
     lax.fori_loop(0, (n + 7) // 8, take, 0)
     for a, ref in enumerate((k0, s0, k1, s1)):
         ref[...] = xf[a * h:(a + 1) * h, :].astype(BF16)
-    zero_wait(z, de_ref, vl // 2, zsem)
 
 
 def dx_kernel(m, xh_ref, z_ref, p0, p1, p2, p3, r0, r1, r2, r3, dres_ref, g_ref, tok_ref, *refs):
@@ -309,21 +305,21 @@
         q1 = perm(p1, sib)
         v1 = perm(r1, sib)
 
-        k0, s0, k1, s1, last, dup, cnt, de = call(
+        k0, s0, k1, s1, last, dup, cnt = call(
             gather_kernel, 60,
-            [S((n, d), BF16)] * 4 + [S((2, 2 * h + 8), jnp.int32)] * 2 + [S((8,), jnp.int32), S((vl, d), F32)],
-            [HBM, SMEM, HBM], [VMEM] * 4 + [SMEM] * 3 + [HBM],
-            [pltpu.VMEM((2 * h, 8, d), BF16), pltpu.VMEM((8, 8, d), F32), pltpu.VMEM((2 * h + 8, d), F32), pltpu.VMEM((256, d), F32)]
-            + [pltpu.SMEM((2 * h + 8,), jnp.int32)] * 3 + [pltpu.SMEM((vl,), jnp.int32), D, D],
-            5_000_000_000, 16 * h * d)(r2, ids, emb)
+            [S((n, d), BF16)] * 4 + [S((2, 2 * h + 8), jnp.int32)] * 2 + [S((8,), jnp.int32)],
+            [HBM, SMEM, HBM], [VMEM] * 4 + [SMEM] * 3,
+            [pltpu.VMEM((2 * h, 8, d), BF16), pltpu.VMEM((8, 8, d), F32), pltpu.VMEM((2 * h + 8, d), F32)]
+            + [pltpu.SMEM((2 * h + 8,), jnp.int32)] * 3 + [pltpu.SMEM((vl,), jnp.int32), D],
+            500_000_000, 16 * h * d)(r2, ids, emb)
         y0 = perm(s0, sib)
         y1 = perm(s1, sib)
         xh0 = k0 + y0
         xh1 = k1 + y1
         z0 = perm(xh0, cross)
         z1 = perm(xh1, cross)
-        de = call(zero_kernel, 8, S((vl, d), F32), [HBM, HBM], HBM,
-                  [pltpu.VMEM((256, d), F32), D], 5_000_000_000, 2 * vl * d, {1: 0})(xh1, de)
+        de = call(zero_kernel, 8, S((vl, d), F32), [SMEM], HBM,
+                  [pltpu.VMEM((256, d), F32), D], 10_000_000_000, 4 * vl * d)(cnt)
 
         def dxk(m, xh, z, tok, more):
             outs = [S((n, d), BF16), S((tl, d), BF16), S((1, d), F32)] + ([S((k, tl, d), BF16)] if m else [])

time: 122 us -> 121 us (level)
  waiting for transfers between devices: 47.6 us -> 33.1 us
  Pallas kernels: 61.2 us -> 73.3 us
  starting transfers between devices: 7.06 us -> 10 us
    ppermute x20, waiting for transfers between devices: 47.6 us -> 33.1 us  [perm(): return lax.ppermute(v, 'tp', p)]
    pallas_call x1, Pallas kernels: 12.3 us -> 24.6 us  [local(): call(zero_kernel, 8, S((vl, d), F32), [SMEM], HBM, [pltpu.VMEM((256, d),...]
    ppermute x20, starting transfers between devices: 7.06 us -> 10 us  [perm(): return lax.ppermute(v, 'tp', p)]
  transfers between devices with their start and end apart: 20 -> 20, of which waited for: 8 -> 8; matrix products, arithmetic and copies ran while one was open for 3% -> 2% of each run, Pallas kernels for 20% -> 31%
where the time goes in v5:
time: 121 us
  Pallas kernels  73.3 us (61%)
  waiting for transfers between devices  33.1 us (27%)
  starting transfers between devices  10 us (8%)
  other arithmetic  1.97 us (2%)
    ppermute x20, waiting for transfers between devices, perm(): return lax.ppermute(v, 'tp', p)  33.1 us
    pallas_call x1, Pallas kernels, local(): call(zero_kernel, 8, S((vl, d), F32), [SMEM], HBM, [pltpu.VMEM((256, d),...  24.6 us
    pallas_call x1, Pallas kernels, local(): call(gather_kernel, 60, [S((n, d), BF16)] * 4 + [S((2, 2 * h + 8), jnp.in...  18.2 us
    ppermute x20, starting transfers between devices, perm(): return lax.ppermute(v, 'tp', p)  10 us
    pallas_call x1, Pallas kernels, local(): call(functools.partial(pdn_kernel, 0, True), 60, [S((n, d1), BF16)] * 4 +...  6.82 us
    pallas_call x1, Pallas kernels, local(): call(proj_kernel, 36, [S((k, t, fc), BF16), S((d, fc), F32), S((8,), jnp....  6.66 us
    pallas_call x1, Pallas kernels, local(): call(functools.partial(pdn_kernel, d1, False), 60, [S((n, d2), BF16)] * 4...  6.16 us
    pallas_call x2, Pallas kernels, scatter(): call(functools.partial(scatter_kernel, m), 16, S((vl, d), F32), [SMEM] *...  5 us
  transfers between devices with their start and end apart: 20, of which 8 were waited for; matrix products, arithmetic and copies ran while one was open for 2% of the time, Pallas kernels for 31%

profile of v5, /device:TPU:0, one launch (start us, length us, event | category | flops | bytes accessed | tf_op | source)
XLA Modules:
  0.0 120.6 jit_solution(9867135206084009885)
XLA Ops:
  0.6 6.8 %shard_map.101 = (bf16[128,1280]{1,0:T(8,128)(2,1)}, bf16[128,1280]{1,0:T(8,128)(2,1)}, bf16[128,1280]{1,0:T(8,128)(2,1)}, bf16[128,1280]{1,0:T(8,128)(2,1)}, bf16[512,1024]{1,0:T(8,128)(2,1)}) custom-call(bf16[2,256,1024]{2,1,0:T(8,128)(2,1)} %du_ref.1, bf16[2304,1024]{1,0:T(8,128)(2,1)} %w_ref.3), custom_call_target="tpu_custom_call" | custom-call | flops 1342177280 | bytes 4980736 | tf_op jit(solution)/shard_map/pallas_call | solution.py:293
  7.5 0.0 copy-start.12
  7.5 6.2 %shard_map.102 = (bf16[128,1024]{1,0:T(8,128)(2,1)}, bf16[128,1024]{1,0:T(8,128)(2,1)}, bf16[128,1024]{1,0:T(8,128)(2,1)}, bf16[128,1024]{1,0:T(8,128)(2,1)}) custom-call(bf16[512,1024]{1,0:T(8,128)(2,1)} %get-tuple-element.34.refs_0_, bf16[2304,1024]{1,0:T(8,128)(2,1)} %w_ref.3), custom_call_target="tpu_custom_call" | custom-call | flops 1073741824 | bytes 4194304 | tf_op jit(solution)/shard_map/pallas_call | solution.py:297
  13.7 18.2 %shard_map.103 = (bf16[128,2304]{1,0:T(8,128)(2,1)}, bf16[128,2304]{1,0:T(8,128)(2,1)}, bf16[128,2304]{1,0:T(8,128)(2,1)}, bf16[128,2304]{1,0:T(8,128)(2,1)}, s3...) custom-call(bf16[128,1024]{1,0:T(8,128)(2,1)} %get-tuple-element.35.tok_ref, s32[2,256]{1,0:T(2,128)} %ids_ref.1, ...), custom_call_target="tpu_custom_call" | custom-call | flops 500000000 | bytes 9437184 | tf_op jit(solution)/shard_map/pallas_call | solution.py:308
  31.9 0.0 collective-permute-start
  31.9 0.5 collective-permute-start.5
  32.4 0.3 collective-permute-start.6
  32.7 0.0 copy-done.14
  32.7 1.1 collective-permute-start.7
  33.8 0.7 collective-permute-start.2
  34.6 0.0 collective-permute-done
  34.6 0.0 copy-done.12
  34.6 0.3 collective-permute-start.3
  34.9 1.2 add.12.xh_ref
  36.1 0.0 collective-permute-done.5.r1
  36.1 1.1 collective-permute-start.4
  37.2 4.4 %collective-permute-done.6.r2 = bf16[128,1024]{1,0:T(8,128)(2,1)S(1)} collective-permute-done((bf16[128,1024]{1,0:T(8,128)(2,1)S(1)}, bf16[128,1024]{1,0:T(8,128)(2,1)S(1)}, u32[]{:S(2)}, u32[]{:S(2)}) %collective-permute-start.6) | collective-permute-done | bytes 262176 | tf_op jit(solution)/shard_map/ppermute | solution.py:289
  41.6 0.0 collective-permute-start.9
  41.6 3.8 %collective-permute-done.7.r3 = bf16[128,1024]{1,0:T(8,128)(2,1)S(1)} collective-permute-done((bf16[128,1024]{1,0:T(8,128)(2,1)S(1)}, bf16[128,1024]{1,0:T(8,128)(2,1)S(1)}, u32[]{:S(2)}, u32[]{:S(2)}) %collective-permute-start.7) | collective-permute-done | bytes 262176 | tf_op jit(solution)/shard_map/ppermute | solution.py:289
  45.4 1.4 %collective-permute-start.1 = (bf16[128,2304]{1,0:T(8,128)(2,1)S(1)}, bf16[128,2304]{1,0:T(8,128)(2,1)S(1)}, u32[]{:S(2)}, u32[]{:S(2)}) collective-permute-start(bf16[128,2304]{1,0:T(8,128)(2,1)S(1)} %add.12.xh_ref), channel_id=1, source_target_pairs={{0,2},{1,3},{2,0},{3,1},{4,6},{5,7},{6,4},{7,5}} | collective-permute-start | bytes 1769480 | tf_op jit(solution)/shard_map/ppermute | solution.py:289
  46.8 0.7 copy-done.6
  47.4 0.0 slice-start
  47.4 24.6 %shard_map.104.tok_ref.refs_5_ = f32[8192,2304]{1,0:T(8,128)} custom-call(s32[8]{0:T(128)S(1)} %copy-done.6), custom_call_target="tpu_custom_call" | custom-call | flops 10000000000 | bytes 75497472 | tf_op jit(solution)/shard_map/pallas_call | solution.py:321
  72.1 0.0 collective-permute-done.2.p1
  72.1 0.0 collective-permute-done.3.p2
  72.1 0.0 collective-permute-done.4.p3
  72.1 0.8 collective-permute-done.1.z_ref
  73.0 0.0 copy-done.2
  73.0 0.0 copy-start.8
  73.0 0.0 slice-start.1
  73.0 0.0 copy-start.3
  73.0 0.0 copy-start.4
  73.0 0.7 shard_map.105
  73.7 0.0 collective-permute-start.8
  73.8 0.0 collective-permute-done.9
  73.8 0.3 copy-done.8
  74.0 0.1 add.13.xh_ref
  74.2 0.9 collective-permute-start.10
  75.1 0.6 collective-permute-done.8.xo_ref
  75.8 3.3 %shard_map.106 = (bf16[2,256,1024]{2,1,0:T(8,128)(2,1)}, bf16[256,2304]{1,0:T(8,128)(2,1)S(1)}, s32[8]{0:T(128)S(1)}) custom-call(bf16[128,2304]{1,0:T(8,128)(2,1)S(1)} %get-tuple-element.46.xm_ref.refs_0_, bf16[128,2304]{1,0:T(8,128)(2,1)S(1)} %collective-permute-done.8.xo_ref, bf16[1,2304]{1,0:T(2,128)(2,1)S(1)} %reshape.16.g_ref, ...), custom_call_target="tpu_custom_call" | custom-call | flops 1207959552 | bytes 4718592 | tf_op jit(solution)/shard_map/pallas_call | solution.py:333
  79.1 10.6 %collective-permute-done.10.z_ref = bf16[128,2304]{1,0:T(8,128)(2,1)S(1)} collective-permute-done((bf16[128,2304]{1,0:T(8,128)(2,1)S(1)}, bf16[128,2304]{1,0:T(8,128)(2,1)S(1)}, u32[]{:S(2)}, u32[]{:S(2)}) %collective-permute-start.10) | collective-permute-done | bytes 589856 | tf_op jit(solution)/shard_map/ppermute | solution.py:289
  89.7 1.9 %shard_map.107 = (bf16[128,2304]{1,0:T(8,128)(2,1)S(1)}, bf16[64,2304]{1,0:T(8,128)(2,1)S(1)}, f32[1,2304]{1,0:T(1,128)S(1)}, bf16[2,64,2304]{2,1,0:T(8,128)(2,1)}) custom-call(bf16[128,2304]{1,0:T(8,128)(2,1)S(1)} %add.13.xh_ref, bf16[128,2304]{1,0:T(8,128)(2,1)S(1)} %collective-permute-done.10.z_ref, bf16[128,1280]{1,0:T(8,128)(2,1)S(1)} %copy-done.1, ...), custom_call_target="tpu_custom_call" | custom-call | flops 8847360 | bytes 4718592 | tf_op jit(solution)/shard_map/pallas_call | solution.py:326
  91.6 0.0 collective-permute-start.11
  91.6 1.0 collective-permute-start.12
  92.6 1.0 collective-permute-start.15
  93.6 0.0 collective-permute-start.18
  93.6 1.2 collective-permute-done.18
  94.8 1.0 collective-permute-start.19
  95.8 0.0 collective-permute-start.13
  95.8 5.6 %collective-permute-done.12.refs_1_ = bf16[64,2304]{1,0:T(8,128)(2,1)S(1)} collective-permute-done((bf16[64,2304]{1,0:T(8,128)(2,1)S(1)}, bf16[64,2304]{1,0:T(8,128)(2,1)S(1)}, u32[]{:S(2)}, u32[]{:S(2)}) %collective-permute-start.12) | collective-permute-done | bytes 294944 | tf_op jit(solution)/shard_map/ppermute | solution.py:289
  101.5 0.0 collective-permute-start.14
  101.5 6.1 %collective-permute-done.19 = f32[1,2304]{1,0:T(1,128)S(1)} collective-permute-done((f32[1,2304]{1,0:T(1,128)S(1)}, f32[1,2304]{1,0:T(1,128)S(1)}, u32[]{:S(2)}, u32[]{:S(2)}) %collective-permute-start.19) | collective-permute-done | bytes 9248 | tf_op jit(solution)/shard_map/ppermute | solution.py:289
  107.5 0.0 collective-permute-start.16
  107.5 0.6 add_reduce_fusion
  108.2 0.0 collective-permute-done.15.refs_5_
  108.2 0.5 collective-permute-start.17
  108.7 0.0 collective-permute-done.11.xo_ref
  108.7 6.7 %shard_map.108 = (bf16[2,256,1024]{2,1,0:T(8,128)(2,1)}, f32[2304,1024]{1,0:T(8,128)}, s32[8]{0:T(128)S(1)}) custom-call(bf16[256,2304]{1,0:T(8,128)(2,1)S(1)} %get-tuple-element.48.n0_ref, bf16[128,2304]{1,0:T(8,128)(2,1)S(1)} %get-tuple-element.52.xm_ref, bf16[128,2304]{1,0:T(8,128)(2,1)S(1)} %collective-permute-done.11.xo_ref, ...), custom_call_target="tpu_custom_call", output_to_operand_aliasing={{0}: (6, {})} | custom-call | flops 3623878656 | bytes 14155776 | tf_op jit(solution)/shard_map/pallas_call | solution.py:345
  115.4 0.0 collective-permute-done.13.refs_2_
  115.4 0.0 collective-permute-done.14.refs_3_
  115.4 2.4 %shard_map.109.refs_9_ = f32[8192,2304]{1,0:T(8,128)} custom-call(s32[2,520]{1,0:T(2,128)S(1)} %copy-done.4, s32[2,520]{1,0:T(2,128)S(1)} %copy-done.5, s32[8]{0:T(128)S(1)} %copy-done.7, bf16[64,2304]{1,0:T(8,128)(2,1)S(1)} %get-tuple-element.59.refs_0_, bf16[64,2304]{1,0:T(8,128)(2,1)S(1)} %collective-permute-done.12.refs_1_, ...), custom_call_target="tpu_custom_call", output_to_operand_aliasing={{}: (8, {})} | custom-call | flops 4718592 | bytes 4718592 | tf_op jit(solution)/shard_map/pallas_call | solution.py:353
  117.8 0.0 collective-permute-done.16.refs_6_
  117.8 0.0 collective-permute-done.17.refs_7_
  117.8 2.6 %shard_map.110 = f32[8192,2304]{1,0:T(8,128)} custom-call(s32[2,520]{1,0:T(2,128)S(1)} %copy-done.4, s32[2,520]{1,0:T(2,128)S(1)} %copy-done.5, s32[8]{0:T(128)S(1)} %copy-done.7, bf16[64,2304]{1,0:T(8,128)(2,1)S(1)} %get-tuple-element.59.refs_0_, bf16[64,2304]{1,0:T(8,128)(2,1)S(1)} %collective-permute-done.12.refs_1_, ...), custom_call_target="tpu_custom_call", output_to_operand_aliasing={{}: (12, {})} | custom-call | flops 4718592 | bytes 4718592 | tf_op jit(solution)/shard_map/pallas_call | solution.py:353
  (28 shorter events, 0.1 us)
Async XLA Ops:
  7.5 26.4 %copy-start.13 = (bf16[128,1280]{1,0:T(8,128)(2,1)S(1)}, bf16[128,1280]{1,0:T(8,128)(2,1)}, u32[]{:S(2)}) copy-start(bf16[128,1280]{1,0:T(8,128)(2,1)} %get-tuple-element.39) | copy-start | bytes 983044
  7.5 27.1 %copy-start.12 = (bf16[128,1280]{1,0:T(8,128)(2,1)S(1)}, bf16[128,1280]{1,0:T(8,128)(2,1)}, u32[]{:S(2)}) copy-start(bf16[128,1280]{1,0:T(8,128)(2,1)} %get-tuple-element.40) | copy-start | bytes 983044
  7.5 28.6 %copy-start.11 = (bf16[128,1280]{1,0:T(8,128)(2,1)S(1)}, bf16[128,1280]{1,0:T(8,128)(2,1)}, u32[]{:S(2)}) copy-start(bf16[128,1280]{1,0:T(8,128)(2,1)} %get-tuple-element.41) | copy-start | bytes 983044
  13.7 18.3 %copy-start.15 = (bf16[128,1024]{1,0:T(8,128)(2,1)S(1)}, bf16[128,1024]{1,0:T(8,128)(2,1)}, u32[]{:S(2)}) copy-start(bf16[128,1024]{1,0:T(8,128)(2,1)} %get-tuple-element.43) | copy-start | bytes 786436
  13.7 18.7 %copy-start.9 = (bf16[128,1024]{1,0:T(8,128)(2,1)S(1)}, bf16[128,1024]{1,0:T(8,128)(2,1)}, u32[]{:S(2)}) copy-start(bf16[128,1024]{1,0:T(8,128)(2,1)} %get-tuple-element.35.tok_ref) | copy-start | bytes 786436
  13.7 19.1 %copy-start.14 = (bf16[128,1024]{1,0:T(8,128)(2,1)S(1)}, bf16[128,1024]{1,0:T(8,128)(2,1)}, u32[]{:S(2)}) copy-start(bf16[128,1024]{1,0:T(8,128)(2,1)} %get-tuple-element.44) | copy-start | bytes 786436
  31.9 2.7 %collective-permute-start = (bf16[128,2304]{1,0:T(8,128)(2,1)}, bf16[128,2304]{1,0:T(8,128)(2,1)S(1)}, u32[]{:S(2)}, u32[]{:S(2)}) collective-permute-start(bf16[128,2304]{1,0:T(8,128)(2,1)} %get-tuple-element.37), channel_id=1, source_target_pairs={{0,1},{1,0},{2,3},{3,2},{4,5},{5,4},{6,7},{7,6}} | collective-permute-start | bytes 1769480 | tf_op jit(solution)/shard_map/ppermute | solution.py:289
  31.9 4.2 %collective-permute-start.5 = (bf16[128,1024]{1,0:T(8,128)(2,1)S(1)}, bf16[128,1024]{1,0:T(8,128)(2,1)S(1)}, u32[]{:S(2)}, u32[]{:S(2)}) collective-permute-start(bf16[128,1024]{1,0:T(8,128)(2,1)S(1)} %copy-done.15), channel_id=1, source_target_pairs={{0,1},{1,0},{2,3},{3,2},{4,5},{5,4},{6,7},{7,6}} | collective-permute-start | bytes 786440 | tf_op jit(solution)/shard_map/ppermute | solution.py:289
  32.4 9.2 %collective-permute-start.6 = (bf16[128,1024]{1,0:T(8,128)(2,1)S(1)}, bf16[128,1024]{1,0:T(8,128)(2,1)S(1)}, u32[]{:S(2)}, u32[]{:S(2)}) collective-permute-start(bf16[128,1024]{1,0:T(8,128)(2,1)S(1)} %copy-done.9), channel_id=1, source_target_pairs={{0,2},{1,3},{2,0},{3,1},{4,6},{5,7},{6,4},{7,5}} | collective-permute-start | bytes 786440 | tf_op jit(solution)/shard_map/ppermute | solution.py:289
  32.7 12.6 %collective-permute-start.7 = (bf16[128,1024]{1,0:T(8,128)(2,1)S(1)}, bf16[128,1024]{1,0:T(8,128)(2,1)S(1)}, u32[]{:S(2)}, u32[]{:S(2)}) collective-permute-start(bf16[128,1024]{1,0:T(8,128)(2,1)S(1)} %copy-done.14), channel_id=1, source_target_pairs={{0,3},{1,2},{2,1},{3,0},{4,7},{5,6},{6,5},{7,4}} | collective-permute-start | bytes 786440 | tf_op jit(solution)/shard_map/ppermute | solution.py:289
  33.8 38.3 %collective-permute-start.2 = (bf16[128,1280]{1,0:T(8,128)(2,1)S(1)}, bf16[128,1280]{1,0:T(8,128)(2,1)S(1)}, u32[]{:S(2)}, u32[]{:S(2)}) collective-permute-start(bf16[128,1280]{1,0:T(8,128)(2,1)S(1)} %copy-done.13), channel_id=1, source_target_pairs={{0,1},{1,0},{2,3},{3,2},{4,5},{5,4},{6,7},{7,6}} | collective-permute-start | bytes 983048 | tf_op jit(solution)/shard_map/ppermute | solution.py:289
  34.6 37.5 %collective-permute-start.3 = (bf16[128,1280]{1,0:T(8,128)(2,1)S(1)}, bf16[128,1280]{1,0:T(8,128)(2,1)S(1)}, u32[]{:S(2)}, u32[]{:S(2)}) collective-permute-start(bf16[128,1280]{1,0:T(8,128)(2,1)S(1)} %copy-done.12), channel_id=1, source_target_pairs={{0,2},{1,3},{2,0},{3,1},{4,6},{5,7},{6,4},{7,5}} | collective-permute-start | bytes 983048 | tf_op jit(solution)/shard_map/ppermute | solution.py:289
  36.1 36.0 %collective-permute-start.4 = (bf16[128,1280]{1,0:T(8,128)(2,1)S(1)}, bf16[128,1280]{1,0:T(8,128)(2,1)S(1)}, u32[]{:S(2)}, u32[]{:S(2)}) collective-permute-start(bf16[128,1280]{1,0:T(8,128)(2,1)S(1)} %copy-done.11), channel_id=1, source_target_pairs={{0,3},{1,2},{2,1},{3,0},{4,7},{5,6},{6,5},{7,4}} | collective-permute-start | bytes 983048 | tf_op jit(solution)/shard_map/ppermute | solution.py:289
  41.6 32.2 %collective-permute-start.9 = (bf16[128,2304]{1,0:T(8,128)(2,1)}, bf16[128,2304]{1,0:T(8,128)(2,1)S(1)}, u32[]{:S(2)}, u32[]{:S(2)}) collective-permute-start(bf16[128,2304]{1,0:T(8,128)(2,1)} %get-tuple-element.50), channel_id=1, source_target_pairs={{0,1},{1,0},{2,3},{3,2},{4,5},{5,4},{6,7},{7,6}} | collective-permute-start | bytes 1769480 | tf_op jit(solution)/shard_map/ppermute | solution.py:289
  45.4 27.6 %collective-permute-start.1 = (bf16[128,2304]{1,0:T(8,128)(2,1)S(1)}, bf16[128,2304]{1,0:T(8,128)(2,1)S(1)}, u32[]{:S(2)}, u32[]{:S(2)}) collective-permute-start(bf16[128,2304]{1,0:T(8,128)(2,1)S(1)} %add.12.xh_ref), channel_id=1, source_target_pairs={{0,2},{1,3},{2,0},{3,1},{4,6},{5,7},{6,4},{7,5}} | collective-permute-start | bytes 1769480 | tf_op jit(solution)/shard_map/ppermute | solution.py:289
  46.8 0.7 copy-start.6
  47.4 24.7 %copy-start.10 = (bf16[2304]{0:T(1024)(128)(2,1)S(1)}, bf16[2304]{0:T(1024)(128)(2,1)}, u32[]{:S(2)}) copy-start(bf16[2304]{0:T(1024)(128)(2,1)} %param.8) | copy-start | bytes 13828
  47.4 25.6 %copy-start = (bf16[2,64,2304]{2,1,0:T(8,128)(2,1)S(1)}, bf16[2,64,2304]{2,1,0:T(8,128)(2,1)}, u32[]{:S(2)}) copy-start(bf16[2,64,2304]{2,1,0:T(8,128)(2,1)} %dres_ref.3) | copy-start | bytes 1769476
  47.4 25.6 %copy-start.1 = (bf16[128,1280]{1,0:T(8,128)(2,1)S(1)}, bf16[128,1280]{1,0:T(8,128)(2,1)}, u32[]{:S(2)}) copy-start(bf16[128,1280]{1,0:T(8,128)(2,1)} %get-tuple-element.38.p0) | copy-start | bytes 983044
  47.4 25.6 %copy-start.2 = (bf16[128,1024]{1,0:T(8,128)(2,1)S(1)}, bf16[128,1024]{1,0:T(8,128)(2,1)}, u32[]{:S(2)}) copy-start(bf16[128,1024]{1,0:T(8,128)(2,1)} %get-tuple-element.42.r0) | copy-start | bytes 786436
  47.4 28.3 %slice-start = ((s8[4718592]{0:T(1024)(128)(4,1)}), s8[4194304]{0:T(1024)(128)(4,1)S(1)}, s32[]{:S(2)}) async-start(s8[4718592]{0:T(1024)(128)(4,1)} %bitcast), calls=%async_computation | async-start | bytes 8388608
  73.0 1.1 copy-start.8
  73.0 2.8 %slice-start.1 = ((s8[4718592]{0:T(1024)(128)(4,1)}), s8[524288]{0:T(1024)(128)(4,1)S(1)}, s32[]{:S(2)}) async-start(s8[4718592]{0:T(1024)(128)(4,1)} %bitcast), calls=%async_computation.1 | async-start | bytes 1048576
  73.0 35.7 %copy-start.3 = (bf16[2,256,1024]{2,1,0:T(8,128)(2,1)S(1)}, bf16[2,256,1024]{2,1,0:T(8,128)(2,1)}, u32[]{:S(2)}) copy-start(bf16[2,256,1024]{2,1,0:T(8,128)(2,1)} %du_ref.1) | copy-start | bytes 3145732
  73.0 42.4 %copy-start.4 = (s32[2,520]{1,0:T(2,128)S(1)}, s32[2,520]{1,0:T(2,128)}, u32[]{:S(2)}) copy-start(s32[2,520]{1,0:T(2,128)} %get-tuple-element.57.last_ref) | copy-start | bytes 12484
  73.0 42.4 %copy-start.5 = (s32[2,520]{1,0:T(2,128)S(1)}, s32[2,520]{1,0:T(2,128)}, u32[]{:S(2)}) copy-start(s32[2,520]{1,0:T(2,128)} %get-tuple-element.58.dup_ref) | copy-start | bytes 12484
  73.0 42.4 %copy-start.7 = (s32[8]{0:T(128)S(1)}, s32[8]{0:T(128)}, u32[]{:S(2)}) copy-start(s32[8]{0:T(128)} %get-tuple-element.45.tok_ref.cnt_ref) | copy-start | bytes 100
  73.7 2.0 %collective-permute-start.8 = (bf16[128,2304]{1,0:T(8,128)(2,1)S(1)}, bf16[128,2304]{1,0:T(8,128)(2,1)S(1)}, u32[]{:S(2)}, u32[]{:S(2)}) collective-permute-start(bf16[128,2304]{1,0:T(8,128)(2,1)S(1)} %get-tuple-element.46.xm_ref.refs_0_), channel_id=1, source_target_pairs={{0,1},{1,0},{2,3},{3,2},{4,5},{5,4},{6,7},{7,6}} | collective-permute-start | bytes 1769480 | tf_op jit(solution)/shard_map/ppermute | solution.py:289
  74.2 15.5 %collective-permute-start.10 = (bf16[128,2304]{1,0:T(8,128)(2,1)S(1)}, bf16[128,2304]{1,0:T(8,128)(2,1)S(1)}, u32[]{:S(2)}, u32[]{:S(2)}) collective-permute-start(bf16[128,2304]{1,0:T(8,128)(2,1)S(1)} %add.13.xh_ref), channel_id=1, source_target_pairs={{0,2},{1,3},{2,0},{3,1},{4,6},{5,7},{6,4},{7,5}} | collective-permute-start | bytes 1769480 | tf_op jit(solution)/shard_map/ppermute | solution.py:289
  91.6 17.1 %collective-permute-start.11 = (bf16[128,2304]{1,0:T(8,128)(2,1)S(1)}, bf16[128,2304]{1,0:T(8,128)(2,1)S(1)}, u32[]{:S(2)}, u32[]{:S(2)}) collective-permute-start(bf16[128,2304]{1,0:T(8,128)(2,1)S(1)} %get-tuple-element.52.xm_ref), channel_id=1, source_target_pairs={{0,1},{1,0},{2,3},{3,2},{4,5},{5,4},{6,7},{7,6}} | collective-permute-start | bytes 1769480 | tf_op jit(solution)/shard_map/ppermute | solution.py:289
  91.6 9.9 %collective-permute-start.12 = (bf16[64,2304]{1,0:T(8,128)(2,1)S(1)}, bf16[64,2304]{1,0:T(8,128)(2,1)S(1)}, u32[]{:S(2)}, u32[]{:S(2)}) collective-permute-start(bf16[64,2304]{1,0:T(8,128)(2,1)S(1)} %get-tuple-element.59.refs_0_), channel_id=1, source_target_pairs={{0,2},{1,3},{2,0},{3,1},{4,6},{5,7},{6,4},{7,5}} | collective-permute-start | bytes 884744 | tf_op jit(solution)/shard_map/ppermute | solution.py:289
  92.6 15.6 %collective-permute-start.15 = (bf16[64,2304]{1,0:T(8,128)(2,1)S(1)}, bf16[64,2304]{1,0:T(8,128)(2,1)S(1)}, u32[]{:S(2)}, u32[]{:S(2)}) collective-permute-start(bf16[64,2304]{1,0:T(8,128)(2,1)S(1)} %get-tuple-element.60.refs_4_), channel_id=1, source_target_pairs={{0,2},{1,3},{2,0},{3,1},{4,6},{5,7},{6,4},{7,5}} | collective-permute-start | bytes 884744 | tf_op jit(solution)/shard_map/ppermute | solution.py:289
  93.6 1.2 collective-permute-start.18
  94.8 12.7 %collective-permute-start.19 = (f32[1,2304]{1,0:T(1,128)S(1)}, f32[1,2304]{1,0:T(1,128)S(1)}, u32[]{:S(2)}, u32[]{:S(2)}) collective-permute-start(f32[1,2304]{1,0:T(1,128)S(1)} %add.14), channel_id=1, source_target_pairs={{0,2},{1,3},{2,0},{3,1},{4,6},{5,7},{6,4},{7,5}} | collective-permute-start | bytes 27656 | tf_op jit(solution)/shard_map/ppermute | solution.py:289
  95.8 19.5 %collective-permute-start.13 = (bf16[64,2304]{1,0:T(8,128)(2,1)S(1)}, bf16[64,2304]{1,0:T(8,128)(2,1)S(1)}, u32[]{:S(2)}, u32[]{:S(2)}) collective-permute-start(bf16[64,2304]{1,0:T(8,128)(2,1)S(1)} %get-tuple-element.59.refs_0_), channel_id=1, source_target_pairs={{0,1},{1,0},{2,3},{3,2},{4,5},{5,4},{6,7},{7,6}} | collective-permute-start | bytes 884744 | tf_op jit(solution)/shard_map/ppermute | solution.py:289
  101.5 13.9 %collective-permute-start.14 = (bf16[64,2304]{1,0:T(8,128)(2,1)S(1)}, bf16[64,2304]{1,0:T(8,128)(2,1)S(1)}, u32[]{:S(2)}, u32[]{:S(2)}) collective-permute-start(bf16[64,2304]{1,0:T(8,128)(2,1)S(1)} %collective-permute-done.12.refs_1_), channel_id=1, source_target_pairs={{0,1},{1,0},{2,3},{3,2},{4,5},{5,4},{6,7},{7,6}} | collective-permute-start | bytes 884744 | tf_op jit(solution)/shard_map/ppermute | solution.py:289
  107.5 10.3 %collective-permute-start.16 = (bf16[64,2304]{1,0:T(8,128)(2,1)S(1)}, bf16[64,2304]{1,0:T(8,128)(2,1)S(1)}, u32[]{:S(2)}, u32[]{:S(2)}) collective-permute-start(bf16[64,2304]{1,0:T(8,128)(2,1)S(1)} %get-tuple-element.60.refs_4_), channel_id=1, source_target_pairs={{0,1},{1,0},{2,3},{3,2},{4,5},{5,4},{6,7},{7,6}} | collective-permute-start | bytes 884744 | tf_op jit(solution)/shard_map/ppermute | solution.py:289
  108.2 9.7 %collective-permute-start.17 = (bf16[64,2304]{1,0:T(8,128)(2,1)S(1)}, bf16[64,2304]{1,0:T(8,128)(2,1)S(1)}, u32[]{:S(2)}, u32[]{:S(2)}) collective-permute-start(bf16[64,2304]{1,0:T(8,128)(2,1)S(1)} %collective-permute-done.15.refs_5_), channel_id=1, source_target_pairs={{0,1},{1,0},{2,3},{3,2},{4,5},{5,4},{6,7},{7,6}} | collective-permute-start | bytes 884744 | tf_op jit(solution)/shard_map/ppermute | solution.py:289

commit v6 on v5

--- a/solution.py
+++ b/solution.py
@@ -69,14 +69,43 @@
         pltpu.make_async_copy(z, de_ref.at[pl.ds(0, step), :], sem).wait()
 
 
-def zero_kernel(tok_ref, de_ref, z, sem):
+def zero_kernel(lpos, lrow, cnt, last_ref, dup_ref, out_ref, de_ref, z, lnxt, tab, sem):
     z[...] = jnp.zeros_like(z)
     zero_start(z, de_ref, 0, de_ref.shape[0], sem)
+    n = cnt[0]
+    t = lnxt.shape[0] - 8
+
+    def link(i, c):
+        v = lrow[i]
+        p = tab[v]
+        ok = jnp.logical_and(p >= 0, p < i)
+        p = jnp.where(ok, p, 0)
+        ok = jnp.logical_and(ok, lrow[p] == v)
+        lnxt[i] = -1
+        lnxt[jnp.where(ok, p, t)] = i
+        tab[v] = i
+        return c
+
+    lax.fori_loop(0, n, link, 0)
+
+    def lists(i, c):
+        nl, nd, n0 = c
+        x = lnxt[i]
+        end = (x < 0).astype(jnp.int32)
+        last_ref[0, nl] = lpos[i]
+        last_ref[1, nl] = lrow[i]
+        dup_ref[0, nd] = lpos[i]
+        dup_ref[1, nd] = lpos[jnp.maximum(x, 0)]
+        return nl + end, nd + 1 - end, n0 + end * (lpos[i] < t // 2).astype(jnp.int32)
+
+    nl, nd, n0 = lax.fori_loop(0, n, lists, (0, 0, 0))
+    out_ref[0] = nl
+    out_ref[1] = nd
+    out_ref[2] = n0
     zero_wait(z, de_ref, de_ref.shape[0], sem)
 
 
-def gather_kernel(tok_ref, ids_ref, emb_ref, k0, s0, k1, s1, last_ref, dup_ref, cnt_ref,
-                  buf, tmp, xf, lpos, lrow, lnxt, tab, sem):
+def gather_kernel(tok_ref, ids_ref, emb_ref, k0, s0, k1, s1, lpos, lrow, cnt, buf, tmp, xf, lst, sem):
     k, t = ids_ref.shape
     vl = emb_ref.shape[0]
     h = k0.shape[0]
@@ -85,19 +114,20 @@
     n = 0
     for m in range(k):
         def scan(i, n):
-            v = ids_ref[m, i] - r * vl
-            q = i // tl
-            lpos[n] = m * t + ((q ^ r) & 1) * h + (q >> 1) * tl + (i & (tl - 1))
-            lrow[n] = v
-            return n + jnp.logical_and(v >= 0, v < vl).astype(jnp.int32)
-
-        n = lax.fori_loop(0, t, scan, n, unroll=8)
+            lst[n] = m * t + i
+            return n + (lax.shift_right_logical(ids_ref[m, i], vl.bit_length() - 1) == r).astype(jnp.int32)
+
+        n = lax.fori_loop(0, t, scan, n, unroll=16)
+    cnt[0] = n
 
     def start(i, c):
-        v = lrow[i]
-        b = pl.multiple_of((v >> 3) << 3, 8)
-        pltpu.make_async_copy(emb_ref.at[pl.ds(b, 8), :], buf.at[i], sem).start()
-        lnxt[i] = -1
+        j = lst[i]
+        m = j // t
+        v = ids_ref[m, j & (t - 1)] - r * vl
+        q = (j & (t - 1)) // tl
+        pltpu.make_async_copy(emb_ref.at[pl.ds(pl.multiple_of((v >> 3) << 3, 8), 8), :], buf.at[i], sem).start()
+        lpos[i] = m * t + ((q ^ r) & 1) * h + (q >> 1) * tl + (j & (tl - 1))
+        lrow[i] = v
         return c
 
     lax.fori_loop(0, n, start, 0)
@@ -105,33 +135,6 @@
         lpos[n + a] = k * t
         lrow[n + a] = 0
     xf[...] = jnp.zeros_like(xf)
-
-    def link(i, c):
-        v = lrow[i]
-        p = tab[v]
-        ok = jnp.logical_and(p >= 0, p < i)
-        p = jnp.where(ok, p, 0)
-        ok = jnp.logical_and(ok, lrow[p] == v)
-        lnxt[jnp.where(ok, p, k * t)] = i
-        tab[v] = i
-        return c
-
-    lax.fori_loop(0, n, link, 0)
-
-    def lists(i, c):
-        nl, nd, n0 = c
-        x = lnxt[i]
-        end = (x < 0).astype(jnp.int32)
-        last_ref[0, nl] = lpos[i]
-        last_ref[1, nl] = lrow[i]
-        dup_ref[0, nd] = lpos[i]
-        dup_ref[1, nd] = lpos[jnp.maximum(x, 0)]
-        return nl + end, nd + 1 - end, n0 + end * (lpos[i] < t).astype(jnp.int32)
-
-    nl, nd, n0 = lax.fori_loop(0, n, lists, (0, 0, 0))
-    cnt_ref[0] = nl
-    cnt_ref[1] = nd
-    cnt_ref[2] = n0
 
     def wait(i, c):
         pltpu.make_async_copy(emb_ref.at[pl.ds(0, 8), :], buf.at[0], sem).wait()
@@ -305,12 +308,12 @@
         q1 = perm(p1, sib)
         v1 = perm(r1, sib)
 
-        k0, s0, k1, s1, last, dup, cnt = call(
+        k0, s0, k1, s1, lpos, lrow, nown = call(
             gather_kernel, 60,
-            [S((n, d), BF16)] * 4 + [S((2, 2 * h + 8), jnp.int32)] * 2 + [S((8,), jnp.int32)],
+            [S((n, d), BF16)] * 4 + [S((2 * h + 8,), jnp.int32)] * 2 + [S((8,), jnp.int32)],
             [HBM, SMEM, HBM], [VMEM] * 4 + [SMEM] * 3,
             [pltpu.VMEM((2 * h, 8, d), BF16), pltpu.VMEM((8, 8, d), F32), pltpu.VMEM((2 * h + 8, d), F32)]
-            + [pltpu.SMEM((2 * h + 8,), jnp.int32)] * 3 + [pltpu.SMEM((vl,), jnp.int32), D],
+            + [pltpu.SMEM((2 * h + 8,), jnp.int32), D],
             500_000_000, 16 * h * d)(r2, ids, emb)
         y0 = perm(s0, sib)
         y1 = perm(s1, sib)
@@ -318,8 +321,11 @@
         xh1 = k1 + y1
         z0 = perm(xh0, cross)
         z1 = perm(xh1, cross)
-        de = call(zero_kernel, 8, S((vl, d), F32), [SMEM], HBM,
-                  [pltpu.VMEM((256, d), F32), D], 10_000_000_000, 4 * vl * d)(cnt)
+        last, dup, cnt, de = call(
+            zero_kernel, 8, [S((2, 2 * h + 8), jnp.int32)] * 2 + [S((8,), jnp.int32), S((vl, d), F32)],
+            [SMEM] * 3, [SMEM] * 3 + [HBM],
+            [pltpu.VMEM((256, d), F32), pltpu.SMEM((2 * h + 8,), jnp.int32), pltpu.SMEM((vl,), jnp.int32), D],
+            10_000_000_000, 4 * vl * d)(lpos, lrow, nown)
 
         def dxk(m, xh, z, tok, more):
             outs = [S((n, d), BF16), S((tl, d), BF16), S((1, d), F32)] + ([S((k, tl, d), BF16)] if m else [])

time: 121 us -> 116 us (0.959)
  Pallas kernels: 73.3 us -> 67 us
    pallas_call x2, Pallas kernels: 42.8 us -> 36.5 us  [the longest x1 25.1 us: local(): call(zero_kernel, 8, [S((2, 2 * h + 8), jnp.int32)] * 2 + [S((8,), jnp.in...]
  transfers between devices with their start and end apart: 20 -> 20, of which waited for: 8 -> 7; matrix products, arithmetic and copies ran while one was open for 2% -> 2% of each run, Pallas kernels for 31% -> 33%
where the time goes in v6:
time: 116 us
  Pallas kernels  67 us (58%)
  waiting for transfers between devices  33.2 us (29%)
  starting transfers between devices  10.4 us (9%)
  local copies, waits for them, and re-layouts  2.06 us (2%)
  other arithmetic  1.97 us (2%)
    ppermute x20, waiting for transfers between devices, perm(): return lax.ppermute(v, 'tp', p)  33.2 us
    pallas_call x1, Pallas kernels, local(): call(zero_kernel, 8, [S((2, 2 * h + 8), jnp.int32)] * 2 + [S((8,), jnp.in...  25.1 us
    pallas_call x1, Pallas kernels, local(): call(gather_kernel, 60, [S((n, d), BF16)] * 4 + [S((2 * h + 8,), jnp.int3...  11.4 us
    ppermute x20, starting transfers between devices, perm(): return lax.ppermute(v, 'tp', p)  10.4 us
    pallas_call x1, Pallas kernels, local(): call(functools.partial(pdn_kernel, 0, True), 60, [S((n, d1), BF16)] * 4 +...  6.82 us
    pallas_call x1, Pallas kernels, local(): call(proj_kernel, 36, [S((k, t, fc), BF16), S((d, fc), F32), S((8,), jnp....  6.67 us
    pallas_call x1, Pallas kernels, local(): call(functools.partial(pdn_kernel, d1, False), 60, [S((n, d2), BF16)] * 4...  6.16 us
    pallas_call x2, Pallas kernels, scatter(): call(functools.partial(scatter_kernel, m), 16, S((vl, d), F32), [SMEM] *...  5 us
  transfers between devices with their start and end apart: 20, of which 7 were waited for; matrix products, arithmetic and copies ran while one was open for 2% of the time, Pallas kernels for 33%

profile of v6, /device:TPU:0, one launch (start us, length us, event | category | flops | bytes accessed | tf_op | source)
XLA Modules:
  0.0 115.7 jit_solution(4181007413899411948)
XLA Ops:
  0.6 6.8 %shard_map.101 = (bf16[128,1280]{1,0:T(8,128)(2,1)}, bf16[128,1280]{1,0:T(8,128)(2,1)}, bf16[128,1280]{1,0:T(8,128)(2,1)}, bf16[128,1280]{1,0:T(8,128)(2,1)}, bf16[512,1024]{1,0:T(8,128)(2,1)}) custom-call(bf16[2,256,1024]{2,1,0:T(8,128)(2,1)} %du_ref.1, bf16[2304,1024]{1,0:T(8,128)(2,1)} %w_ref.3), custom_call_target="tpu_custom_call" | custom-call | flops 1342177280 | bytes 4980736 | tf_op jit(solution)/shard_map/pallas_call | solution.py:296
  7.5 0.0 copy-start.11
  7.5 6.2 %shard_map.102 = (bf16[128,1024]{1,0:T(8,128)(2,1)}, bf16[128,1024]{1,0:T(8,128)(2,1)}, bf16[128,1024]{1,0:T(8,128)(2,1)}, bf16[128,1024]{1,0:T(8,128)(2,1)}) custom-call(bf16[512,1024]{1,0:T(8,128)(2,1)} %get-tuple-element.38.refs_0_, bf16[2304,1024]{1,0:T(8,128)(2,1)} %w_ref.3), custom_call_target="tpu_custom_call" | custom-call | flops 1073741824 | bytes 4194304 | tf_op jit(solution)/shard_map/pallas_call | solution.py:300
  13.7 0.0 copy-start.9
  13.7 0.0 copy-start
  13.7 0.0 copy-start.1
  13.7 0.0 copy-start.2
  13.7 11.4 %shard_map.103 = (bf16[128,2304]{1,0:T(8,128)(2,1)}, bf16[128,2304]{1,0:T(8,128)(2,1)}, bf16[128,2304]{1,0:T(8,128)(2,1)}, bf16[128,2304]{1,0:T(8,128)(2,1)}, s3...) custom-call(bf16[128,1024]{1,0:T(8,128)(2,1)} %get-tuple-element.39.tok_ref, s32[2,256]{1,0:T(2,128)} %ids_ref.1, ...), custom_call_target="tpu_custom_call" | custom-call | flops 500000000 | bytes 9437184 | tf_op jit(solution)/shard_map/pallas_call | solution.py:311
  25.1 0.1 collective-permute-start
  25.3 0.4 collective-permute-start.5
  25.7 1.2 %collective-permute-start.6 = (bf16[128,1024]{1,0:T(8,128)(2,1)S(1)}, bf16[128,1024]{1,0:T(8,128)(2,1)S(1)}, u32[]{:S(2)}, u32[]{:S(2)}) collective-permute-start(bf16[128,1024]{1,0:T(8,128)(2,1)S(1)} %copy-done.8), channel_id=1, source_target_pairs={{0,2},{1,3},{2,0},{3,1},{4,6},{5,7},{6,4},{7,5}} | collective-permute-start | bytes 786440 | tf_op jit(solution)/shard_map/ppermute | solution.py:292
  26.8 0.3 collective-permute-start.7
  27.1 0.7 collective-permute-start.2
  27.8 0.0 collective-permute-done
  27.8 1.2 %collective-permute-start.3 = (bf16[128,1280]{1,0:T(8,128)(2,1)S(1)}, bf16[128,1280]{1,0:T(8,128)(2,1)S(1)}, u32[]{:S(2)}, u32[]{:S(2)}) collective-permute-start(bf16[128,1280]{1,0:T(8,128)(2,1)S(1)} %copy-done.11), channel_id=1, source_target_pairs={{0,2},{1,3},{2,0},{3,1},{4,6},{5,7},{6,4},{7,5}} | collective-permute-start | bytes 983048 | tf_op jit(solution)/shard_map/ppermute | solution.py:292
  29.0 1.2 %add.12.xh_ref = bf16[128,2304]{1,0:T(8,128)(2,1)S(1)} add(bf16[128,2304]{1,0:T(8,128)(2,1)} %get-tuple-element.40, bf16[128,2304]{1,0:T(8,128)(2,1)S(1)} %collective-permute-done) | non-fusion elementwise | flops 294912 | bytes 1769472 | tf_op jit(solution)/shard_map/add | solution.py:320
  30.2 0.0 collective-permute-done.5.r1
  30.2 0.2 collective-permute-start.4
  30.4 4.4 %collective-permute-done.6.r2 = bf16[128,1024]{1,0:T(8,128)(2,1)S(1)} collective-permute-done((bf16[128,1024]{1,0:T(8,128)(2,1)S(1)}, bf16[128,1024]{1,0:T(8,128)(2,1)S(1)}, u32[]{:S(2)}, u32[]{:S(2)}) %collective-permute-start.6) | collective-permute-done | bytes 262176 | tf_op jit(solution)/shard_map/ppermute | solution.py:292
  34.8 0.0 collective-permute-start.9
  34.8 4.3 %collective-permute-done.7.r3 = bf16[128,1024]{1,0:T(8,128)(2,1)S(1)} collective-permute-done((bf16[128,1024]{1,0:T(8,128)(2,1)S(1)}, bf16[128,1024]{1,0:T(8,128)(2,1)S(1)}, u32[]{:S(2)}, u32[]{:S(2)}) %collective-permute-start.7) | collective-permute-done | bytes 262176 | tf_op jit(solution)/shard_map/ppermute | solution.py:292
  39.2 0.8 collective-permute-start.1
  40.0 0.7 copy-done.4
  40.7 0.7 copy-done.5
  41.4 0.6 copy-done.6
  42.0 25.1 %shard_map.104 = (s32[2,520]{1,0:T(2,128)S(1)}, s32[2,520]{1,0:T(2,128)S(1)}, s32[8]{0:T(128)S(1)}, f32[8192,2304]{1,0:T(8,128)}) custom-call(s32[520]{0:T(1024)S(1)} %copy-done.4, s32[520]{0:T(1024)S(1)} %copy-done.5, s32[8]{0:T(128)S(1)} %copy-done.6), custom_call_target="tpu_custom_call" | custom-call | flops 10000000000 | bytes 75497472 | tf_op jit(solution)/shard_map/pallas_call | solution.py:324
  67.1 0.0 collective-permute-done.2.p1
  67.1 0.0 collective-permute-done.3.p2
  67.1 0.0 collective-permute-done.4.p3
  67.1 0.0 collective-permute-done.1.z_ref
  67.2 0.0 copy-start.7
  67.2 0.0 slice-start.1
  67.2 0.0 copy-start.3
  67.2 0.7 shard_map.105
  67.9 1.2 %collective-permute-start.8 = (bf16[128,2304]{1,0:T(8,128)(2,1)S(1)}, bf16[128,2304]{1,0:T(8,128)(2,1)S(1)}, u32[]{:S(2)}, u32[]{:S(2)}) collective-permute-start(bf16[128,2304]{1,0:T(8,128)(2,1)S(1)} %get-tuple-element.53.xm_ref.refs_0_), channel_id=1, source_target_pairs={{0,1},{1,0},{2,3},{3,2},{4,5},{5,4},{6,7},{7,6}} | collective-permute-start | bytes 1769480 | tf_op jit(solution)/shard_map/ppermute | solution.py:292
  69.1 0.0 collective-permute-done.9
  69.1 0.1 add.13.xh_ref
  69.2 0.9 collective-permute-start.10
  70.1 0.6 collective-permute-done.8.xo_ref
  70.7 3.3 %shard_map.106 = (bf16[2,256,1024]{2,1,0:T(8,128)(2,1)}, bf16[256,2304]{1,0:T(8,128)(2,1)S(1)}, s32[8]{0:T(128)S(1)}) custom-call(bf16[128,2304]{1,0:T(8,128)(2,1)S(1)} %get-tuple-element.53.xm_ref.refs_0_, bf16[128,2304]{1,0:T(8,128)(2,1)S(1)} %collective-permute-done.8.xo_ref, bf16[1,2304]{1,0:T(2,128)(2,1)S(1)} %reshape.16.g_ref, ...), custom_call_target="tpu_custom_call" | custom-call | flops 1207959552 | bytes 4718592 | tf_op jit(solution)/shard_map/pallas_call | solution.py:339
  74.0 10.8 %collective-permute-done.10.z_ref = bf16[128,2304]{1,0:T(8,128)(2,1)S(1)} collective-permute-done((bf16[128,2304]{1,0:T(8,128)(2,1)S(1)}, bf16[128,2304]{1,0:T(8,128)(2,1)S(1)}, u32[]{:S(2)}, u32[]{:S(2)}) %collective-permute-start.10) | collective-permute-done | bytes 589856 | tf_op jit(solution)/shard_map/ppermute | solution.py:292
  84.8 1.9 %shard_map.107 = (bf16[128,2304]{1,0:T(8,128)(2,1)S(1)}, bf16[64,2304]{1,0:T(8,128)(2,1)S(1)}, f32[1,2304]{1,0:T(1,128)S(1)}, bf16[2,64,2304]{2,1,0:T(8,128)(2,1)}) custom-call(bf16[128,2304]{1,0:T(8,128)(2,1)S(1)} %add.13.xh_ref, bf16[128,2304]{1,0:T(8,128)(2,1)S(1)} %collective-permute-done.10.z_ref, bf16[128,1280]{1,0:T(8,128)(2,1)S(1)} %copy-done.1, ...), custom_call_target="tpu_custom_call" | custom-call | flops 8847360 | bytes 4718592 | tf_op jit(solution)/shard_map/pallas_call | solution.py:332
  86.7 0.0 collective-permute-start.11
  86.7 0.8 collective-permute-start.12
  87.6 1.2 %collective-permute-start.15 = (bf16[64,2304]{1,0:T(8,128)(2,1)S(1)}, bf16[64,2304]{1,0:T(8,128)(2,1)S(1)}, u32[]{:S(2)}, u32[]{:S(2)}) collective-permute-start(bf16[64,2304]{1,0:T(8,128)(2,1)S(1)} %get-tuple-element.68.refs_4_), channel_id=1, source_target_pairs={{0,2},{1,3},{2,0},{3,1},{4,6},{5,7},{6,4},{7,5}} | collective-permute-start | bytes 884744 | tf_op jit(solution)/shard_map/ppermute | solution.py:292
  88.8 0.0 collective-permute-start.18
  88.8 1.2 %collective-permute-done.18 = f32[1,2304]{1,0:T(1,128)S(1)} collective-permute-done((f32[1,2304]{1,0:T(1,128)S(1)}, f32[1,2304]{1,0:T(1,128)S(1)}, u32[]{:S(2)}, u32[]{:S(2)}) %collective-permute-start.18) | collective-permute-done | bytes 9248 | tf_op jit(solution)/shard_map/ppermute | solution.py:292
  90.0 0.9 collective-permute-start.19
  90.8 0.0 collective-permute-start.13
  90.8 5.8 %collective-permute-done.12.refs_1_ = bf16[64,2304]{1,0:T(8,128)(2,1)S(1)} collective-permute-done((bf16[64,2304]{1,0:T(8,128)(2,1)S(1)}, bf16[64,2304]{1,0:T(8,128)(2,1)S(1)}, u32[]{:S(2)}, u32[]{:S(2)}) %collective-permute-start.12) | collective-permute-done | bytes 294944 | tf_op jit(solution)/shard_map/ppermute | solution.py:292
  96.6 0.0 collective-permute-start.14
  96.6 6.1 %collective-permute-done.19 = f32[1,2304]{1,0:T(1,128)S(1)} collective-permute-done((f32[1,2304]{1,0:T(1,128)S(1)}, f32[1,2304]{1,0:T(1,128)S(1)}, u32[]{:S(2)}, u32[]{:S(2)}) %collective-permute-start.19) | collective-permute-done | bytes 9248 | tf_op jit(solution)/shard_map/ppermute | solution.py:292
  102.7 0.0 collective-permute-start.16
  102.7 0.6 add_reduce_fusion
  103.3 0.0 collective-permute-done.15.refs_5_
  103.3 0.5 collective-permute-start.17
  103.8 0.0 collective-permute-done.11.xo_ref
  103.8 6.7 %shard_map.108 = (bf16[2,256,1024]{2,1,0:T(8,128)(2,1)}, f32[2304,1024]{1,0:T(8,128)}, s32[8]{0:T(128)S(1)}) custom-call(bf16[256,2304]{1,0:T(8,128)(2,1)S(1)} %get-tuple-element.55.n0_ref, bf16[128,2304]{1,0:T(8,128)(2,1)S(1)} %get-tuple-element.59.xm_ref, bf16[128,2304]{1,0:T(8,128)(2,1)S(1)} %collective-permute-done.11.xo_ref, ...), custom_call_target="tpu_custom_call", output_to_operand_aliasing={{0}: (6, {})} | custom-call | flops 3623878656 | bytes 14155776 | tf_op jit(solution)/shard_map/pallas_call | solution.py:351
  110.5 0.0 collective-permute-done.13.refs_2_
  110.5 0.0 collective-permute-done.14.refs_3_
  110.5 2.4 %shard_map.109.refs_9_ = f32[8192,2304]{1,0:T(8,128)} custom-call(s32[2,520]{1,0:T(2,128)S(1)} %get-tuple-element.64.last_ref, s32[2,520]{1,0:T(2,128)S(1)} %get-tuple-element.65.dup_ref, s32[8]{0:T(128)S(1)} %get-tuple-element.66.cnt_ref, bf16[64,2304]{1,0:T(8,128)(2,1)S(1)} %get-tuple-element.67.refs_0_, ...), custom_call_target="tpu_custom_call", output_to_operand_aliasing={{}: (8, {})} | custom-call | flops 4718592 | bytes 4718592 | tf_op jit(solution)/shard_map/pallas_call | solution.py:359
  112.9 0.0 collective-permute-done.16.refs_6_
  112.9 0.0 collective-permute-done.17.refs_7_
  113.0 2.6 %shard_map.110 = f32[8192,2304]{1,0:T(8,128)} custom-call(s32[2,520]{1,0:T(2,128)S(1)} %get-tuple-element.64.last_ref, s32[2,520]{1,0:T(2,128)S(1)} %get-tuple-element.65.dup_ref, s32[8]{0:T(128)S(1)} %get-tuple-element.66.cnt_ref, bf16[64,2304]{1,0:T(8,128)(2,1)S(1)} %get-tuple-element.67.refs_0_, ...), custom_call_target="tpu_custom_call", output_to_operand_aliasing={{}: (12, {})} | custom-call | flops 4718592 | bytes 4718592 | tf_op jit(solution)/shard_map/pallas_call | solution.py:359
  (26 shorter events, 0.1 us)
Async XLA Ops:
  7.5 19.7 %copy-start.12 = (bf16[128,1280]{1,0:T(8,128)(2,1)S(1)}, bf16[128,1280]{1,0:T(8,128)(2,1)}, u32[]{:S(2)}) copy-start(bf16[128,1280]{1,0:T(8,128)(2,1)} %get-tuple-element.43) | copy-start | bytes 983044
  7.5 20.3 %copy-start.11 = (bf16[128,1280]{1,0:T(8,128)(2,1)S(1)}, bf16[128,1280]{1,0:T(8,128)(2,1)}, u32[]{:S(2)}) copy-start(bf16[128,1280]{1,0:T(8,128)(2,1)} %get-tuple-element.44) | copy-start | bytes 983044
  7.5 22.7 %copy-start.10 = (bf16[128,1280]{1,0:T(8,128)(2,1)S(1)}, bf16[128,1280]{1,0:T(8,128)(2,1)}, u32[]{:S(2)}) copy-start(bf16[128,1280]{1,0:T(8,128)(2,1)} %get-tuple-element.45) | copy-start | bytes 983044
  13.7 11.6 %copy-start.14 = (bf16[128,1024]{1,0:T(8,128)(2,1)S(1)}, bf16[128,1024]{1,0:T(8,128)(2,1)}, u32[]{:S(2)}) copy-start(bf16[128,1024]{1,0:T(8,128)(2,1)} %get-tuple-element.47) | copy-start | bytes 786436
  13.7 12.0 %copy-start.8 = (bf16[128,1024]{1,0:T(8,128)(2,1)S(1)}, bf16[128,1024]{1,0:T(8,128)(2,1)}, u32[]{:S(2)}) copy-start(bf16[128,1024]{1,0:T(8,128)(2,1)} %get-tuple-element.39.tok_ref) | copy-start | bytes 786436
  13.7 13.2 %copy-start.13 = (bf16[128,1024]{1,0:T(8,128)(2,1)S(1)}, bf16[128,1024]{1,0:T(8,128)(2,1)}, u32[]{:S(2)}) copy-start(bf16[128,1024]{1,0:T(8,128)(2,1)} %get-tuple-element.48) | copy-start | bytes 786436
  13.7 53.4 %copy-start.9 = (bf16[2304]{0:T(1024)(128)(2,1)S(1)}, bf16[2304]{0:T(1024)(128)(2,1)}, u32[]{:S(2)}) copy-start(bf16[2304]{0:T(1024)(128)(2,1)} %param.8) | copy-start | bytes 13828
  13.7 53.4 %copy-start = (bf16[2,64,2304]{2,1,0:T(8,128)(2,1)S(1)}, bf16[2,64,2304]{2,1,0:T(8,128)(2,1)}, u32[]{:S(2)}) copy-start(bf16[2,64,2304]{2,1,0:T(8,128)(2,1)} %dres_ref.3) | copy-start | bytes 1769476
  13.7 53.4 %copy-start.1 = (bf16[128,1280]{1,0:T(8,128)(2,1)S(1)}, bf16[128,1280]{1,0:T(8,128)(2,1)}, u32[]{:S(2)}) copy-start(bf16[128,1280]{1,0:T(8,128)(2,1)} %get-tuple-element.42.p0) | copy-start | bytes 983044
  13.7 53.4 %copy-start.2 = (bf16[128,1024]{1,0:T(8,128)(2,1)S(1)}, bf16[128,1024]{1,0:T(8,128)(2,1)}, u32[]{:S(2)}) copy-start(bf16[128,1024]{1,0:T(8,128)(2,1)} %get-tuple-element.46.r0) | copy-start | bytes 786436
  25.1 2.7 %collective-permute-start = (bf16[128,2304]{1,0:T(8,128)(2,1)}, bf16[128,2304]{1,0:T(8,128)(2,1)S(1)}, u32[]{:S(2)}, u32[]{:S(2)}) collective-permute-start(bf16[128,2304]{1,0:T(8,128)(2,1)} %get-tuple-element.41), channel_id=1, source_target_pairs={{0,1},{1,0},{2,3},{3,2},{4,5},{5,4},{6,7},{7,6}} | collective-permute-start | bytes 1769480 | tf_op jit(solution)/shard_map/ppermute | solution.py:292
  25.3 4.9 %collective-permute-start.5 = (bf16[128,1024]{1,0:T(8,128)(2,1)S(1)}, bf16[128,1024]{1,0:T(8,128)(2,1)S(1)}, u32[]{:S(2)}, u32[]{:S(2)}) collective-permute-start(bf16[128,1024]{1,0:T(8,128)(2,1)S(1)} %copy-done.14), channel_id=1, source_target_pairs={{0,1},{1,0},{2,3},{3,2},{4,5},{5,4},{6,7},{7,6}} | collective-permute-start | bytes 786440 | tf_op jit(solution)/shard_map/ppermute | solution.py:292
  25.7 9.2 %collective-permute-start.6 = (bf16[128,1024]{1,0:T(8,128)(2,1)S(1)}, bf16[128,1024]{1,0:T(8,128)(2,1)S(1)}, u32[]{:S(2)}, u32[]{:S(2)}) collective-permute-start(bf16[128,1024]{1,0:T(8,128)(2,1)S(1)} %copy-done.8), channel_id=1, source_target_pairs={{0,2},{1,3},{2,0},{3,1},{4,6},{5,7},{6,4},{7,5}} | collective-permute-start | bytes 786440 | tf_op jit(solution)/shard_map/ppermute | solution.py:292
  26.8 12.3 %collective-permute-start.7 = (bf16[128,1024]{1,0:T(8,128)(2,1)S(1)}, bf16[128,1024]{1,0:T(8,128)(2,1)S(1)}, u32[]{:S(2)}, u32[]{:S(2)}) collective-permute-start(bf16[128,1024]{1,0:T(8,128)(2,1)S(1)} %copy-done.13), channel_id=1, source_target_pairs={{0,3},{1,2},{2,1},{3,0},{4,7},{5,6},{6,5},{7,4}} | collective-permute-start | bytes 786440 | tf_op jit(solution)/shard_map/ppermute | solution.py:292
  27.1 40.0 %collective-permute-start.2 = (bf16[128,1280]{1,0:T(8,128)(2,1)S(1)}, bf16[128,1280]{1,0:T(8,128)(2,1)S(1)}, u32[]{:S(2)}, u32[]{:S(2)}) collective-permute-start(bf16[128,1280]{1,0:T(8,128)(2,1)S(1)} %copy-done.12), channel_id=1, source_target_pairs={{0,1},{1,0},{2,3},{3,2},{4,5},{5,4},{6,7},{7,6}} | collective-permute-start | bytes 983048 | tf_op jit(solution)/shard_map/ppermute | solution.py:292
  27.8 39.3 %collective-permute-start.3 = (bf16[128,1280]{1,0:T(8,128)(2,1)S(1)}, bf16[128,1280]{1,0:T(8,128)(2,1)S(1)}, u32[]{:S(2)}, u32[]{:S(2)}) collective-permute-start(bf16[128,1280]{1,0:T(8,128)(2,1)S(1)} %copy-done.11), channel_id=1, source_target_pairs={{0,2},{1,3},{2,0},{3,1},{4,6},{5,7},{6,4},{7,5}} | collective-permute-start | bytes 983048 | tf_op jit(solution)/shard_map/ppermute | solution.py:292
  30.2 36.9 %collective-permute-start.4 = (bf16[128,1280]{1,0:T(8,128)(2,1)S(1)}, bf16[128,1280]{1,0:T(8,128)(2,1)S(1)}, u32[]{:S(2)}, u32[]{:S(2)}) collective-permute-start(bf16[128,1280]{1,0:T(8,128)(2,1)S(1)} %copy-done.10), channel_id=1, source_target_pairs={{0,3},{1,2},{2,1},{3,0},{4,7},{5,6},{6,5},{7,4}} | collective-permute-start | bytes 983048 | tf_op jit(solution)/shard_map/ppermute | solution.py:292
  34.8 34.3 %collective-permute-start.9 = (bf16[128,2304]{1,0:T(8,128)(2,1)}, bf16[128,2304]{1,0:T(8,128)(2,1)S(1)}, u32[]{:S(2)}, u32[]{:S(2)}) collective-permute-start(bf16[128,2304]{1,0:T(8,128)(2,1)} %get-tuple-element.57), channel_id=1, source_target_pairs={{0,1},{1,0},{2,3},{3,2},{4,5},{5,4},{6,7},{7,6}} | collective-permute-start | bytes 1769480 | tf_op jit(solution)/shard_map/ppermute | solution.py:292
  39.2 28.0 %collective-permute-start.1 = (bf16[128,2304]{1,0:T(8,128)(2,1)S(1)}, bf16[128,2304]{1,0:T(8,128)(2,1)S(1)}, u32[]{:S(2)}, u32[]{:S(2)}) collective-permute-start(bf16[128,2304]{1,0:T(8,128)(2,1)S(1)} %add.12.xh_ref), channel_id=1, source_target_pairs={{0,2},{1,3},{2,0},{3,1},{4,6},{5,7},{6,4},{7,5}} | collective-permute-start | bytes 1769480 | tf_op jit(solution)/shard_map/ppermute | solution.py:292
  40.0 0.7 copy-start.4
  40.7 0.7 copy-start.5
  41.4 0.6 copy-start.6
  42.0 28.7 %slice-start = ((s8[4718592]{0:T(1024)(128)(4,1)}), s8[4194304]{0:T(1024)(128)(4,1)S(1)}, s32[]{:S(2)}) async-start(s8[4718592]{0:T(1024)(128)(4,1)} %bitcast), calls=%async_computation | async-start | bytes 8388608
  67.2 1.9 %copy-start.7 = (bf16[128,2304]{1,0:T(8,128)(2,1)S(1)}, bf16[128,2304]{1,0:T(8,128)(2,1)}, u32[]{:S(2)}) copy-start(bf16[128,2304]{1,0:T(8,128)(2,1)} %get-tuple-element.56) | copy-start | bytes 1769476
  67.2 3.5 %slice-start.1 = ((s8[4718592]{0:T(1024)(128)(4,1)}), s8[524288]{0:T(1024)(128)(4,1)S(1)}, s32[]{:S(2)}) async-start(s8[4718592]{0:T(1024)(128)(4,1)} %bitcast), calls=%async_computation.1 | async-start | bytes 1048576
  67.2 36.6 %copy-start.3 = (bf16[2,256,1024]{2,1,0:T(8,128)(2,1)S(1)}, bf16[2,256,1024]{2,1,0:T(8,128)(2,1)}, u32[]{:S(2)}) copy-start(bf16[2,256,1024]{2,1,0:T(8,128)(2,1)} %du_ref.1) | copy-start | bytes 3145732
  67.9 2.8 %collective-permute-start.8 = (bf16[128,2304]{1,0:T(8,128)(2,1)S(1)}, bf16[128,2304]{1,0:T(8,128)(2,1)S(1)}, u32[]{:S(2)}, u32[]{:S(2)}) collective-permute-start(bf16[128,2304]{1,0:T(8,128)(2,1)S(1)} %get-tuple-element.53.xm_ref.refs_0_), channel_id=1, source_target_pairs={{0,1},{1,0},{2,3},{3,2},{4,5},{5,4},{6,7},{7,6}} | collective-permute-start | bytes 1769480 | tf_op jit(solution)/shard_map/ppermute | solution.py:292
  69.2 15.6 %collective-permute-start.10 = (bf16[128,2304]{1,0:T(8,128)(2,1)S(1)}, bf16[128,2304]{1,0:T(8,128)(2,1)S(1)}, u32[]{:S(2)}, u32[]{:S(2)}) collective-permute-start(bf16[128,2304]{1,0:T(8,128)(2,1)S(1)} %add.13.xh_ref), channel_id=1, source_target_pairs={{0,2},{1,3},{2,0},{3,1},{4,6},{5,7},{6,4},{7,5}} | collective-permute-start | bytes 1769480 | tf_op jit(solution)/shard_map/ppermute | solution.py:292
  86.7 17.1 %collective-permute-start.11 = (bf16[128,2304]{1,0:T(8,128)(2,1)S(1)}, bf16[128,2304]{1,0:T(8,128)(2,1)S(1)}, u32[]{:S(2)}, u32[]{:S(2)}) collective-permute-start(bf16[128,2304]{1,0:T(8,128)(2,1)S(1)} %get-tuple-element.59.xm_ref), channel_id=1, source_target_pairs={{0,1},{1,0},{2,3},{3,2},{4,5},{5,4},{6,7},{7,6}} | collective-permute-start | bytes 1769480 | tf_op jit(solution)/shard_map/ppermute | solution.py:292
  86.7 9.9 %collective-permute-start.12 = (bf16[64,2304]{1,0:T(8,128)(2,1)S(1)}, bf16[64,2304]{1,0:T(8,128)(2,1)S(1)}, u32[]{:S(2)}, u32[]{:S(2)}) collective-permute-start(bf16[64,2304]{1,0:T(8,128)(2,1)S(1)} %get-tuple-element.67.refs_0_), channel_id=1, source_target_pairs={{0,2},{1,3},{2,0},{3,1},{4,6},{5,7},{6,4},{7,5}} | collective-permute-start | bytes 884744 | tf_op jit(solution)/shard_map/ppermute | solution.py:292
  87.6 15.7 %collective-permute-start.15 = (bf16[64,2304]{1,0:T(8,128)(2,1)S(1)}, bf16[64,2304]{1,0:T(8,128)(2,1)S(1)}, u32[]{:S(2)}, u32[]{:S(2)}) collective-permute-start(bf16[64,2304]{1,0:T(8,128)(2,1)S(1)} %get-tuple-element.68.refs_4_), channel_id=1, source_target_pairs={{0,2},{1,3},{2,0},{3,1},{4,6},{5,7},{6,4},{7,5}} | collective-permute-start | bytes 884744 | tf_op jit(solution)/shard_map/ppermute | solution.py:292
  88.8 1.2 %collective-permute-start.18 = (f32[1,2304]{1,0:T(1,128)S(1)}, f32[1,2304]{1,0:T(1,128)S(1)}, u32[]{:S(2)}, u32[]{:S(2)}) collective-permute-start(f32[1,2304]{1,0:T(1,128)S(1)} %get-tuple-element.61.tok_ref), channel_id=1, source_target_pairs={{0,1},{1,0},{2,3},{3,2},{4,5},{5,4},{6,7},{7,6}} | collective-permute-start | bytes 27656 | tf_op jit(solution)/shard_map/ppermute | solution.py:292
  90.0 12.7 %collective-permute-start.19 = (f32[1,2304]{1,0:T(1,128)S(1)}, f32[1,2304]{1,0:T(1,128)S(1)}, u32[]{:S(2)}, u32[]{:S(2)}) collective-permute-start(f32[1,2304]{1,0:T(1,128)S(1)} %add.14), channel_id=1, source_target_pairs={{0,2},{1,3},{2,0},{3,1},{4,6},{5,7},{6,4},{7,5}} | collective-permute-start | bytes 27656 | tf_op jit(solution)/shard_map/ppermute | solution.py:292
  90.8 19.7 %collective-permute-start.13 = (bf16[64,2304]{1,0:T(8,128)(2,1)S(1)}, bf16[64,2304]{1,0:T(8,128)(2,1)S(1)}, u32[]{:S(2)}, u32[]{:S(2)}) collective-permute-start(bf16[64,2304]{1,0:T(8,128)(2,1)S(1)} %get-tuple-element.67.refs_0_), channel_id=1, source_target_pairs={{0,1},{1,0},{2,3},{3,2},{4,5},{5,4},{6,7},{7,6}} | collective-permute-start | bytes 884744 | tf_op jit(solution)/shard_map/ppermute | solution.py:292
  96.6 13.9 %collective-permute-start.14 = (bf16[64,2304]{1,0:T(8,128)(2,1)S(1)}, bf16[64,2304]{1,0:T(8,128)(2,1)S(1)}, u32[]{:S(2)}, u32[]{:S(2)}) collective-permute-start(bf16[64,2304]{1,0:T(8,128)(2,1)S(1)} %collective-permute-done.12.refs_1_), channel_id=1, source_target_pairs={{0,1},{1,0},{2,3},{3,2},{4,5},{5,4},{6,7},{7,6}} | collective-permute-start | bytes 884744 | tf_op jit(solution)/shard_map/ppermute | solution.py:292
  102.7 10.3 %collective-permute-start.16 = (bf16[64,2304]{1,0:T(8,128)(2,1)S(1)}, bf16[64,2304]{1,0:T(8,128)(2,1)S(1)}, u32[]{:S(2)}, u32[]{:S(2)}) collective-permute-start(bf16[64,2304]{1,0:T(8,128)(2,1)S(1)} %get-tuple-element.68.refs_4_), channel_id=1, source_target_pairs={{0,1},{1,0},{2,3},{3,2},{4,5},{5,4},{6,7},{7,6}} | collective-permute-start | bytes 884744 | tf_op jit(solution)/shard_map/ppermute | solution.py:292
  103.3 9.6 %collective-permute-start.17 = (bf16[64,2304]{1,0:T(8,128)(2,1)S(1)}, bf16[64,2304]{1,0:T(8,128)(2,1)S(1)}, u32[]{:S(2)}, u32[]{:S(2)}) collective-permute-start(bf16[64,2304]{1,0:T(8,128)(2,1)S(1)} %collective-permute-done.15.refs_5_), channel_id=1, source_target_pairs={{0,1},{1,0},{2,3},{3,2},{4,5},{5,4},{6,7},{7,6}} | collective-permute-start | bytes 884744 | tf_op jit(solution)/shard_map/ppermute | solution.py:292

commit v7 on v6

--- a/solution.py
+++ b/solution.py
@@ -33,13 +33,16 @@
     if first:
         du_ref, w_ref, *outs, dup_ref, dub, wb, dsem, wsem = refs
     else:
-        dup_ref, w_ref, *outs, wb, wsem = refs
+        dup_ref, w_ref, *outs, de_ref, wb, z, wsem, zsem = refs
     width = outs[0].shape[1]
     n = outs[0].shape[0]
     blk = 256
     nb = width // blk
     for i in range(nb):
         pltpu.make_async_copy(w_ref.at[pl.ds(lo + i * blk, blk), :], wb.at[pl.ds(i * blk, blk), :], wsem.at[i]).start()
+    if not first:
+        z[...] = jnp.zeros_like(z)
+        zero_start(z, de_ref, *FILL[0], zsem)
     if first:
         k, tl = dub.shape[0], dub.shape[1] // 4
         dc = pltpu.make_async_copy(du_ref, dub, dsem)
@@ -55,23 +58,29 @@
         p = lax.dot_general(dup_ref[...], wb[i * blk:(i + 1) * blk, :], (((1,), (1,)), ((), ())), preferred_element_type=F32)
         for a in range(4):
             outs[a][:, i * blk:(i + 1) * blk] = p[a * n:(a + 1) * n].astype(BF16)
-
-
-def zero_start(z, de_ref, lo, rows, sem):
+    if not first:
+        zero_wait(z, de_ref, *FILL[0], zsem)
+
+
+FILL = ((0, 3), (3, 6), (6, 9), (9, 16))
+
+
+def zero_start(z, de_ref, lo, hi, sem):
     step = z.shape[0]
-    for i in range(rows // step):
-        pltpu.make_async_copy(z, de_ref.at[pl.ds(lo + i * step, step), :], sem).start()
-
-
-def zero_wait(z, de_ref, rows, sem):
+    per = de_ref.shape[0] // 16
+    for i in range((hi - lo) * per // step):
+        pltpu.make_async_copy(z, de_ref.at[pl.ds(lo * per + i * step, step), :], sem).start()
+
+
+def zero_wait(z, de_ref, lo, hi, sem):
     step = z.shape[0]
-    for _ in range(rows // step):
+    for _ in range((hi - lo) * (de_ref.shape[0] // 16) // step):
         pltpu.make_async_copy(z, de_ref.at[pl.ds(0, step), :], sem).wait()
 
 
-def zero_kernel(lpos, lrow, cnt, last_ref, dup_ref, out_ref, de_ref, z, lnxt, tab, sem):
+def zero_kernel(lpos, lrow, cnt, de_in, last_ref, dup_ref, out_ref, de_ref, z, lnxt, tab, sem):
     z[...] = jnp.zeros_like(z)
-    zero_start(z, de_ref, 0, de_ref.shape[0], sem)
+    zero_start(z, de_ref, *FILL[3], sem)
     n = cnt[0]
     t = lnxt.shape[0] - 8
 
@@ -102,15 +111,17 @@
     out_ref[0] = nl
     out_ref[1] = nd
     out_ref[2] = n0
-    zero_wait(z, de_ref, de_ref.shape[0], sem)
-
-
-def gather_kernel(tok_ref, ids_ref, emb_ref, k0, s0, k1, s1, lpos, lrow, cnt, buf, tmp, xf, lst, sem):
+    zero_wait(z, de_ref, *FILL[3], sem)
+
+
+def gather_kernel(ids_ref, emb_ref, de_in, k0, s0, k1, s1, lpos, lrow, cnt, de_ref, buf, tmp, xf, z, lst, sem, zsem):
     k, t = ids_ref.shape
     vl = emb_ref.shape[0]
     h = k0.shape[0]
     tl = t // 4
     r = lax.axis_index("tp")
+    z[...] = jnp.zeros_like(z)
+    zero_start(z, de_ref, *FILL[1], zsem)
     n = 0
     for m in range(k):
         def scan(i, n):
@@ -131,6 +142,7 @@
         return c
 
     lax.fori_loop(0, n, start, 0)
+    zero_start(z, de_ref, *FILL[2], zsem)
     for a in range(8):
         lpos[n + a] = k * t
         lrow[n + a] = 0
@@ -153,6 +165,7 @@
     lax.fori_loop(0, (n + 7) // 8, take, 0)
     for a, ref in enumerate((k0, s0, k1, s1)):
         ref[...] = xf[a * h:(a + 1) * h, :].astype(BF16)
+    zero_wait(z, de_ref, FILL[1][0], FILL[2][1], zsem)
 
 
 def dx_kernel(m, xh_ref, z_ref, p0, p1, p2, p3, r0, r1, r2, r3, dres_ref, g_ref, tok_ref, *refs):
@@ -297,9 +310,9 @@
             functools.partial(pdn_kernel, 0, True), 60, [S((n, d1), BF16)] * 4 + [S((4 * n, fc), BF16)],
             [HBM] * 2, [VMEM] * 5, [pltpu.VMEM((k, t, fc), BF16), pltpu.VMEM((d1, fc), BF16), D, D((d1 // 256,))],
             8 * n * fc * d1, 2 * d1 * fc + 8 * n * (fc + d1))(du, w)
-        r2, r3, r1, r0 = call(
-            functools.partial(pdn_kernel, d1, False), 60, [S((n, d2), BF16)] * 4,
-            [VMEM, HBM], [VMEM] * 4, [pltpu.VMEM((d2, fc), BF16), D((d2 // 256,))],
+        r2, r3, r1, r0, de = call(
+            functools.partial(pdn_kernel, d1, False), 60, [S((n, d2), BF16)] * 4 + [S((vl, d), F32)],
+            [VMEM, HBM], [VMEM] * 4 + [HBM], [pltpu.VMEM((d2, fc), BF16), pltpu.VMEM((256, d), F32), D((d2 // 256,)), D],
             8 * n * fc * d2, 2 * d2 * fc + 8 * n * (fc + d2))(dup4, w)
         q2 = perm(p2, cross)
         q3 = perm(p3, diag)
@@ -308,13 +321,13 @@
         q1 = perm(p1, sib)
         v1 = perm(r1, sib)
 
-        k0, s0, k1, s1, lpos, lrow, nown = call(
+        k0, s0, k1, s1, lpos, lrow, nown, de = call(
             gather_kernel, 60,
-            [S((n, d), BF16)] * 4 + [S((2 * h + 8,), jnp.int32)] * 2 + [S((8,), jnp.int32)],
-            [HBM, SMEM, HBM], [VMEM] * 4 + [SMEM] * 3,
-            [pltpu.VMEM((2 * h, 8, d), BF16), pltpu.VMEM((8, 8, d), F32), pltpu.VMEM((2 * h + 8, d), F32)]
-            + [pltpu.SMEM((2 * h + 8,), jnp.int32), D],
-            500_000_000, 16 * h * d)(r2, ids, emb)
+            [S((n, d), BF16)] * 4 + [S((2 * h + 8,), jnp.int32)] * 2 + [S((8,), jnp.int32), S((vl, d), F32)],
+            [SMEM, HBM, HBM], [VMEM] * 4 + [SMEM] * 3 + [HBM],
+            [pltpu.VMEM((2 * h, 8, d), BF16), pltpu.VMEM((8, 8, d), F32), pltpu.VMEM((2 * h + 8, d), F32), pltpu.VMEM((256, d), F32)]
+            + [pltpu.SMEM((2 * h + 8,), jnp.int32), D, D],
+            500_000_000, 16 * h * d, {2: 7})(ids, emb, de)
         y0 = perm(s0, sib)
         y1 = perm(s1, sib)
         xh0 = k0 + y0
@@ -323,9 +336,9 @@
         z1 = perm(xh1, cross)
         last, dup, cnt, de = call(
             zero_kernel, 8, [S((2, 2 * h + 8), jnp.int32)] * 2 + [S((8,), jnp.int32), S((vl, d), F32)],
-            [SMEM] * 3, [SMEM] * 3 + [HBM],
+            [SMEM] * 3 + [HBM], [SMEM] * 3 + [HBM],
             [pltpu.VMEM((256, d), F32), pltpu.SMEM((2 * h + 8,), jnp.int32), pltpu.SMEM((vl,), jnp.int32), D],
-            10_000_000_000, 4 * vl * d)(lpos, lrow, nown)
+            10_000_000_000, 4 * vl * d, {3: 3})(lpos, lrow, nown, de)
 
         def dxk(m, xh, z, tok, more):
             outs = [S((n, d), BF16), S((tl, d), BF16), S((1, d), F32)] + ([S((k, tl, d), BF16)] if m else [])

time: 116 us -> 119 us (1.026)
  waiting for transfers between devices: 33.2 us -> 42.7 us
  Pallas kernels: 67 us -> 58.4 us
  starting transfers between devices: 10.4 us -> 11.8 us
    pallas_call x1, Pallas kernels: 25.1 us -> 12.8 us  [local(): call(zero_kernel, 8, [S((2, 2 * h + 8), jnp.int32)] * 2 + [S((8,), jnp.in...]
    ppermute x20, waiting for transfers between devices: 33.2 us -> 42.7 us  [perm(): return lax.ppermute(v, 'tp', p)]
    pallas_call x1, Pallas kernels: 11.4 us -> 13.7 us  [local(): call(gather_kernel, 60, [S((n, d), BF16)] * 4 + [S((2 * h + 8,), jnp.int3...]
    ppermute x20, starting transfers between devices: 10.4 us -> 11.8 us  [perm(): return lax.ppermute(v, 'tp', p)]
    pallas_call x1, Pallas kernels: 6.16 us -> 7.57 us  [local(): call(functools.partial(pdn_kernel, d1, False), 60, [S((n, d2), BF16)] * 4...]
  transfers between devices with their start and end apart: 20 -> 20, of which waited for: 7 -> 8; matrix products, arithmetic and copies ran while one was open for 2% -> 2% of each run, Pallas kernels for 33% -> 22%
where the time goes in v7:
time: 119 us; the launch traced here: 118 us
  Pallas kernels  58.4 us (49%)
  waiting for transfers between devices  42.7 us (36%)
  starting transfers between devices  11.8 us (10%)
  local copies, waits for them, and re-layouts  2.11 us (2%)
  other arithmetic  1.98 us (2%)
    ppermute x20, waiting for transfers between devices, perm(): return lax.ppermute(v, 'tp', p)  42.7 us
    pallas_call x1, Pallas kernels, local(): call(gather_kernel, 60, [S((n, d), BF16)] * 4 + [S((2 * h + 8,), jnp.int3...  13.7 us
    pallas_call x1, Pallas kernels, local(): call(zero_kernel, 8, [S((2, 2 * h + 8), jnp.int32)] * 2 + [S((8,), jnp.in...  12.8 us
    ppermute x20, starting transfers between devices, perm(): return lax.ppermute(v, 'tp', p)  11.8 us
    pallas_call x1, Pallas kernels, local(): call(functools.partial(pdn_kernel, d1, False), 60, [S((n, d2), BF16)] * 4...  7.57 us
    pallas_call x1, Pallas kernels, local(): call(functools.partial(pdn_kernel, 0, True), 60, [S((n, d1), BF16)] * 4 +...  6.82 us
    pallas_call x1, Pallas kernels, local(): call(proj_kernel, 36, [S((k, t, fc), BF16), S((d, fc), F32), S((8,), jnp....  6.66 us
    pallas_call x2, Pallas kernels, scatter(): call(functools.partial(scatter_kernel, m), 16, S((vl, d), F32), [SMEM] *...  5 us
  transfers between devices with their start and end apart: 20, of which 8 were waited for; matrix products, arithmetic and copies ran while one was open for 2% of the time, Pallas kernels for 22%

profile of v7, /device:TPU:0, one launch (start us, length us, event | category | flops | bytes accessed | tf_op | source)
XLA Modules:
  0.0 118.1 jit_solution(17734037781446514631)
XLA Ops:
  0.6 6.8 %shard_map.101 = (bf16[128,1280]{1,0:T(8,128)(2,1)}, bf16[128,1280]{1,0:T(8,128)(2,1)}, bf16[128,1280]{1,0:T(8,128)(2,1)}, bf16[128,1280]{1,0:T(8,128)(2,1)}, bf16[512,1024]{1,0:T(8,128)(2,1)}) custom-call(bf16[2,256,1024]{2,1,0:T(8,128)(2,1)} %du_ref.1, bf16[2304,1024]{1,0:T(8,128)(2,1)} %w_ref.3), custom_call_target="tpu_custom_call" | custom-call | flops 1342177280 | bytes 4980736 | tf_op jit(solution)/shard_map/pallas_call | solution.py:309
  7.5 0.0 copy-start.11
  7.5 0.0 copy-start.10
  7.5 7.6 %shard_map.102 = (bf16[128,1024]{1,0:T(8,128)(2,1)}, bf16[128,1024]{1,0:T(8,128)(2,1)}, bf16[128,1024]{1,0:T(8,128)(2,1)}, bf16[128,1024]{1,0:T(8,128)(2,1)}, f32[8192,2304]{1,0:T(8,128)}) custom-call(bf16[512,1024]{1,0:T(8,128)(2,1)} %get-tuple-element.40.refs_0_, bf16[2304,1024]{1,0:T(8,128)(2,1)} %w_ref.3), custom_call_target="tpu_custom_call" | custom-call | flops 1073741824 | bytes 4194304 | tf_op jit(solution)/shard_map/pallas_call | solution.py:313
  15.1 0.0 copy-start.8
  15.1 0.0 copy-start
  15.1 13.7 %shard_map.103 = (bf16[128,2304]{1,0:T(8,128)(2,1)}, bf16[128,2304]{1,0:T(8,128)(2,1)}, bf16[128,2304]{1,0:T(8,128)(2,1)}, bf16[128,2304]{1,0:T(8,128)(2,1)}, s3...) custom-call(s32[2,256]{1,0:T(2,128)} %ids_ref.1, ...), custom_call_target="tpu_custom_call", output_to_operand_aliasing={{7}: (2, {})} | custom-call | flops 500000000 | bytes 9437184 | tf_op jit(solution)/shard_map/pallas_call | solution.py:324
  28.8 0.6 collective-permute-start
  29.4 0.0 collective-permute-start.5
  29.4 2.3 %collective-permute-start.6 = (bf16[128,1024]{1,0:T(8,128)(2,1)S(1)}, bf16[128,1024]{1,0:T(8,128)(2,1)S(1)}, u32[]{:S(2)}, u32[]{:S(2)}) collective-permute-start(bf16[128,1024]{1,0:T(8,128)(2,1)S(1)} %copy-done.13), channel_id=1, source_target_pairs={{0,2},{1,3},{2,0},{3,1},{4,6},{5,7},{6,4},{7,5}} | collective-permute-start | bytes 786440 | tf_op jit(solution)/shard_map/ppermute | solution.py:305
  31.8 0.0 copy-done.12
  31.8 0.0 collective-permute-start.7
  31.8 0.1 collective-permute-start.2
  31.9 0.0 collective-permute-done
  31.9 2.0 %collective-permute-start.3 = (bf16[128,1280]{1,0:T(8,128)(2,1)S(1)}, bf16[128,1280]{1,0:T(8,128)(2,1)S(1)}, u32[]{:S(2)}, u32[]{:S(2)}) collective-permute-start(bf16[128,1280]{1,0:T(8,128)(2,1)S(1)} %copy-done.10), channel_id=1, source_target_pairs={{0,2},{1,3},{2,0},{3,1},{4,6},{5,7},{6,4},{7,5}} | collective-permute-start | bytes 983048 | tf_op jit(solution)/shard_map/ppermute | solution.py:305
  33.9 1.2 %add.12.xh_ref = bf16[128,2304]{1,0:T(8,128)(2,1)S(1)} add(bf16[128,2304]{1,0:T(8,128)(2,1)} %get-tuple-element.42, bf16[128,2304]{1,0:T(8,128)(2,1)S(1)} %collective-permute-done) | non-fusion elementwise | flops 294912 | bytes 1769472 | tf_op jit(solution)/shard_map/add | solution.py:333
  35.1 0.0 collective-permute-done.5.r1
  35.2 0.0 collective-permute-start.4
  35.2 3.7 %collective-permute-done.6.r2 = bf16[128,1024]{1,0:T(8,128)(2,1)S(1)} collective-permute-done((bf16[128,1024]{1,0:T(8,128)(2,1)S(1)}, bf16[128,1024]{1,0:T(8,128)(2,1)S(1)}, u32[]{:S(2)}, u32[]{:S(2)}) %collective-permute-start.6) | collective-permute-done | bytes 262176 | tf_op jit(solution)/shard_map/ppermute | solution.py:305
  38.9 0.0 collective-permute-start.9
  38.9 5.2 %collective-permute-done.7.r3 = bf16[128,1024]{1,0:T(8,128)(2,1)S(1)} collective-permute-done((bf16[128,1024]{1,0:T(8,128)(2,1)S(1)}, bf16[128,1024]{1,0:T(8,128)(2,1)S(1)}, u32[]{:S(2)}, u32[]{:S(2)}) %collective-permute-start.7) | collective-permute-done | bytes 262176 | tf_op jit(solution)/shard_map/ppermute | solution.py:305
  44.1 0.6 collective-permute-start.1
  44.7 0.7 copy-done.4
  45.4 0.7 copy-done.5
  46.1 0.7 copy-done.6
  46.8 12.8 %shard_map.104 = (s32[2,520]{1,0:T(2,128)S(1)}, s32[2,520]{1,0:T(2,128)S(1)}, s32[8]{0:T(128)S(1)}, f32[8192,2304]{1,0:T(8,128)}) custom-call(s32[520]{0:T(1024)S(1)} %copy-done.4, s32[520]{0:T(1024)S(1)} %copy-done.5, s32[8]{0:T(128)S(1)} %copy-done.6, f32[8192,2304]{1,0:T(8,128)} %get-tuple-element.55.de_in), custom_call_target="tpu_custom_call", output_to_operand_aliasing={{3}: (3, {})} | custom-call | flops 10000000000 | bytes 75497472 | tf_op jit(solution)/shard_map/pallas_call | solution.py:337
  59.6 0.0 collective-permute-done.2.p1
  59.6 0.0 collective-permute-done.3.p2
  59.6 0.0 collective-permute-done.4.p3
  59.6 11.0 %collective-permute-done.1.z_ref = bf16[128,2304]{1,0:T(8,128)(2,1)S(1)} collective-permute-done((bf16[128,2304]{1,0:T(8,128)(2,1)S(1)}, bf16[128,2304]{1,0:T(8,128)(2,1)S(1)}, u32[]{:S(2)}, u32[]{:S(2)}) %collective-permute-start.1) | collective-permute-done | bytes 589856 | tf_op jit(solution)/shard_map/ppermute | solution.py:305
  70.6 0.0 slice-start.1
  70.6 0.7 shard_map.105
  71.3 0.0 collective-permute-start.8
  71.3 0.0 collective-permute-done.9
  71.4 0.0 copy-done.7
  71.4 0.1 add.13.xh_ref
  71.5 1.8 %collective-permute-start.10 = (bf16[128,2304]{1,0:T(8,128)(2,1)S(1)}, bf16[128,2304]{1,0:T(8,128)(2,1)S(1)}, u32[]{:S(2)}, u32[]{:S(2)}) collective-permute-start(bf16[128,2304]{1,0:T(8,128)(2,1)S(1)} %add.13.xh_ref), channel_id=1, source_target_pairs={{0,2},{1,3},{2,0},{3,1},{4,6},{5,7},{6,4},{7,5}} | collective-permute-start | bytes 1769480 | tf_op jit(solution)/shard_map/ppermute | solution.py:305
  73.3 0.1 collective-permute-done.8.xo_ref
  73.3 0.0 slice-done.1
  73.3 3.3 %shard_map.106 = (bf16[2,256,1024]{2,1,0:T(8,128)(2,1)}, bf16[256,2304]{1,0:T(8,128)(2,1)S(1)}, s32[8]{0:T(128)S(1)}) custom-call(bf16[128,2304]{1,0:T(8,128)(2,1)S(1)} %get-tuple-element.57.xm_ref.refs_0_, bf16[128,2304]{1,0:T(8,128)(2,1)S(1)} %collective-permute-done.8.xo_ref, bf16[1,2304]{1,0:T(2,128)(2,1)S(1)} %reshape.16.g_ref, ...), custom_call_target="tpu_custom_call" | custom-call | flops 1207959552 | bytes 4718592 | tf_op jit(solution)/shard_map/pallas_call | solution.py:352
  76.6 10.6 %collective-permute-done.10.z_ref = bf16[128,2304]{1,0:T(8,128)(2,1)S(1)} collective-permute-done((bf16[128,2304]{1,0:T(8,128)(2,1)S(1)}, bf16[128,2304]{1,0:T(8,128)(2,1)S(1)}, u32[]{:S(2)}, u32[]{:S(2)}) %collective-permute-start.10) | collective-permute-done | bytes 589856 | tf_op jit(solution)/shard_map/ppermute | solution.py:305
  87.2 1.9 %shard_map.107 = (bf16[128,2304]{1,0:T(8,128)(2,1)S(1)}, bf16[64,2304]{1,0:T(8,128)(2,1)S(1)}, f32[1,2304]{1,0:T(1,128)S(1)}, bf16[2,64,2304]{2,1,0:T(8,128)(2,1)}) custom-call(bf16[128,2304]{1,0:T(8,128)(2,1)S(1)} %add.13.xh_ref, bf16[128,2304]{1,0:T(8,128)(2,1)S(1)} %collective-permute-done.10.z_ref, bf16[128,1280]{1,0:T(8,128)(2,1)S(1)} %copy-done.1, ...), custom_call_target="tpu_custom_call" | custom-call | flops 8847360 | bytes 4718592 | tf_op jit(solution)/shard_map/pallas_call | solution.py:345
  89.2 0.0 collective-permute-start.11
  89.2 1.7 %collective-permute-start.12 = (bf16[64,2304]{1,0:T(8,128)(2,1)S(1)}, bf16[64,2304]{1,0:T(8,128)(2,1)S(1)}, u32[]{:S(2)}, u32[]{:S(2)}) collective-permute-start(bf16[64,2304]{1,0:T(8,128)(2,1)S(1)} %get-tuple-element.71.refs_0_), channel_id=1, source_target_pairs={{0,2},{1,3},{2,0},{3,1},{4,6},{5,7},{6,4},{7,5}} | collective-permute-start | bytes 884744 | tf_op jit(solution)/shard_map/ppermute | solution.py:305
  90.9 0.3 collective-permute-start.15
  91.2 0.0 collective-permute-start.18
  91.2 1.2 collective-permute-done.18
  92.4 1.8 %collective-permute-start.19 = (f32[1,2304]{1,0:T(1,128)S(1)}, f32[1,2304]{1,0:T(1,128)S(1)}, u32[]{:S(2)}, u32[]{:S(2)}) collective-permute-start(f32[1,2304]{1,0:T(1,128)S(1)} %add.14), channel_id=1, source_target_pairs={{0,2},{1,3},{2,0},{3,1},{4,6},{5,7},{6,4},{7,5}} | collective-permute-start | bytes 27656 | tf_op jit(solution)/shard_map/ppermute | solution.py:305
  94.2 0.0 collective-permute-start.13
  94.2 4.9 %collective-permute-done.12.refs_1_ = bf16[64,2304]{1,0:T(8,128)(2,1)S(1)} collective-permute-done((bf16[64,2304]{1,0:T(8,128)(2,1)S(1)}, bf16[64,2304]{1,0:T(8,128)(2,1)S(1)}, u32[]{:S(2)}, u32[]{:S(2)}) %collective-permute-start.12) | collective-permute-done | bytes 294944 | tf_op jit(solution)/shard_map/ppermute | solution.py:305
  99.1 0.0 collective-permute-start.14
  99.1 6.1 %collective-permute-done.19 = f32[1,2304]{1,0:T(1,128)S(1)} collective-permute-done((f32[1,2304]{1,0:T(1,128)S(1)}, f32[1,2304]{1,0:T(1,128)S(1)}, u32[]{:S(2)}, u32[]{:S(2)}) %collective-permute-start.19) | collective-permute-done | bytes 9248 | tf_op jit(solution)/shard_map/ppermute | solution.py:305
  105.1 0.0 collective-permute-start.16
  105.1 0.6 add_reduce_fusion
  105.7 0.0 collective-permute-done.15.refs_5_
  105.7 0.5 collective-permute-start.17
  106.3 0.0 collective-permute-done.11.xo_ref
  106.3 6.7 %shard_map.108 = (bf16[2,256,1024]{2,1,0:T(8,128)(2,1)}, f32[2304,1024]{1,0:T(8,128)}, s32[8]{0:T(128)S(1)}) custom-call(bf16[256,2304]{1,0:T(8,128)(2,1)S(1)} %get-tuple-element.59.n0_ref, bf16[128,2304]{1,0:T(8,128)(2,1)S(1)} %get-tuple-element.63.xm_ref, bf16[128,2304]{1,0:T(8,128)(2,1)S(1)} %collective-permute-done.11.xo_ref, ...), custom_call_target="tpu_custom_call", output_to_operand_aliasing={{0}: (6, {})} | custom-call | flops 3623878656 | bytes 14155776 | tf_op jit(solution)/shard_map/pallas_call | solution.py:364
  112.9 0.0 collective-permute-done.13.refs_2_
  112.9 0.0 collective-permute-done.14.refs_3_
  112.9 2.4 %shard_map.109.refs_9_ = f32[8192,2304]{1,0:T(8,128)} custom-call(s32[2,520]{1,0:T(2,128)S(1)} %get-tuple-element.68.last_ref, s32[2,520]{1,0:T(2,128)S(1)} %get-tuple-element.69.dup_ref, s32[8]{0:T(128)S(1)} %get-tuple-element.70.cnt_ref, bf16[64,2304]{1,0:T(8,128)(2,1)S(1)} %get-tuple-element.71.refs_0_, ...), custom_call_target="tpu_custom_call", output_to_operand_aliasing={{}: (8, {})} | custom-call | flops 4718592 | bytes 4718592 | tf_op jit(solution)/shard_map/pallas_call | solution.py:372
  115.4 0.0 collective-permute-done.16.refs_6_
  115.4 0.0 collective-permute-done.17.refs_7_
  115.4 2.6 %shard_map.110 = f32[8192,2304]{1,0:T(8,128)} custom-call(s32[2,520]{1,0:T(2,128)S(1)} %get-tuple-element.68.last_ref, s32[2,520]{1,0:T(2,128)S(1)} %get-tuple-element.69.dup_ref, s32[8]{0:T(128)S(1)} %get-tuple-element.70.cnt_ref, bf16[64,2304]{1,0:T(8,128)(2,1)S(1)} %get-tuple-element.71.refs_0_, ...), custom_call_target="tpu_custom_call", output_to_operand_aliasing={{}: (12, {})} | custom-call | flops 4718592 | bytes 4718592 | tf_op jit(solution)/shard_map/pallas_call | solution.py:372
  (26 shorter events, 0.1 us)
Async XLA Ops:
  7.5 24.3 %copy-start.11 = (bf16[128,1280]{1,0:T(8,128)(2,1)S(1)}, bf16[128,1280]{1,0:T(8,128)(2,1)}, u32[]{:S(2)}) copy-start(bf16[128,1280]{1,0:T(8,128)(2,1)} %get-tuple-element.45) | copy-start | bytes 983044
  7.5 24.5 %copy-start.10 = (bf16[128,1280]{1,0:T(8,128)(2,1)S(1)}, bf16[128,1280]{1,0:T(8,128)(2,1)}, u32[]{:S(2)}) copy-start(bf16[128,1280]{1,0:T(8,128)(2,1)} %get-tuple-element.46) | copy-start | bytes 983044
  7.5 27.7 %copy-start.9 = (bf16[128,1280]{1,0:T(8,128)(2,1)S(1)}, bf16[128,1280]{1,0:T(8,128)(2,1)}, u32[]{:S(2)}) copy-start(bf16[128,1280]{1,0:T(8,128)(2,1)} %get-tuple-element.47) | copy-start | bytes 983044
  15.1 14.3 %copy-start.14 = (bf16[128,1024]{1,0:T(8,128)(2,1)S(1)}, bf16[128,1024]{1,0:T(8,128)(2,1)}, u32[]{:S(2)}) copy-start(bf16[128,1024]{1,0:T(8,128)(2,1)} %get-tuple-element.49) | copy-start | bytes 786436
  15.1 14.4 %copy-start.13 = (bf16[128,1024]{1,0:T(8,128)(2,1)S(1)}, bf16[128,1024]{1,0:T(8,128)(2,1)}, u32[]{:S(2)}) copy-start(bf16[128,1024]{1,0:T(8,128)(2,1)} %get-tuple-element.50) | copy-start | bytes 786436
  15.1 16.7 %copy-start.12 = (bf16[128,1024]{1,0:T(8,128)(2,1)S(1)}, bf16[128,1024]{1,0:T(8,128)(2,1)}, u32[]{:S(2)}) copy-start(bf16[128,1024]{1,0:T(8,128)(2,1)} %get-tuple-element.51) | copy-start | bytes 786436
  15.1 44.5 %copy-start.8 = (bf16[2304]{0:T(1024)(128)(2,1)S(1)}, bf16[2304]{0:T(1024)(128)(2,1)}, u32[]{:S(2)}) copy-start(bf16[2304]{0:T(1024)(128)(2,1)} %param.8) | copy-start | bytes 13828
  15.1 55.5 %copy-start = (bf16[2,64,2304]{2,1,0:T(8,128)(2,1)S(1)}, bf16[2,64,2304]{2,1,0:T(8,128)(2,1)}, u32[]{:S(2)}) copy-start(bf16[2,64,2304]{2,1,0:T(8,128)(2,1)} %dres_ref.3) | copy-start | bytes 1769476
  15.1 55.5 %copy-start.1 = (bf16[128,1280]{1,0:T(8,128)(2,1)S(1)}, bf16[128,1280]{1,0:T(8,128)(2,1)}, u32[]{:S(2)}) copy-start(bf16[128,1280]{1,0:T(8,128)(2,1)} %get-tuple-element.44.p0) | copy-start | bytes 983044
  15.1 55.5 %copy-start.2 = (bf16[128,1024]{1,0:T(8,128)(2,1)S(1)}, bf16[128,1024]{1,0:T(8,128)(2,1)}, u32[]{:S(2)}) copy-start(bf16[128,1024]{1,0:T(8,128)(2,1)} %get-tuple-element.48.r0) | copy-start | bytes 786436
  28.8 3.1 %collective-permute-start = (bf16[128,2304]{1,0:T(8,128)(2,1)}, bf16[128,2304]{1,0:T(8,128)(2,1)S(1)}, u32[]{:S(2)}, u32[]{:S(2)}) collective-permute-start(bf16[128,2304]{1,0:T(8,128)(2,1)} %get-tuple-element.43), channel_id=1, source_target_pairs={{0,1},{1,0},{2,3},{3,2},{4,5},{5,4},{6,7},{7,6}} | collective-permute-start | bytes 1769480 | tf_op jit(solution)/shard_map/ppermute | solution.py:305
  29.4 5.8 %collective-permute-start.5 = (bf16[128,1024]{1,0:T(8,128)(2,1)S(1)}, bf16[128,1024]{1,0:T(8,128)(2,1)S(1)}, u32[]{:S(2)}, u32[]{:S(2)}) collective-permute-start(bf16[128,1024]{1,0:T(8,128)(2,1)S(1)} %copy-done.14), channel_id=1, source_target_pairs={{0,1},{1,0},{2,3},{3,2},{4,5},{5,4},{6,7},{7,6}} | collective-permute-start | bytes 786440 | tf_op jit(solution)/shard_map/ppermute | solution.py:305
  29.4 9.5 %collective-permute-start.6 = (bf16[128,1024]{1,0:T(8,128)(2,1)S(1)}, bf16[128,1024]{1,0:T(8,128)(2,1)S(1)}, u32[]{:S(2)}, u32[]{:S(2)}) collective-permute-start(bf16[128,1024]{1,0:T(8,128)(2,1)S(1)} %copy-done.13), channel_id=1, source_target_pairs={{0,2},{1,3},{2,0},{3,1},{4,6},{5,7},{6,4},{7,5}} | collective-permute-start | bytes 786440 | tf_op jit(solution)/shard_map/ppermute | solution.py:305
  31.8 12.3 %collective-permute-start.7 = (bf16[128,1024]{1,0:T(8,128)(2,1)S(1)}, bf16[128,1024]{1,0:T(8,128)(2,1)S(1)}, u32[]{:S(2)}, u32[]{:S(2)}) collective-permute-start(bf16[128,1024]{1,0:T(8,128)(2,1)S(1)} %copy-done.12), channel_id=1, source_target_pairs={{0,3},{1,2},{2,1},{3,0},{4,7},{5,6},{6,5},{7,4}} | collective-permute-start | bytes 786440 | tf_op jit(solution)/shard_map/ppermute | solution.py:305
  31.8 27.8 %collective-permute-start.2 = (bf16[128,1280]{1,0:T(8,128)(2,1)S(1)}, bf16[128,1280]{1,0:T(8,128)(2,1)S(1)}, u32[]{:S(2)}, u32[]{:S(2)}) collective-permute-start(bf16[128,1280]{1,0:T(8,128)(2,1)S(1)} %copy-done.11), channel_id=1, source_target_pairs={{0,1},{1,0},{2,3},{3,2},{4,5},{5,4},{6,7},{7,6}} | collective-permute-start | bytes 983048 | tf_op jit(solution)/shard_map/ppermute | solution.py:305
  31.9 27.7 %collective-permute-start.3 = (bf16[128,1280]{1,0:T(8,128)(2,1)S(1)}, bf16[128,1280]{1,0:T(8,128)(2,1)S(1)}, u32[]{:S(2)}, u32[]{:S(2)}) collective-permute-start(bf16[128,1280]{1,0:T(8,128)(2,1)S(1)} %copy-done.10), channel_id=1, source_target_pairs={{0,2},{1,3},{2,0},{3,1},{4,6},{5,7},{6,4},{7,5}} | collective-permute-start | bytes 983048 | tf_op jit(solution)/shard_map/ppermute | solution.py:305
  35.2 24.4 %collective-permute-start.4 = (bf16[128,1280]{1,0:T(8,128)(2,1)S(1)}, bf16[128,1280]{1,0:T(8,128)(2,1)S(1)}, u32[]{:S(2)}, u32[]{:S(2)}) collective-permute-start(bf16[128,1280]{1,0:T(8,128)(2,1)S(1)} %copy-done.9), channel_id=1, source_target_pairs={{0,3},{1,2},{2,1},{3,0},{4,7},{5,6},{6,5},{7,4}} | collective-permute-start | bytes 983048 | tf_op jit(solution)/shard_map/ppermute | solution.py:305
  38.9 32.4 %collective-permute-start.9 = (bf16[128,2304]{1,0:T(8,128)(2,1)}, bf16[128,2304]{1,0:T(8,128)(2,1)S(1)}, u32[]{:S(2)}, u32[]{:S(2)}) collective-permute-start(bf16[128,2304]{1,0:T(8,128)(2,1)} %get-tuple-element.61), channel_id=1, source_target_pairs={{0,1},{1,0},{2,3},{3,2},{4,5},{5,4},{6,7},{7,6}} | collective-permute-start | bytes 1769480 | tf_op jit(solution)/shard_map/ppermute | solution.py:305
  44.1 26.5 %collective-permute-start.1 = (bf16[128,2304]{1,0:T(8,128)(2,1)S(1)}, bf16[128,2304]{1,0:T(8,128)(2,1)S(1)}, u32[]{:S(2)}, u32[]{:S(2)}) collective-permute-start(bf16[128,2304]{1,0:T(8,128)(2,1)S(1)} %add.12.xh_ref), channel_id=1, source_target_pairs={{0,2},{1,3},{2,0},{3,1},{4,6},{5,7},{6,4},{7,5}} | collective-permute-start | bytes 1769480 | tf_op jit(solution)/shard_map/ppermute | solution.py:305
  44.7 0.7 copy-start.4
  45.4 0.7 copy-start.5
  46.1 0.7 copy-start.6
  46.8 24.6 %copy-start.7 = (bf16[128,2304]{1,0:T(8,128)(2,1)S(1)}, bf16[128,2304]{1,0:T(8,128)(2,1)}, u32[]{:S(2)}) copy-start(bf16[128,2304]{1,0:T(8,128)(2,1)} %get-tuple-element.60) | copy-start | bytes 1769476
  46.8 26.6 %slice-start = ((s8[4718592]{0:T(1024)(128)(4,1)}), s8[4194304]{0:T(1024)(128)(4,1)S(1)}, s32[]{:S(2)}) async-start(s8[4718592]{0:T(1024)(128)(4,1)} %bitcast), calls=%async_computation | async-start | bytes 8388608
  46.8 59.5 %copy-start.3 = (bf16[2,256,1024]{2,1,0:T(8,128)(2,1)S(1)}, bf16[2,256,1024]{2,1,0:T(8,128)(2,1)}, u32[]{:S(2)}) copy-start(bf16[2,256,1024]{2,1,0:T(8,128)(2,1)} %du_ref.1) | copy-start | bytes 3145732
  70.6 2.7 %slice-start.1 = ((s8[4718592]{0:T(1024)(128)(4,1)}), s8[524288]{0:T(1024)(128)(4,1)S(1)}, s32[]{:S(2)}) async-start(s8[4718592]{0:T(1024)(128)(4,1)} %bitcast), calls=%async_computation.1 | async-start | bytes 1048576
  71.3 2.0 %collective-permute-start.8 = (bf16[128,2304]{1,0:T(8,128)(2,1)S(1)}, bf16[128,2304]{1,0:T(8,128)(2,1)S(1)}, u32[]{:S(2)}, u32[]{:S(2)}) collective-permute-start(bf16[128,2304]{1,0:T(8,128)(2,1)S(1)} %get-tuple-element.57.xm_ref.refs_0_), channel_id=1, source_target_pairs={{0,1},{1,0},{2,3},{3,2},{4,5},{5,4},{6,7},{7,6}} | collective-permute-start | bytes 1769480 | tf_op jit(solution)/shard_map/ppermute | solution.py:305
  71.5 15.7 %collective-permute-start.10 = (bf16[128,2304]{1,0:T(8,128)(2,1)S(1)}, bf16[128,2304]{1,0:T(8,128)(2,1)S(1)}, u32[]{:S(2)}, u32[]{:S(2)}) collective-permute-start(bf16[128,2304]{1,0:T(8,128)(2,1)S(1)} %add.13.xh_ref), channel_id=1, source_target_pairs={{0,2},{1,3},{2,0},{3,1},{4,6},{5,7},{6,4},{7,5}} | collective-permute-start | bytes 1769480 | tf_op jit(solution)/shard_map/ppermute | solution.py:305
  89.2 17.1 %collective-permute-start.11 = (bf16[128,2304]{1,0:T(8,128)(2,1)S(1)}, bf16[128,2304]{1,0:T(8,128)(2,1)S(1)}, u32[]{:S(2)}, u32[]{:S(2)}) collective-permute-start(bf16[128,2304]{1,0:T(8,128)(2,1)S(1)} %get-tuple-element.63.xm_ref), channel_id=1, source_target_pairs={{0,1},{1,0},{2,3},{3,2},{4,5},{5,4},{6,7},{7,6}} | collective-permute-start | bytes 1769480 | tf_op jit(solution)/shard_map/ppermute | solution.py:305
  89.2 9.9 %collective-permute-start.12 = (bf16[64,2304]{1,0:T(8,128)(2,1)S(1)}, bf16[64,2304]{1,0:T(8,128)(2,1)S(1)}, u32[]{:S(2)}, u32[]{:S(2)}) collective-permute-start(bf16[64,2304]{1,0:T(8,128)(2,1)S(1)} %get-tuple-element.71.refs_0_), channel_id=1, source_target_pairs={{0,2},{1,3},{2,0},{3,1},{4,6},{5,7},{6,4},{7,5}} | collective-permute-start | bytes 884744 | tf_op jit(solution)/shard_map/ppermute | solution.py:305
  90.9 14.8 %collective-permute-start.15 = (bf16[64,2304]{1,0:T(8,128)(2,1)S(1)}, bf16[64,2304]{1,0:T(8,128)(2,1)S(1)}, u32[]{:S(2)}, u32[]{:S(2)}) collective-permute-start(bf16[64,2304]{1,0:T(8,128)(2,1)S(1)} %get-tuple-element.72.refs_4_), channel_id=1, source_target_pairs={{0,2},{1,3},{2,0},{3,1},{4,6},{5,7},{6,4},{7,5}} | collective-permute-start | bytes 884744 | tf_op jit(solution)/shard_map/ppermute | solution.py:305
  91.2 1.2 collective-permute-start.18
  92.4 12.7 %collective-permute-start.19 = (f32[1,2304]{1,0:T(1,128)S(1)}, f32[1,2304]{1,0:T(1,128)S(1)}, u32[]{:S(2)}, u32[]{:S(2)}) collective-permute-start(f32[1,2304]{1,0:T(1,128)S(1)} %add.14), channel_id=1, source_target_pairs={{0,2},{1,3},{2,0},{3,1},{4,6},{5,7},{6,4},{7,5}} | collective-permute-start | bytes 27656 | tf_op jit(solution)/shard_map/ppermute | solution.py:305
  94.2 18.8 %collective-permute-start.13 = (bf16[64,2304]{1,0:T(8,128)(2,1)S(1)}, bf16[64,2304]{1,0:T(8,128)(2,1)S(1)}, u32[]{:S(2)}, u32[]{:S(2)}) collective-permute-start(bf16[64,2304]{1,0:T(8,128)(2,1)S(1)} %get-tuple-element.71.refs_0_), channel_id=1, source_target_pairs={{0,1},{1,0},{2,3},{3,2},{4,5},{5,4},{6,7},{7,6}} | collective-permute-start | bytes 884744 | tf_op jit(solution)/shard_map/ppermute | solution.py:305
  99.1 13.9 %collective-permute-start.14 = (bf16[64,2304]{1,0:T(8,128)(2,1)S(1)}, bf16[64,2304]{1,0:T(8,128)(2,1)S(1)}, u32[]{:S(2)}, u32[]{:S(2)}) collective-permute-start(bf16[64,2304]{1,0:T(8,128)(2,1)S(1)} %collective-permute-done.12.refs_1_), channel_id=1, source_target_pairs={{0,1},{1,0},{2,3},{3,2},{4,5},{5,4},{6,7},{7,6}} | collective-permute-start | bytes 884744 | tf_op jit(solution)/shard_map/ppermute | solution.py:305
  105.1 10.2 %collective-permute-start.16 = (bf16[64,2304]{1,0:T(8,128)(2,1)S(1)}, bf16[64,2304]{1,0:T(8,128)(2,1)S(1)}, u32[]{:S(2)}, u32[]{:S(2)}) collective-permute-start(bf16[64,2304]{1,0:T(8,128)(2,1)S(1)} %get-tuple-element.72.refs_4_), channel_id=1, source_target_pairs={{0,1},{1,0},{2,3},{3,2},{4,5},{5,4},{6,7},{7,6}} | collective-permute-start | bytes 884744 | tf_op jit(solution)/shard_map/ppermute | solution.py:305
  105.7 9.6 %collective-permute-start.17 = (bf16[64,2304]{1,0:T(8,128)(2,1)S(1)}, bf16[64,2304]{1,0:T(8,128)(2,1)S(1)}, u32[]{:S(2)}, u32[]{:S(2)}) collective-permute-start(bf16[64,2304]{1,0:T(8,128)(2,1)S(1)} %collective-permute-done.15.refs_5_), channel_id=1, source_target_pairs={{0,1},{1,0},{2,3},{3,2},{4,5},{5,4},{6,7},{7,6}} | collective-permute-start | bytes 884744 | tf_op jit(solution)/shard_map/ppermute | solution.py:305

commit v8 on v7

--- a/solution.py
+++ b/solution.py
@@ -33,11 +33,14 @@
     if first:
         du_ref, w_ref, *outs, dup_ref, dub, wb, dsem, wsem = refs
     else:
-        dup_ref, w_ref, *outs, de_ref, wb, z, wsem, zsem = refs
+        dup_ref, w_ref, de_in, *outs, de_ref, wb, z, wsem, zsem = refs
     width = outs[0].shape[1]
     n = outs[0].shape[0]
     blk = 256
     nb = width // blk
+    if first:
+        dc = pltpu.make_async_copy(du_ref, dub, dsem)
+        dc.start()
     for i in range(nb):
         pltpu.make_async_copy(w_ref.at[pl.ds(lo + i * blk, blk), :], wb.at[pl.ds(i * blk, blk), :], wsem.at[i]).start()
     if not first:
@@ -45,8 +48,6 @@
         zero_start(z, de_ref, *FILL[0], zsem)
     if first:
         k, tl = dub.shape[0], dub.shape[1] // 4
-        dc = pltpu.make_async_copy(du_ref, dub, dsem)
-        dc.start()
         r = lax.axis_index("tp")
         dc.wait()
         for a, j in enumerate((2, 3, 1, 0)):
@@ -62,7 +63,7 @@
         zero_wait(z, de_ref, *FILL[0], zsem)
 
 
-FILL = ((0, 3), (3, 6), (6, 9), (9, 16))
+FILL = ((0, 2), (2, 4), (4, 6), (6, 16))
 
 
 def zero_start(z, de_ref, lo, hi, sem):
@@ -98,23 +99,22 @@
     lax.fori_loop(0, n, link, 0)
 
     def lists(i, c):
-        nl, nd, n0 = c
+        nl, nd = c
         x = lnxt[i]
         end = (x < 0).astype(jnp.int32)
         last_ref[0, nl] = lpos[i]
         last_ref[1, nl] = lrow[i]
         dup_ref[0, nd] = lpos[i]
         dup_ref[1, nd] = lpos[jnp.maximum(x, 0)]
-        return nl + end, nd + 1 - end, n0 + end * (lpos[i] < t // 2).astype(jnp.int32)
-
-    nl, nd, n0 = lax.fori_loop(0, n, lists, (0, 0, 0))
+        return nl + end, nd + 1 - end
+
+    nl, nd = lax.fori_loop(0, n, lists, (0, 0))
     out_ref[0] = nl
     out_ref[1] = nd
-    out_ref[2] = n0
     zero_wait(z, de_ref, *FILL[3], sem)
 
 
-def gather_kernel(ids_ref, emb_ref, de_in, k0, s0, k1, s1, lpos, lrow, cnt, de_ref, buf, tmp, xf, z, lst, sem, zsem):
+def gather_kernel(ids_ref, emb_ref, k0, s0, k1, s1, lpos, lrow, cnt, de_ref, buf, tmp, xf, z, lst, sem, zsem):
     k, t = ids_ref.shape
     vl = emb_ref.shape[0]
     h = k0.shape[0]
@@ -250,9 +250,8 @@
         c.wait()
 
 
-def scatter_kernel(m, last_ref, dup_ref, cnt_ref, *refs):
-    nd = 4 * (m + 1)
-    ds, de_ref, xf, sem = refs[:nd], refs[-3], refs[-2], refs[-1]
+def scatter_kernel(last_ref, dup_ref, cnt_ref, *refs):
+    ds, de_ref, xf, sem = refs[:8], refs[-3], refs[-2], refs[-1]
     tl = ds[0].shape[0]
     chip = lax.axis_index("tp") >> 1
     for a, ref in enumerate(ds):
@@ -262,11 +261,7 @@
     def add(i, c):
         a = dup_ref[0, i]
         b = dup_ref[1, i]
-
-        @pl.when(b < 4 * tl * (m + 1))
-        def _():
-            xf[pl.ds(b, 1), :] = xf[pl.ds(b, 1), :] + xf[pl.ds(a, 1), :]
-
+        xf[pl.ds(b, 1), :] = xf[pl.ds(b, 1), :] + xf[pl.ds(a, 1), :]
         return c
 
     lax.fori_loop(0, cnt_ref[1], add, 0)
@@ -279,9 +274,8 @@
         pltpu.make_async_copy(xf.at[pl.ds(0, 1), :], de_ref.at[pl.ds(0, 1), :], sem).wait()
         return c
 
-    n0, n1 = (0, cnt_ref[2]) if m == 0 else (cnt_ref[2], cnt_ref[0])
-    lax.fori_loop(n0, n1, put, 0)
-    lax.fori_loop(n0, n1, wait, 0)
+    lax.fori_loop(0, cnt_ref[0], put, 0)
+    lax.fori_loop(0, cnt_ref[0], wait, 0)
 
 
 def solution(mesh):
@@ -304,32 +298,31 @@
         def perm(v, p):
             return lax.ppermute(v, "tp", p)
 
-        d1 = 5 * 256
+        d1 = 7 * 256
         d2 = d - d1
         p2, p3, p1, p0, dup4 = call(
             functools.partial(pdn_kernel, 0, True), 60, [S((n, d1), BF16)] * 4 + [S((4 * n, fc), BF16)],
             [HBM] * 2, [VMEM] * 5, [pltpu.VMEM((k, t, fc), BF16), pltpu.VMEM((d1, fc), BF16), D, D((d1 // 256,))],
             8 * n * fc * d1, 2 * d1 * fc + 8 * n * (fc + d1))(du, w)
+        q2 = perm(p2, cross)
+        q3 = perm(p3, diag)
+        k0, s0, k1, s1, lpos, lrow, nown, de = call(
+            gather_kernel, 60,
+            [S((n, d), BF16)] * 4 + [S((2 * h + 8,), jnp.int32)] * 2 + [S((8,), jnp.int32), S((vl, d), F32)],
+            [SMEM, HBM], [VMEM] * 4 + [SMEM] * 3 + [HBM],
+            [pltpu.VMEM((2 * h, 8, d), BF16), pltpu.VMEM((8, 8, d), F32), pltpu.VMEM((2 * h + 8, d), F32), pltpu.VMEM((256, d), F32)]
+            + [pltpu.SMEM((2 * h + 8,), jnp.int32), D, D],
+            500_000_000, 16 * h * d)(ids, emb)
+        y0 = perm(s0, sib)
+        y1 = perm(s1, sib)
         r2, r3, r1, r0, de = call(
             functools.partial(pdn_kernel, d1, False), 60, [S((n, d2), BF16)] * 4 + [S((vl, d), F32)],
-            [VMEM, HBM], [VMEM] * 4 + [HBM], [pltpu.VMEM((d2, fc), BF16), pltpu.VMEM((256, d), F32), D((d2 // 256,)), D],
-            8 * n * fc * d2, 2 * d2 * fc + 8 * n * (fc + d2))(dup4, w)
-        q2 = perm(p2, cross)
-        q3 = perm(p3, diag)
+            [VMEM, HBM, HBM], [VMEM] * 4 + [HBM], [pltpu.VMEM((d2, fc), BF16), pltpu.VMEM((256, d), F32), D((d2 // 256,)), D],
+            8 * n * fc * d2, 2 * d2 * fc + 8 * n * (fc + d2), {2: 4})(dup4, w, de)
         v2 = perm(r2, cross)
         v3 = perm(r3, diag)
         q1 = perm(p1, sib)
         v1 = perm(r1, sib)
-
-        k0, s0, k1, s1, lpos, lrow, nown, de = call(
-            gather_kernel, 60,
-            [S((n, d), BF16)] * 4 + [S((2 * h + 8,), jnp.int32)] * 2 + [S((8,), jnp.int32), S((vl, d), F32)],
-            [SMEM, HBM, HBM], [VMEM] * 4 + [SMEM] * 3 + [HBM],
-            [pltpu.VMEM((2 * h, 8, d), BF16), pltpu.VMEM((8, 8, d), F32), pltpu.VMEM((2 * h + 8, d), F32), pltpu.VMEM((256, d), F32)]
-            + [pltpu.SMEM((2 * h + 8,), jnp.int32), D, D],
-            500_000_000, 16 * h * d, {2: 7})(ids, emb, de)
-        y0 = perm(s0, sib)
-        y1 = perm(s1, sib)
         xh0 = k0 + y0
         xh1 = k1 + y1
         z0 = perm(xh0, cross)
@@ -368,14 +361,9 @@
              pltpu.VMEM((d // 256, 256, fc), F32), D, D],
             3 * k * t * d * fc, 6 * d * fc, {6: 0})(n0, xm1, xo1, g2, w, du, u, dg)
 
-        def scatter(m, parts, de, tok):
-            return call(functools.partial(scatter_kernel, m), 16, S((vl, d), F32),
-                        [SMEM] * 3 + [VMEM] * len(parts) + [SMEM, HBM], HBM,
-                        [pltpu.VMEM((h * (m + 1), d), F32), D], 8 * h * d, 8 * h * d,
-                        {4 + len(parts): 0})(last, dup, cnt, *parts, tok, de)
-
-        de = scatter(0, (dx0, c0, a0, b0), de, done1)
-        de = scatter(1, (dx0, c0, a0, b0, dx1, c1, a1, b1), de, done1)
+        de = call(scatter_kernel, 16, S((vl, d), F32), [SMEM] * 3 + [VMEM] * 8 + [SMEM, HBM], HBM,
+                  [pltpu.VMEM((2 * h, d), F32), D], 8 * h * d, 8 * h * d,
+                  {12: 0})(last, dup, cnt, dx0, c0, a0, b0, dx1, c1, a1, b1, done1, de)
         return u, x, de, dw, dgs.reshape(d)
 
     return jax.shard_map(

time: 119 us -> 116 us (0.975)
  local copies, waits for them, and re-layouts: 2.11 us -> 0.09 us
  Pallas kernels: 58.4 us -> 60.2 us
    pallas_call x1, Pallas kernels: 12.8 us -> 17 us  [local(): call(zero_kernel, 8, [S((2, 2 * h + 8), jnp.int32)] * 2 + [S((8,), jnp.in...]
    unnamed x34 -> x30, local copies, waits for them, and re-layouts: 2.1 us -> 0.08 us
    pallas_call x1, Pallas kernels: 6.82 us -> 8.61 us  [local(): call(functools.partial(pdn_kernel, 0, True), 60, [S((n, d1), BF16)] * 4 +...]
    pallas_call x1, Pallas kernels: 7.57 us -> 6.01 us  [local(): call(functools.partial(pdn_kernel, d1, False), 60, [S((n, d2), BF16)] * 4...]
    pallas_call x1, Pallas kernels: 13.7 us -> 12.2 us  [local(): call(gather_kernel, 60, [S((n, d), BF16)] * 4 + [S((2 * h + 8,), jnp.int3...]
    pallas_call x2 -> x1, Pallas kernels: 5 us -> 3.85 us  [local(): call(scatter_kernel, 16, S((vl, d), F32), [SMEM] * 3 + [VMEM] * 8 + [SMEM...]
  transfers between devices with their start and end apart: 20 -> 20, of which waited for: 8 -> 9; matrix products, arithmetic and copies ran while one was open for 2% -> 1% of each run, Pallas kernels for 22% -> 37%
where the time goes in v8:
time: 116 us
  Pallas kernels  60.2 us (52%)
  waiting for transfers between devices  41.9 us (36%)
  starting transfers between devices  11.4 us (10%)
    ppermute x20, waiting for transfers between devices, perm(): return lax.ppermute(v, 'tp', p)  41.9 us
    pallas_call x1, Pallas kernels, local(): call(zero_kernel, 8, [S((2, 2 * h + 8), jnp.int32)] * 2 + [S((8,), jnp.in...  17 us
    pallas_call x1, Pallas kernels, local(): call(gather_kernel, 60, [S((n, d), BF16)] * 4 + [S((2 * h + 8,), jnp.int3...  12.2 us
    ppermute x20, starting transfers between devices, perm(): return lax.ppermute(v, 'tp', p)  11.4 us
    pallas_call x1, Pallas kernels, local(): call(functools.partial(pdn_kernel, 0, True), 60, [S((n, d1), BF16)] * 4 +...  8.61 us
    pallas_call x1, Pallas kernels, local(): call(proj_kernel, 36, [S((k, t, fc), BF16), S((d, fc), F32), S((8,), jnp....  6.65 us
    pallas_call x1, Pallas kernels, local(): call(functools.partial(pdn_kernel, d1, False), 60, [S((n, d2), BF16)] * 4...  6.01 us
    pallas_call x1, Pallas kernels, local(): call(scatter_kernel, 16, S((vl, d), F32), [SMEM] * 3 + [VMEM] * 8 + [SMEM...  3.85 us
  transfers between devices with their start and end apart: 20, of which 9 were waited for; matrix products, arithmetic and copies ran while one was open for 1% of the time, Pallas kernels for 37%

profile of v8, /device:TPU:0, one launch (start us, length us, event | category | flops | bytes accessed | tf_op | source)
XLA Modules:
  0.0 115.6 jit_solution(2799940782015489348)
XLA Ops:
  0.6 12.2 %shard_map.101 = (bf16[128,2304]{1,0:T(8,128)(2,1)}, bf16[128,2304]{1,0:T(8,128)(2,1)}, bf16[128,2304]{1,0:T(8,128)(2,1)}, bf16[128,2304]{1,0:T(8,128)(2,1)}, s3...) custom-call(s32[2,256]{1,0:T(2,128)} %ids_ref.1, bf16[8192,2304]{1,0:T(8,128)(2,1)} %emb_ref.1), custom_call_target="tpu_custom_call" | custom-call | flops 500000000 | bytes 9437184 | tf_op jit(solution)/shard_map/pallas_call | solution.py:309
  12.8 0.0 copy-start.8
  12.8 0.0 copy-start.3
  12.8 0.0 copy-start.4
  12.8 0.0 copy-start.5
  12.8 0.4 collective-permute-start
  13.2 8.6 %shard_map.102 = (bf16[128,1792]{1,0:T(8,128)(2,1)}, bf16[128,1792]{1,0:T(8,128)(2,1)}, bf16[128,1792]{1,0:T(8,128)(2,1)}, bf16[128,1792]{1,0:T(8,128)(2,1)}, bf16[512,1024]{1,0:T(8,128)(2,1)}) custom-call(bf16[2,256,1024]{2,1,0:T(8,128)(2,1)} %du_ref.1, bf16[2304,1024]{1,0:T(8,128)(2,1)} %w_ref.3), custom_call_target="tpu_custom_call" | custom-call | flops 1879048192 | bytes 6553600 | tf_op jit(solution)/shard_map/pallas_call | solution.py:303
  21.9 0.0 copy-start.9
  21.9 0.0 copy-start
  21.9 6.0 %shard_map.103 = (bf16[128,512]{1,0:T(8,128)(2,1)}, bf16[128,512]{1,0:T(8,128)(2,1)}, bf16[128,512]{1,0:T(8,128)(2,1)}, bf16[128,512]{1,0:T(8,128)(2,1)}, f32[8192,2304]{1,0:T(8,128)}) custom-call(bf16[512,1024]{1,0:T(8,128)(2,1)} %get-tuple-element.46.refs_0_, bf16[2304,1024]{1,0:T(8,128)(2,1)} %w_ref.3, ...), custom_call_target="tpu_custom_call", output_to_operand_aliasing={{4}: (2, {})} | custom-call | flops 536870912 | bytes 2621440 | tf_op jit(solution)/shard_map/pallas_call | solution.py:318
  27.9 0.2 collective-permute-start.5
  28.2 1.9 %collective-permute-start.6 = (bf16[128,512]{1,0:T(8,128)(2,1)}, bf16[128,512]{1,0:T(8,128)(2,1)S(1)}, u32[]{:S(2)}, u32[]{:S(2)}) collective-permute-start(bf16[128,512]{1,0:T(8,128)(2,1)} %get-tuple-element.50), channel_id=1, source_target_pairs={{0,2},{1,3},{2,0},{3,1},{4,6},{5,7},{6,4},{7,5}} | collective-permute-start | bytes 393224 | tf_op jit(solution)/shard_map/ppermute | solution.py:299
  30.1 0.0 collective-permute-start.7
  30.1 0.2 collective-permute-start.2
  30.3 0.0 collective-permute-done
  30.3 0.0 copy-done.12
  30.3 1.9 %collective-permute-start.3 = (bf16[128,1792]{1,0:T(8,128)(2,1)S(1)}, bf16[128,1792]{1,0:T(8,128)(2,1)S(1)}, u32[]{:S(2)}, u32[]{:S(2)}) collective-permute-start(bf16[128,1792]{1,0:T(8,128)(2,1)S(1)} %copy-done.12), channel_id=1, source_target_pairs={{0,2},{1,3},{2,0},{3,1},{4,6},{5,7},{6,4},{7,5}} | collective-permute-start | bytes 1376264 | tf_op jit(solution)/shard_map/ppermute | solution.py:299
  32.2 0.1 add.12.xh_ref
  32.4 0.0 collective-permute-done.5.r1
  32.4 0.0 collective-permute-start.4
  32.4 2.3 %collective-permute-done.6.r2 = bf16[128,512]{1,0:T(8,128)(2,1)S(1)} collective-permute-done((bf16[128,512]{1,0:T(8,128)(2,1)}, bf16[128,512]{1,0:T(8,128)(2,1)S(1)}, u32[]{:S(2)}, u32[]{:S(2)}) %collective-permute-start.6) | collective-permute-done | bytes 131104 | tf_op jit(solution)/shard_map/ppermute | solution.py:299
  34.8 0.0 collective-permute-start.9
  34.8 2.3 %collective-permute-done.7.r3 = bf16[128,512]{1,0:T(8,128)(2,1)S(1)} collective-permute-done((bf16[128,512]{1,0:T(8,128)(2,1)}, bf16[128,512]{1,0:T(8,128)(2,1)S(1)}, u32[]{:S(2)}, u32[]{:S(2)}) %collective-permute-start.7) | collective-permute-done | bytes 131104 | tf_op jit(solution)/shard_map/ppermute | solution.py:299
  37.1 0.6 collective-permute-start.1
  37.7 0.0 copy-done.3
  37.7 0.0 slice-start
  37.8 0.0 copy-start.6
  37.8 17.0 %shard_map.104 = (s32[2,520]{1,0:T(2,128)S(1)}, s32[2,520]{1,0:T(2,128)S(1)}, s32[8]{0:T(128)S(1)}, f32[8192,2304]{1,0:T(8,128)}) custom-call(s32[520]{0:T(1024)S(1)} %copy-done.3, s32[520]{0:T(1024)S(1)} %copy-done.4, s32[8]{0:T(128)S(1)} %copy-done.5, f32[8192,2304]{1,0:T(8,128)} %get-tuple-element.55.de_in), custom_call_target="tpu_custom_call", output_to_operand_aliasing={{3}: (3, {})} | custom-call | flops 10000000000 | bytes 75497472 | tf_op jit(solution)/shard_map/pallas_call | solution.py:330
  54.8 0.0 collective-permute-done.2.p1
  54.8 0.0 collective-permute-done.3.p2
  54.8 1.8 %collective-permute-done.4.p3 = bf16[128,1792]{1,0:T(8,128)(2,1)S(1)} collective-permute-done((bf16[128,1792]{1,0:T(8,128)(2,1)S(1)}, bf16[128,1792]{1,0:T(8,128)(2,1)S(1)}, u32[]{:S(2)}, u32[]{:S(2)}) %collective-permute-start.4) | collective-permute-done | bytes 458784 | tf_op jit(solution)/shard_map/ppermute | solution.py:299
  56.7 12.5 %collective-permute-done.1.z_ref = bf16[128,2304]{1,0:T(8,128)(2,1)S(1)} collective-permute-done((bf16[128,2304]{1,0:T(8,128)(2,1)S(1)}, bf16[128,2304]{1,0:T(8,128)(2,1)S(1)}, u32[]{:S(2)}, u32[]{:S(2)}) %collective-permute-start.1) | collective-permute-done | bytes 589856 | tf_op jit(solution)/shard_map/ppermute | solution.py:299
  69.2 0.0 slice-start.1
  69.2 0.7 shard_map.105
  69.9 0.0 collective-permute-start.8
  69.9 0.0 collective-permute-done.9
  69.9 0.0 copy-done.7
  70.0 0.1 add.13.xh_ref
  70.1 1.7 %collective-permute-start.10 = (bf16[128,2304]{1,0:T(8,128)(2,1)S(1)}, bf16[128,2304]{1,0:T(8,128)(2,1)S(1)}, u32[]{:S(2)}, u32[]{:S(2)}) collective-permute-start(bf16[128,2304]{1,0:T(8,128)(2,1)S(1)} %add.13.xh_ref), channel_id=1, source_target_pairs={{0,2},{1,3},{2,0},{3,1},{4,6},{5,7},{6,4},{7,5}} | collective-permute-start | bytes 1769480 | tf_op jit(solution)/shard_map/ppermute | solution.py:299
  71.8 0.1 collective-permute-done.8.xo_ref
  71.9 3.3 %shard_map.106 = (bf16[2,256,1024]{2,1,0:T(8,128)(2,1)}, bf16[256,2304]{1,0:T(8,128)(2,1)S(1)}, s32[8]{0:T(128)S(1)}) custom-call(bf16[128,2304]{1,0:T(8,128)(2,1)S(1)} %get-tuple-element.57.xm_ref.refs_0_, bf16[128,2304]{1,0:T(8,128)(2,1)S(1)} %collective-permute-done.8.xo_ref, bf16[1,2304]{1,0:T(2,128)(2,1)S(1)} %reshape.16.g_ref, ...), custom_call_target="tpu_custom_call" | custom-call | flops 1207959552 | bytes 4718592 | tf_op jit(solution)/shard_map/pallas_call | solution.py:345
  75.2 10.6 %collective-permute-done.10.z_ref = bf16[128,2304]{1,0:T(8,128)(2,1)S(1)} collective-permute-done((bf16[128,2304]{1,0:T(8,128)(2,1)S(1)}, bf16[128,2304]{1,0:T(8,128)(2,1)S(1)}, u32[]{:S(2)}, u32[]{:S(2)}) %collective-permute-start.10) | collective-permute-done | bytes 589856 | tf_op jit(solution)/shard_map/ppermute | solution.py:299
  85.8 1.9 %shard_map.107 = (bf16[128,2304]{1,0:T(8,128)(2,1)S(1)}, bf16[64,2304]{1,0:T(8,128)(2,1)S(1)}, f32[1,2304]{1,0:T(1,128)S(1)}, bf16[2,64,2304]{2,1,0:T(8,128)(2,1)}) custom-call(bf16[128,2304]{1,0:T(8,128)(2,1)S(1)} %add.13.xh_ref, bf16[128,2304]{1,0:T(8,128)(2,1)S(1)} %collective-permute-done.10.z_ref, bf16[128,1792]{1,0:T(8,128)(2,1)S(1)} %copy-done.1, ...), custom_call_target="tpu_custom_call" | custom-call | flops 8847360 | bytes 4718592 | tf_op jit(solution)/shard_map/pallas_call | solution.py:338
  87.8 0.0 collective-permute-start.11
  87.8 1.7 %collective-permute-start.12 = (bf16[64,2304]{1,0:T(8,128)(2,1)S(1)}, bf16[64,2304]{1,0:T(8,128)(2,1)S(1)}, u32[]{:S(2)}, u32[]{:S(2)}) collective-permute-start(bf16[64,2304]{1,0:T(8,128)(2,1)S(1)} %get-tuple-element.71.refs_0_), channel_id=1, source_target_pairs={{0,2},{1,3},{2,0},{3,1},{4,6},{5,7},{6,4},{7,5}} | collective-permute-start | bytes 884744 | tf_op jit(solution)/shard_map/ppermute | solution.py:299
  89.5 0.3 collective-permute-start.15
  89.8 0.0 collective-permute-start.18
  89.8 1.2 %collective-permute-done.18 = f32[1,2304]{1,0:T(1,128)S(1)} collective-permute-done((f32[1,2304]{1,0:T(1,128)S(1)}, f32[1,2304]{1,0:T(1,128)S(1)}, u32[]{:S(2)}, u32[]{:S(2)}) %collective-permute-start.18) | collective-permute-done | bytes 9248 | tf_op jit(solution)/shard_map/ppermute | solution.py:299
  91.0 1.7 %collective-permute-start.19 = (f32[1,2304]{1,0:T(1,128)S(1)}, f32[1,2304]{1,0:T(1,128)S(1)}, u32[]{:S(2)}, u32[]{:S(2)}) collective-permute-start(f32[1,2304]{1,0:T(1,128)S(1)} %add.14), channel_id=1, source_target_pairs={{0,2},{1,3},{2,0},{3,1},{4,6},{5,7},{6,4},{7,5}} | collective-permute-start | bytes 27656 | tf_op jit(solution)/shard_map/ppermute | solution.py:299
  92.7 0.0 collective-permute-start.13
  92.7 4.9 %collective-permute-done.12.refs_1_ = bf16[64,2304]{1,0:T(8,128)(2,1)S(1)} collective-permute-done((bf16[64,2304]{1,0:T(8,128)(2,1)S(1)}, bf16[64,2304]{1,0:T(8,128)(2,1)S(1)}, u32[]{:S(2)}, u32[]{:S(2)}) %collective-permute-start.12) | collective-permute-done | bytes 294944 | tf_op jit(solution)/shard_map/ppermute | solution.py:299
  97.6 0.0 collective-permute-start.14
  97.6 6.1 %collective-permute-done.19 = f32[1,2304]{1,0:T(1,128)S(1)} collective-permute-done((f32[1,2304]{1,0:T(1,128)S(1)}, f32[1,2304]{1,0:T(1,128)S(1)}, u32[]{:S(2)}, u32[]{:S(2)}) %collective-permute-start.19) | collective-permute-done | bytes 9248 | tf_op jit(solution)/shard_map/ppermute | solution.py:299
  103.7 0.0 collective-permute-start.16
  103.7 0.6 add_reduce_fusion
  104.3 0.0 collective-permute-done.15.refs_5_
  104.3 0.5 collective-permute-start.17
  104.8 0.0 collective-permute-done.11.xo_ref
  104.8 6.6 %shard_map.108 = (bf16[2,256,1024]{2,1,0:T(8,128)(2,1)}, f32[2304,1024]{1,0:T(8,128)}, s32[8]{0:T(128)S(1)}) custom-call(bf16[256,2304]{1,0:T(8,128)(2,1)S(1)} %get-tuple-element.59.n0_ref, bf16[128,2304]{1,0:T(8,128)(2,1)S(1)} %get-tuple-element.63.xm_ref, bf16[128,2304]{1,0:T(8,128)(2,1)S(1)} %collective-permute-done.11.xo_ref, ...), custom_call_target="tpu_custom_call", output_to_operand_aliasing={{0}: (6, {})} | custom-call | flops 3623878656 | bytes 14155776 | tf_op jit(solution)/shard_map/pallas_call | solution.py:357
  111.5 0.0 collective-permute-done.13.refs_2_
  111.5 0.0 collective-permute-done.14.refs_3_
  111.5 0.0 collective-permute-done.16.refs_6_
  111.5 0.0 collective-permute-done.17.refs_7_
  111.5 3.9 %shard_map.109 = f32[8192,2304]{1,0:T(8,128)} custom-call(s32[2,520]{1,0:T(2,128)S(1)} %get-tuple-element.68.last_ref, s32[2,520]{1,0:T(2,128)S(1)} %get-tuple-element.69.dup_ref, s32[8]{0:T(128)S(1)} %get-tuple-element.70.cnt_ref, bf16[64,2304]{1,0:T(8,128)(2,1)S(1)} %get-tuple-element.71.refs_0_, ...), custom_call_target="tpu_custom_call", output_to_operand_aliasing={{}: (12, {})} | custom-call | flops 4718592 | bytes 4718592 | tf_op jit(solution)/shard_map/pallas_call | solution.py:364
  (21 shorter events, 0.1 us)
Async XLA Ops:
  12.8 19.5 %copy-start.8 = (bf16[128,2304]{1,0:T(8,128)(2,1)S(1)}, bf16[128,2304]{1,0:T(8,128)(2,1)}, u32[]{:S(2)}) copy-start(bf16[128,2304]{1,0:T(8,128)(2,1)} %get-tuple-element.40) | copy-start | bytes 1769476
  12.8 22.0 %copy-start.10 = (bf16[128,2304]{1,0:T(8,128)(2,1)S(1)}, bf16[128,2304]{1,0:T(8,128)(2,1)}, u32[]{:S(2)}) copy-start(bf16[128,2304]{1,0:T(8,128)(2,1)} %get-tuple-element.61) | copy-start | bytes 1769476
  12.8 24.9 %copy-start.3 = (s32[520]{0:T(1024)S(1)}, s32[520]{0:T(1024)}, u32[]{:S(2)}) copy-start(s32[520]{0:T(1024)} %get-tuple-element.52.lpos) | copy-start | bytes 6244
  12.8 24.9 %copy-start.4 = (s32[520]{0:T(1024)S(1)}, s32[520]{0:T(1024)}, u32[]{:S(2)}) copy-start(s32[520]{0:T(1024)} %get-tuple-element.53.lrow) | copy-start | bytes 6244
  12.8 24.9 %copy-start.5 = (s32[8]{0:T(128)S(1)}, s32[8]{0:T(128)}, u32[]{:S(2)}) copy-start(s32[8]{0:T(128)} %get-tuple-element.54.cnt) | copy-start | bytes 100
  12.8 17.5 %collective-permute-start = (bf16[128,2304]{1,0:T(8,128)(2,1)}, bf16[128,2304]{1,0:T(8,128)(2,1)S(1)}, u32[]{:S(2)}, u32[]{:S(2)}) collective-permute-start(bf16[128,2304]{1,0:T(8,128)(2,1)} %get-tuple-element.41), channel_id=1, source_target_pairs={{0,1},{1,0},{2,3},{3,2},{4,5},{5,4},{6,7},{7,6}} | collective-permute-start | bytes 1769480 | tf_op jit(solution)/shard_map/ppermute | solution.py:299
  21.9 8.5 %copy-start.12 = (bf16[128,1792]{1,0:T(8,128)(2,1)S(1)}, bf16[128,1792]{1,0:T(8,128)(2,1)}, u32[]{:S(2)}) copy-start(bf16[128,1792]{1,0:T(8,128)(2,1)} %get-tuple-element.44) | copy-start | bytes 1376260
  21.9 10.5 %copy-start.11 = (bf16[128,1792]{1,0:T(8,128)(2,1)S(1)}, bf16[128,1792]{1,0:T(8,128)(2,1)}, u32[]{:S(2)}) copy-start(bf16[128,1792]{1,0:T(8,128)(2,1)} %get-tuple-element.45) | copy-start | bytes 1376260
  21.9 32.9 %copy-start.9 = (bf16[2304]{0:T(1024)(128)(2,1)S(1)}, bf16[2304]{0:T(1024)(128)(2,1)}, u32[]{:S(2)}) copy-start(bf16[2304]{0:T(1024)(128)(2,1)} %param.8) | copy-start | bytes 13828
  21.9 47.3 %copy-start = (bf16[2,64,2304]{2,1,0:T(8,128)(2,1)S(1)}, bf16[2,64,2304]{2,1,0:T(8,128)(2,1)}, u32[]{:S(2)}) copy-start(bf16[2,64,2304]{2,1,0:T(8,128)(2,1)} %dres_ref.3) | copy-start | bytes 1769476
  21.9 47.3 %copy-start.1 = (bf16[128,1792]{1,0:T(8,128)(2,1)S(1)}, bf16[128,1792]{1,0:T(8,128)(2,1)}, u32[]{:S(2)}) copy-start(bf16[128,1792]{1,0:T(8,128)(2,1)} %get-tuple-element.42.p0) | copy-start | bytes 1376260
  27.9 41.3 %copy-start.2 = (bf16[128,512]{1,0:T(8,128)(2,1)S(1)}, bf16[128,512]{1,0:T(8,128)(2,1)}, u32[]{:S(2)}) copy-start(bf16[128,512]{1,0:T(8,128)(2,1)} %get-tuple-element.48.r0) | copy-start | bytes 393220
  27.9 4.5 %collective-permute-start.5 = (bf16[128,512]{1,0:T(8,128)(2,1)}, bf16[128,512]{1,0:T(8,128)(2,1)S(1)}, u32[]{:S(2)}, u32[]{:S(2)}) collective-permute-start(bf16[128,512]{1,0:T(8,128)(2,1)} %get-tuple-element.49), channel_id=1, source_target_pairs={{0,1},{1,0},{2,3},{3,2},{4,5},{5,4},{6,7},{7,6}} | collective-permute-start | bytes 393224 | tf_op jit(solution)/shard_map/ppermute | solution.py:299
  28.2 6.6 %collective-permute-start.6 = (bf16[128,512]{1,0:T(8,128)(2,1)}, bf16[128,512]{1,0:T(8,128)(2,1)S(1)}, u32[]{:S(2)}, u32[]{:S(2)}) collective-permute-start(bf16[128,512]{1,0:T(8,128)(2,1)} %get-tuple-element.50), channel_id=1, source_target_pairs={{0,2},{1,3},{2,0},{3,1},{4,6},{5,7},{6,4},{7,5}} | collective-permute-start | bytes 393224 | tf_op jit(solution)/shard_map/ppermute | solution.py:299
  30.1 7.0 %collective-permute-start.7 = (bf16[128,512]{1,0:T(8,128)(2,1)}, bf16[128,512]{1,0:T(8,128)(2,1)S(1)}, u32[]{:S(2)}, u32[]{:S(2)}) collective-permute-start(bf16[128,512]{1,0:T(8,128)(2,1)} %get-tuple-element.51), channel_id=1, source_target_pairs={{0,3},{1,2},{2,1},{3,0},{4,7},{5,6},{6,5},{7,4}} | collective-permute-start | bytes 393224 | tf_op jit(solution)/shard_map/ppermute | solution.py:299
  30.1 24.7 %collective-permute-start.2 = (bf16[128,1792]{1,0:T(8,128)(2,1)}, bf16[128,1792]{1,0:T(8,128)(2,1)S(1)}, u32[]{:S(2)}, u32[]{:S(2)}) collective-permute-start(bf16[128,1792]{1,0:T(8,128)(2,1)} %get-tuple-element.43), channel_id=1, source_target_pairs={{0,1},{1,0},{2,3},{3,2},{4,5},{5,4},{6,7},{7,6}} | collective-permute-start | bytes 1376264 | tf_op jit(solution)/shard_map/ppermute | solution.py:299
  30.3 24.5 %collective-permute-start.3 = (bf16[128,1792]{1,0:T(8,128)(2,1)S(1)}, bf16[128,1792]{1,0:T(8,128)(2,1)S(1)}, u32[]{:S(2)}, u32[]{:S(2)}) collective-permute-start(bf16[128,1792]{1,0:T(8,128)(2,1)S(1)} %copy-done.12), channel_id=1, source_target_pairs={{0,2},{1,3},{2,0},{3,1},{4,6},{5,7},{6,4},{7,5}} | collective-permute-start | bytes 1376264 | tf_op jit(solution)/shard_map/ppermute | solution.py:299
  32.4 24.3 %collective-permute-start.4 = (bf16[128,1792]{1,0:T(8,128)(2,1)S(1)}, bf16[128,1792]{1,0:T(8,128)(2,1)S(1)}, u32[]{:S(2)}, u32[]{:S(2)}) collective-permute-start(bf16[128,1792]{1,0:T(8,128)(2,1)S(1)} %copy-done.11), channel_id=1, source_target_pairs={{0,3},{1,2},{2,1},{3,0},{4,7},{5,6},{6,5},{7,4}} | collective-permute-start | bytes 1376264 | tf_op jit(solution)/shard_map/ppermute | solution.py:299
  34.8 35.2 %collective-permute-start.9 = (bf16[128,2304]{1,0:T(8,128)(2,1)S(1)}, bf16[128,2304]{1,0:T(8,128)(2,1)S(1)}, u32[]{:S(2)}, u32[]{:S(2)}) collective-permute-start(bf16[128,2304]{1,0:T(8,128)(2,1)S(1)} %copy-done.10), channel_id=1, source_target_pairs={{0,1},{1,0},{2,3},{3,2},{4,5},{5,4},{6,7},{7,6}} | collective-permute-start | bytes 1769480 | tf_op jit(solution)/shard_map/ppermute | solution.py:299
  37.1 32.1 %collective-permute-start.1 = (bf16[128,2304]{1,0:T(8,128)(2,1)S(1)}, bf16[128,2304]{1,0:T(8,128)(2,1)S(1)}, u32[]{:S(2)}, u32[]{:S(2)}) collective-permute-start(bf16[128,2304]{1,0:T(8,128)(2,1)S(1)} %add.12.xh_ref), channel_id=1, source_target_pairs={{0,2},{1,3},{2,0},{3,1},{4,6},{5,7},{6,4},{7,5}} | collective-permute-start | bytes 1769480 | tf_op jit(solution)/shard_map/ppermute | solution.py:299
  37.7 32.2 %copy-start.7 = (bf16[128,2304]{1,0:T(8,128)(2,1)S(1)}, bf16[128,2304]{1,0:T(8,128)(2,1)}, u32[]{:S(2)}) copy-start(bf16[128,2304]{1,0:T(8,128)(2,1)} %get-tuple-element.60) | copy-start | bytes 1769476
  37.7 34.2 %slice-start = ((s8[4718592]{0:T(1024)(128)(4,1)}), s8[4194304]{0:T(1024)(128)(4,1)S(1)}, s32[]{:S(2)}) async-start(s8[4718592]{0:T(1024)(128)(4,1)} %bitcast), calls=%async_computation | async-start | bytes 8388608
  37.8 67.1 %copy-start.6 = (bf16[2,256,1024]{2,1,0:T(8,128)(2,1)S(1)}, bf16[2,256,1024]{2,1,0:T(8,128)(2,1)}, u32[]{:S(2)}) copy-start(bf16[2,256,1024]{2,1,0:T(8,128)(2,1)} %du_ref.1) | copy-start | bytes 3145732
  69.2 2.7 %slice-start.1 = ((s8[4718592]{0:T(1024)(128)(4,1)}), s8[524288]{0:T(1024)(128)(4,1)S(1)}, s32[]{:S(2)}) async-start(s8[4718592]{0:T(1024)(128)(4,1)} %bitcast), calls=%async_computation.1 | async-start | bytes 1048576
  69.9 2.0 %collective-permute-start.8 = (bf16[128,2304]{1,0:T(8,128)(2,1)S(1)}, bf16[128,2304]{1,0:T(8,128)(2,1)S(1)}, u32[]{:S(2)}, u32[]{:S(2)}) collective-permute-start(bf16[128,2304]{1,0:T(8,128)(2,1)S(1)} %get-tuple-element.57.xm_ref.refs_0_), channel_id=1, source_target_pairs={{0,1},{1,0},{2,3},{3,2},{4,5},{5,4},{6,7},{7,6}} | collective-permute-start | bytes 1769480 | tf_op jit(solution)/shard_map/ppermute | solution.py:299
  70.1 15.7 %collective-permute-start.10 = (bf16[128,2304]{1,0:T(8,128)(2,1)S(1)}, bf16[128,2304]{1,0:T(8,128)(2,1)S(1)}, u32[]{:S(2)}, u32[]{:S(2)}) collective-permute-start(bf16[128,2304]{1,0:T(8,128)(2,1)S(1)} %add.13.xh_ref), channel_id=1, source_target_pairs={{0,2},{1,3},{2,0},{3,1},{4,6},{5,7},{6,4},{7,5}} | collective-permute-start | bytes 1769480 | tf_op jit(solution)/shard_map/ppermute | solution.py:299
  87.8 17.1 %collective-permute-start.11 = (bf16[128,2304]{1,0:T(8,128)(2,1)S(1)}, bf16[128,2304]{1,0:T(8,128)(2,1)S(1)}, u32[]{:S(2)}, u32[]{:S(2)}) collective-permute-start(bf16[128,2304]{1,0:T(8,128)(2,1)S(1)} %get-tuple-element.63.xm_ref), channel_id=1, source_target_pairs={{0,1},{1,0},{2,3},{3,2},{4,5},{5,4},{6,7},{7,6}} | collective-permute-start | bytes 1769480 | tf_op jit(solution)/shard_map/ppermute | solution.py:299
  87.8 9.9 %collective-permute-start.12 = (bf16[64,2304]{1,0:T(8,128)(2,1)S(1)}, bf16[64,2304]{1,0:T(8,128)(2,1)S(1)}, u32[]{:S(2)}, u32[]{:S(2)}) collective-permute-start(bf16[64,2304]{1,0:T(8,128)(2,1)S(1)} %get-tuple-element.71.refs_0_), channel_id=1, source_target_pairs={{0,2},{1,3},{2,0},{3,1},{4,6},{5,7},{6,4},{7,5}} | collective-permute-start | bytes 884744 | tf_op jit(solution)/shard_map/ppermute | solution.py:299
  89.5 14.9 %collective-permute-start.15 = (bf16[64,2304]{1,0:T(8,128)(2,1)S(1)}, bf16[64,2304]{1,0:T(8,128)(2,1)S(1)}, u32[]{:S(2)}, u32[]{:S(2)}) collective-permute-start(bf16[64,2304]{1,0:T(8,128)(2,1)S(1)} %get-tuple-element.72.refs_4_), channel_id=1, source_target_pairs={{0,2},{1,3},{2,0},{3,1},{4,6},{5,7},{6,4},{7,5}} | collective-permute-start | bytes 884744 | tf_op jit(solution)/shard_map/ppermute | solution.py:299
  89.8 1.2 %collective-permute-start.18 = (f32[1,2304]{1,0:T(1,128)S(1)}, f32[1,2304]{1,0:T(1,128)S(1)}, u32[]{:S(2)}, u32[]{:S(2)}) collective-permute-start(f32[1,2304]{1,0:T(1,128)S(1)} %get-tuple-element.65.tok_ref), channel_id=1, source_target_pairs={{0,1},{1,0},{2,3},{3,2},{4,5},{5,4},{6,7},{7,6}} | collective-permute-start | bytes 27656 | tf_op jit(solution)/shard_map/ppermute | solution.py:299
  91.0 12.7 %collective-permute-start.19 = (f32[1,2304]{1,0:T(1,128)S(1)}, f32[1,2304]{1,0:T(1,128)S(1)}, u32[]{:S(2)}, u32[]{:S(2)}) collective-permute-start(f32[1,2304]{1,0:T(1,128)S(1)} %add.14), channel_id=1, source_target_pairs={{0,2},{1,3},{2,0},{3,1},{4,6},{5,7},{6,4},{7,5}} | collective-permute-start | bytes 27656 | tf_op jit(solution)/shard_map/ppermute | solution.py:299
  92.7 18.8 %collective-permute-start.13 = (bf16[64,2304]{1,0:T(8,128)(2,1)S(1)}, bf16[64,2304]{1,0:T(8,128)(2,1)S(1)}, u32[]{:S(2)}, u32[]{:S(2)}) collective-permute-start(bf16[64,2304]{1,0:T(8,128)(2,1)S(1)} %get-tuple-element.71.refs_0_), channel_id=1, source_target_pairs={{0,1},{1,0},{2,3},{3,2},{4,5},{5,4},{6,7},{7,6}} | collective-permute-start | bytes 884744 | tf_op jit(solution)/shard_map/ppermute | solution.py:299
  97.6 13.9 %collective-permute-start.14 = (bf16[64,2304]{1,0:T(8,128)(2,1)S(1)}, bf16[64,2304]{1,0:T(8,128)(2,1)S(1)}, u32[]{:S(2)}, u32[]{:S(2)}) collective-permute-start(bf16[64,2304]{1,0:T(8,128)(2,1)S(1)} %collective-permute-done.12.refs_1_), channel_id=1, source_target_pairs={{0,1},{1,0},{2,3},{3,2},{4,5},{5,4},{6,7},{7,6}} | collective-permute-start | bytes 884744 | tf_op jit(solution)/shard_map/ppermute | solution.py:299
  103.7 7.8 %collective-permute-start.16 = (bf16[64,2304]{1,0:T(8,128)(2,1)S(1)}, bf16[64,2304]{1,0:T(8,128)(2,1)S(1)}, u32[]{:S(2)}, u32[]{:S(2)}) collective-permute-start(bf16[64,2304]{1,0:T(8,128)(2,1)S(1)} %get-tuple-element.72.refs_4_), channel_id=1, source_target_pairs={{0,1},{1,0},{2,3},{3,2},{4,5},{5,4},{6,7},{7,6}} | collective-permute-start | bytes 884744 | tf_op jit(solution)/shard_map/ppermute | solution.py:299
  104.3 7.2 %collective-permute-start.17 = (bf16[64,2304]{1,0:T(8,128)(2,1)S(1)}, bf16[64,2304]{1,0:T(8,128)(2,1)S(1)}, u32[]{:S(2)}, u32[]{:S(2)}) collective-permute-start(bf16[64,2304]{1,0:T(8,128)(2,1)S(1)} %collective-permute-done.15.refs_5_), channel_id=1, source_target_pairs={{0,1},{1,0},{2,3},{3,2},{4,5},{5,4},{6,7},{7,6}} | collective-permute-start | bytes 884744 | tf_op jit(solution)/shard_map/ppermute | solution.py:299

commit v9 on v8

--- a/solution.py
+++ b/solution.py
@@ -63,7 +63,7 @@
         zero_wait(z, de_ref, *FILL[0], zsem)
 
 
-FILL = ((0, 2), (2, 4), (4, 6), (6, 16))
+FILL = ((0, 2), (2, 4), (4, 6), (6, 10), (10, 13), (13, 16))
 
 
 def zero_start(z, de_ref, lo, hi, sem):
@@ -112,6 +112,12 @@
     out_ref[0] = nl
     out_ref[1] = nd
     zero_wait(z, de_ref, *FILL[3], sem)
+
+
+def zero2_kernel(tok_ref, de_in, de_ref, z, sem):
+    z[...] = jnp.zeros_like(z)
+    zero_start(z, de_ref, *FILL[4], sem)
+    zero_wait(z, de_ref, *FILL[4], sem)
 
 
 def gather_kernel(ids_ref, emb_ref, k0, s0, k1, s1, lpos, lrow, cnt, de_ref, buf, tmp, xf, z, lst, sem, zsem):
@@ -137,7 +143,7 @@
         v = ids_ref[m, j & (t - 1)] - r * vl
         q = (j & (t - 1)) // tl
         pltpu.make_async_copy(emb_ref.at[pl.ds(pl.multiple_of((v >> 3) << 3, 8), 8), :], buf.at[i], sem).start()
-        lpos[i] = m * t + ((q ^ r) & 1) * h + (q >> 1) * tl + (j & (tl - 1))
+        lpos[i] = m * t + ((q ^ r) & 1) * h + ((q ^ r) >> 1) * tl + (j & (tl - 1))
         lrow[i] = v
         return c
 
@@ -168,19 +174,35 @@
     zero_wait(z, de_ref, FILL[1][0], FILL[2][1], zsem)
 
 
-def dx_kernel(m, xh_ref, z_ref, p0, p1, p2, p3, r0, r1, r2, r3, dres_ref, g_ref, tok_ref, *refs):
+def sum_kernel(k0, y0, k1, y1, a0, t0, a1, t1):
+    tl = a0.shape[0]
+    for x, y, a, t in ((k0, y0, a0, t0), (k1, y1, a1, t1)):
+        a[...] = x[0:tl, :] + y[0:tl, :]
+        t[...] = x[tl:2 * tl, :] + y[tl:2 * tl, :]
+
+
+def chip_mask(ids_ref, m, q, tl, chip_rows):
+    t = ids_ref.shape[1]
+    row = lax.broadcasted_iota(jnp.int32, (tl, t), 0) + q * tl
+    lane = lax.broadcasted_iota(jnp.int32, (tl, t), 1)
+    ids = jnp.broadcast_to(ids_ref[m:m + 1, :].astype(F32), (tl, t))
+    col = jnp.sum(jnp.where(row == lane, ids, 0.0), axis=1, keepdims=True)
+    lo = ((lax.axis_index("tp") >> 1) * chip_rows).astype(F32)
+    return jnp.logical_and(col >= lo, col < lo + chip_rows)
+
+
+def dx_kernel(m, chip_rows, xh_ref, z_ref, p0, p1, p2, p3, r0, r1, r2, r3, dres_ref, g_ref, ids_ref, tok_ref, *refs):
     if m == 1:
-        xm0_ref, dg0_ref, xm_ref, dx_ref, dg_ref, x_ref = refs
+        x0_ref, dg0_ref, x_ref, dx_ref, slot_ref, dg_ref, xs_ref = refs
     else:
-        xm_ref, dx_ref, dg_ref = refs
+        x_ref, dx_ref, slot_ref, dg_ref = refs
     tl = dx_ref.shape[0]
-    chip = lax.axis_index("tp") >> 1
-    mine = pl.ds(pl.multiple_of(chip * tl, tl), tl)
-    xm_ref[...] = xh_ref[...] + z_ref[...]
+    xh = xh_ref[...].astype(F32)
+    x = xh + z_ref[...].astype(F32)
+    x_ref[...] = x.astype(BF16)
     if m == 1:
-        x_ref[0] = xm0_ref[mine, :]
-        x_ref[1] = xm_ref[mine, :]
-    x = xm_ref[mine, :].astype(F32)
+        xs_ref[0] = x0_ref[...]
+        xs_ref[1] = x.astype(BF16)
     g = g_ref[...].astype(F32)
     rs = lax.rsqrt(jnp.mean(x * x, axis=-1, keepdims=True) + EPS)
     nh = x * rs
@@ -191,54 +213,78 @@
     gdn = g * dn
     mean = jnp.mean(nh * gdn, axis=-1, keepdims=True)
     dxn = rs * (gdn - nh * mean)
-    dx_ref[...] = (dres_ref[m].astype(F32) + dxn).astype(BF16)
+    dx = (dres_ref[m].astype(F32) + dxn).astype(BF16)
+    dx_ref[...] = dx
+    own = chip_mask(ids_ref, m, lax.axis_index("tp"), tl, chip_rows)
+    slot_ref[...] = jnp.where(own, xh, dx.astype(F32)).astype(BF16)
     dg = jnp.sum(dn * nh, axis=0, keepdims=True)
     dg_ref[...] = dg if m == 0 else dg + dg0_ref[...]
 
 
-def fill_n(xm_ref, xo_ref, g_ref, n_ref, off):
+def norm(x, g_ref):
+    rs = lax.rsqrt(jnp.mean(x * x, axis=-1, keepdims=True) + EPS)
+    return ((x * rs) * g_ref[...].astype(F32)).astype(BF16)
+
+
+def umat(n, w_ref, ub, u_ref, q0, q1, sem):
+    blk = 256
+    for i in range(ub.shape[1] // blk):
+        ub[:, i * blk:(i + 1) * blk] = jnp.dot(n, w_ref[:, i * blk:(i + 1) * blk], preferred_element_type=F32).astype(BF16)
+    k = u_ref.shape[0]
+    tl = u_ref.shape[1] // 4
+    copies = []
+    for m in range(k):
+        for a, q in enumerate((q0, q1)):
+            c = pltpu.make_async_copy(ub.at[pl.ds((m * 2 + a) * tl, tl), :],
+                                      u_ref.at[m, pl.ds(pl.multiple_of(q * tl, tl), tl), :], sem)
+            c.start()
+            copies.append(c)
+    return copies
+
+
+def u_kernel(x0, y0, x1, y1, g_ref, w_ref, tok_ref, de_in, u_ref, n_ref, flag_ref, de_ref, ub, z, usem, zsem):
+    flag_ref[0] = 0
+    z[...] = jnp.zeros_like(z)
+    zero_start(z, de_ref, *FILL[5], zsem)
     r = lax.axis_index("tp")
-    par = r & 1
-    tl = xm_ref.shape[0] // 2
-    g = g_ref[...].astype(F32)
-    for side, ref in ((0, xm_ref), (1, xo_ref)):
-        for c in range(2):
-            q = 2 * c + (par ^ side)
-            x = ref[c * tl:(c + 1) * tl, :].astype(F32)
-            rs = lax.rsqrt(jnp.mean(x * x, axis=-1, keepdims=True) + EPS)
-            n_ref[pl.ds(pl.multiple_of(off + q * tl, tl), tl), :] = ((x * rs) * g).astype(BF16)
-
-
-def umat(n_ref, w_ref, u_ref, lo):
-    t = u_ref.shape[0]
-    blk = 256
-    for i in range(u_ref.shape[1] // blk):
-        u_ref[:, i * blk:(i + 1) * blk] = jnp.dot(
-            n_ref[lo:lo + t, :], w_ref[:, i * blk:(i + 1) * blk], preferred_element_type=F32).astype(BF16)
-
-
-def u_kernel(xm_ref, xo_ref, g_ref, w_ref, tok_ref, u_ref, n_ref, flag_ref, ub, usem):
-    flag_ref[0] = 0
-    fill_n(xm_ref, xo_ref, g_ref, n_ref, 0)
-    umat(n_ref, w_ref, ub, 0)
-    c = pltpu.make_async_copy(ub, u_ref.at[0], usem)
-    c.start()
-    c.wait()
-
-
-def proj_kernel(n0_ref, xm_ref, xo_ref, g_ref, w_ref, du_ref, u_in, tok_ref, u_ref, dw_ref, flag_ref, n_ref, du2, ub, dwb, usem, wsem):
-    flag_ref[0] = 0
-    k, t = du_ref.shape[0], du_ref.shape[1]
+    tl = x0.shape[0]
+    for a, x in enumerate((x0, y0, x1, y1)):
+        n_ref[a * tl:(a + 1) * tl, :] = norm(x[...].astype(F32), g_ref)
+    for c in umat(n_ref[...], w_ref, ub, u_ref, r, r ^ 1, usem):
+        c.wait()
+    zero_wait(z, de_ref, *FILL[5], zsem)
+
+
+def last_kernel(chip_rows, last_ref, dup_ref, cnt_ref, d0, c0, a0, b0, d1, c1, a1, b1, t0, w0, t1, w1, n0_ref, ids_ref, g_ref,
+                w_ref, du_ref, u_in, de_in, u_ref, dw_ref, de_ref, xf, n_ref, du2, ub, dwb, usem, wsem, sem):
+    t = du_ref.shape[1]
     d, _ = w_ref.shape
-    copies = []
+    tl = d0.shape[0]
+    r = lax.axis_index("tp")
+    for a, ref in enumerate((d0, c0, a0, b0, d1, c1, a1, b1)):
+        xf[a * tl:(a + 1) * tl, :] = ref[...].astype(F32)
+
+    def add(i, c):
+        a = dup_ref[0, i]
+        b = dup_ref[1, i]
+        xf[pl.ds(b, 1), :] = xf[pl.ds(b, 1), :] + xf[pl.ds(a, 1), :]
+        return c
+
+    lax.fori_loop(0, cnt_ref[1], add, 0)
+
     n_ref[0:t, :] = n0_ref[...]
-    fill_n(xm_ref, xo_ref, g_ref, n_ref, t)
-    for m in range(k):
-        du2[m * t:(m + 1) * t, :] = du_ref[m]
-    umat(n_ref, w_ref, ub, t)
-    c = pltpu.make_async_copy(ub, u_ref.at[1], usem)
-    c.start()
-    copies.append(c)
+    for a, (m, q, own, got) in enumerate(((0, r ^ 2, t0, c0), (0, r ^ 3, w0, b0), (1, r ^ 2, t1, c1), (1, r ^ 3, w1, b1))):
+        x = jnp.where(chip_mask(ids_ref, m, q, tl, chip_rows), own[...].astype(F32), got[...].astype(F32))
+        n_ref[t + a * tl:t + (a + 1) * tl, :] = norm(x, g_ref)
+
+    def put(i, c):
+        pltpu.make_async_copy(xf.at[pl.ds(last_ref[0, i], 1), :], de_ref.at[pl.ds(last_ref[1, i], 1), :], sem).start()
+        return c
+
+    lax.fori_loop(0, cnt_ref[0], put, 0)
+    for a, (m, q) in enumerate(((0, r), (0, r ^ 1), (1, r), (1, r ^ 1), (0, r ^ 2), (0, r ^ 3), (1, r ^ 2), (1, r ^ 3))):
+        du2[a * tl:(a + 1) * tl, :] = du_ref[m, pl.ds(pl.multiple_of(q * tl, tl), tl), :]
+    copies = umat(n_ref[t:2 * t, :], w_ref, ub, u_ref, r ^ 2, r ^ 3, usem)
     blk = 256
     for i in range(d // blk):
         dwb[i] = lax.dot_general(n_ref[:, i * blk:(i + 1) * blk], du2[...], (((0,), (0,)), ((), ())),
@@ -246,36 +292,14 @@
         c = pltpu.make_async_copy(dwb.at[i], dw_ref.at[pl.ds(i * blk, blk), :], wsem)
         c.start()
         copies.append(c)
+
+    def wait(i, c):
+        pltpu.make_async_copy(xf.at[pl.ds(0, 1), :], de_ref.at[pl.ds(0, 1), :], sem).wait()
+        return c
+
+    lax.fori_loop(0, cnt_ref[0], wait, 0)
     for c in copies:
         c.wait()
-
-
-def scatter_kernel(last_ref, dup_ref, cnt_ref, *refs):
-    ds, de_ref, xf, sem = refs[:8], refs[-3], refs[-2], refs[-1]
-    tl = ds[0].shape[0]
-    chip = lax.axis_index("tp") >> 1
-    for a, ref in enumerate(ds):
-        c = chip if a % 2 == 0 else 1 - chip
-        xf[pl.ds(pl.multiple_of((a // 2) * 2 * tl + c * tl, tl), tl), :] = ref[...].astype(F32)
-
-    def add(i, c):
-        a = dup_ref[0, i]
-        b = dup_ref[1, i]
-        xf[pl.ds(b, 1), :] = xf[pl.ds(b, 1), :] + xf[pl.ds(a, 1), :]
-        return c
-
-    lax.fori_loop(0, cnt_ref[1], add, 0)
-
-    def put(i, c):
-        pltpu.make_async_copy(xf.at[pl.ds(last_ref[0, i], 1), :], de_ref.at[pl.ds(last_ref[1, i], 1), :], sem).start()
-        return c
-
-    def wait(i, c):
-        pltpu.make_async_copy(xf.at[pl.ds(0, 1), :], de_ref.at[pl.ds(0, 1), :], sem).wait()
-        return c
-
-    lax.fori_loop(0, cnt_ref[0], put, 0)
-    lax.fori_loop(0, cnt_ref[0], wait, 0)
 
 
 def solution(mesh):
@@ -323,47 +347,52 @@
         v3 = perm(r3, diag)
         q1 = perm(p1, sib)
         v1 = perm(r1, sib)
-        xh0 = k0 + y0
-        xh1 = k1 + y1
-        z0 = perm(xh0, cross)
-        z1 = perm(xh1, cross)
+        own0, oth0, own1, oth1 = call(sum_kernel, 16, [S((tl, d), BF16)] * 4, [VMEM] * 4, [VMEM] * 4, [],
+                                      8 * tl * d, 24 * tl * d)(k0, y0, k1, y1)
+        z0 = perm(oth0, cross)
+        z1 = perm(oth1, cross)
+        w0 = perm(oth0, sib)
+        w1 = perm(oth1, sib)
         last, dup, cnt, de = call(
             zero_kernel, 8, [S((2, 2 * h + 8), jnp.int32)] * 2 + [S((8,), jnp.int32), S((vl, d), F32)],
             [SMEM] * 3 + [HBM], [SMEM] * 3 + [HBM],
             [pltpu.VMEM((256, d), F32), pltpu.SMEM((2 * h + 8,), jnp.int32), pltpu.SMEM((vl,), jnp.int32), D],
-            10_000_000_000, 4 * vl * d, {3: 3})(lpos, lrow, nown, de)
+            3_000_000_000, vl * d, {3: 3})(lpos, lrow, nown, de)
 
         def dxk(m, xh, z, tok, more):
-            outs = [S((n, d), BF16), S((tl, d), BF16), S((1, d), F32)] + ([S((k, tl, d), BF16)] if m else [])
-            return call(functools.partial(dx_kernel, m), 16, outs, [VMEM] * 12 + [SMEM if m else HBM] + [VMEM] * len(more),
-                        [VMEM] * len(outs), [], 30 * n * d, 16 * n * d)(xh, z, p0, q1, q2, q3, r0, v1, v2, v3, dres, g2, tok, *more)
-
-        xm0, dx0, dg0 = dxk(0, xh0, z0, de, ())
-        c0 = perm(dx0, cross)
-        xo0 = perm(xm0, sib)
+            outs = [S((tl, d), BF16)] * 3 + [S((1, d), F32)] + ([S((k, tl, d), BF16)] if m else [])
+            return call(functools.partial(dx_kernel, m, 2 * vl), 16, outs,
+                        [VMEM] * 13 + [HBM] + [VMEM] * len(more),
+                        [VMEM] * len(outs), [], 30 * n * d, 16 * n * d)(
+                            xh, z, p0, q1, q2, q3, r0, v1, v2, v3, dres, g2, ids, tok, *more)
+
+        x0, dx0, slot0, dg0 = dxk(0, own0, z0, de, ())
+        c0 = perm(slot0, cross)
+        de = call(zero2_kernel, 8, S((vl, d), F32), [VMEM, HBM], HBM, [pltpu.VMEM((256, d), F32), D],
+                  2_000_000_000, vl * d, {1: 0})(dg0, de)
+        x1, dx1, slot1, dg, x = dxk(1, own1, z1, de, (x0, dg0))
+        c1 = perm(slot1, cross)
+        xo0 = perm(x0, sib)
+        xo1 = perm(x1, sib)
         a0 = perm(dx0, sib)
-        u, n0, done0 = call(
-            u_kernel, 24, [S((k, t, fc), BF16), S((t, d), BF16), S((8,), jnp.int32)], [VMEM] * 5, [HBM, VMEM, SMEM],
-            [pltpu.VMEM((t, fc), BF16), D], 2 * t * d * fc, 2 * d * fc)(xm0, xo0, g2, w, dg0)
-        xm1, dx1, dg, x = dxk(1, xh1, z1, done0, (xm0, dg0))
-        c1 = perm(dx1, cross)
-        xo1 = perm(xm1, sib)
         a1 = perm(dx1, sib)
+        u, nown2, _, de = call(
+            u_kernel, 28, [S((k, t, fc), BF16), S((t, d), BF16), S((8,), jnp.int32), S((vl, d), F32)],
+            [VMEM] * 7 + [HBM], [HBM, VMEM, SMEM, HBM],
+            [pltpu.VMEM((t, fc), BF16), pltpu.VMEM((256, d), F32), D, D], 2 * t * d * fc, 2 * d * fc,
+            {7: 3})(x0, xo0, x1, xo1, g2, w, dg, de)
         b0 = perm(c0, sib)
         b1 = perm(c1, sib)
         dgs = dg + perm(dg, sib)
         dgs = dgs + perm(dgs, cross)
 
-        u, dw, done1 = call(
-            proj_kernel, 36, [S((k, t, fc), BF16), S((d, fc), F32), S((8,), jnp.int32)],
-            [VMEM] * 6 + [HBM, VMEM], [HBM, HBM, SMEM],
-            [pltpu.VMEM((k * t, d), BF16), pltpu.VMEM((k * t, fc), BF16), pltpu.VMEM((t, fc), BF16),
-             pltpu.VMEM((d // 256, 256, fc), F32), D, D],
-            3 * k * t * d * fc, 6 * d * fc, {6: 0})(n0, xm1, xo1, g2, w, du, u, dg)
-
-        de = call(scatter_kernel, 16, S((vl, d), F32), [SMEM] * 3 + [VMEM] * 8 + [SMEM, HBM], HBM,
-                  [pltpu.VMEM((2 * h, d), F32), D], 8 * h * d, 8 * h * d,
-                  {12: 0})(last, dup, cnt, dx0, c0, a0, b0, dx1, c1, a1, b1, done1, de)
+        u, dw, de = call(
+            functools.partial(last_kernel, 2 * vl), 44, [S((k, t, fc), BF16), S((d, fc), F32), S((vl, d), F32)],
+            [SMEM] * 3 + [VMEM] * 17 + [HBM] * 2, [HBM] * 3,
+            [pltpu.VMEM((2 * h, d), F32), pltpu.VMEM((k * t, d), BF16), pltpu.VMEM((k * t, fc), BF16), pltpu.VMEM((t, fc), BF16),
+             pltpu.VMEM((d // 256, 256, fc), F32), D, D, D],
+            3 * k * t * d * fc, 6 * d * fc, {20: 0, 21: 2})(
+                last, dup, cnt, dx0, c0, a0, b0, dx1, c1, a1, b1, oth0, w0, oth1, w1, nown2, ids, g2, w, du, u, de)
         return u, x, de, dw, dgs.reshape(d)
 
     return jax.shard_map(

time: 116 us -> 112 us (0.966)
  waiting for transfers between devices: 41.9 us -> 34.8 us
  starting transfers between devices: 11.4 us -> 13.7 us
    pallas_call x5 -> x6, Pallas kernels: 16.4 us -> 26 us  [the longest x1 10.9 us: local(): call(functools.partial(last_kernel, 2 * vl), 44, [S((k, t, fc), BF16), S(...]
    pallas_call x1, Pallas kernels: 17 us -> 8.05 us  [local(): call(zero_kernel, 8, [S((2, 2 * h + 8), jnp.int32)] * 2 + [S((8,), jnp.in...]
    ppermute x20 -> x22, waiting for transfers between devices: 41.9 us -> 34.8 us  [perm(): return lax.ppermute(v, 'tp', p)]
    ppermute x20 -> x22, starting transfers between devices: 11.4 us -> 13.7 us  [perm(): return lax.ppermute(v, 'tp', p)]
  transfers between devices with their start and end apart: 20 -> 22, of which waited for: 9 -> 3; matrix products, arithmetic and copies ran while one was open for 1% -> 1% of each run, Pallas kernels for 37% -> 34%
where the time goes in v9:
time: 112 us; the launch traced here: 111 us
  Pallas kernels  60.8 us (54%)
  waiting for transfers between devices  34.8 us (31%)
  starting transfers between devices  13.7 us (12%)
    ppermute x22, waiting for transfers between devices, perm(): return lax.ppermute(v, 'tp', p)  34.8 us
    ppermute x22, starting transfers between devices, perm(): return lax.ppermute(v, 'tp', p)  13.7 us
    pallas_call x1, Pallas kernels, local(): call(gather_kernel, 60, [S((n, d), BF16)] * 4 + [S((2 * h + 8,), jnp.int3...  12.2 us
    pallas_call x1, Pallas kernels, local(): call(functools.partial(last_kernel, 2 * vl), 44, [S((k, t, fc), BF16), S(...  10.9 us
    pallas_call x1, Pallas kernels, local(): call(functools.partial(pdn_kernel, 0, True), 60, [S((n, d1), BF16)] * 4 +...  8.62 us
    pallas_call x1, Pallas kernels, local(): call(zero_kernel, 8, [S((2, 2 * h + 8), jnp.int32)] * 2 + [S((8,), jnp.in...  8.05 us
    pallas_call x1, Pallas kernels, local(): call(u_kernel, 28, [S((k, t, fc), BF16), S((t, d), BF16), S((8,), jnp.int...  7.44 us
    pallas_call x1, Pallas kernels, local(): call(functools.partial(pdn_kernel, d1, False), 60, [S((n, d2), BF16)] * 4...  5.97 us
  transfers between devices with their start and end apart: 22, of which 3 were waited for; matrix products, arithmetic and copies ran while one was open for 1% of the time, Pallas kernels for 34%

profile of v9, /device:TPU:0, one launch (start us, length us, event | category | flops | bytes accessed | tf_op | source)
XLA Modules:
  0.0 111.2 jit_solution(2182845786605253477)
XLA Ops:
  0.6 12.2 %shard_map.101 = (bf16[128,2304]{1,0:T(8,128)(2,1)}, bf16[128,2304]{1,0:T(8,128)(2,1)}, bf16[128,2304]{1,0:T(8,128)(2,1)}, bf16[128,2304]{1,0:T(8,128)(2,1)}, s3...) custom-call(s32[2,256]{1,0:T(2,128)} %ids_ref.7, bf16[8192,2304]{1,0:T(8,128)(2,1)} %emb_ref.1), custom_call_target="tpu_custom_call" | custom-call | flops 500000000 | bytes 9437184 | tf_op jit(solution)/shard_map/pallas_call | solution.py:333
  12.9 0.0 copy-start.3
  12.9 0.0 copy-start.4
  12.9 0.0 copy-start.7
  12.9 0.4 collective-permute-start
  13.3 0.1 collective-permute-start.1
  13.5 8.6 %shard_map.102 = (bf16[128,1792]{1,0:T(8,128)(2,1)}, bf16[128,1792]{1,0:T(8,128)(2,1)}, bf16[128,1792]{1,0:T(8,128)(2,1)}, bf16[128,1792]{1,0:T(8,128)(2,1)}, bf16[512,1024]{1,0:T(8,128)(2,1)}) custom-call(bf16[2,256,1024]{2,1,0:T(8,128)(2,1)} %du_ref.1, bf16[2304,1024]{1,0:T(8,128)(2,1)} %w_ref.3), custom_call_target="tpu_custom_call" | custom-call | flops 1879048192 | bytes 6553600 | tf_op jit(solution)/shard_map/pallas_call | solution.py:327
  22.1 0.0 copy-start.10
  22.1 0.0 copy-start
  22.1 0.0 copy-start.6
  22.1 6.0 %shard_map.103 = (bf16[128,512]{1,0:T(8,128)(2,1)}, bf16[128,512]{1,0:T(8,128)(2,1)}, bf16[128,512]{1,0:T(8,128)(2,1)}, bf16[128,512]{1,0:T(8,128)(2,1)}, f32[8192,2304]{1,0:T(8,128)}) custom-call(bf16[512,1024]{1,0:T(8,128)(2,1)} %get-tuple-element.49.refs_0_, bf16[2304,1024]{1,0:T(8,128)(2,1)} %w_ref.3, ...), custom_call_target="tpu_custom_call", output_to_operand_aliasing={{4}: (2, {})} | custom-call | flops 536870912 | bytes 2621440 | tf_op jit(solution)/shard_map/pallas_call | solution.py:342
  28.1 0.4 collective-permute-start.6
  28.5 0.2 collective-permute-start.3
  28.7 2.0 %collective-permute-start.4 = (bf16[128,1792]{1,0:T(8,128)(2,1)}, bf16[128,1792]{1,0:T(8,128)(2,1)S(1)}, u32[]{:S(2)}, u32[]{:S(2)}) collective-permute-start(bf16[128,1792]{1,0:T(8,128)(2,1)} %get-tuple-element.63), channel_id=1, source_target_pairs={{0,2},{1,3},{2,0},{3,1},{4,6},{5,7},{6,4},{7,5}} | collective-permute-start | bytes 1376264 | tf_op jit(solution)/shard_map/ppermute | solution.py:323
  30.6 0.0 collective-permute-done.6.r1
  30.6 0.8 collective-permute-start.5
  31.4 0.0 collective-permute-done.y0
  31.4 0.6 collective-permute-start.7
  32.0 0.0 collective-permute-done.1.y1
  32.0 1.1 %collective-permute-start.8 = (bf16[128,512]{1,0:T(8,128)(2,1)}, bf16[128,512]{1,0:T(8,128)(2,1)S(1)}, u32[]{:S(2)}, u32[]{:S(2)}) collective-permute-start(bf16[128,512]{1,0:T(8,128)(2,1)} %get-tuple-element.68), channel_id=1, source_target_pairs={{0,3},{1,2},{2,1},{3,0},{4,7},{5,6},{6,5},{7,4}} | collective-permute-start | bytes 393224 | tf_op jit(solution)/shard_map/ppermute | solution.py:323
  33.2 0.1 shard_map.105
  33.3 21.6 %collective-permute-done.7.r2 = bf16[128,512]{1,0:T(8,128)(2,1)S(1)} collective-permute-done((bf16[128,512]{1,0:T(8,128)(2,1)}, bf16[128,512]{1,0:T(8,128)(2,1)S(1)}, u32[]{:S(2)}, u32[]{:S(2)}) %collective-permute-start.7) | collective-permute-done | bytes 131104 | tf_op jit(solution)/shard_map/ppermute | solution.py:323
  54.9 2.0 %collective-permute-start.2 = (bf16[64,2304]{1,0:T(8,128)(2,1)S(1)}, bf16[64,2304]{1,0:T(8,128)(2,1)S(1)}, u32[]{:S(2)}, u32[]{:S(2)}) collective-permute-start(bf16[64,2304]{1,0:T(8,128)(2,1)S(1)} %get-tuple-element.60.t0), channel_id=1, source_target_pairs={{0,2},{1,3},{2,0},{3,1},{4,6},{5,7},{6,4},{7,5}} | collective-permute-start | bytes 884744 | tf_op jit(solution)/shard_map/ppermute | solution.py:323
  56.9 0.4 collective-permute-done.8.r3
  57.3 0.5 collective-permute-start.12
  57.8 8.0 %shard_map.104 = (s32[2,520]{1,0:T(2,128)S(1)}, s32[2,520]{1,0:T(2,128)S(1)}, s32[8]{0:T(128)S(1)}, f32[8192,2304]{1,0:T(8,128)}) custom-call(s32[520]{0:T(1024)S(1)} %copy-done.7, s32[520]{0:T(1024)S(1)} %copy-done.8, s32[8]{0:T(128)S(1)} %copy-done.9, f32[8192,2304]{1,0:T(8,128)} %get-tuple-element.51.de_in), custom_call_target="tpu_custom_call", output_to_operand_aliasing={{3}: (3, {})} | custom-call | flops 3000000000 | bytes 18874368 | tf_op jit(solution)/shard_map/pallas_call | solution.py:356
  65.9 0.0 collective-permute-done.3.p1
  65.9 1.4 %collective-permute-start.16 = (bf16[64,2304]{1,0:T(8,128)(2,1)S(1)}, bf16[64,2304]{1,0:T(8,128)(2,1)S(1)}, u32[]{:S(2)}, u32[]{:S(2)}) collective-permute-start(bf16[64,2304]{1,0:T(8,128)(2,1)S(1)} %get-tuple-element.60.t0), channel_id=1, source_target_pairs={{0,1},{1,0},{2,3},{3,2},{4,5},{5,4},{6,7},{7,6}} | collective-permute-start | bytes 884744 | tf_op jit(solution)/shard_map/ppermute | solution.py:323
  67.3 0.0 collective-permute-done.4.p2
  67.3 0.0 collective-permute-done.5.p3
  67.3 0.0 collective-permute-done.2.z_ref
  67.4 0.8 shard_map.106
  68.2 5.2 %shard_map.107.tok_ref.de_in = f32[8192,2304]{1,0:T(8,128)} custom-call(f32[1,2304]{1,0:T(1,128)S(1)} %get-tuple-element.74.tok_ref.refs_1_, f32[8192,2304]{1,0:T(8,128)} %get-tuple-element.69.tok_ref.de_in), custom_call_target="tpu_custom_call", output_to_operand_aliasing={{}: (1, {})} | custom-call | flops 2000000000 | bytes 18874368 | tf_op jit(solution)/shard_map/pallas_call | solution.py:371
  73.4 0.0 slice-start
  73.4 0.0 collective-permute-done.12.z_ref
  73.4 0.0 slice-start.1
  73.5 0.0 copy-start.2
  73.5 1.5 %shard_map.108 = (bf16[64,2304]{1,0:T(8,128)(2,1)S(1)}, bf16[64,2304]{1,0:T(8,128)(2,1)S(1)}, bf16[64,2304]{1,0:T(8,128)(2,1)S(1)}, f32[1,2304]{1,0:T(1,128)S(1)}, bf16[2,64,2304]{2,1,0:T(8,128)(2,1)}) custom-call(bf16[64,2304]{1,0:T(8,128)(2,1)S(1)} %get-tuple-element.72.xh_ref, bf16[64,2304]{1,0:T(8,128)(2,1)S(1)} %collective-permute-done.12.z_ref, ...), custom_call_target="tpu_custom_call" | custom-call | flops 8847360 | bytes 4718592 | tf_op jit(solution)/shard_map/pallas_call | solution.py:364
  74.9 0.0 collective-permute-start.20
  75.0 0.6 collective-permute-start.9
  75.6 1.4 %collective-permute-start.13 = (bf16[64,2304]{1,0:T(8,128)(2,1)S(1)}, bf16[64,2304]{1,0:T(8,128)(2,1)S(1)}, u32[]{:S(2)}, u32[]{:S(2)}) collective-permute-start(bf16[64,2304]{1,0:T(8,128)(2,1)S(1)} %get-tuple-element.77), channel_id=1, source_target_pairs={{0,2},{1,3},{2,0},{3,1},{4,6},{5,7},{6,4},{7,5}} | collective-permute-start | bytes 884744 | tf_op jit(solution)/shard_map/ppermute | solution.py:323
  77.0 0.0 collective-permute-start.18
  77.0 0.0 collective-permute-done.20
  77.0 0.5 collective-permute-start.19
  77.5 0.0 collective-permute-done.16.w0
  77.5 0.6 collective-permute-start.21
  78.2 12.7 %collective-permute-done.21 = f32[1,2304]{1,0:T(1,128)S(1)} collective-permute-done((f32[1,2304]{1,0:T(1,128)S(1)}, f32[1,2304]{1,0:T(1,128)S(1)}, u32[]{:S(2)}, u32[]{:S(2)}) %collective-permute-start.21) | collective-permute-done | bytes 9248 | tf_op jit(solution)/shard_map/ppermute | solution.py:323
  90.9 0.0 collective-permute-start.17
  90.9 0.0 collective-permute-done.9.c0
  90.9 0.5 collective-permute-start.10
  91.4 0.0 collective-permute-done.13.c1
  91.4 0.0 collective-permute-start.14
  91.4 0.0 collective-permute-done.18.y0
  91.4 0.5 collective-permute-start.11
  91.9 0.0 collective-permute-done.19.y1
  91.9 0.0 collective-permute-start.15
  91.9 0.6 add_reduce_fusion
  92.6 7.4 %shard_map.109 = (bf16[2,256,1024]{2,1,0:T(8,128)(2,1)}, bf16[256,2304]{1,0:T(8,128)(2,1)S(1)}, s32[8]{0:T(128)}, f32[8192,2304]{1,0:T(8,128)}) custom-call(bf16[64,2304]{1,0:T(8,128)(2,1)S(1)} %get-tuple-element.75.refs_0_.x0, bf16[64,2304]{1,0:T(8,128)(2,1)S(1)} %collective-permute-done.18.y0, ...), custom_call_target="tpu_custom_call", output_to_operand_aliasing={{3}: (7, {})} | custom-call | flops 1207959552 | bytes 4718592 | tf_op jit(solution)/shard_map/pallas_call | solution.py:379
  100.0 0.0 collective-permute-done.17.w1
  100.0 0.0 collective-permute-done.10.a0
  100.1 0.0 collective-permute-done.14.a1
  100.1 0.0 collective-permute-done.11.b0
  100.1 0.0 collective-permute-done.15.b1
  100.1 10.9 %shard_map.110 = (bf16[2,256,1024]{2,1,0:T(8,128)(2,1)}, f32[2304,1024]{1,0:T(8,128)}, f32[8192,2304]{1,0:T(8,128)}) custom-call(s32[2,520]{1,0:T(2,128)S(1)} %get-tuple-element.52.last_ref, s32[2,520]{1,0:T(2,128)S(1)} %get-tuple-element.53.dup_ref, s32[8]{0:T(128)S(1)} %get-tuple-element.54.cnt_ref, ...), custom_call_target="tpu_custom_call", output_to_operand_aliasing={{0}: (20, {}), {2}: (21, {})} | custom-call | flops 3623878656 | bytes 14155776 | tf_op jit(solution)/shard_map/pallas_call | solution.py:389
  (22 shorter events, 0.1 us)
Async XLA Ops:
  12.9 20.3 %copy-start.3 = (bf16[128,2304]{1,0:T(8,128)(2,1)S(1)}, bf16[128,2304]{1,0:T(8,128)(2,1)}, u32[]{:S(2)}) copy-start(bf16[128,2304]{1,0:T(8,128)(2,1)} %get-tuple-element.55.k0) | copy-start | bytes 1769476
  12.9 20.3 %copy-start.4 = (bf16[128,2304]{1,0:T(8,128)(2,1)S(1)}, bf16[128,2304]{1,0:T(8,128)(2,1)}, u32[]{:S(2)}) copy-start(bf16[128,2304]{1,0:T(8,128)(2,1)} %get-tuple-element.57.k1) | copy-start | bytes 1769476
  12.9 44.9 %copy-start.7 = (s32[520]{0:T(1024)S(1)}, s32[520]{0:T(1024)}, u32[]{:S(2)}) copy-start(s32[520]{0:T(1024)} %get-tuple-element.46.lpos) | copy-start | bytes 6244
  12.9 44.9 %copy-start.8 = (s32[520]{0:T(1024)S(1)}, s32[520]{0:T(1024)}, u32[]{:S(2)}) copy-start(s32[520]{0:T(1024)} %get-tuple-element.47.lrow) | copy-start | bytes 6244
  12.9 44.9 %copy-start.9 = (s32[8]{0:T(128)S(1)}, s32[8]{0:T(128)}, u32[]{:S(2)}) copy-start(s32[8]{0:T(128)} %get-tuple-element.48.cnt) | copy-start | bytes 100
  12.9 18.5 %collective-permute-start = (bf16[128,2304]{1,0:T(8,128)(2,1)}, bf16[128,2304]{1,0:T(8,128)(2,1)S(1)}, u32[]{:S(2)}, u32[]{:S(2)}) collective-permute-start(bf16[128,2304]{1,0:T(8,128)(2,1)} %get-tuple-element.56), channel_id=1, source_target_pairs={{0,1},{1,0},{2,3},{3,2},{4,5},{5,4},{6,7},{7,6}} | collective-permute-start | bytes 1769480 | tf_op jit(solution)/shard_map/ppermute | solution.py:323
  13.3 18.7 %collective-permute-start.1 = (bf16[128,2304]{1,0:T(8,128)(2,1)}, bf16[128,2304]{1,0:T(8,128)(2,1)S(1)}, u32[]{:S(2)}, u32[]{:S(2)}) collective-permute-start(bf16[128,2304]{1,0:T(8,128)(2,1)} %get-tuple-element.58), channel_id=1, source_target_pairs={{0,1},{1,0},{2,3},{3,2},{4,5},{5,4},{6,7},{7,6}} | collective-permute-start | bytes 1769480 | tf_op jit(solution)/shard_map/ppermute | solution.py:323
  22.1 8.6 %copy-start.11 = (bf16[128,1792]{1,0:T(8,128)(2,1)S(1)}, bf16[128,1792]{1,0:T(8,128)(2,1)}, u32[]{:S(2)}) copy-start(bf16[128,1792]{1,0:T(8,128)(2,1)} %get-tuple-element.64) | copy-start | bytes 1376260
  22.1 43.8 %copy-start.10 = (bf16[2304]{0:T(1024)(128)(2,1)S(1)}, bf16[2304]{0:T(1024)(128)(2,1)}, u32[]{:S(2)}) copy-start(bf16[2304]{0:T(1024)(128)(2,1)} %param.8) | copy-start | bytes 13828
  22.1 45.3 %copy-start = (bf16[2,64,2304]{2,1,0:T(8,128)(2,1)S(1)}, bf16[2,64,2304]{2,1,0:T(8,128)(2,1)}, u32[]{:S(2)}) copy-start(bf16[2,64,2304]{2,1,0:T(8,128)(2,1)} %dres_ref.3) | copy-start | bytes 1769476
  22.1 45.2 %copy-start.1 = (bf16[128,1792]{1,0:T(8,128)(2,1)S(1)}, bf16[128,1792]{1,0:T(8,128)(2,1)}, u32[]{:S(2)}) copy-start(bf16[128,1792]{1,0:T(8,128)(2,1)} %get-tuple-element.61.p0) | copy-start | bytes 1376260
  22.1 45.2 %copy-start.6 = (s32[2,256]{1,0:T(2,128)S(1)}, s32[2,256]{1,0:T(2,128)}, u32[]{:S(2)}) copy-start(s32[2,256]{1,0:T(2,128)} %ids_ref.7) | copy-start | bytes 6148
  28.1 39.3 %copy-start.5 = (bf16[128,512]{1,0:T(8,128)(2,1)S(1)}, bf16[128,512]{1,0:T(8,128)(2,1)}, u32[]{:S(2)}) copy-start(bf16[128,512]{1,0:T(8,128)(2,1)} %get-tuple-element.65.r0) | copy-start | bytes 393220
  28.1 2.5 %collective-permute-start.6 = (bf16[128,512]{1,0:T(8,128)(2,1)}, bf16[128,512]{1,0:T(8,128)(2,1)S(1)}, u32[]{:S(2)}, u32[]{:S(2)}) collective-permute-start(bf16[128,512]{1,0:T(8,128)(2,1)} %get-tuple-element.66), channel_id=1, source_target_pairs={{0,1},{1,0},{2,3},{3,2},{4,5},{5,4},{6,7},{7,6}} | collective-permute-start | bytes 393224 | tf_op jit(solution)/shard_map/ppermute | solution.py:323
  28.5 37.4 %collective-permute-start.3 = (bf16[128,1792]{1,0:T(8,128)(2,1)}, bf16[128,1792]{1,0:T(8,128)(2,1)S(1)}, u32[]{:S(2)}, u32[]{:S(2)}) collective-permute-start(bf16[128,1792]{1,0:T(8,128)(2,1)} %get-tuple-element.62), channel_id=1, source_target_pairs={{0,1},{1,0},{2,3},{3,2},{4,5},{5,4},{6,7},{7,6}} | collective-permute-start | bytes 1376264 | tf_op jit(solution)/shard_map/ppermute | solution.py:323
  28.7 38.7 %collective-permute-start.4 = (bf16[128,1792]{1,0:T(8,128)(2,1)}, bf16[128,1792]{1,0:T(8,128)(2,1)S(1)}, u32[]{:S(2)}, u32[]{:S(2)}) collective-permute-start(bf16[128,1792]{1,0:T(8,128)(2,1)} %get-tuple-element.63), channel_id=1, source_target_pairs={{0,2},{1,3},{2,0},{3,1},{4,6},{5,7},{6,4},{7,5}} | collective-permute-start | bytes 1376264 | tf_op jit(solution)/shard_map/ppermute | solution.py:323
  30.6 36.7 %collective-permute-start.5 = (bf16[128,1792]{1,0:T(8,128)(2,1)S(1)}, bf16[128,1792]{1,0:T(8,128)(2,1)S(1)}, u32[]{:S(2)}, u32[]{:S(2)}) collective-permute-start(bf16[128,1792]{1,0:T(8,128)(2,1)S(1)} %copy-done.11), channel_id=1, source_target_pairs={{0,3},{1,2},{2,1},{3,0},{4,7},{5,6},{6,5},{7,4}} | collective-permute-start | bytes 1376264 | tf_op jit(solution)/shard_map/ppermute | solution.py:323
  31.4 23.5 %collective-permute-start.7 = (bf16[128,512]{1,0:T(8,128)(2,1)}, bf16[128,512]{1,0:T(8,128)(2,1)S(1)}, u32[]{:S(2)}, u32[]{:S(2)}) collective-permute-start(bf16[128,512]{1,0:T(8,128)(2,1)} %get-tuple-element.67), channel_id=1, source_target_pairs={{0,2},{1,3},{2,0},{3,1},{4,6},{5,7},{6,4},{7,5}} | collective-permute-start | bytes 393224 | tf_op jit(solution)/shard_map/ppermute | solution.py:323
  32.0 25.3 %collective-permute-start.8 = (bf16[128,512]{1,0:T(8,128)(2,1)}, bf16[128,512]{1,0:T(8,128)(2,1)S(1)}, u32[]{:S(2)}, u32[]{:S(2)}) collective-permute-start(bf16[128,512]{1,0:T(8,128)(2,1)} %get-tuple-element.68), channel_id=1, source_target_pairs={{0,3},{1,2},{2,1},{3,0},{4,7},{5,6},{6,5},{7,4}} | collective-permute-start | bytes 393224 | tf_op jit(solution)/shard_map/ppermute | solution.py:323
  54.9 12.4 %collective-permute-start.2 = (bf16[64,2304]{1,0:T(8,128)(2,1)S(1)}, bf16[64,2304]{1,0:T(8,128)(2,1)S(1)}, u32[]{:S(2)}, u32[]{:S(2)}) collective-permute-start(bf16[64,2304]{1,0:T(8,128)(2,1)S(1)} %get-tuple-element.60.t0), channel_id=1, source_target_pairs={{0,2},{1,3},{2,0},{3,1},{4,6},{5,7},{6,4},{7,5}} | collective-permute-start | bytes 884744 | tf_op jit(solution)/shard_map/ppermute | solution.py:323
  57.3 16.1 %collective-permute-start.12 = (bf16[64,2304]{1,0:T(8,128)(2,1)S(1)}, bf16[64,2304]{1,0:T(8,128)(2,1)S(1)}, u32[]{:S(2)}, u32[]{:S(2)}) collective-permute-start(bf16[64,2304]{1,0:T(8,128)(2,1)S(1)} %get-tuple-element.73.t1), channel_id=1, source_target_pairs={{0,2},{1,3},{2,0},{3,1},{4,6},{5,7},{6,4},{7,5}} | collective-permute-start | bytes 884744 | tf_op jit(solution)/shard_map/ppermute | solution.py:323
  65.9 11.6 %collective-permute-start.16 = (bf16[64,2304]{1,0:T(8,128)(2,1)S(1)}, bf16[64,2304]{1,0:T(8,128)(2,1)S(1)}, u32[]{:S(2)}, u32[]{:S(2)}) collective-permute-start(bf16[64,2304]{1,0:T(8,128)(2,1)S(1)} %get-tuple-element.60.t0), channel_id=1, source_target_pairs={{0,1},{1,0},{2,3},{3,2},{4,5},{5,4},{6,7},{7,6}} | collective-permute-start | bytes 884744 | tf_op jit(solution)/shard_map/ppermute | solution.py:323
  73.4 19.2 %slice-start = ((s8[4718592]{0:T(1024)(128)(4,1)}), s8[4194304]{0:T(1024)(128)(4,1)S(1)}, s32[]{:S(2)}) async-start(s8[4718592]{0:T(1024)(128)(4,1)} %bitcast), calls=%async_computation | async-start | bytes 8388608
  73.4 19.1 %slice-start.1 = ((s8[4718592]{0:T(1024)(128)(4,1)}), s8[524288]{0:T(1024)(128)(4,1)S(1)}, s32[]{:S(2)}) async-start(s8[4718592]{0:T(1024)(128)(4,1)} %bitcast), calls=%async_computation.1 | async-start | bytes 1048576
  73.5 26.6 %copy-start.2 = (bf16[2,256,1024]{2,1,0:T(8,128)(2,1)S(1)}, bf16[2,256,1024]{2,1,0:T(8,128)(2,1)}, u32[]{:S(2)}) copy-start(bf16[2,256,1024]{2,1,0:T(8,128)(2,1)} %du_ref.1) | copy-start | bytes 3145732
  74.9 2.1 %collective-permute-start.20 = (f32[1,2304]{1,0:T(1,128)S(1)}, f32[1,2304]{1,0:T(1,128)S(1)}, u32[]{:S(2)}, u32[]{:S(2)}) collective-permute-start(f32[1,2304]{1,0:T(1,128)S(1)} %get-tuple-element.79.tok_ref), channel_id=1, source_target_pairs={{0,1},{1,0},{2,3},{3,2},{4,5},{5,4},{6,7},{7,6}} | collective-permute-start | bytes 27656 | tf_op jit(solution)/shard_map/ppermute | solution.py:323
  75.0 15.9 %collective-permute-start.9 = (bf16[64,2304]{1,0:T(8,128)(2,1)S(1)}, bf16[64,2304]{1,0:T(8,128)(2,1)S(1)}, u32[]{:S(2)}, u32[]{:S(2)}) collective-permute-start(bf16[64,2304]{1,0:T(8,128)(2,1)S(1)} %get-tuple-element.71), channel_id=1, source_target_pairs={{0,2},{1,3},{2,0},{3,1},{4,6},{5,7},{6,4},{7,5}} | collective-permute-start | bytes 884744 | tf_op jit(solution)/shard_map/ppermute | solution.py:323
  75.6 15.8 %collective-permute-start.13 = (bf16[64,2304]{1,0:T(8,128)(2,1)S(1)}, bf16[64,2304]{1,0:T(8,128)(2,1)S(1)}, u32[]{:S(2)}, u32[]{:S(2)}) collective-permute-start(bf16[64,2304]{1,0:T(8,128)(2,1)S(1)} %get-tuple-element.77), channel_id=1, source_target_pairs={{0,2},{1,3},{2,0},{3,1},{4,6},{5,7},{6,4},{7,5}} | collective-permute-start | bytes 884744 | tf_op jit(solution)/shard_map/ppermute | solution.py:323
  77.0 14.4 %collective-permute-start.18 = (bf16[64,2304]{1,0:T(8,128)(2,1)S(1)}, bf16[64,2304]{1,0:T(8,128)(2,1)S(1)}, u32[]{:S(2)}, u32[]{:S(2)}) collective-permute-start(bf16[64,2304]{1,0:T(8,128)(2,1)S(1)} %get-tuple-element.75.refs_0_.x0), channel_id=1, source_target_pairs={{0,1},{1,0},{2,3},{3,2},{4,5},{5,4},{6,7},{7,6}} | collective-permute-start | bytes 884744 | tf_op jit(solution)/shard_map/ppermute | solution.py:323
  77.0 14.9 %collective-permute-start.19 = (bf16[64,2304]{1,0:T(8,128)(2,1)S(1)}, bf16[64,2304]{1,0:T(8,128)(2,1)S(1)}, u32[]{:S(2)}, u32[]{:S(2)}) collective-permute-start(bf16[64,2304]{1,0:T(8,128)(2,1)S(1)} %get-tuple-element.78.x1), channel_id=1, source_target_pairs={{0,1},{1,0},{2,3},{3,2},{4,5},{5,4},{6,7},{7,6}} | collective-permute-start | bytes 884744 | tf_op jit(solution)/shard_map/ppermute | solution.py:323
  77.5 13.3 %collective-permute-start.21 = (f32[1,2304]{1,0:T(1,128)S(1)}, f32[1,2304]{1,0:T(1,128)S(1)}, u32[]{:S(2)}, u32[]{:S(2)}) collective-permute-start(f32[1,2304]{1,0:T(1,128)S(1)} %add.6), channel_id=1, source_target_pairs={{0,2},{1,3},{2,0},{3,1},{4,6},{5,7},{6,4},{7,5}} | collective-permute-start | bytes 27656 | tf_op jit(solution)/shard_map/ppermute | solution.py:323
  90.9 9.1 %collective-permute-start.17 = (bf16[64,2304]{1,0:T(8,128)(2,1)S(1)}, bf16[64,2304]{1,0:T(8,128)(2,1)S(1)}, u32[]{:S(2)}, u32[]{:S(2)}) collective-permute-start(bf16[64,2304]{1,0:T(8,128)(2,1)S(1)} %get-tuple-element.73.t1), channel_id=1, source_target_pairs={{0,1},{1,0},{2,3},{3,2},{4,5},{5,4},{6,7},{7,6}} | collective-permute-start | bytes 884744 | tf_op jit(solution)/shard_map/ppermute | solution.py:323
  90.9 9.2 %collective-permute-start.10 = (bf16[64,2304]{1,0:T(8,128)(2,1)S(1)}, bf16[64,2304]{1,0:T(8,128)(2,1)S(1)}, u32[]{:S(2)}, u32[]{:S(2)}) collective-permute-start(bf16[64,2304]{1,0:T(8,128)(2,1)S(1)} %get-tuple-element.70.d0), channel_id=1, source_target_pairs={{0,1},{1,0},{2,3},{3,2},{4,5},{5,4},{6,7},{7,6}} | collective-permute-start | bytes 884744 | tf_op jit(solution)/shard_map/ppermute | solution.py:323
  91.4 8.7 %collective-permute-start.14 = (bf16[64,2304]{1,0:T(8,128)(2,1)S(1)}, bf16[64,2304]{1,0:T(8,128)(2,1)S(1)}, u32[]{:S(2)}, u32[]{:S(2)}) collective-permute-start(bf16[64,2304]{1,0:T(8,128)(2,1)S(1)} %get-tuple-element.76.d1), channel_id=1, source_target_pairs={{0,1},{1,0},{2,3},{3,2},{4,5},{5,4},{6,7},{7,6}} | collective-permute-start | bytes 884744 | tf_op jit(solution)/shard_map/ppermute | solution.py:323
  91.4 8.6 %collective-permute-start.11 = (bf16[64,2304]{1,0:T(8,128)(2,1)S(1)}, bf16[64,2304]{1,0:T(8,128)(2,1)S(1)}, u32[]{:S(2)}, u32[]{:S(2)}) collective-permute-start(bf16[64,2304]{1,0:T(8,128)(2,1)S(1)} %collective-permute-done.9.c0), channel_id=1, source_target_pairs={{0,1},{1,0},{2,3},{3,2},{4,5},{5,4},{6,7},{7,6}} | collective-permute-start | bytes 884744 | tf_op jit(solution)/shard_map/ppermute | solution.py:323
  91.9 8.2 %collective-permute-start.15 = (bf16[64,2304]{1,0:T(8,128)(2,1)S(1)}, bf16[64,2304]{1,0:T(8,128)(2,1)S(1)}, u32[]{:S(2)}, u32[]{:S(2)}) collective-permute-start(bf16[64,2304]{1,0:T(8,128)(2,1)S(1)} %collective-permute-done.13.c1), channel_id=1, source_target_pairs={{0,1},{1,0},{2,3},{3,2},{4,5},{5,4},{6,7},{7,6}} | collective-permute-start | bytes 884744 | tf_op jit(solution)/shard_map/ppermute | solution.py:323

commit v10 on v9

v10 whole, which is shorter than its diff:
```python
import functools

import jax
import jax.numpy as jnp
from jax import lax
from jax.experimental import pallas as pl
from jax.experimental.pallas import tpu as pltpu
from jax.sharding import PartitionSpec as P


EPS = 1e-6
F32 = jnp.float32
BF16 = jnp.bfloat16
HBM = pl.BlockSpec(memory_space=pltpu.HBM)
VMEM = pl.BlockSpec(memory_space=pltpu.VMEM)
SMEM = pl.BlockSpec(memory_space=pltpu.SMEM)


def call(body, mib, outs, ins, out_specs, scratch, flops, nbytes, aliases=None):
    return pl.pallas_call(
        body,
        out_shape=outs,
        in_specs=ins,
        out_specs=out_specs,
        scratch_shapes=scratch,
        input_output_aliases=aliases or {},
        cost_estimate=pl.CostEstimate(flops=flops, bytes_accessed=nbytes, transcendentals=0),
        compiler_params=pltpu.CompilerParams(vmem_limit_bytes=mib << 20),
    )


def pdn_kernel(du_ref, w_ref, *refs):
    outs = refs[:4]
    de_ref, dub, dup, wb, z, dsem, wsem, zsem = refs[4:]
    n, d = outs[0].shape
    k, tl = dub.shape[0], dub.shape[1] // 4
    blk = 256
    nb = d // blk
    dc = pltpu.make_async_copy(du_ref, dub, dsem)
    dc.start()
    for i in range(nb):
        pltpu.make_async_copy(w_ref.at[pl.ds(i * blk, blk), :], wb.at[pl.ds(i * blk, blk), :], wsem.at[i]).start()
    z[...] = jnp.zeros_like(z)
    zero_start(z, de_ref, *FILL[0], zsem)
    r = lax.axis_index("tp")
    dc.wait()
    for a, j in enumerate((2, 3, 1, 0)):
        q = r ^ j
        for m in range(k):
            dup[pl.ds(a * n + m * tl, tl), :] = dub[m, pl.ds(pl.multiple_of(q * tl, tl), tl), :]
    for i in range(nb):
        pltpu.make_async_copy(w_ref.at[pl.ds(i * blk, blk), :], wb.at[pl.ds(i * blk, blk), :], wsem.at[i]).wait()
        p = lax.dot_general(dup[...], wb[i * blk:(i + 1) * blk, :], (((1,), (1,)), ((), ())), preferred_element_type=F32)
        for a in range(4):
            outs[a][:, i * blk:(i + 1) * blk] = p[a * n:(a + 1) * n].astype(BF16)
    zero_wait(z, de_ref, *FILL[0], zsem)


FILL = ((0, 4), (4, 6), (6, 8), (8, 16))


def zero_start(z, de_ref, lo, hi, sem):
    step = z.shape[0]
    per = de_ref.shape[0] // 16
    for i in range((hi - lo) * per // step):
        pltpu.make_async_copy(z, de_ref.at[pl.ds(lo * per + i * step, step), :], sem).start()


def zero_wait(z, de_ref, lo, hi, sem):
    step = z.shape[0]
    for _ in range((hi - lo) * (de_ref.shape[0] // 16) // step):
        pltpu.make_async_copy(z, de_ref.at[pl.ds(0, step), :], sem).wait()


def zero_kernel(own_ref, de_in, list_ref, de_ref, z, lnxt, tab, sem):
    z[...] = jnp.zeros_like(z)
    zero_start(z, de_ref, *FILL[3], sem)
    n = own_ref[0, own_ref.shape[1] - 1]
    t = lnxt.shape[0] - 8

    def link(i, c):
        v = own_ref[1, i]
        p = tab[v]
        ok = jnp.logical_and(p >= 0, p < i)
        p = jnp.where(ok, p, 0)
        ok = jnp.logical_and(ok, own_ref[1, p] == v)
        lnxt[i] = -1
        lnxt[jnp.where(ok, p, t)] = i
        tab[v] = i
        return c

    lax.fori_loop(0, n, link, 0)

    def lists(i, c):
        nl, nd = c
        x = lnxt[i]
        end = (x < 0).astype(jnp.int32)
        pos = own_ref[0, i]
        list_ref[0, nl] = pos
        list_ref[1, nl] = own_ref[1, i]
        list_ref[2, nd] = pos
        list_ref[3, nd] = own_ref[0, jnp.maximum(x, 0)]
        return nl + end, nd + 1 - end

    nl, nd = lax.fori_loop(0, n, lists, (0, 0))
    list_ref[0, list_ref.shape[1] - 1] = nl
    list_ref[2, list_ref.shape[1] - 1] = nd
    zero_wait(z, de_ref, *FILL[3], sem)


def gather_kernel(ids_ref, emb_ref, de_in, k0, s0, k1, s1, own_ref, de_ref, buf, tmp, xf, z, lst, sem, zsem):
    k, t = ids_ref.shape
    vl = emb_ref.shape[0]
    h = k0.shape[0]
    tl = t // 4
    r = lax.axis_index("tp")
    z[...] = jnp.zeros_like(z)
    zero_start(z, de_ref, *FILL[1], zsem)
    n = 0
    for m in range(k):
        def scan(i, n):
            lst[n] = m * t + i
            return n + (lax.shift_right_logical(ids_ref[m, i], vl.bit_length() - 1) == r).astype(jnp.int32)

        n = lax.fori_loop(0, t, scan, n, unroll=16)
    own_ref[0, own_ref.shape[1] - 1] = n

    def start(i, c):
        j = lst[i]
        m = j // t
        v = ids_ref[m, j & (t - 1)] - r * vl
        q = (j & (t - 1)) // tl
        pltpu.make_async_copy(emb_ref.at[pl.ds(pl.multiple_of((v >> 3) << 3, 8), 8), :], buf.at[i], sem).start()
        own_ref[0, i] = m * t + ((q ^ r) & 1) * h + ((q ^ r) >> 1) * tl + (j & (tl - 1))
        own_ref[1, i] = v
        return c

    lax.fori_loop(0, n, start, 0)
    zero_start(z, de_ref, *FILL[2], zsem)
    for a in range(8):
        own_ref[0, n + a] = k * t
        own_ref[1, n + a] = 0
    xf[...] = jnp.zeros_like(xf)

    def wait(i, c):
        pltpu.make_async_copy(emb_ref.at[pl.ds(0, 8), :], buf.at[0], sem).wait()
        return c

    lax.fori_loop(0, n, wait, 0)

    def take(g, c):
        for a in range(8):
            tmp[a] = buf[g * 8 + a].astype(F32)
        for a in range(8):
            i = g * 8 + a
            xf[pl.ds(own_ref[0, i], 1), :] = tmp[a, pl.ds(own_ref[1, i] & 7, 1), :]
        return c

    lax.fori_loop(0, (n + 7) // 8, take, 0)
    for a, ref in enumerate((k0, s0, k1, s1)):
        ref[...] = xf[a * h:(a + 1) * h, :].astype(BF16)
    zero_wait(z, de_ref, FILL[1][0], FILL[2][1], zsem)


def sum_kernel(k0, y0, k1, y1, a0, t0, a1, t1):
    tl = a0.shape[0]
    for x, y, a, t in ((k0, y0, a0, t0), (k1, y1, a1, t1)):
        a[...] = x[0:tl, :] + y[0:tl, :]
        t[...] = x[tl:2 * tl, :] + y[tl:2 * tl, :]


def chip_mask(ids_ref, m, q, tl, chip_rows):
    t = ids_ref.shape[1]
    row = lax.broadcasted_iota(jnp.int32, (tl, t), 0) + q * tl
    lane = lax.broadcasted_iota(jnp.int32, (tl, t), 1)
    ids = jnp.broadcast_to(ids_ref[m:m + 1, :].astype(F32), (tl, t))
    col = jnp.sum(jnp.where(row == lane, ids, 0.0), axis=1, keepdims=True)
    lo = ((lax.axis_index("tp") >> 1) * chip_rows).astype(F32)
    return jnp.logical_and(col >= lo, col < lo + chip_rows)


def dx_kernel(m, chip_rows, xh_ref, z_ref, p0, p1, p2, p3, dres_ref, g_ref, ids_ref, tok_ref, *refs):
    if m == 1:
        x0_ref, dg0_ref, x_ref, dx_ref, slot_ref, dg_ref, xs_ref = refs
    else:
        x_ref, dx_ref, slot_ref, dg_ref = refs
    tl = dx_ref.shape[0]
    xh = xh_ref[...].astype(F32)
    x = xh + z_ref[...].astype(F32)
    x_ref[...] = x.astype(BF16)
    if m == 1:
        xs_ref[0] = x0_ref[...]
        xs_ref[1] = x.astype(BF16)
    g = g_ref[...].astype(F32)
    rs = lax.rsqrt(jnp.mean(x * x, axis=-1, keepdims=True) + EPS)
    nh = x * rs
    s = slice(m * tl, (m + 1) * tl)
    dn = (p0[s, :].astype(F32) + p1[s, :].astype(F32)) + (p2[s, :].astype(F32) + p3[s, :].astype(F32))
    gdn = g * dn
    mean = jnp.mean(nh * gdn, axis=-1, keepdims=True)
    dxn = rs * (gdn - nh * mean)
    dx = (dres_ref[m].astype(F32) + dxn).astype(BF16)
    dx_ref[...] = dx
    own = chip_mask(ids_ref, m, lax.axis_index("tp"), tl, chip_rows)
    slot_ref[...] = jnp.where(own, xh, dx.astype(F32)).astype(BF16)
    dg = jnp.sum(dn * nh, axis=0, keepdims=True)
    dg_ref[...] = dg if m == 0 else dg + dg0_ref[...]


def norm(x, g_ref):
    rs = lax.rsqrt(jnp.mean(x * x, axis=-1, keepdims=True) + EPS)
    return ((x * rs) * g_ref[...].astype(F32)).astype(BF16)


def umat(n, w_ref, ub, u_ref, q0, q1, sem):
    blk = 256
    for i in range(ub.shape[1] // blk):
        ub[:, i * blk:(i + 1) * blk] = jnp.dot(n, w_ref[:, i * blk:(i + 1) * blk], preferred_element_type=F32).astype(BF16)
    k = u_ref.shape[0]
    tl = u_ref.shape[1] // 4
    copies = []
    for m in range(k):
        for a, q in enumerate((q0, q1)):
            c = pltpu.make_async_copy(ub.at[pl.ds((m * 2 + a) * tl, tl), :],
                                      u_ref.at[m, pl.ds(pl.multiple_of(q * tl, tl), tl), :], sem)
            c.start()
            copies.append(c)
    return copies


def take_du(du_ref, out_ref, tl, order):
    for a, (m, q) in enumerate(order):
        out_ref[a * tl:(a + 1) * tl, :] = du_ref[m, pl.ds(pl.multiple_of(q * tl, tl), tl), :]


def dw_tile(n_ref, du2, i, blk):
    return lax.dot_general(n_ref[:, i * blk:(i + 1) * blk], du2[...], (((0,), (0,)), ((), ())), preferred_element_type=F32)


def u_kernel(x0, y0, x1, y1, g_ref, w_ref, du_ref, tok_ref, u_ref, dwp_ref, n_ref, du2, ub, usem):
    r = lax.axis_index("tp")
    tl = x0.shape[0]
    for a, x in enumerate((x0, y0, x1, y1)):
        n_ref[a * tl:(a + 1) * tl, :] = norm(x[...].astype(F32), g_ref)
    take_du(du_ref, du2, tl, ((0, r), (0, r ^ 1), (1, r), (1, r ^ 1)))
    copies = umat(n_ref[...], w_ref, ub, u_ref, r, r ^ 1, usem)
    blk = 256
    for i in range(dwp_ref.shape[0] // blk):
        dwp_ref[i * blk:(i + 1) * blk, :] = dw_tile(n_ref, du2, i, blk)
    for c in copies:
        c.wait()


def last_kernel(chip_rows, list_ref, d0, c0, a0, b0, d1, c1, a1, b1, t0, w0, t1, w1, dwp_ref, ids_ref, g_ref,
                w_ref, du_ref, u_in, de_in, u_ref, dw_ref, de_ref, xf, n_ref, du2, ub, dwb, usem, wsem, sem):
    d = w_ref.shape[0]
    tl = d0.shape[0]
    r = lax.axis_index("tp")
    for a, ref in enumerate((d0, c0, a0, b0, d1, c1, a1, b1)):
        xf[a * tl:(a + 1) * tl, :] = ref[...].astype(F32)

    def add(i, c):
        a = list_ref[2, i]
        b = list_ref[3, i]
        xf[pl.ds(b, 1), :] = xf[pl.ds(b, 1), :] + xf[pl.ds(a, 1), :]
        return c

    lax.fori_loop(0, list_ref[2, list_ref.shape[1] - 1], add, 0)

    for a, (m, q, own, got) in enumerate(((0, r ^ 2, t0, c0), (0, r ^ 3, w0, b0), (1, r ^ 2, t1, c1), (1, r ^ 3, w1, b1))):
        x = jnp.where(chip_mask(ids_ref, m, q, tl, chip_rows), own[...].astype(F32), got[...].astype(F32))
        n_ref[a * tl:(a + 1) * tl, :] = norm(x, g_ref)

    def put(i, c):
        pltpu.make_async_copy(xf.at[pl.ds(list_ref[0, i], 1), :], de_ref.at[pl.ds(list_ref[1, i], 1), :], sem).start()
        return c

    lax.fori_loop(0, list_ref[0, list_ref.shape[1] - 1], put, 0)
    take_du(du_ref, du2, tl, ((0, r ^ 2), (0, r ^ 3), (1, r ^ 2), (1, r ^ 3)))
    copies = umat(n_ref[...], w_ref, ub, u_ref, r ^ 2, r ^ 3, usem)
    blk = 256
    for i in range(d // blk):
        dwb[i] = dwp_ref[i * blk:(i + 1) * blk, :] + dw_tile(n_ref, du2, i, blk)
        c = pltpu.make_async_copy(dwb.at[i], dw_ref.at[pl.ds(i * blk, blk), :], wsem)
        c.start()
        copies.append(c)

    def wait(i, c):
        pltpu.make_async_copy(xf.at[pl.ds(0, 1), :], de_ref.at[pl.ds(0, 1), :], sem).wait()
        return c

    lax.fori_loop(0, list_ref[0, list_ref.shape[1] - 1], wait, 0)
    for c in copies:
        c.wait()


def solution(mesh):
    groups = mesh.shape["tp"]
    sib = [(i, i ^ 1) for i in range(groups)]
    cross = [(i, i ^ 2) for i in range(groups)]
    diag = [(i, i ^ 3) for i in range(groups)]

    def local(ids, emb, g, w, du, dres):
        k, t = ids.shape
        vl, d = emb.shape
        fc = w.shape[1]
        tl = t // groups
        n = k * tl
        h = 2 * n
        g2 = g.reshape(1, d)
        S = jax.ShapeDtypeStruct
        D = pltpu.SemaphoreType.DMA

        def perm(v, p):
            return lax.ppermute(v, "tp", p)

        p2, p3, p1, p0, de = call(
            pdn_kernel, 60, [S((n, d), BF16)] * 4 + [S((vl, d), F32)], [HBM] * 2, [VMEM] * 4 + [HBM],
            [pltpu.VMEM((k, t, fc), BF16), pltpu.VMEM((4 * n, fc), BF16), pltpu.VMEM((d, fc), BF16), pltpu.VMEM((256, d), F32),
             D, D((d // 256,)), D], 8 * n * fc * d, 2 * d * fc + 8 * n * (fc + d))(du, w)
        q2 = perm(p2, cross)
        q3 = perm(p3, diag)
        k0, s0, k1, s1, owned, de = call(
            gather_kernel, 60,
            [S((n, d), BF16)] * 4 + [S((2, 2 * h + 16), jnp.int32), S((vl, d), F32)],
            [SMEM, HBM, HBM], [VMEM] * 4 + [SMEM, HBM],
            [pltpu.VMEM((2 * h, 8, d), BF16), pltpu.VMEM((8, 8, d), F32), pltpu.VMEM((2 * h + 8, d), F32), pltpu.VMEM((256, d), F32)]
            + [pltpu.SMEM((2 * h + 8,), jnp.int32), D, D],
            500_000_000, 16 * h * d, {2: 5})(ids, emb, de)
        y0 = perm(s0, sib)
        y1 = perm(s1, sib)
        q1 = perm(p1, sib)
        own0, oth0, own1, oth1 = call(sum_kernel, 16, [S((tl, d), BF16)] * 4, [VMEM] * 4, [VMEM] * 4, [],
                                      8 * tl * d, 24 * tl * d)(k0, y0, k1, y1)
        z0 = perm(oth0, cross)
        z1 = perm(oth1, cross)
        w0 = perm(oth0, sib)
        w1 = perm(oth1, sib)
        lists, de = call(
            zero_kernel, 8, [S((4, 2 * h + 16), jnp.int32), S((vl, d), F32)], [SMEM, HBM], [SMEM, HBM],
            [pltpu.VMEM((256, d), F32), pltpu.SMEM((2 * h + 8,), jnp.int32), pltpu.SMEM((vl,), jnp.int32), D],
            6_000_000_000, 2 * vl * d, {1: 1})(owned, de)

        def dxk(m, xh, z, tok, more):
            outs = [S((tl, d), BF16)] * 3 + [S((1, d), F32)] + ([S((k, tl, d), BF16)] if m else [])
            return call(functools.partial(dx_kernel, m, 2 * vl), 16, outs,
                        [VMEM] * 9 + [SMEM if m else HBM] + [VMEM] * len(more),
                        [VMEM] * len(outs), [], 30 * n * d, 16 * n * d)(
                            xh, z, p0, q1, q2, q3, dres, g2, ids, tok, *more)

        x0, dx0, slot0, dg0 = dxk(0, own0, z0, de, ())
        c0 = perm(slot0, cross)
        x1, dx1, slot1, dg, x = dxk(1, own1, z1, lists, (x0, dg0))
        c1 = perm(slot1, cross)
        xo0 = perm(x0, sib)
        xo1 = perm(x1, sib)
        a0 = perm(dx0, sib)
        a1 = perm(dx1, sib)
        u, dwp = call(
            u_kernel, 32, [S((k, t, fc), BF16), S((d, fc), F32)], [VMEM] * 8, [HBM, VMEM],
            [pltpu.VMEM((t, d), BF16), pltpu.VMEM((t, fc), BF16), pltpu.VMEM((t, fc), BF16), D],
            4 * t * d * fc, 2 * d * fc)(x0, xo0, x1, xo1, g2, w, du, dg)
        b0 = perm(c0, sib)
        b1 = perm(c1, sib)
        dgs = dg + perm(dg, sib)
        dgs = dgs + perm(dgs, cross)

        u, dw, de = call(
            functools.partial(last_kernel, 2 * vl), 36, [S((k, t, fc), BF16), S((d, fc), F32), S((vl, d), F32)],
            [SMEM] + [VMEM] * 17 + [HBM] * 2, [HBM] * 3,
            [pltpu.VMEM((2 * h, d), F32), pltpu.VMEM((t, d), BF16), pltpu.VMEM((t, fc), BF16), pltpu.VMEM((t, fc), BF16),
             pltpu.VMEM((d // 256, 256, fc), F32), D, D, D],
            4 * t * d * fc, 6 * d * fc, {18: 0, 19: 2})(
                lists, dx0, c0, a0, b0, dx1, c1, a1, b1, oth0, w0, oth1, w1, dwp, ids, g2, w, du, u, de)
        return u, x, de, dw, dgs.reshape(d)

    return jax.shard_map(
        local,
        mesh=mesh,
        in_specs=(P("dp", None), P("tp", None), P(None), P(None, "tp"), P("dp", None, "tp"), P("dp", "tp", None)),
        out_specs=(P("dp", None, "tp"), P("dp", "tp", None), P(("dp", "tp"), None), P(None, ("dp", "tp")), P("dp")),
        check_vma=False,
    )
```

time: 112 us -> 101 us (0.902)
  Pallas kernels: 60.8 us -> 54.5 us
  waiting for transfers between devices: 34.8 us -> 30.8 us
  starting transfers between devices: 13.7 us -> 10.3 us
  local copies, waits for them, and re-layouts: 0.09 us -> 2.88 us
    pallas_call x9 -> x7, Pallas kernels: 60.7 us -> 54.3 us  [the longest x1 14 us: local(): call(zero_kernel, 8, [S((4, 2 * h + 16), jnp.int32), S((vl, d), F32)], [S...]
    ppermute x22 -> x19, waiting for transfers between devices: 34.8 us -> 30.8 us  [perm(): return lax.ppermute(v, 'tp', p)]
    ppermute x22 -> x19, starting transfers between devices: 13.7 us -> 10.3 us  [perm(): return lax.ppermute(v, 'tp', p)]
    unnamed x28 -> x26, local copies, waits for them, and re-layouts: 0.08 us -> 2.87 us
  transfers between devices with their start and end apart: 22 -> 19, of which waited for: 3 -> 5; matrix products, arithmetic and copies ran while one was open for 1% -> 1% of each run, Pallas kernels for 34% -> 20%
where the time goes in v10:
time: 101 us; the launch traced here: 100 us
  Pallas kernels  54.5 us (54%)
  waiting for transfers between devices  30.8 us (30%)
  starting transfers between devices  10.3 us (10%)
  local copies, waits for them, and re-layouts  2.88 us (3%)
    ppermute x19, waiting for transfers between devices, perm(): return lax.ppermute(v, 'tp', p)  30.8 us
    pallas_call x1, Pallas kernels, local(): call(zero_kernel, 8, [S((4, 2 * h + 16), jnp.int32), S((vl, d), F32)], [S...  14 us
    pallas_call x1, Pallas kernels, local(): call(pdn_kernel, 60, [S((n, d), BF16)] * 4 + [S((vl, d), F32)], [HBM] * 2...  13.8 us
    pallas_call x1, Pallas kernels, local(): call(gather_kernel, 60, [S((n, d), BF16)] * 4 + [S((2, 2 * h + 16), jnp.i...  11.8 us
    ppermute x19, starting transfers between devices, perm(): return lax.ppermute(v, 'tp', p)  10.3 us
    pallas_call x1, Pallas kernels, local(): call(functools.partial(last_kernel, 2 * vl), 36, [S((k, t, fc), BF16), S(...  8.95 us
    pallas_call x1, Pallas kernels, local(): call(u_kernel, 32, [S((k, t, fc), BF16), S((d, fc), F32)], [VMEM] * 8, [H...  2.93 us
    pallas_call x2, Pallas kernels, dxk(): call(functools.partial(dx_kernel, m, 2 * vl), 16, outs, [VMEM] * 9 + [SME...  2.92 us
  transfers between devices with their start and end apart: 19, of which 5 were waited for; matrix products, arithmetic and copies ran while one was open for 1% of the time, Pallas kernels for 20%

profile of v10, /device:TPU:0, one launch (start us, length us, event | category | flops | bytes accessed | tf_op | source)
XLA Modules:
  0.0 100.0 jit_solution(9242052515318625070)
XLA Ops:
  0.6 0.0 copy-start.7
  0.6 13.8 %shard_map.101 = (bf16[128,2304]{1,0:T(8,128)(2,1)}, bf16[128,2304]{1,0:T(8,128)(2,1)}, bf16[128,2304]{1,0:T(8,128)(2,1)}, bf16[128,2304]{1,0:T(8,128)(2,1)}, f32[8192,2304]{1,0:T(8,128)}) custom-call(bf16[2,256,1024]{2,1,0:T(8,128)(2,1)} %du_ref.5, bf16[2304,1024]{1,0:T(8,128)(2,1)} %w_ref.5), custom_call_target="tpu_custom_call" | custom-call | flops 2415919104 | bytes 8126464 | tf_op jit(solution)/shard_map/pallas_call | solution.py:317
  14.4 0.0 copy-start.10
  14.4 0.0 copy-start.9
  14.4 0.0 copy-start.8
  14.4 0.0 copy-start
  14.5 0.0 copy-start.1
  14.5 0.0 copy-start.5
  14.5 11.8 %shard_map.102 = (bf16[128,2304]{1,0:T(8,128)(2,1)}, bf16[128,2304]{1,0:T(8,128)(2,1)}, bf16[128,2304]{1,0:T(8,128)(2,1)}, bf16[128,2304]{1,0:T(8,128)(2,1)}, s32[2,528]{1,0:T(2,128)}, /*index=5*/f32[8192,2304]{1,0:T(8,128)}) custom-call(s32[2,256]{1,0:T(2,128)} %ids_ref.7, bf16[8192,2304]{1,0:T(8,128)(2,1)} %emb_ref.1, ...), custom_call_target="tpu_custom_call", output_to_operand_aliasing={{5}: (2, {})} | custom-call | flops 500000000 | bytes 9437184 | tf_op jit(solution)/shard_map/pallas_call | solution.py:323
  26.3 0.4 collective-permute-start
  26.7 0.1 collective-permute-start.1
  26.8 0.0 copy-done.10
  26.8 0.4 collective-permute-start.3
  27.2 0.0 copy-done.9
  27.2 1.8 %collective-permute-start.4 = (bf16[128,2304]{1,0:T(8,128)(2,1)S(1)}, bf16[128,2304]{1,0:T(8,128)(2,1)S(1)}, u32[]{:S(2)}, u32[]{:S(2)}) collective-permute-start(bf16[128,2304]{1,0:T(8,128)(2,1)S(1)} %copy-done.9), channel_id=1, source_target_pairs={{0,2},{1,3},{2,0},{3,1},{4,6},{5,7},{6,4},{7,5}} | collective-permute-start | bytes 1769480 | tf_op jit(solution)/shard_map/ppermute | solution.py:315
  29.0 0.0 copy-done.8
  29.0 0.1 collective-permute-start.5
  29.1 0.0 copy-done.7
  29.1 0.0 collective-permute-done.y0
  29.1 0.3 collective-permute-done.1.y1
  29.4 1.1 %copy-done.3 = bf16[128,2304]{1,0:T(8,128)(2,1)S(1)} copy-done((bf16[128,2304]{1,0:T(8,128)(2,1)S(1)}, bf16[128,2304]{1,0:T(8,128)(2,1)}, u32[]{:S(2)}) %copy-start.3) | copy-done | bytes 589848
  30.5 1.1 %copy-done.4 = bf16[128,2304]{1,0:T(8,128)(2,1)S(1)} copy-done((bf16[128,2304]{1,0:T(8,128)(2,1)S(1)}, bf16[128,2304]{1,0:T(8,128)(2,1)}, u32[]{:S(2)}) %copy-start.4) | copy-done | bytes 589848
  31.5 0.1 shard_map.104
  31.7 2.1 %collective-permute-start.2 = (bf16[64,2304]{1,0:T(8,128)(2,1)S(1)}, bf16[64,2304]{1,0:T(8,128)(2,1)S(1)}, u32[]{:S(2)}, u32[]{:S(2)}) collective-permute-start(bf16[64,2304]{1,0:T(8,128)(2,1)S(1)} %get-tuple-element.45.t0), channel_id=1, source_target_pairs={{0,2},{1,3},{2,0},{3,1},{4,6},{5,7},{6,4},{7,5}} | collective-permute-start | bytes 884744 | tf_op jit(solution)/shard_map/ppermute | solution.py:315
  33.8 0.0 collective-permute-start.9
  33.8 0.7 copy-done.6
  34.5 14.0 %shard_map.103 = (s32[4,528]{1,0:T(4,128)S(1)}, f32[8192,2304]{1,0:T(8,128)}) custom-call(s32[2,528]{1,0:T(2,128)S(1)} %copy-done.6, f32[8192,2304]{1,0:T(8,128)} %get-tuple-element.38.de_in), custom_call_target="tpu_custom_call", output_to_operand_aliasing={{1}: (1, {})} | custom-call | flops 6000000000 | bytes 37748736 | tf_op jit(solution)/shard_map/pallas_call | solution.py:339
  48.5 0.0 collective-permute-done.3.p1
  48.5 0.0 collective-permute-start.13
  48.6 0.0 collective-permute-done.4.p2
  48.6 6.8 %collective-permute-done.5.p3 = bf16[128,2304]{1,0:T(8,128)(2,1)S(1)} collective-permute-done((bf16[128,2304]{1,0:T(8,128)(2,1)S(1)}, bf16[128,2304]{1,0:T(8,128)(2,1)S(1)}, u32[]{:S(2)}, u32[]{:S(2)}) %collective-permute-start.5) | collective-permute-done | bytes 589856 | tf_op jit(solution)/shard_map/ppermute | solution.py:315
  55.4 7.0 %collective-permute-done.2.z_ref = bf16[64,2304]{1,0:T(8,128)(2,1)S(1)} collective-permute-done((bf16[64,2304]{1,0:T(8,128)(2,1)S(1)}, bf16[64,2304]{1,0:T(8,128)(2,1)S(1)}, u32[]{:S(2)}, u32[]{:S(2)}) %collective-permute-start.2) | collective-permute-done | bytes 294944 | tf_op jit(solution)/shard_map/ppermute | solution.py:315
  62.4 0.0 copy-done
  62.4 0.0 copy-done.1
  62.4 0.0 slice-start.1
  62.4 0.8 shard_map.105
  63.2 5.1 %collective-permute-done.9.z_ref = bf16[64,2304]{1,0:T(8,128)(2,1)S(1)} collective-permute-done((bf16[64,2304]{1,0:T(8,128)(2,1)S(1)}, bf16[64,2304]{1,0:T(8,128)(2,1)S(1)}, u32[]{:S(2)}, u32[]{:S(2)}) %collective-permute-start.9) | collective-permute-done | bytes 294944 | tf_op jit(solution)/shard_map/ppermute | solution.py:315
  68.3 2.2 %shard_map.106 = (bf16[64,2304]{1,0:T(8,128)(2,1)S(1)}, bf16[64,2304]{1,0:T(8,128)(2,1)S(1)}, bf16[64,2304]{1,0:T(8,128)(2,1)S(1)}, f32[1,2304]{1,0:T(1,128)S(1)}, bf16[2,64,2304]{2,1,0:T(8,128)(2,1)}) custom-call(bf16[64,2304]{1,0:T(8,128)(2,1)S(1)} %get-tuple-element.53.xh_ref, bf16[64,2304]{1,0:T(8,128)(2,1)S(1)} %collective-permute-done.9.z_ref, ...), custom_call_target="tpu_custom_call" | custom-call | flops 8847360 | bytes 4718592 | tf_op jit(solution)/shard_map/pallas_call | solution.py:346
  70.4 0.0 collective-permute-start.17
  70.4 1.7 %collective-permute-start.6 = (bf16[64,2304]{1,0:T(8,128)(2,1)S(1)}, bf16[64,2304]{1,0:T(8,128)(2,1)S(1)}, u32[]{:S(2)}, u32[]{:S(2)}) collective-permute-start(bf16[64,2304]{1,0:T(8,128)(2,1)S(1)} %get-tuple-element.52), channel_id=1, source_target_pairs={{0,2},{1,3},{2,0},{3,1},{4,6},{5,7},{6,4},{7,5}} | collective-permute-start | bytes 884744 | tf_op jit(solution)/shard_map/ppermute | solution.py:315
  72.2 0.3 collective-permute-start.10
  72.4 0.0 collective-permute-start.15
  72.5 0.0 collective-permute-done.17
  72.5 0.5 collective-permute-start.16
  73.0 0.0 collective-permute-done.13.w0
  73.0 1.8 %collective-permute-start.18 = (f32[1,2304]{1,0:T(1,128)S(1)}, f32[1,2304]{1,0:T(1,128)S(1)}, u32[]{:S(2)}, u32[]{:S(2)}) collective-permute-start(f32[1,2304]{1,0:T(1,128)S(1)} %add.6), channel_id=1, source_target_pairs={{0,2},{1,3},{2,0},{3,1},{4,6},{5,7},{6,4},{7,5}} | collective-permute-start | bytes 27656 | tf_op jit(solution)/shard_map/ppermute | solution.py:315
  74.8 11.6 %collective-permute-done.18 = f32[1,2304]{1,0:T(1,128)S(1)} collective-permute-done((f32[1,2304]{1,0:T(1,128)S(1)}, f32[1,2304]{1,0:T(1,128)S(1)}, u32[]{:S(2)}, u32[]{:S(2)}) %collective-permute-start.18) | collective-permute-done | bytes 9248 | tf_op jit(solution)/shard_map/ppermute | solution.py:315
  86.4 0.0 collective-permute-start.14
  86.4 0.0 collective-permute-done.6.c0
  86.4 0.5 collective-permute-start.7
  86.9 0.0 collective-permute-done.10.c1
  86.9 0.0 collective-permute-start.11
  86.9 0.0 collective-permute-done.15.y0
  86.9 0.5 collective-permute-start.8
  87.4 0.0 collective-permute-done.16.y1
  87.4 0.0 collective-permute-start.12
  87.4 0.6 add_reduce_fusion
  88.1 2.9 %shard_map.107 = (bf16[2,256,1024]{2,1,0:T(8,128)(2,1)}, f32[2304,1024]{1,0:T(8,128)S(1)}) custom-call(bf16[64,2304]{1,0:T(8,128)(2,1)S(1)} %get-tuple-element.55.refs_0_.x0, bf16[64,2304]{1,0:T(8,128)(2,1)S(1)} %collective-permute-done.15.y0, bf16[64,2304]{1,0:T(8,128)(2,1)S(1)} %get-tuple-element.59.x1, bf16[64,2304]{1,0:T(8,128)(2,1)S(1)} %collective-permute-done.16.y1, ...), custom_call_target="tpu_custom_call" | custom-call | flops 2415919104 | bytes 4718592 | tf_op jit(solution)/shard_map/pallas_call | solution.py:359
  91.0 0.0 collective-permute-done.14.w1
  91.0 0.0 collective-permute-done.7.a0
  91.0 0.0 collective-permute-done.11.a1
  91.0 0.0 collective-permute-done.8.b0
  91.0 0.0 collective-permute-done.12.b1
  91.0 8.9 %shard_map.108 = (bf16[2,256,1024]{2,1,0:T(8,128)(2,1)}, f32[2304,1024]{1,0:T(8,128)}, f32[8192,2304]{1,0:T(8,128)}) custom-call(s32[4,528]{1,0:T(4,128)S(1)} %get-tuple-element.39.tok_ref.list_ref, bf16[64,2304]{1,0:T(8,128)(2,1)S(1)} %get-tuple-element.51.d0, ...), custom_call_target="tpu_custom_call", output_to_operand_aliasing={{0}: (18, {}), {2}: (19, {})} | custom-call | flops 2415919104 | bytes 14155776 | tf_op jit(solution)/shard_map/pallas_call | solution.py:368
  (12 shorter events, 0.0 us)
Async XLA Ops:
  0.6 28.5 %copy-start.7 = (bf16[2304]{0:T(1024)(128)(2,1)S(1)}, bf16[2304]{0:T(1024)(128)(2,1)}, u32[]{:S(2)}) copy-start(bf16[2304]{0:T(1024)(128)(2,1)} %param.8) | copy-start | bytes 13828
  14.4 12.4 %copy-start.10 = (bf16[128,2304]{1,0:T(8,128)(2,1)S(1)}, bf16[128,2304]{1,0:T(8,128)(2,1)}, u32[]{:S(2)}) copy-start(bf16[128,2304]{1,0:T(8,128)(2,1)} %get-tuple-element.47) | copy-start | bytes 1769476
  14.4 12.8 %copy-start.9 = (bf16[128,2304]{1,0:T(8,128)(2,1)S(1)}, bf16[128,2304]{1,0:T(8,128)(2,1)}, u32[]{:S(2)}) copy-start(bf16[128,2304]{1,0:T(8,128)(2,1)} %get-tuple-element.48) | copy-start | bytes 1769476
  14.4 14.6 %copy-start.8 = (bf16[128,2304]{1,0:T(8,128)(2,1)S(1)}, bf16[128,2304]{1,0:T(8,128)(2,1)}, u32[]{:S(2)}) copy-start(bf16[128,2304]{1,0:T(8,128)(2,1)} %get-tuple-element.49) | copy-start | bytes 1769476
  14.4 48.0 %copy-start = (bf16[2,64,2304]{2,1,0:T(8,128)(2,1)S(1)}, bf16[2,64,2304]{2,1,0:T(8,128)(2,1)}, u32[]{:S(2)}) copy-start(bf16[2,64,2304]{2,1,0:T(8,128)(2,1)} %dres_ref.3) | copy-start | bytes 1769476
  14.5 48.0 %copy-start.1 = (bf16[128,2304]{1,0:T(8,128)(2,1)S(1)}, bf16[128,2304]{1,0:T(8,128)(2,1)}, u32[]{:S(2)}) copy-start(bf16[128,2304]{1,0:T(8,128)(2,1)} %get-tuple-element.46.p0) | copy-start | bytes 1769476
  14.5 48.0 %copy-start.5 = (s32[2,256]{1,0:T(2,128)S(1)}, s32[2,256]{1,0:T(2,128)}, u32[]{:S(2)}) copy-start(s32[2,256]{1,0:T(2,128)} %ids_ref.7) | copy-start | bytes 6148
  26.3 2.8 %collective-permute-start = (bf16[128,2304]{1,0:T(8,128)(2,1)}, bf16[128,2304]{1,0:T(8,128)(2,1)S(1)}, u32[]{:S(2)}, u32[]{:S(2)}) collective-permute-start(bf16[128,2304]{1,0:T(8,128)(2,1)} %get-tuple-element.41), channel_id=1, source_target_pairs={{0,1},{1,0},{2,3},{3,2},{4,5},{5,4},{6,7},{7,6}} | collective-permute-start | bytes 1769480 | tf_op jit(solution)/shard_map/ppermute | solution.py:315
  26.7 2.7 %collective-permute-start.1 = (bf16[128,2304]{1,0:T(8,128)(2,1)}, bf16[128,2304]{1,0:T(8,128)(2,1)S(1)}, u32[]{:S(2)}, u32[]{:S(2)}) collective-permute-start(bf16[128,2304]{1,0:T(8,128)(2,1)} %get-tuple-element.43), channel_id=1, source_target_pairs={{0,1},{1,0},{2,3},{3,2},{4,5},{5,4},{6,7},{7,6}} | collective-permute-start | bytes 1769480 | tf_op jit(solution)/shard_map/ppermute | solution.py:315
  26.8 21.7 %collective-permute-start.3 = (bf16[128,2304]{1,0:T(8,128)(2,1)S(1)}, bf16[128,2304]{1,0:T(8,128)(2,1)S(1)}, u32[]{:S(2)}, u32[]{:S(2)}) collective-permute-start(bf16[128,2304]{1,0:T(8,128)(2,1)S(1)} %copy-done.10), channel_id=1, source_target_pairs={{0,1},{1,0},{2,3},{3,2},{4,5},{5,4},{6,7},{7,6}} | collective-permute-start | bytes 1769480 | tf_op jit(solution)/shard_map/ppermute | solution.py:315
  27.2 21.3 %collective-permute-start.4 = (bf16[128,2304]{1,0:T(8,128)(2,1)S(1)}, bf16[128,2304]{1,0:T(8,128)(2,1)S(1)}, u32[]{:S(2)}, u32[]{:S(2)}) collective-permute-start(bf16[128,2304]{1,0:T(8,128)(2,1)S(1)} %copy-done.9), channel_id=1, source_target_pairs={{0,2},{1,3},{2,0},{3,1},{4,6},{5,7},{6,4},{7,5}} | collective-permute-start | bytes 1769480 | tf_op jit(solution)/shard_map/ppermute | solution.py:315
  29.0 26.4 %collective-permute-start.5 = (bf16[128,2304]{1,0:T(8,128)(2,1)S(1)}, bf16[128,2304]{1,0:T(8,128)(2,1)S(1)}, u32[]{:S(2)}, u32[]{:S(2)}) collective-permute-start(bf16[128,2304]{1,0:T(8,128)(2,1)S(1)} %copy-done.8), channel_id=1, source_target_pairs={{0,3},{1,2},{2,1},{3,0},{4,7},{5,6},{6,5},{7,4}} | collective-permute-start | bytes 1769480 | tf_op jit(solution)/shard_map/ppermute | solution.py:315
  29.4 1.1 %copy-start.3 = (bf16[128,2304]{1,0:T(8,128)(2,1)S(1)}, bf16[128,2304]{1,0:T(8,128)(2,1)}, u32[]{:S(2)}) copy-start(bf16[128,2304]{1,0:T(8,128)(2,1)} %get-tuple-element.40.k0) | copy-start | bytes 1769476
  30.5 1.1 %copy-start.4 = (bf16[128,2304]{1,0:T(8,128)(2,1)S(1)}, bf16[128,2304]{1,0:T(8,128)(2,1)}, u32[]{:S(2)}) copy-start(bf16[128,2304]{1,0:T(8,128)(2,1)} %get-tuple-element.42.k1) | copy-start | bytes 1769476
  31.7 30.7 %collective-permute-start.2 = (bf16[64,2304]{1,0:T(8,128)(2,1)S(1)}, bf16[64,2304]{1,0:T(8,128)(2,1)S(1)}, u32[]{:S(2)}, u32[]{:S(2)}) collective-permute-start(bf16[64,2304]{1,0:T(8,128)(2,1)S(1)} %get-tuple-element.45.t0), channel_id=1, source_target_pairs={{0,2},{1,3},{2,0},{3,1},{4,6},{5,7},{6,4},{7,5}} | collective-permute-start | bytes 884744 | tf_op jit(solution)/shard_map/ppermute | solution.py:315
  33.8 34.5 %collective-permute-start.9 = (bf16[64,2304]{1,0:T(8,128)(2,1)S(1)}, bf16[64,2304]{1,0:T(8,128)(2,1)S(1)}, u32[]{:S(2)}, u32[]{:S(2)}) collective-permute-start(bf16[64,2304]{1,0:T(8,128)(2,1)S(1)} %get-tuple-element.54.t1), channel_id=1, source_target_pairs={{0,2},{1,3},{2,0},{3,1},{4,6},{5,7},{6,4},{7,5}} | collective-permute-start | bytes 884744 | tf_op jit(solution)/shard_map/ppermute | solution.py:315
  33.8 0.7 copy-start.6
  34.5 53.5 %slice-start = ((s8[4718592]{0:T(1024)(128)(4,1)}), s8[4194304]{0:T(1024)(128)(4,1)S(1)}, s32[]{:S(2)}) async-start(s8[4718592]{0:T(1024)(128)(4,1)} %bitcast), calls=%async_computation | async-start | bytes 8388608
  34.5 53.5 %copy-start.2 = (bf16[2,256,1024]{2,1,0:T(8,128)(2,1)S(1)}, bf16[2,256,1024]{2,1,0:T(8,128)(2,1)}, u32[]{:S(2)}) copy-start(bf16[2,256,1024]{2,1,0:T(8,128)(2,1)} %du_ref.5) | copy-start | bytes 3145732
  48.5 24.5 %collective-permute-start.13 = (bf16[64,2304]{1,0:T(8,128)(2,1)S(1)}, bf16[64,2304]{1,0:T(8,128)(2,1)S(1)}, u32[]{:S(2)}, u32[]{:S(2)}) collective-permute-start(bf16[64,2304]{1,0:T(8,128)(2,1)S(1)} %get-tuple-element.45.t0), channel_id=1, source_target_pairs={{0,1},{1,0},{2,3},{3,2},{4,5},{5,4},{6,7},{7,6}} | collective-permute-start | bytes 884744 | tf_op jit(solution)/shard_map/ppermute | solution.py:315
  62.4 25.6 %slice-start.1 = ((s8[4718592]{0:T(1024)(128)(4,1)}), s8[524288]{0:T(1024)(128)(4,1)S(1)}, s32[]{:S(2)}) async-start(s8[4718592]{0:T(1024)(128)(4,1)} %bitcast), calls=%async_computation.1 | async-start | bytes 1048576
  70.4 2.0 %collective-permute-start.17 = (f32[1,2304]{1,0:T(1,128)S(1)}, f32[1,2304]{1,0:T(1,128)S(1)}, u32[]{:S(2)}, u32[]{:S(2)}) collective-permute-start(f32[1,2304]{1,0:T(1,128)S(1)} %get-tuple-element.60.tok_ref), channel_id=1, source_target_pairs={{0,1},{1,0},{2,3},{3,2},{4,5},{5,4},{6,7},{7,6}} | collective-permute-start | bytes 27656 | tf_op jit(solution)/shard_map/ppermute | solution.py:315
  70.4 15.9 %collective-permute-start.6 = (bf16[64,2304]{1,0:T(8,128)(2,1)S(1)}, bf16[64,2304]{1,0:T(8,128)(2,1)S(1)}, u32[]{:S(2)}, u32[]{:S(2)}) collective-permute-start(bf16[64,2304]{1,0:T(8,128)(2,1)S(1)} %get-tuple-element.52), channel_id=1, source_target_pairs={{0,2},{1,3},{2,0},{3,1},{4,6},{5,7},{6,4},{7,5}} | collective-permute-start | bytes 884744 | tf_op jit(solution)/shard_map/ppermute | solution.py:315
  72.2 14.7 %collective-permute-start.10 = (bf16[64,2304]{1,0:T(8,128)(2,1)S(1)}, bf16[64,2304]{1,0:T(8,128)(2,1)S(1)}, u32[]{:S(2)}, u32[]{:S(2)}) collective-permute-start(bf16[64,2304]{1,0:T(8,128)(2,1)S(1)} %get-tuple-element.58), channel_id=1, source_target_pairs={{0,2},{1,3},{2,0},{3,1},{4,6},{5,7},{6,4},{7,5}} | collective-permute-start | bytes 884744 | tf_op jit(solution)/shard_map/ppermute | solution.py:315
  72.4 14.5 %collective-permute-start.15 = (bf16[64,2304]{1,0:T(8,128)(2,1)S(1)}, bf16[64,2304]{1,0:T(8,128)(2,1)S(1)}, u32[]{:S(2)}, u32[]{:S(2)}) collective-permute-start(bf16[64,2304]{1,0:T(8,128)(2,1)S(1)} %get-tuple-element.55.refs_0_.x0), channel_id=1, source_target_pairs={{0,1},{1,0},{2,3},{3,2},{4,5},{5,4},{6,7},{7,6}} | collective-permute-start | bytes 884744 | tf_op jit(solution)/shard_map/ppermute | solution.py:315
  72.5 14.9 %collective-permute-start.16 = (bf16[64,2304]{1,0:T(8,128)(2,1)S(1)}, bf16[64,2304]{1,0:T(8,128)(2,1)S(1)}, u32[]{:S(2)}, u32[]{:S(2)}) collective-permute-start(bf16[64,2304]{1,0:T(8,128)(2,1)S(1)} %get-tuple-element.59.x1), channel_id=1, source_target_pairs={{0,1},{1,0},{2,3},{3,2},{4,5},{5,4},{6,7},{7,6}} | collective-permute-start | bytes 884744 | tf_op jit(solution)/shard_map/ppermute | solution.py:315
  73.0 13.4 %collective-permute-start.18 = (f32[1,2304]{1,0:T(1,128)S(1)}, f32[1,2304]{1,0:T(1,128)S(1)}, u32[]{:S(2)}, u32[]{:S(2)}) collective-permute-start(f32[1,2304]{1,0:T(1,128)S(1)} %add.6), channel_id=1, source_target_pairs={{0,2},{1,3},{2,0},{3,1},{4,6},{5,7},{6,4},{7,5}} | collective-permute-start | bytes 27656 | tf_op jit(solution)/shard_map/ppermute | solution.py:315
  86.4 4.6 %collective-permute-start.14 = (bf16[64,2304]{1,0:T(8,128)(2,1)S(1)}, bf16[64,2304]{1,0:T(8,128)(2,1)S(1)}, u32[]{:S(2)}, u32[]{:S(2)}) collective-permute-start(bf16[64,2304]{1,0:T(8,128)(2,1)S(1)} %get-tuple-element.54.t1), channel_id=1, source_target_pairs={{0,1},{1,0},{2,3},{3,2},{4,5},{5,4},{6,7},{7,6}} | collective-permute-start | bytes 884744 | tf_op jit(solution)/shard_map/ppermute | solution.py:315
  86.4 4.6 %collective-permute-start.7 = (bf16[64,2304]{1,0:T(8,128)(2,1)S(1)}, bf16[64,2304]{1,0:T(8,128)(2,1)S(1)}, u32[]{:S(2)}, u32[]{:S(2)}) collective-permute-start(bf16[64,2304]{1,0:T(8,128)(2,1)S(1)} %get-tuple-element.51.d0), channel_id=1, source_target_pairs={{0,1},{1,0},{2,3},{3,2},{4,5},{5,4},{6,7},{7,6}} | collective-permute-start | bytes 884744 | tf_op jit(solution)/shard_map/ppermute | solution.py:315
  86.9 4.1 %collective-permute-start.11 = (bf16[64,2304]{1,0:T(8,128)(2,1)S(1)}, bf16[64,2304]{1,0:T(8,128)(2,1)S(1)}, u32[]{:S(2)}, u32[]{:S(2)}) collective-permute-start(bf16[64,2304]{1,0:T(8,128)(2,1)S(1)} %get-tuple-element.57.d1), channel_id=1, source_target_pairs={{0,1},{1,0},{2,3},{3,2},{4,5},{5,4},{6,7},{7,6}} | collective-permute-start | bytes 884744 | tf_op jit(solution)/shard_map/ppermute | solution.py:315
  86.9 4.1 %collective-permute-start.8 = (bf16[64,2304]{1,0:T(8,128)(2,1)S(1)}, bf16[64,2304]{1,0:T(8,128)(2,1)S(1)}, u32[]{:S(2)}, u32[]{:S(2)}) collective-permute-start(bf16[64,2304]{1,0:T(8,128)(2,1)S(1)} %collective-permute-done.6.c0), channel_id=1, source_target_pairs={{0,1},{1,0},{2,3},{3,2},{4,5},{5,4},{6,7},{7,6}} | collective-permute-start | bytes 884744 | tf_op jit(solution)/shard_map/ppermute | solution.py:315
  87.4 3.6 %collective-permute-start.12 = (bf16[64,2304]{1,0:T(8,128)(2,1)S(1)}, bf16[64,2304]{1,0:T(8,128)(2,1)S(1)}, u32[]{:S(2)}, u32[]{:S(2)}) collective-permute-start(bf16[64,2304]{1,0:T(8,128)(2,1)S(1)} %collective-permute-done.10.c1), channel_id=1, source_target_pairs={{0,1},{1,0},{2,3},{3,2},{4,5},{5,4},{6,7},{7,6}} | collective-permute-start | bytes 884744 | tf_op jit(solution)/shard_map/ppermute | solution.py:315

commit v11 on v10

--- a/solution.py
+++ b/solution.py
@@ -31,7 +31,7 @@
 
 def pdn_kernel(du_ref, w_ref, *refs):
     outs = refs[:4]
-    de_ref, dub, dup, wb, z, dsem, wsem, zsem = refs[4:]
+    dub, dup, wb, ob, dsem, wsem, osem = refs[4:]
     n, d = outs[0].shape
     k, tl = dub.shape[0], dub.shape[1] // 4
     blk = 256
@@ -40,23 +40,27 @@
     dc.start()
     for i in range(nb):
         pltpu.make_async_copy(w_ref.at[pl.ds(i * blk, blk), :], wb.at[pl.ds(i * blk, blk), :], wsem.at[i]).start()
-    z[...] = jnp.zeros_like(z)
-    zero_start(z, de_ref, *FILL[0], zsem)
     r = lax.axis_index("tp")
     dc.wait()
     for a, j in enumerate((2, 3, 1, 0)):
         q = r ^ j
         for m in range(k):
             dup[pl.ds(a * n + m * tl, tl), :] = dub[m, pl.ds(pl.multiple_of(q * tl, tl), tl), :]
+    copies = []
     for i in range(nb):
-        pltpu.make_async_copy(w_ref.at[pl.ds(i * blk, blk), :], wb.at[pl.ds(i * blk, blk), :], wsem.at[i]).wait()
+        cols = pl.ds(i * blk, blk)
+        pltpu.make_async_copy(w_ref.at[cols, :], wb.at[cols, :], wsem.at[i]).wait()
         p = lax.dot_general(dup[...], wb[i * blk:(i + 1) * blk, :], (((1,), (1,)), ((), ())), preferred_element_type=F32)
+        ob[:, i * blk:(i + 1) * blk] = p.astype(BF16)
         for a in range(4):
-            outs[a][:, i * blk:(i + 1) * blk] = p[a * n:(a + 1) * n].astype(BF16)
-    zero_wait(z, de_ref, *FILL[0], zsem)
-
-
-FILL = ((0, 4), (4, 6), (6, 8), (8, 16))
+            c = pltpu.make_async_copy(ob.at[pl.ds(a * n, n), cols], outs[a].at[:, cols], osem)
+            c.start()
+            copies.append(c)
+    for c in copies:
+        c.wait()
+
+
+FILL = ((0, 3), (3, 6), (6, 16))
 
 
 def zero_start(z, de_ref, lo, hi, sem):
@@ -74,7 +78,7 @@
 
 def zero_kernel(own_ref, de_in, list_ref, de_ref, z, lnxt, tab, sem):
     z[...] = jnp.zeros_like(z)
-    zero_start(z, de_ref, *FILL[3], sem)
+    zero_start(z, de_ref, *FILL[2], sem)
     n = own_ref[0, own_ref.shape[1] - 1]
     t = lnxt.shape[0] - 8
 
@@ -92,7 +96,7 @@
     lax.fori_loop(0, n, link, 0)
 
     def lists(i, c):
-        nl, nd = c
+        nl, nd, nl0, nd0 = c
         x = lnxt[i]
         end = (x < 0).astype(jnp.int32)
         pos = own_ref[0, i]
@@ -100,29 +104,34 @@
         list_ref[1, nl] = own_ref[1, i]
         list_ref[2, nd] = pos
         list_ref[3, nd] = own_ref[0, jnp.maximum(x, 0)]
-        return nl + end, nd + 1 - end
-
-    nl, nd = lax.fori_loop(0, n, lists, (0, 0))
-    list_ref[0, list_ref.shape[1] - 1] = nl
-    list_ref[2, list_ref.shape[1] - 1] = nd
-    zero_wait(z, de_ref, *FILL[3], sem)
-
-
-def gather_kernel(ids_ref, emb_ref, de_in, k0, s0, k1, s1, own_ref, de_ref, buf, tmp, xf, z, lst, sem, zsem):
+        near = (pos < t // 2).astype(jnp.int32)
+        near2 = (list_ref[3, nd] < t // 2).astype(jnp.int32)
+        return nl + end, nd + 1 - end, nl0 + end * near, nd0 + (1 - end) * near2
+
+    nl, nd, nl0, nd0 = lax.fori_loop(0, n, lists, (0, 0, 0, 0))
+    for a, v in enumerate((nl, nl0, nd, nd0)):
+        list_ref[a, list_ref.shape[1] - 1] = v
+    zero_wait(z, de_ref, *FILL[2], sem)
+
+
+def gather_kernel(ids_ref, emb_ref, k0, s0, k1, s1, own_ref, de_ref, buf, tmp, xf, z, lst, sem, zsem):
     k, t = ids_ref.shape
     vl = emb_ref.shape[0]
     h = k0.shape[0]
     tl = t // 4
     r = lax.axis_index("tp")
     z[...] = jnp.zeros_like(z)
-    zero_start(z, de_ref, *FILL[1], zsem)
+    zero_start(z, de_ref, *FILL[0], zsem)
     n = 0
-    for m in range(k):
-        def scan(i, n):
-            lst[n] = m * t + i
-            return n + (lax.shift_right_logical(ids_ref[m, i], vl.bit_length() - 1) == r).astype(jnp.int32)
-
-        n = lax.fori_loop(0, t, scan, n, unroll=16)
+    for c in range(2):
+        lo = ((r >> 1) ^ c) * h
+        for m in range(k):
+            def scan(i, n):
+                j = lo + i
+                lst[n] = m * t + j
+                return n + (lax.shift_right_logical(ids_ref[m, j], vl.bit_length() - 1) == r).astype(jnp.int32)
+
+            n = lax.fori_loop(0, h, scan, n, unroll=16)
     own_ref[0, own_ref.shape[1] - 1] = n
 
     def start(i, c):
@@ -131,12 +140,12 @@
         v = ids_ref[m, j & (t - 1)] - r * vl
         q = (j & (t - 1)) // tl
         pltpu.make_async_copy(emb_ref.at[pl.ds(pl.multiple_of((v >> 3) << 3, 8), 8), :], buf.at[i], sem).start()
-        own_ref[0, i] = m * t + ((q ^ r) & 1) * h + ((q ^ r) >> 1) * tl + (j & (tl - 1))
+        own_ref[0, i] = ((q ^ r) >> 1) * 2 * h + m * h + ((q ^ r) & 1) * tl + (j & (tl - 1))
         own_ref[1, i] = v
         return c
 
     lax.fori_loop(0, n, start, 0)
-    zero_start(z, de_ref, *FILL[2], zsem)
+    zero_start(z, de_ref, *FILL[1], zsem)
     for a in range(8):
         own_ref[0, n + a] = k * t
         own_ref[1, n + a] = 0
@@ -158,8 +167,9 @@
 
     lax.fori_loop(0, (n + 7) // 8, take, 0)
     for a, ref in enumerate((k0, s0, k1, s1)):
-        ref[...] = xf[a * h:(a + 1) * h, :].astype(BF16)
-    zero_wait(z, de_ref, FILL[1][0], FILL[2][1], zsem)
+        for c in range(2):
+            ref[c * tl:(c + 1) * tl, :] = xf[c * 2 * h + a * tl:c * 2 * h + (a + 1) * tl, :].astype(BF16)
+    zero_wait(z, de_ref, FILL[0][0], FILL[1][1], zsem)
 
 
 def sum_kernel(k0, y0, k1, y1, a0, t0, a1, t1):
@@ -251,45 +261,76 @@
         c.wait()
 
 
-def last_kernel(chip_rows, list_ref, d0, c0, a0, b0, d1, c1, a1, b1, t0, w0, t1, w1, dwp_ref, ids_ref, g_ref,
-                w_ref, du_ref, u_in, de_in, u_ref, dw_ref, de_ref, xf, n_ref, du2, ub, dwb, usem, wsem, sem):
-    d = w_ref.shape[0]
-    tl = d0.shape[0]
-    r = lax.axis_index("tp")
-    for a, ref in enumerate((d0, c0, a0, b0, d1, c1, a1, b1)):
-        xf[a * tl:(a + 1) * tl, :] = ref[...].astype(F32)
+def scatter(near, list_ref, xf, de_ref, sem):
+    e = list_ref.shape[1] - 1
+    split = xf.shape[0] if near else xf.shape[0] // 2
 
     def add(i, c):
         a = list_ref[2, i]
         b = list_ref[3, i]
-        xf[pl.ds(b, 1), :] = xf[pl.ds(b, 1), :] + xf[pl.ds(a, 1), :]
-        return c
-
-    lax.fori_loop(0, list_ref[2, list_ref.shape[1] - 1], add, 0)
-
+
+        @pl.when((b < split) if near else (b >= split))
+        def _():
+            xf[pl.ds(b, 1), :] = xf[pl.ds(b, 1), :] + xf[pl.ds(a, 1), :]
+
+        return c
+
+    @pl.when((list_ref[3, e] > 0) if near else (list_ref[2, e] > list_ref[3, e]))
+    def _():
+        lax.fori_loop(0, list_ref[2, e], add, 0)
+
+    def put(i, c):
+        pltpu.make_async_copy(xf.at[pl.ds(list_ref[0, i], 1), :], de_ref.at[pl.ds(list_ref[1, i], 1), :], sem).start()
+        return c
+
+    lax.fori_loop(*((0, list_ref[1, e]) if near else (list_ref[1, e], list_ref[0, e])), put, 0)
+
+
+def scatter_wait(near, list_ref, xf, de_ref, sem):
+    e = list_ref.shape[1] - 1
+
+    def wait(i, c):
+        pltpu.make_async_copy(xf.at[pl.ds(0, 1), :], de_ref.at[pl.ds(0, 1), :], sem).wait()
+        return c
+
+    lax.fori_loop(*((0, list_ref[1, e]) if near else (list_ref[1, e], list_ref[0, e])), wait, 0)
+
+
+def near_kernel(list_ref, d0, a0, d1, a1, tok_ref, de_in, xn_ref, de_ref, sem):
+    tl = d0.shape[0]
+    for a, ref in enumerate((d0, a0, d1, a1)):
+        xn_ref[a * tl:(a + 1) * tl, :] = ref[...].astype(F32)
+    scatter(True, list_ref, xn_ref, de_ref, sem)
+    scatter_wait(True, list_ref, xn_ref, de_ref, sem)
+
+
+def last_kernel(chip_rows, list_ref, xn_ref, c0, b0, c1, b1, t0, w0, t1, w1, dwp_ref, ids_ref, g_ref,
+                w_ref, du_ref, u_in, de_in, u_ref, dw_ref, de_ref, xf, n_ref, du2, ub, dwb, usem, wsem, sem):
+    d = w_ref.shape[0]
+    tl = c0.shape[0]
+    r = lax.axis_index("tp")
+    h = xn_ref.shape[0]
+
+    @pl.when(list_ref[2, list_ref.shape[1] - 1] > list_ref[3, list_ref.shape[1] - 1])
+    def _():
+        xf[0:h, :] = xn_ref[...]
+
+    for a, ref in enumerate((c0, b0, c1, b1)):
+        xf[h + a * tl:h + (a + 1) * tl, :] = ref[...].astype(F32)
+    scatter(False, list_ref, xf, de_ref, sem)
+    take_du(du_ref, du2, tl, ((0, r ^ 2), (0, r ^ 3), (1, r ^ 2), (1, r ^ 3)))
     for a, (m, q, own, got) in enumerate(((0, r ^ 2, t0, c0), (0, r ^ 3, w0, b0), (1, r ^ 2, t1, c1), (1, r ^ 3, w1, b1))):
         x = jnp.where(chip_mask(ids_ref, m, q, tl, chip_rows), own[...].astype(F32), got[...].astype(F32))
         n_ref[a * tl:(a + 1) * tl, :] = norm(x, g_ref)
-
-    def put(i, c):
-        pltpu.make_async_copy(xf.at[pl.ds(list_ref[0, i], 1), :], de_ref.at[pl.ds(list_ref[1, i], 1), :], sem).start()
-        return c
-
-    lax.fori_loop(0, list_ref[0, list_ref.shape[1] - 1], put, 0)
-    take_du(du_ref, du2, tl, ((0, r ^ 2), (0, r ^ 3), (1, r ^ 2), (1, r ^ 3)))
-    copies = umat(n_ref[...], w_ref, ub, u_ref, r ^ 2, r ^ 3, usem)
     blk = 256
+    copies = []
     for i in range(d // blk):
         dwb[i] = dwp_ref[i * blk:(i + 1) * blk, :] + dw_tile(n_ref, du2, i, blk)
         c = pltpu.make_async_copy(dwb.at[i], dw_ref.at[pl.ds(i * blk, blk), :], wsem)
         c.start()
         copies.append(c)
-
-    def wait(i, c):
-        pltpu.make_async_copy(xf.at[pl.ds(0, 1), :], de_ref.at[pl.ds(0, 1), :], sem).wait()
-        return c
-
-    lax.fori_loop(0, list_ref[0, list_ref.shape[1] - 1], wait, 0)
+    copies += umat(n_ref[...], w_ref, ub, u_ref, r ^ 2, r ^ 3, usem)
+    scatter_wait(False, list_ref, xf, de_ref, sem)
     for c in copies:
         c.wait()
 
@@ -314,19 +355,19 @@
         def perm(v, p):
             return lax.ppermute(v, "tp", p)
 
-        p2, p3, p1, p0, de = call(
-            pdn_kernel, 60, [S((n, d), BF16)] * 4 + [S((vl, d), F32)], [HBM] * 2, [VMEM] * 4 + [HBM],
-            [pltpu.VMEM((k, t, fc), BF16), pltpu.VMEM((4 * n, fc), BF16), pltpu.VMEM((d, fc), BF16), pltpu.VMEM((256, d), F32),
+        p2, p3, p1, p0 = call(
+            pdn_kernel, 60, [S((n, d), BF16)] * 4, [HBM] * 2, [HBM] * 4,
+            [pltpu.VMEM((k, t, fc), BF16), pltpu.VMEM((4 * n, fc), BF16), pltpu.VMEM((d, fc), BF16), pltpu.VMEM((4 * n, d), BF16),
              D, D((d // 256,)), D], 8 * n * fc * d, 2 * d * fc + 8 * n * (fc + d))(du, w)
         q2 = perm(p2, cross)
         q3 = perm(p3, diag)
         k0, s0, k1, s1, owned, de = call(
-            gather_kernel, 60,
+            gather_kernel, 36,
             [S((n, d), BF16)] * 4 + [S((2, 2 * h + 16), jnp.int32), S((vl, d), F32)],
-            [SMEM, HBM, HBM], [VMEM] * 4 + [SMEM, HBM],
+            [SMEM, HBM], [VMEM] * 4 + [SMEM, HBM],
             [pltpu.VMEM((2 * h, 8, d), BF16), pltpu.VMEM((8, 8, d), F32), pltpu.VMEM((2 * h + 8, d), F32), pltpu.VMEM((256, d), F32)]
             + [pltpu.SMEM((2 * h + 8,), jnp.int32), D, D],
-            500_000_000, 16 * h * d, {2: 5})(ids, emb, de)
+            500_000_000, 16 * h * d)(ids, emb)
         y0 = perm(s0, sib)
         y1 = perm(s1, sib)
         q1 = perm(p1, sib)
@@ -360,6 +401,8 @@
             u_kernel, 32, [S((k, t, fc), BF16), S((d, fc), F32)], [VMEM] * 8, [HBM, VMEM],
             [pltpu.VMEM((t, d), BF16), pltpu.VMEM((t, fc), BF16), pltpu.VMEM((t, fc), BF16), D],
             4 * t * d * fc, 2 * d * fc)(x0, xo0, x1, xo1, g2, w, du, dg)
+        xn, de = call(near_kernel, 12, [S((t, d), F32), S((vl, d), F32)], [SMEM] + [VMEM] * 5 + [HBM], [VMEM, HBM],
+                      [D], 8 * h * d, 8 * h * d, {6: 1})(lists, dx0, a0, dx1, a1, dg, de)
         b0 = perm(c0, sib)
         b1 = perm(c1, sib)
         dgs = dg + perm(dg, sib)
@@ -367,11 +410,11 @@
 
         u, dw, de = call(
             functools.partial(last_kernel, 2 * vl), 36, [S((k, t, fc), BF16), S((d, fc), F32), S((vl, d), F32)],
-            [SMEM] + [VMEM] * 17 + [HBM] * 2, [HBM] * 3,
+            [SMEM] + [VMEM] * 14 + [HBM] * 2, [HBM] * 3,
             [pltpu.VMEM((2 * h, d), F32), pltpu.VMEM((t, d), BF16), pltpu.VMEM((t, fc), BF16), pltpu.VMEM((t, fc), BF16),
              pltpu.VMEM((d // 256, 256, fc), F32), D, D, D],
-            4 * t * d * fc, 6 * d * fc, {18: 0, 19: 2})(
-                lists, dx0, c0, a0, b0, dx1, c1, a1, b1, oth0, w0, oth1, w1, dwp, ids, g2, w, du, u, de)
+            4 * t * d * fc, 6 * d * fc, {15: 0, 16: 2})(
+                lists, xn, c0, b0, c1, b1, oth0, w0, oth1, w1, dwp, ids, g2, w, du, u, de)
         return u, x, de, dw, dgs.reshape(d)
 
     return jax.shard_map(

time: 101 us -> 108 us (1.069)
  waiting for transfers between devices: 30.8 us -> 34.1 us
  Pallas kernels: 54.5 us -> 57.1 us
  local copies, waits for them, and re-layouts: 2.88 us -> 4.37 us
    ppermute x19, waiting for transfers between devices: 30.8 us -> 34.1 us  [perm(): return lax.ppermute(v, 'tp', p)]
    pallas_call x1, Pallas kernels: 14 us -> 16.6 us  [local(): call(zero_kernel, 8, [S((4, 2 * h + 16), jnp.int32), S((vl, d), F32)], [S...]
    unnamed x26 -> x18, local copies, waits for them, and re-layouts: 2.87 us -> 4.36 us
    pallas_call x2 -> x3, Pallas kernels: 25.6 us -> 24.8 us  [the longest x1 12.7 us: local(): call(gather_kernel, 36, [S((n, d), BF16)] * 4 + [S((2, 2 * h + 16), jnp.i...]
  transfers between devices with their start and end apart: 19 -> 19, of which waited for: 5 -> 6; matrix products, arithmetic and copies ran while one was open for 1% -> 1% of each run, Pallas kernels for 20% -> 32%
where the time goes in v11:
time: 108 us; the launch traced here: 107 us
  Pallas kernels  57.1 us (53%)
  waiting for transfers between devices  34.1 us (32%)
  starting transfers between devices  9.94 us (9%)
  local copies, waits for them, and re-layouts  4.37 us (4%)
    ppermute x19, waiting for transfers between devices, perm(): return lax.ppermute(v, 'tp', p)  34.1 us
    pallas_call x1, Pallas kernels, local(): call(zero_kernel, 8, [S((4, 2 * h + 16), jnp.int32), S((vl, d), F32)], [S...  16.6 us
    pallas_call x1, Pallas kernels, local(): call(gather_kernel, 36, [S((n, d), BF16)] * 4 + [S((2, 2 * h + 16), jnp.i...  12.7 us
    ppermute x19, starting transfers between devices, perm(): return lax.ppermute(v, 'tp', p)  9.94 us
    pallas_call x1, Pallas kernels, local(): call(functools.partial(last_kernel, 2 * vl), 36, [S((k, t, fc), BF16), S(...  9.85 us
    pallas_call x1, Pallas kernels, local(): call(pdn_kernel, 60, [S((n, d), BF16)] * 4, [HBM] * 2, [HBM] * 4, [pltpu....  9.64 us
    unnamed x18, local copies, waits for them, and re-layouts  4.36 us
    pallas_call x1, Pallas kernels, local(): call(u_kernel, 32, [S((k, t, fc), BF16), S((d, fc), F32)], [VMEM] * 8, [H...  2.92 us
  transfers between devices with their start and end apart: 19, of which 6 were waited for; matrix products, arithmetic and copies ran while one was open for 1% of the time, Pallas kernels for 32%

profile of v11, /device:TPU:0, one launch (start us, length us, event | category | flops | bytes accessed | tf_op | source)
XLA Modules:
  0.0 107.2 jit_solution(1144028352633733052)
XLA Ops:
  0.6 0.0 copy-start.4
  0.6 0.7 copy-done.4
  1.3 12.7 %shard_map.101 = (bf16[128,2304]{1,0:T(8,128)(2,1)S(1)}, bf16[128,2304]{1,0:T(8,128)(2,1)S(1)}, bf16[128,2304]{1,0:T(8,128)(2,1)S(1)}, bf16[128,2304]{1,0:T(8,12...) custom-call(s32[2,256]{1,0:T(2,128)S(1)} %copy-done.4, bf16[8192,2304]{1,0:T(8,128)(2,1)} %emb_ref.1), custom_call_target="tpu_custom_call" | custom-call | flops 500000000 | bytes 9437184 | tf_op jit(solution)/shard_map/pallas_call | solution.py:364
  14.1 0.5 collective-permute-start
  14.6 0.0 collective-permute-start.1
  14.6 9.6 %shard_map.104 = (bf16[128,2304]{1,0:T(8,128)(2,1)}, bf16[128,2304]{1,0:T(8,128)(2,1)}, bf16[128,2304]{1,0:T(8,128)(2,1)}, bf16[128,2304]{1,0:T(8,128)(2,1)}) custom-call(bf16[2,256,1024]{2,1,0:T(8,128)(2,1)} %du_ref.5, bf16[2304,1024]{1,0:T(8,128)(2,1)} %w_ref.5), custom_call_target="tpu_custom_call" | custom-call | flops 2415919104 | bytes 8126464 | tf_op jit(solution)/shard_map/pallas_call | solution.py:358
  24.3 0.5 collective-permute-start.3
  24.7 1.9 %collective-permute-start.4 = (bf16[128,2304]{1,0:T(8,128)(2,1)}, bf16[128,2304]{1,0:T(8,128)(2,1)S(1)}, u32[]{:S(2)}, u32[]{:S(2)}) collective-permute-start(bf16[128,2304]{1,0:T(8,128)(2,1)} %get-tuple-element.48), channel_id=1, source_target_pairs={{0,2},{1,3},{2,0},{3,1},{4,6},{5,7},{6,4},{7,5}} | collective-permute-start | bytes 1769480 | tf_op jit(solution)/shard_map/ppermute | solution.py:356
  26.7 0.1 collective-permute-start.5
  26.7 0.0 collective-permute-done.y0
  26.7 0.0 collective-permute-done.1.y1
  26.7 0.1 shard_map.103
  26.9 1.8 %collective-permute-start.2 = (bf16[64,2304]{1,0:T(8,128)(2,1)S(1)}, bf16[64,2304]{1,0:T(8,128)(2,1)S(1)}, u32[]{:S(2)}, u32[]{:S(2)}) collective-permute-start(bf16[64,2304]{1,0:T(8,128)(2,1)S(1)} %get-tuple-element.45.t0), channel_id=1, source_target_pairs={{0,2},{1,3},{2,0},{3,1},{4,6},{5,7},{6,4},{7,5}} | collective-permute-start | bytes 884744 | tf_op jit(solution)/shard_map/ppermute | solution.py:356
  28.6 0.3 collective-permute-start.7
  28.9 0.0 copy-start.6
  28.9 0.0 copy-start.1
  28.9 0.0 copy-start.2
  28.9 0.0 copy-start.5
  28.9 16.6 %shard_map.102 = (s32[4,528]{1,0:T(4,128)S(1)}, f32[8192,2304]{1,0:T(8,128)}) custom-call(s32[2,528]{1,0:T(2,128)S(1)} %get-tuple-element.37.own_ref, f32[8192,2304]{1,0:T(8,128)} %get-tuple-element.38.de_in), custom_call_target="tpu_custom_call", output_to_operand_aliasing={{1}: (1, {})} | custom-call | flops 6000000000 | bytes 37748736 | tf_op jit(solution)/shard_map/pallas_call | solution.py:380
  45.5 0.0 copy-done.6
  45.5 0.0 collective-permute-done.3.p1
  45.5 0.0 collective-permute-done.4.p2
  45.5 7.8 %collective-permute-done.5.p3 = bf16[128,2304]{1,0:T(8,128)(2,1)S(1)} collective-permute-done((bf16[128,2304]{1,0:T(8,128)(2,1)}, bf16[128,2304]{1,0:T(8,128)(2,1)S(1)}, u32[]{:S(2)}, u32[]{:S(2)}) %collective-permute-start.5) | collective-permute-done | bytes 589856 | tf_op jit(solution)/shard_map/ppermute | solution.py:356
  53.3 6.8 %collective-permute-done.2.z_ref = bf16[64,2304]{1,0:T(8,128)(2,1)S(1)} collective-permute-done((bf16[64,2304]{1,0:T(8,128)(2,1)S(1)}, bf16[64,2304]{1,0:T(8,128)(2,1)S(1)}, u32[]{:S(2)}, u32[]{:S(2)}) %collective-permute-start.2) | collective-permute-done | bytes 294944 | tf_op jit(solution)/shard_map/ppermute | solution.py:356
  60.1 0.0 copy-done.1
  60.1 0.0 copy-done.2
  60.1 0.0 copy-done.5
  60.1 0.7 shard_map.105
  60.9 0.0 collective-permute-start.6
  60.9 5.2 %collective-permute-done.7.z_ref = bf16[64,2304]{1,0:T(8,128)(2,1)S(1)} collective-permute-done((bf16[64,2304]{1,0:T(8,128)(2,1)S(1)}, bf16[64,2304]{1,0:T(8,128)(2,1)S(1)}, u32[]{:S(2)}, u32[]{:S(2)}) %collective-permute-start.7) | collective-permute-done | bytes 294944 | tf_op jit(solution)/shard_map/ppermute | solution.py:356
  66.1 0.0 slice-start
  66.1 2.1 %shard_map.106 = (bf16[64,2304]{1,0:T(8,128)(2,1)S(1)}, bf16[64,2304]{1,0:T(8,128)(2,1)S(1)}, bf16[64,2304]{1,0:T(8,128)(2,1)S(1)}, f32[1,2304]{1,0:T(1,128)S(1)}, bf16[2,64,2304]{2,1,0:T(8,128)(2,1)}) custom-call(bf16[64,2304]{1,0:T(8,128)(2,1)S(1)} %get-tuple-element.52.xh_ref, bf16[64,2304]{1,0:T(8,128)(2,1)S(1)} %collective-permute-done.7.z_ref, ...), custom_call_target="tpu_custom_call" | custom-call | flops 8847360 | bytes 4718592 | tf_op jit(solution)/shard_map/pallas_call | solution.py:387
  68.3 0.0 collective-permute-start.17
  68.3 1.2 %collective-permute-done.17 = f32[1,2304]{1,0:T(1,128)S(1)} collective-permute-done((f32[1,2304]{1,0:T(1,128)S(1)}, f32[1,2304]{1,0:T(1,128)S(1)}, u32[]{:S(2)}, u32[]{:S(2)}) %collective-permute-start.17) | collective-permute-done | bytes 9248 | tf_op jit(solution)/shard_map/ppermute | solution.py:356
  69.4 1.8 %collective-permute-start.18 = (f32[1,2304]{1,0:T(1,128)S(1)}, f32[1,2304]{1,0:T(1,128)S(1)}, u32[]{:S(2)}, u32[]{:S(2)}) collective-permute-start(f32[1,2304]{1,0:T(1,128)S(1)} %add.6), channel_id=1, source_target_pairs={{0,2},{1,3},{2,0},{3,1},{4,6},{5,7},{6,4},{7,5}} | collective-permute-start | bytes 27656 | tf_op jit(solution)/shard_map/ppermute | solution.py:356
  71.2 0.0 collective-permute-start.8
  71.2 0.3 collective-permute-start.9
  71.5 1.7 %collective-permute-start.11 = (bf16[64,2304]{1,0:T(8,128)(2,1)S(1)}, bf16[64,2304]{1,0:T(8,128)(2,1)S(1)}, u32[]{:S(2)}, u32[]{:S(2)}) collective-permute-start(bf16[64,2304]{1,0:T(8,128)(2,1)S(1)} %get-tuple-element.60), channel_id=1, source_target_pairs={{0,2},{1,3},{2,0},{3,1},{4,6},{5,7},{6,4},{7,5}} | collective-permute-start | bytes 884744 | tf_op jit(solution)/shard_map/ppermute | solution.py:356
  73.2 0.0 collective-permute-done.18
  73.2 0.0 collective-permute-start.15
  73.2 0.0 collective-permute-done.6.a0
  73.3 0.5 collective-permute-start.16
  73.8 0.0 collective-permute-done.8.a1
  73.8 0.0 collective-permute-start.13
  73.8 7.3 %collective-permute-done.9.c0 = bf16[64,2304]{1,0:T(8,128)(2,1)S(1)} collective-permute-done((bf16[64,2304]{1,0:T(8,128)(2,1)S(1)}, bf16[64,2304]{1,0:T(8,128)(2,1)S(1)}, u32[]{:S(2)}, u32[]{:S(2)}) %collective-permute-start.9) | collective-permute-done | bytes 294944 | tf_op jit(solution)/shard_map/ppermute | solution.py:356
  81.1 0.0 collective-permute-start.14
  81.1 5.9 %collective-permute-done.11.c1 = bf16[64,2304]{1,0:T(8,128)(2,1)S(1)} collective-permute-done((bf16[64,2304]{1,0:T(8,128)(2,1)S(1)}, bf16[64,2304]{1,0:T(8,128)(2,1)S(1)}, u32[]{:S(2)}, u32[]{:S(2)}) %collective-permute-start.11) | collective-permute-done | bytes 294944 | tf_op jit(solution)/shard_map/ppermute | solution.py:356
  87.0 0.0 collective-permute-start.10
  87.0 0.0 collective-permute-done.15.y0
  87.0 0.5 collective-permute-start.12
  87.5 0.6 add_reduce_fusion
  88.1 2.4 %shard_map.107 = (f32[256,2304]{1,0:T(8,128)S(1)}, f32[8192,2304]{1,0:T(8,128)}) custom-call(s32[4,528]{1,0:T(4,128)S(1)} %get-tuple-element.39.tok_ref.list_ref, bf16[64,2304]{1,0:T(8,128)(2,1)S(1)} %get-tuple-element.51.d0, bf16[64,2304]{1,0:T(8,128)(2,1)S(1)} %collective-permute-done.6.a0, ...), custom_call_target="tpu_custom_call", output_to_operand_aliasing={{1}: (6, {})} | custom-call | flops 4718592 | bytes 4718592 | tf_op jit(solution)/shard_map/pallas_call | solution.py:404
  90.5 0.0 collective-permute-done.16.y1
  90.5 0.0 slice-done
  90.5 0.0 slice-done.1
  90.5 0.0 copy-done.3
  90.6 2.9 %shard_map.108 = (bf16[2,256,1024]{2,1,0:T(8,128)(2,1)}, f32[2304,1024]{1,0:T(8,128)S(1)}) custom-call(bf16[64,2304]{1,0:T(8,128)(2,1)S(1)} %get-tuple-element.54.refs_0_.x0, bf16[64,2304]{1,0:T(8,128)(2,1)S(1)} %collective-permute-done.15.y0, bf16[64,2304]{1,0:T(8,128)(2,1)S(1)} %get-tuple-element.61.x1, bf16[64,2304]{1,0:T(8,128)(2,1)S(1)} %collective-permute-done.16.y1, ...), custom_call_target="tpu_custom_call" | custom-call | flops 2415919104 | bytes 4718592 | tf_op jit(solution)/shard_map/pallas_call | solution.py:400
  93.5 0.0 copy-start
  93.5 3.7 %copy-done = f32[2304,1024]{1,0:T(8,128)} copy-done((f32[2304,1024]{1,0:T(8,128)}, f32[2304,1024]{1,0:T(8,128)S(1)}, u32[]{:S(2)}) %copy-start) | copy-done | bytes 9437208
  97.2 0.0 collective-permute-done.13.w0
  97.2 0.0 collective-permute-done.14.w1
  97.2 0.0 collective-permute-done.10.b0
  97.2 0.0 collective-permute-done.12.b1
  97.2 9.8 %shard_map.109 = (bf16[2,256,1024]{2,1,0:T(8,128)(2,1)}, f32[2304,1024]{1,0:T(8,128)}, f32[8192,2304]{1,0:T(8,128)}) custom-call(s32[4,528]{1,0:T(4,128)S(1)} %get-tuple-element.39.tok_ref.list_ref, f32[256,2304]{1,0:T(8,128)S(1)} %get-tuple-element.58.xn_ref, ...), custom_call_target="tpu_custom_call", output_to_operand_aliasing={{0}: (15, {}), {2}: (16, {})} | custom-call | flops 2415919104 | bytes 14155776 | tf_op jit(solution)/shard_map/pallas_call | solution.py:411
  (5 shorter events, 0.0 us)
Async XLA Ops:
  0.6 0.7 copy-start.4
  14.1 12.7 %collective-permute-start = (bf16[128,2304]{1,0:T(8,128)(2,1)S(1)}, bf16[128,2304]{1,0:T(8,128)(2,1)S(1)}, u32[]{:S(2)}, u32[]{:S(2)}) collective-permute-start(bf16[128,2304]{1,0:T(8,128)(2,1)S(1)} %get-tuple-element.41), channel_id=1, source_target_pairs={{0,1},{1,0},{2,3},{3,2},{4,5},{5,4},{6,7},{7,6}} | collective-permute-start | bytes 1769480 | tf_op jit(solution)/shard_map/ppermute | solution.py:356
  14.6 12.2 %collective-permute-start.1 = (bf16[128,2304]{1,0:T(8,128)(2,1)S(1)}, bf16[128,2304]{1,0:T(8,128)(2,1)S(1)}, u32[]{:S(2)}, u32[]{:S(2)}) collective-permute-start(bf16[128,2304]{1,0:T(8,128)(2,1)S(1)} %get-tuple-element.43), channel_id=1, source_target_pairs={{0,1},{1,0},{2,3},{3,2},{4,5},{5,4},{6,7},{7,6}} | collective-permute-start | bytes 1769480 | tf_op jit(solution)/shard_map/ppermute | solution.py:356
  24.3 21.3 %collective-permute-start.3 = (bf16[128,2304]{1,0:T(8,128)(2,1)}, bf16[128,2304]{1,0:T(8,128)(2,1)S(1)}, u32[]{:S(2)}, u32[]{:S(2)}) collective-permute-start(bf16[128,2304]{1,0:T(8,128)(2,1)} %get-tuple-element.47), channel_id=1, source_target_pairs={{0,1},{1,0},{2,3},{3,2},{4,5},{5,4},{6,7},{7,6}} | collective-permute-start | bytes 1769480 | tf_op jit(solution)/shard_map/ppermute | solution.py:356
  24.7 20.8 %collective-permute-start.4 = (bf16[128,2304]{1,0:T(8,128)(2,1)}, bf16[128,2304]{1,0:T(8,128)(2,1)S(1)}, u32[]{:S(2)}, u32[]{:S(2)}) collective-permute-start(bf16[128,2304]{1,0:T(8,128)(2,1)} %get-tuple-element.48), channel_id=1, source_target_pairs={{0,2},{1,3},{2,0},{3,1},{4,6},{5,7},{6,4},{7,5}} | collective-permute-start | bytes 1769480 | tf_op jit(solution)/shard_map/ppermute | solution.py:356
  26.7 26.7 %collective-permute-start.5 = (bf16[128,2304]{1,0:T(8,128)(2,1)}, bf16[128,2304]{1,0:T(8,128)(2,1)S(1)}, u32[]{:S(2)}, u32[]{:S(2)}) collective-permute-start(bf16[128,2304]{1,0:T(8,128)(2,1)} %get-tuple-element.49), channel_id=1, source_target_pairs={{0,3},{1,2},{2,1},{3,0},{4,7},{5,6},{6,5},{7,4}} | collective-permute-start | bytes 1769480 | tf_op jit(solution)/shard_map/ppermute | solution.py:356
  26.9 33.3 %collective-permute-start.2 = (bf16[64,2304]{1,0:T(8,128)(2,1)S(1)}, bf16[64,2304]{1,0:T(8,128)(2,1)S(1)}, u32[]{:S(2)}, u32[]{:S(2)}) collective-permute-start(bf16[64,2304]{1,0:T(8,128)(2,1)S(1)} %get-tuple-element.45.t0), channel_id=1, source_target_pairs={{0,2},{1,3},{2,0},{3,1},{4,6},{5,7},{6,4},{7,5}} | collective-permute-start | bytes 884744 | tf_op jit(solution)/shard_map/ppermute | solution.py:356
  28.6 37.5 %collective-permute-start.7 = (bf16[64,2304]{1,0:T(8,128)(2,1)S(1)}, bf16[64,2304]{1,0:T(8,128)(2,1)S(1)}, u32[]{:S(2)}, u32[]{:S(2)}) collective-permute-start(bf16[64,2304]{1,0:T(8,128)(2,1)S(1)} %get-tuple-element.53.t1), channel_id=1, source_target_pairs={{0,2},{1,3},{2,0},{3,1},{4,6},{5,7},{6,4},{7,5}} | collective-permute-start | bytes 884744 | tf_op jit(solution)/shard_map/ppermute | solution.py:356
  28.9 16.6 %copy-start.6 = (bf16[2304]{0:T(1024)(128)(2,1)S(1)}, bf16[2304]{0:T(1024)(128)(2,1)}, u32[]{:S(2)}) copy-start(bf16[2304]{0:T(1024)(128)(2,1)} %param.8) | copy-start | bytes 13828
  28.9 31.2 %copy-start.1 = (bf16[2,64,2304]{2,1,0:T(8,128)(2,1)S(1)}, bf16[2,64,2304]{2,1,0:T(8,128)(2,1)}, u32[]{:S(2)}) copy-start(bf16[2,64,2304]{2,1,0:T(8,128)(2,1)} %dres_ref.3) | copy-start | bytes 1769476
  28.9 31.2 %copy-start.2 = (bf16[128,2304]{1,0:T(8,128)(2,1)S(1)}, bf16[128,2304]{1,0:T(8,128)(2,1)}, u32[]{:S(2)}) copy-start(bf16[128,2304]{1,0:T(8,128)(2,1)} %get-tuple-element.46.p0) | copy-start | bytes 1769476
  28.9 31.2 %copy-start.5 = (s32[2,256]{1,0:T(2,128)S(1)}, s32[2,256]{1,0:T(2,128)}, u32[]{:S(2)}) copy-start(s32[2,256]{1,0:T(2,128)} %ids_ref.7) | copy-start | bytes 6148
  60.9 12.4 %collective-permute-start.6 = (bf16[64,2304]{1,0:T(8,128)(2,1)S(1)}, bf16[64,2304]{1,0:T(8,128)(2,1)S(1)}, u32[]{:S(2)}, u32[]{:S(2)}) collective-permute-start(bf16[64,2304]{1,0:T(8,128)(2,1)S(1)} %get-tuple-element.51.d0), channel_id=1, source_target_pairs={{0,1},{1,0},{2,3},{3,2},{4,5},{5,4},{6,7},{7,6}} | collective-permute-start | bytes 884744 | tf_op jit(solution)/shard_map/ppermute | solution.py:356
  66.1 24.4 %slice-start = ((s8[4718592]{0:T(1024)(128)(4,1)}), s8[4194304]{0:T(1024)(128)(4,1)S(1)}, s32[]{:S(2)}) async-start(s8[4718592]{0:T(1024)(128)(4,1)} %bitcast), calls=%async_computation | async-start | bytes 8388608
  68.3 1.2 %collective-permute-start.17 = (f32[1,2304]{1,0:T(1,128)S(1)}, f32[1,2304]{1,0:T(1,128)S(1)}, u32[]{:S(2)}, u32[]{:S(2)}) collective-permute-start(f32[1,2304]{1,0:T(1,128)S(1)} %get-tuple-element.57.tok_ref), channel_id=1, source_target_pairs={{0,1},{1,0},{2,3},{3,2},{4,5},{5,4},{6,7},{7,6}} | collective-permute-start | bytes 27656 | tf_op jit(solution)/shard_map/ppermute | solution.py:356
  69.4 3.8 %collective-permute-start.18 = (f32[1,2304]{1,0:T(1,128)S(1)}, f32[1,2304]{1,0:T(1,128)S(1)}, u32[]{:S(2)}, u32[]{:S(2)}) collective-permute-start(f32[1,2304]{1,0:T(1,128)S(1)} %add.6), channel_id=1, source_target_pairs={{0,2},{1,3},{2,0},{3,1},{4,6},{5,7},{6,4},{7,5}} | collective-permute-start | bytes 27656 | tf_op jit(solution)/shard_map/ppermute | solution.py:356
  71.2 2.6 %collective-permute-start.8 = (bf16[64,2304]{1,0:T(8,128)(2,1)S(1)}, bf16[64,2304]{1,0:T(8,128)(2,1)S(1)}, u32[]{:S(2)}, u32[]{:S(2)}) collective-permute-start(bf16[64,2304]{1,0:T(8,128)(2,1)S(1)} %get-tuple-element.56.d1), channel_id=1, source_target_pairs={{0,1},{1,0},{2,3},{3,2},{4,5},{5,4},{6,7},{7,6}} | collective-permute-start | bytes 884744 | tf_op jit(solution)/shard_map/ppermute | solution.py:356
  71.2 9.9 %collective-permute-start.9 = (bf16[64,2304]{1,0:T(8,128)(2,1)S(1)}, bf16[64,2304]{1,0:T(8,128)(2,1)S(1)}, u32[]{:S(2)}, u32[]{:S(2)}) collective-permute-start(bf16[64,2304]{1,0:T(8,128)(2,1)S(1)} %get-tuple-element.59), channel_id=1, source_target_pairs={{0,2},{1,3},{2,0},{3,1},{4,6},{5,7},{6,4},{7,5}} | collective-permute-start | bytes 884744 | tf_op jit(solution)/shard_map/ppermute | solution.py:356
  71.5 15.5 %collective-permute-start.11 = (bf16[64,2304]{1,0:T(8,128)(2,1)S(1)}, bf16[64,2304]{1,0:T(8,128)(2,1)S(1)}, u32[]{:S(2)}, u32[]{:S(2)}) collective-permute-start(bf16[64,2304]{1,0:T(8,128)(2,1)S(1)} %get-tuple-element.60), channel_id=1, source_target_pairs={{0,2},{1,3},{2,0},{3,1},{4,6},{5,7},{6,4},{7,5}} | collective-permute-start | bytes 884744 | tf_op jit(solution)/shard_map/ppermute | solution.py:356
  73.2 13.7 %collective-permute-start.15 = (bf16[64,2304]{1,0:T(8,128)(2,1)S(1)}, bf16[64,2304]{1,0:T(8,128)(2,1)S(1)}, u32[]{:S(2)}, u32[]{:S(2)}) collective-permute-start(bf16[64,2304]{1,0:T(8,128)(2,1)S(1)} %get-tuple-element.54.refs_0_.x0), channel_id=1, source_target_pairs={{0,1},{1,0},{2,3},{3,2},{4,5},{5,4},{6,7},{7,6}} | collective-permute-start | bytes 884744 | tf_op jit(solution)/shard_map/ppermute | solution.py:356
  73.3 17.3 %collective-permute-start.16 = (bf16[64,2304]{1,0:T(8,128)(2,1)S(1)}, bf16[64,2304]{1,0:T(8,128)(2,1)S(1)}, u32[]{:S(2)}, u32[]{:S(2)}) collective-permute-start(bf16[64,2304]{1,0:T(8,128)(2,1)S(1)} %get-tuple-element.61.x1), channel_id=1, source_target_pairs={{0,1},{1,0},{2,3},{3,2},{4,5},{5,4},{6,7},{7,6}} | collective-permute-start | bytes 884744 | tf_op jit(solution)/shard_map/ppermute | solution.py:356
  73.8 23.4 %collective-permute-start.13 = (bf16[64,2304]{1,0:T(8,128)(2,1)S(1)}, bf16[64,2304]{1,0:T(8,128)(2,1)S(1)}, u32[]{:S(2)}, u32[]{:S(2)}) collective-permute-start(bf16[64,2304]{1,0:T(8,128)(2,1)S(1)} %get-tuple-element.45.t0), channel_id=1, source_target_pairs={{0,1},{1,0},{2,3},{3,2},{4,5},{5,4},{6,7},{7,6}} | collective-permute-start | bytes 884744 | tf_op jit(solution)/shard_map/ppermute | solution.py:356
  81.1 16.1 %collective-permute-start.14 = (bf16[64,2304]{1,0:T(8,128)(2,1)S(1)}, bf16[64,2304]{1,0:T(8,128)(2,1)S(1)}, u32[]{:S(2)}, u32[]{:S(2)}) collective-permute-start(bf16[64,2304]{1,0:T(8,128)(2,1)S(1)} %get-tuple-element.53.t1), channel_id=1, source_target_pairs={{0,1},{1,0},{2,3},{3,2},{4,5},{5,4},{6,7},{7,6}} | collective-permute-start | bytes 884744 | tf_op jit(solution)/shard_map/ppermute | solution.py:356
  87.0 10.2 %collective-permute-start.10 = (bf16[64,2304]{1,0:T(8,128)(2,1)S(1)}, bf16[64,2304]{1,0:T(8,128)(2,1)S(1)}, u32[]{:S(2)}, u32[]{:S(2)}) collective-permute-start(bf16[64,2304]{1,0:T(8,128)(2,1)S(1)} %collective-permute-done.9.c0), channel_id=1, source_target_pairs={{0,1},{1,0},{2,3},{3,2},{4,5},{5,4},{6,7},{7,6}} | collective-permute-start | bytes 884744 | tf_op jit(solution)/shard_map/ppermute | solution.py:356
  87.0 10.2 %collective-permute-start.12 = (bf16[64,2304]{1,0:T(8,128)(2,1)S(1)}, bf16[64,2304]{1,0:T(8,128)(2,1)S(1)}, u32[]{:S(2)}, u32[]{:S(2)}) collective-permute-start(bf16[64,2304]{1,0:T(8,128)(2,1)S(1)} %collective-permute-done.11.c1), channel_id=1, source_target_pairs={{0,1},{1,0},{2,3},{3,2},{4,5},{5,4},{6,7},{7,6}} | collective-permute-start | bytes 884744 | tf_op jit(solution)/shard_map/ppermute | solution.py:356
  88.1 2.4 %slice-start.1 = ((s8[4718592]{0:T(1024)(128)(4,1)}), s8[524288]{0:T(1024)(128)(4,1)S(1)}, s32[]{:S(2)}) async-start(s8[4718592]{0:T(1024)(128)(4,1)} %bitcast), calls=%async_computation.1 | async-start | bytes 1048576
  88.1 2.4 %copy-start.3 = (bf16[2,256,1024]{2,1,0:T(8,128)(2,1)S(1)}, bf16[2,256,1024]{2,1,0:T(8,128)(2,1)}, u32[]{:S(2)}) copy-start(bf16[2,256,1024]{2,1,0:T(8,128)(2,1)} %du_ref.5) | copy-start | bytes 3145732
  93.5 3.7 %copy-start = (f32[2304,1024]{1,0:T(8,128)}, f32[2304,1024]{1,0:T(8,128)S(1)}, u32[]{:S(2)}) copy-start(f32[2304,1024]{1,0:T(8,128)S(1)} %get-tuple-element.62.dwp_ref) | copy-start | bytes 28311556

commit v12 on v11

--- a/solution.py
+++ b/solution.py
@@ -46,18 +46,19 @@
         q = r ^ j
         for m in range(k):
             dup[pl.ds(a * n + m * tl, tl), :] = dub[m, pl.ds(pl.multiple_of(q * tl, tl), tl), :]
-    copies = []
-    for i in range(nb):
-        cols = pl.ds(i * blk, blk)
+
+    def tile(i, c):
+        cols = pl.ds(pl.multiple_of(i * blk, blk), blk)
         pltpu.make_async_copy(w_ref.at[cols, :], wb.at[cols, :], wsem.at[i]).wait()
-        p = lax.dot_general(dup[...], wb[i * blk:(i + 1) * blk, :], (((1,), (1,)), ((), ())), preferred_element_type=F32)
-        ob[:, i * blk:(i + 1) * blk] = p.astype(BF16)
+        p = lax.dot_general(dup[...], wb[cols, :], (((1,), (1,)), ((), ())), preferred_element_type=F32)
+        ob[:, cols] = p.astype(BF16)
         for a in range(4):
-            c = pltpu.make_async_copy(ob.at[pl.ds(a * n, n), cols], outs[a].at[:, cols], osem)
-            c.start()
-            copies.append(c)
-    for c in copies:
-        c.wait()
+            pltpu.make_async_copy(ob.at[pl.ds(a * n, n), cols], outs[a].at[:, cols], osem).start()
+        return c
+
+    lax.fori_loop(0, nb, tile, 0)
+    for a in range(4):
+        pltpu.make_async_copy(ob.at[pl.ds(a * n, n), :], outs[a], osem).wait()
 
 
 FILL = ((0, 3), (3, 6), (6, 16))
@@ -191,15 +192,15 @@
 
 def dx_kernel(m, chip_rows, xh_ref, z_ref, p0, p1, p2, p3, dres_ref, g_ref, ids_ref, tok_ref, *refs):
     if m == 1:
-        x0_ref, dg0_ref, x_ref, dx_ref, slot_ref, dg_ref, xs_ref = refs
+        both0_ref, dg0_ref, both_ref, slot_ref, dg_ref, xs_ref = refs
     else:
-        x_ref, dx_ref, slot_ref, dg_ref = refs
-    tl = dx_ref.shape[0]
+        both_ref, slot_ref, dg_ref = refs
+    tl = slot_ref.shape[0]
     xh = xh_ref[...].astype(F32)
     x = xh + z_ref[...].astype(F32)
-    x_ref[...] = x.astype(BF16)
+    both_ref[0:tl, :] = x.astype(BF16)
     if m == 1:
-        xs_ref[0] = x0_ref[...]
+        xs_ref[0] = both0_ref[0:tl, :]
         xs_ref[1] = x.astype(BF16)
     g = g_ref[...].astype(F32)
     rs = lax.rsqrt(jnp.mean(x * x, axis=-1, keepdims=True) + EPS)
@@ -210,7 +211,7 @@
     mean = jnp.mean(nh * gdn, axis=-1, keepdims=True)
     dxn = rs * (gdn - nh * mean)
     dx = (dres_ref[m].astype(F32) + dxn).astype(BF16)
-    dx_ref[...] = dx
+    both_ref[tl:2 * tl, :] = dx
     own = chip_mask(ids_ref, m, lax.axis_index("tp"), tl, chip_rows)
     slot_ref[...] = jnp.where(own, xh, dx.astype(F32)).astype(BF16)
     dg = jnp.sum(dn * nh, axis=0, keepdims=True)
@@ -222,10 +223,15 @@
     return ((x * rs) * g_ref[...].astype(F32)).astype(BF16)
 
 
-def umat(n, w_ref, ub, u_ref, q0, q1, sem):
+def umat(n_ref, w_ref, ub, u_ref, q0, q1, sem):
     blk = 256
-    for i in range(ub.shape[1] // blk):
-        ub[:, i * blk:(i + 1) * blk] = jnp.dot(n, w_ref[:, i * blk:(i + 1) * blk], preferred_element_type=F32).astype(BF16)
+
+    def tile(i, c):
+        cols = pl.ds(pl.multiple_of(i * blk, blk), blk)
+        ub[:, cols] = jnp.dot(n_ref[...], w_ref[:, cols], preferred_element_type=F32).astype(BF16)
+        return c
+
+    lax.fori_loop(0, ub.shape[1] // blk, tile, 0)
     k = u_ref.shape[0]
     tl = u_ref.shape[1] // 4
     copies = []
@@ -244,19 +250,23 @@
 
 
 def dw_tile(n_ref, du2, i, blk):
-    return lax.dot_general(n_ref[:, i * blk:(i + 1) * blk], du2[...], (((0,), (0,)), ((), ())), preferred_element_type=F32)
+    return lax.dot_general(n_ref[:, pl.ds(pl.multiple_of(i * blk, blk), blk)], du2[...], (((0,), (0,)), ((), ())), preferred_element_type=F32)
 
 
 def u_kernel(x0, y0, x1, y1, g_ref, w_ref, du_ref, tok_ref, u_ref, dwp_ref, n_ref, du2, ub, usem):
     r = lax.axis_index("tp")
-    tl = x0.shape[0]
+    tl = x0.shape[0] // 2
     for a, x in enumerate((x0, y0, x1, y1)):
-        n_ref[a * tl:(a + 1) * tl, :] = norm(x[...].astype(F32), g_ref)
+        n_ref[a * tl:(a + 1) * tl, :] = norm(x[0:tl, :].astype(F32), g_ref)
     take_du(du_ref, du2, tl, ((0, r), (0, r ^ 1), (1, r), (1, r ^ 1)))
-    copies = umat(n_ref[...], w_ref, ub, u_ref, r, r ^ 1, usem)
+    copies = umat(n_ref, w_ref, ub, u_ref, r, r ^ 1, usem)
     blk = 256
-    for i in range(dwp_ref.shape[0] // blk):
-        dwp_ref[i * blk:(i + 1) * blk, :] = dw_tile(n_ref, du2, i, blk)
+
+    def tile(i, c):
+        dwp_ref[pl.ds(pl.multiple_of(i * blk, blk), blk), :] = dw_tile(n_ref, du2, i, blk)
+        return c
+
+    lax.fori_loop(0, dwp_ref.shape[0] // blk, tile, 0)
     for c in copies:
         c.wait()
 
@@ -297,9 +307,9 @@
 
 
 def near_kernel(list_ref, d0, a0, d1, a1, tok_ref, de_in, xn_ref, de_ref, sem):
-    tl = d0.shape[0]
+    tl = d0.shape[0] // 2
     for a, ref in enumerate((d0, a0, d1, a1)):
-        xn_ref[a * tl:(a + 1) * tl, :] = ref[...].astype(F32)
+        xn_ref[a * tl:(a + 1) * tl, :] = ref[tl:2 * tl, :].astype(F32)
     scatter(True, list_ref, xn_ref, de_ref, sem)
     scatter_wait(True, list_ref, xn_ref, de_ref, sem)
 
@@ -323,14 +333,17 @@
         x = jnp.where(chip_mask(ids_ref, m, q, tl, chip_rows), own[...].astype(F32), got[...].astype(F32))
         n_ref[a * tl:(a + 1) * tl, :] = norm(x, g_ref)
     blk = 256
-    copies = []
-    for i in range(d // blk):
-        dwb[i] = dwp_ref[i * blk:(i + 1) * blk, :] + dw_tile(n_ref, du2, i, blk)
-        c = pltpu.make_async_copy(dwb.at[i], dw_ref.at[pl.ds(i * blk, blk), :], wsem)
-        c.start()
-        copies.append(c)
-    copies += umat(n_ref[...], w_ref, ub, u_ref, r ^ 2, r ^ 3, usem)
+
+    def tile(i, c):
+        rows = pl.ds(pl.multiple_of(i * blk, blk), blk)
+        dwb[rows, :] = dwp_ref[rows, :] + dw_tile(n_ref, du2, i, blk)
+        pltpu.make_async_copy(dwb.at[rows, :], dw_ref.at[rows, :], wsem).start()
+        return c
+
+    lax.fori_loop(0, d // blk, tile, 0)
+    copies = umat(n_ref, w_ref, ub, u_ref, r ^ 2, r ^ 3, usem)
     scatter_wait(False, list_ref, xf, de_ref, sem)
+    pltpu.make_async_copy(dwb, dw_ref, wsem).wait()
     for c in copies:
         c.wait()
 
@@ -383,36 +396,34 @@
             6_000_000_000, 2 * vl * d, {1: 1})(owned, de)
 
         def dxk(m, xh, z, tok, more):
-            outs = [S((tl, d), BF16)] * 3 + [S((1, d), F32)] + ([S((k, tl, d), BF16)] if m else [])
+            outs = [S((n, d), BF16), S((tl, d), BF16), S((1, d), F32)] + ([S((k, tl, d), BF16)] if m else [])
             return call(functools.partial(dx_kernel, m, 2 * vl), 16, outs,
                         [VMEM] * 9 + [SMEM if m else HBM] + [VMEM] * len(more),
                         [VMEM] * len(outs), [], 30 * n * d, 16 * n * d)(
                             xh, z, p0, q1, q2, q3, dres, g2, ids, tok, *more)
 
-        x0, dx0, slot0, dg0 = dxk(0, own0, z0, de, ())
+        mine0, slot0, dg0 = dxk(0, own0, z0, de, ())
         c0 = perm(slot0, cross)
-        x1, dx1, slot1, dg, x = dxk(1, own1, z1, lists, (x0, dg0))
+        next0 = perm(mine0, sib)
+        mine1, slot1, dg, x = dxk(1, own1, z1, lists, (mine0, dg0))
         c1 = perm(slot1, cross)
-        xo0 = perm(x0, sib)
-        xo1 = perm(x1, sib)
-        a0 = perm(dx0, sib)
-        a1 = perm(dx1, sib)
+        next1 = perm(mine1, sib)
         u, dwp = call(
             u_kernel, 32, [S((k, t, fc), BF16), S((d, fc), F32)], [VMEM] * 8, [HBM, VMEM],
             [pltpu.VMEM((t, d), BF16), pltpu.VMEM((t, fc), BF16), pltpu.VMEM((t, fc), BF16), D],
-            4 * t * d * fc, 2 * d * fc)(x0, xo0, x1, xo1, g2, w, du, dg)
-        xn, de = call(near_kernel, 12, [S((t, d), F32), S((vl, d), F32)], [SMEM] + [VMEM] * 5 + [HBM], [VMEM, HBM],
-                      [D], 8 * h * d, 8 * h * d, {6: 1})(lists, dx0, a0, dx1, a1, dg, de)
+            4 * t * d * fc, 2 * d * fc)(mine0, next0, mine1, next1, g2, w, du, dg)
+        xn, de = call(near_kernel, 8, [S((t, d), F32), S((vl, d), F32)], [SMEM] + [VMEM] * 5 + [HBM], [VMEM, HBM],
+                      [D], 8 * h * d, 8 * h * d, {6: 1})(lists, mine0, next0, mine1, next1, dg, de)
         b0 = perm(c0, sib)
         b1 = perm(c1, sib)
         dgs = dg + perm(dg, sib)
         dgs = dgs + perm(dgs, cross)
 
         u, dw, de = call(
-            functools.partial(last_kernel, 2 * vl), 36, [S((k, t, fc), BF16), S((d, fc), F32), S((vl, d), F32)],
+            functools.partial(last_kernel, 2 * vl), 20, [S((k, t, fc), BF16), S((d, fc), F32), S((vl, d), F32)],
             [SMEM] + [VMEM] * 14 + [HBM] * 2, [HBM] * 3,
             [pltpu.VMEM((2 * h, d), F32), pltpu.VMEM((t, d), BF16), pltpu.VMEM((t, fc), BF16), pltpu.VMEM((t, fc), BF16),
-             pltpu.VMEM((d // 256, 256, fc), F32), D, D, D],
+             pltpu.VMEM((d, fc), F32), D, D, D],
             4 * t * d * fc, 6 * d * fc, {15: 0, 16: 2})(
                 lists, xn, c0, b0, c1, b1, oth0, w0, oth1, w1, dwp, ids, g2, w, du, u, de)
         return u, x, de, dw, dgs.reshape(d)

time: 108 us -> 101 us (0.935)
  local copies, waits for them, and re-layouts: 4.37 us -> 0.71 us
  waiting for transfers between devices: 34.1 us -> 31.9 us
    unnamed x18 -> x16, local copies, waits for them, and re-layouts: 4.36 us -> 0.7 us
    pallas_call x1, Pallas kernels: 2.92 us -> 5.59 us  [local(): call(u_kernel, 32, [S((k, t, fc), BF16), S((d, fc), F32)], [VMEM] * 8, [H...]
    ppermute x19 -> x17, waiting for transfers between devices: 34.1 us -> 31.9 us  [perm(): return lax.ppermute(v, 'tp', p)]
    pallas_call x1, Pallas kernels: 9.64 us -> 7.68 us  [local(): call(pdn_kernel, 60, [S((n, d), BF16)] * 4, [HBM] * 2, [HBM] * 4, [pltpu....]
    pallas_call x2, Pallas kernels: 12.3 us -> 10.8 us  [the longest x1 8.44 us: local(): call(functools.partial(last_kernel, 2 * vl), 20, [S((k, t, fc), BF16), S(...]
    ppermute x19 -> x17, starting transfers between devices: 9.94 us -> 9.91 us  [perm(): return lax.ppermute(v, 'tp', p)]
  transfers between devices with their start and end apart: 19 -> 17, of which waited for: 6 -> 5; matrix products, arithmetic and copies ran while one was open for 1% -> 1% of each run, Pallas kernels for 32% -> 35%
where the time goes in v12:
time: 101 us; the launch traced here: 100 us
  Pallas kernels  56.4 us (56%)
  waiting for transfers between devices  31.9 us (32%)
  starting transfers between devices  9.91 us (10%)
    ppermute x17, waiting for transfers between devices, perm(): return lax.ppermute(v, 'tp', p)  31.9 us
    pallas_call x1, Pallas kernels, local(): call(zero_kernel, 8, [S((4, 2 * h + 16), jnp.int32), S((vl, d), F32)], [S...  16.6 us
    pallas_call x1, Pallas kernels, local(): call(gather_kernel, 36, [S((n, d), BF16)] * 4 + [S((2, 2 * h + 16), jnp.i...  12.7 us
    ppermute x17, starting transfers between devices, perm(): return lax.ppermute(v, 'tp', p)  9.91 us
    pallas_call x1, Pallas kernels, local(): call(functools.partial(last_kernel, 2 * vl), 20, [S((k, t, fc), BF16), S(...  8.44 us
    pallas_call x1, Pallas kernels, local(): call(pdn_kernel, 60, [S((n, d), BF16)] * 4, [HBM] * 2, [HBM] * 4, [pltpu....  7.68 us
    pallas_call x1, Pallas kernels, local(): call(u_kernel, 32, [S((k, t, fc), BF16), S((d, fc), F32)], [VMEM] * 8, [H...  5.59 us
    pallas_call x2, Pallas kernels, dxk(): call(functools.partial(dx_kernel, m, 2 * vl), 16, outs, [VMEM] * 9 + [SME...  2.92 us
  transfers between devices with their start and end apart: 17, of which 5 were waited for; matrix products, arithmetic and copies ran while one was open for 1% of the time, Pallas kernels for 35%

profile of v12, /device:TPU:0, one launch (start us, length us, event | category | flops | bytes accessed | tf_op | source)
XLA Modules:
  0.0 100.5 jit_solution(14098538120922232210)
XLA Ops:
  0.6 0.0 copy-start.3
  0.6 0.7 copy-done.3
  1.3 12.7 %shard_map.101 = (bf16[128,2304]{1,0:T(8,128)(2,1)S(1)}, bf16[128,2304]{1,0:T(8,128)(2,1)S(1)}, bf16[128,2304]{1,0:T(8,128)(2,1)S(1)}, bf16[128,2304]{1,0:T(8,12...) custom-call(s32[2,256]{1,0:T(2,128)S(1)} %copy-done.3, bf16[8192,2304]{1,0:T(8,128)(2,1)} %emb_ref.1), custom_call_target="tpu_custom_call" | custom-call | flops 500000000 | bytes 9437184 | tf_op jit(solution)/shard_map/pallas_call | solution.py:377
  14.1 0.5 collective-permute-start
  14.6 0.0 collective-permute-start.1
  14.6 7.7 %shard_map.104 = (bf16[128,2304]{1,0:T(8,128)(2,1)}, bf16[128,2304]{1,0:T(8,128)(2,1)}, bf16[128,2304]{1,0:T(8,128)(2,1)}, bf16[128,2304]{1,0:T(8,128)(2,1)}) custom-call(bf16[2,256,1024]{2,1,0:T(8,128)(2,1)} %du_ref.5, bf16[2304,1024]{1,0:T(8,128)(2,1)} %w_ref.5), custom_call_target="tpu_custom_call" | custom-call | flops 2415919104 | bytes 8126464 | tf_op jit(solution)/shard_map/pallas_call | solution.py:371
  22.3 0.5 collective-permute-start.3
  22.8 1.9 %collective-permute-start.4 = (bf16[128,2304]{1,0:T(8,128)(2,1)}, bf16[128,2304]{1,0:T(8,128)(2,1)S(1)}, u32[]{:S(2)}, u32[]{:S(2)}) collective-permute-start(bf16[128,2304]{1,0:T(8,128)(2,1)} %get-tuple-element.46), channel_id=1, source_target_pairs={{0,2},{1,3},{2,0},{3,1},{4,6},{5,7},{6,4},{7,5}} | collective-permute-start | bytes 1769480 | tf_op jit(solution)/shard_map/ppermute | solution.py:369
  24.7 0.1 collective-permute-start.5
  24.8 0.0 collective-permute-done.y0
  24.8 0.0 collective-permute-done.1.y1
  24.8 0.1 shard_map.103
  24.9 1.8 %collective-permute-start.2 = (bf16[64,2304]{1,0:T(8,128)(2,1)S(1)}, bf16[64,2304]{1,0:T(8,128)(2,1)S(1)}, u32[]{:S(2)}, u32[]{:S(2)}) collective-permute-start(bf16[64,2304]{1,0:T(8,128)(2,1)S(1)} %get-tuple-element.43.t0), channel_id=1, source_target_pairs={{0,2},{1,3},{2,0},{3,1},{4,6},{5,7},{6,4},{7,5}} | collective-permute-start | bytes 884744 | tf_op jit(solution)/shard_map/ppermute | solution.py:369
  26.7 0.3 collective-permute-start.7
  26.9 0.0 copy-start.5
  27.0 0.0 copy-start
  27.0 0.0 copy-start.1
  27.0 0.0 copy-start.4
  27.0 16.6 %shard_map.102 = (s32[4,528]{1,0:T(4,128)S(1)}, f32[8192,2304]{1,0:T(8,128)}) custom-call(s32[2,528]{1,0:T(2,128)S(1)} %get-tuple-element.35.own_ref, f32[8192,2304]{1,0:T(8,128)} %get-tuple-element.36.de_in), custom_call_target="tpu_custom_call", output_to_operand_aliasing={{1}: (1, {})} | custom-call | flops 6000000000 | bytes 37748736 | tf_op jit(solution)/shard_map/pallas_call | solution.py:393
  43.5 0.0 copy-done.5
  43.5 0.0 collective-permute-done.3.p1
  43.6 0.0 collective-permute-done.4.p2
  43.6 7.8 %collective-permute-done.5.p3 = bf16[128,2304]{1,0:T(8,128)(2,1)S(1)} collective-permute-done((bf16[128,2304]{1,0:T(8,128)(2,1)}, bf16[128,2304]{1,0:T(8,128)(2,1)S(1)}, u32[]{:S(2)}, u32[]{:S(2)}) %collective-permute-start.5) | collective-permute-done | bytes 589856 | tf_op jit(solution)/shard_map/ppermute | solution.py:369
  51.4 6.8 %collective-permute-done.2.z_ref = bf16[64,2304]{1,0:T(8,128)(2,1)S(1)} collective-permute-done((bf16[64,2304]{1,0:T(8,128)(2,1)S(1)}, bf16[64,2304]{1,0:T(8,128)(2,1)S(1)}, u32[]{:S(2)}, u32[]{:S(2)}) %collective-permute-start.2) | collective-permute-done | bytes 294944 | tf_op jit(solution)/shard_map/ppermute | solution.py:369
  58.2 0.0 copy-done
  58.2 0.0 copy-done.1
  58.2 0.0 copy-done.4
  58.2 0.8 shard_map.105
  58.9 0.0 collective-permute-start.6
  59.0 5.2 %collective-permute-done.7.z_ref = bf16[64,2304]{1,0:T(8,128)(2,1)S(1)} collective-permute-done((bf16[64,2304]{1,0:T(8,128)(2,1)S(1)}, bf16[64,2304]{1,0:T(8,128)(2,1)S(1)}, u32[]{:S(2)}, u32[]{:S(2)}) %collective-permute-start.7) | collective-permute-done | bytes 294944 | tf_op jit(solution)/shard_map/ppermute | solution.py:369
  64.1 2.2 %shard_map.106 = (bf16[128,2304]{1,0:T(8,128)(2,1)S(1)}, bf16[64,2304]{1,0:T(8,128)(2,1)S(1)}, f32[1,2304]{1,0:T(1,128)S(1)}, bf16[2,64,2304]{2,1,0:T(8,128)(2,1)}) custom-call(bf16[64,2304]{1,0:T(8,128)(2,1)S(1)} %get-tuple-element.50.xh_ref, bf16[64,2304]{1,0:T(8,128)(2,1)S(1)} %collective-permute-done.7.z_ref, bf16[128,2304]{1,0:T(8,128)(2,1)S(1)} %copy-done.1, ...), custom_call_target="tpu_custom_call" | custom-call | flops 8847360 | bytes 4718592 | tf_op jit(solution)/shard_map/pallas_call | solution.py:400
  66.3 0.0 collective-permute-start.8
  66.3 1.7 %collective-permute-start.9 = (bf16[64,2304]{1,0:T(8,128)(2,1)S(1)}, bf16[64,2304]{1,0:T(8,128)(2,1)S(1)}, u32[]{:S(2)}, u32[]{:S(2)}) collective-permute-start(bf16[64,2304]{1,0:T(8,128)(2,1)S(1)} %get-tuple-element.56), channel_id=1, source_target_pairs={{0,2},{1,3},{2,0},{3,1},{4,6},{5,7},{6,4},{7,5}} | collective-permute-start | bytes 884744 | tf_op jit(solution)/shard_map/ppermute | solution.py:369
  68.1 0.3 collective-permute-start.11
  68.3 0.0 collective-permute-start.15
  68.3 1.2 %collective-permute-done.15 = f32[1,2304]{1,0:T(1,128)S(1)} collective-permute-done((f32[1,2304]{1,0:T(1,128)S(1)}, f32[1,2304]{1,0:T(1,128)S(1)}, u32[]{:S(2)}, u32[]{:S(2)}) %collective-permute-start.15) | collective-permute-done | bytes 9248 | tf_op jit(solution)/shard_map/ppermute | solution.py:369
  69.5 1.8 %collective-permute-start.16 = (f32[1,2304]{1,0:T(1,128)S(1)}, f32[1,2304]{1,0:T(1,128)S(1)}, u32[]{:S(2)}, u32[]{:S(2)}) collective-permute-start(f32[1,2304]{1,0:T(1,128)S(1)} %add.6), channel_id=1, source_target_pairs={{0,2},{1,3},{2,0},{3,1},{4,6},{5,7},{6,4},{7,5}} | collective-permute-start | bytes 27656 | tf_op jit(solution)/shard_map/ppermute | solution.py:369
  71.3 11.0 %collective-permute-done.16 = f32[1,2304]{1,0:T(1,128)S(1)} collective-permute-done((f32[1,2304]{1,0:T(1,128)S(1)}, f32[1,2304]{1,0:T(1,128)S(1)}, u32[]{:S(2)}, u32[]{:S(2)}) %collective-permute-start.16) | collective-permute-done | bytes 9248 | tf_op jit(solution)/shard_map/ppermute | solution.py:369
  82.2 0.0 collective-permute-start.13
  82.3 0.0 collective-permute-done.9.c0
  82.3 0.5 collective-permute-start.14
  82.8 0.0 collective-permute-done.11.c1
  82.8 0.0 collective-permute-start.10
  82.8 0.0 collective-permute-done.6.a0.y0
  82.8 0.5 collective-permute-start.12
  83.3 0.0 slice-start
  83.3 0.6 add_reduce_fusion
  83.9 0.0 slice-start.1
  83.9 0.0 copy-start.2
  83.9 0.0 collective-permute-done.8.a1.y1
  83.9 2.4 %shard_map.107 = (f32[256,2304]{1,0:T(8,128)S(1)}, f32[8192,2304]{1,0:T(8,128)}) custom-call(s32[4,528]{1,0:T(4,128)S(1)} %get-tuple-element.37.tok_ref.list_ref, bf16[128,2304]{1,0:T(8,128)(2,1)S(1)} %get-tuple-element.49.refs_0_.d0.x0, bf16[128,2304]{1,0:T(8,128)(2,1)S(1)} %collective-permute-done.6.a0.y0, ...), custom_call_target="tpu_custom_call", output_to_operand_aliasing={{1}: (6, {})} | custom-call | flops 4718592 | bytes 4718592 | tf_op jit(solution)/shard_map/pallas_call | solution.py:415
  86.3 0.0 slice-done
  86.3 0.0 slice-done.1
  86.4 0.0 copy-done.2
  86.4 5.6 %shard_map.108 = (bf16[2,256,1024]{2,1,0:T(8,128)(2,1)}, f32[2304,1024]{1,0:T(8,128)S(1)}) custom-call(bf16[128,2304]{1,0:T(8,128)(2,1)S(1)} %get-tuple-element.49.refs_0_.d0.x0, bf16[128,2304]{1,0:T(8,128)(2,1)S(1)} %collective-permute-done.6.a0.y0, bf16[128,2304]{1,0:T(8,128)(2,1)S(1)} %get-tuple-element.53.d1.x1, ...), custom_call_target="tpu_custom_call" | custom-call | flops 2415919104 | bytes 4718592 | tf_op jit(solution)/shard_map/pallas_call | solution.py:411
  92.0 0.0 collective-permute-done.13.w0
  92.0 0.0 collective-permute-done.14.w1
  92.0 0.0 collective-permute-done.10.b0
  92.0 0.0 collective-permute-done.12.b1
  92.0 8.4 %shard_map.109 = (bf16[2,256,1024]{2,1,0:T(8,128)(2,1)}, f32[2304,1024]{1,0:T(8,128)}, f32[8192,2304]{1,0:T(8,128)}) custom-call(s32[4,528]{1,0:T(4,128)S(1)} %get-tuple-element.37.tok_ref.list_ref, f32[256,2304]{1,0:T(8,128)S(1)} %get-tuple-element.55.xn_ref, ...), custom_call_target="tpu_custom_call", output_to_operand_aliasing={{0}: (15, {}), {2}: (16, {})} | custom-call | flops 2415919104 | bytes 14155776 | tf_op jit(solution)/shard_map/pallas_call | solution.py:422
  (3 shorter events, 0.0 us)
Async XLA Ops:
  0.6 0.7 copy-start.3
  14.1 10.7 %collective-permute-start = (bf16[128,2304]{1,0:T(8,128)(2,1)S(1)}, bf16[128,2304]{1,0:T(8,128)(2,1)S(1)}, u32[]{:S(2)}, u32[]{:S(2)}) collective-permute-start(bf16[128,2304]{1,0:T(8,128)(2,1)S(1)} %get-tuple-element.39), channel_id=1, source_target_pairs={{0,1},{1,0},{2,3},{3,2},{4,5},{5,4},{6,7},{7,6}} | collective-permute-start | bytes 1769480 | tf_op jit(solution)/shard_map/ppermute | solution.py:369
  14.6 10.2 %collective-permute-start.1 = (bf16[128,2304]{1,0:T(8,128)(2,1)S(1)}, bf16[128,2304]{1,0:T(8,128)(2,1)S(1)}, u32[]{:S(2)}, u32[]{:S(2)}) collective-permute-start(bf16[128,2304]{1,0:T(8,128)(2,1)S(1)} %get-tuple-element.41), channel_id=1, source_target_pairs={{0,1},{1,0},{2,3},{3,2},{4,5},{5,4},{6,7},{7,6}} | collective-permute-start | bytes 1769480 | tf_op jit(solution)/shard_map/ppermute | solution.py:369
  22.3 21.3 %collective-permute-start.3 = (bf16[128,2304]{1,0:T(8,128)(2,1)}, bf16[128,2304]{1,0:T(8,128)(2,1)S(1)}, u32[]{:S(2)}, u32[]{:S(2)}) collective-permute-start(bf16[128,2304]{1,0:T(8,128)(2,1)} %get-tuple-element.45), channel_id=1, source_target_pairs={{0,1},{1,0},{2,3},{3,2},{4,5},{5,4},{6,7},{7,6}} | collective-permute-start | bytes 1769480 | tf_op jit(solution)/shard_map/ppermute | solution.py:369
  22.8 20.8 %collective-permute-start.4 = (bf16[128,2304]{1,0:T(8,128)(2,1)}, bf16[128,2304]{1,0:T(8,128)(2,1)S(1)}, u32[]{:S(2)}, u32[]{:S(2)}) collective-permute-start(bf16[128,2304]{1,0:T(8,128)(2,1)} %get-tuple-element.46), channel_id=1, source_target_pairs={{0,2},{1,3},{2,0},{3,1},{4,6},{5,7},{6,4},{7,5}} | collective-permute-start | bytes 1769480 | tf_op jit(solution)/shard_map/ppermute | solution.py:369
  24.7 26.7 %collective-permute-start.5 = (bf16[128,2304]{1,0:T(8,128)(2,1)}, bf16[128,2304]{1,0:T(8,128)(2,1)S(1)}, u32[]{:S(2)}, u32[]{:S(2)}) collective-permute-start(bf16[128,2304]{1,0:T(8,128)(2,1)} %get-tuple-element.47), channel_id=1, source_target_pairs={{0,3},{1,2},{2,1},{3,0},{4,7},{5,6},{6,5},{7,4}} | collective-permute-start | bytes 1769480 | tf_op jit(solution)/shard_map/ppermute | solution.py:369
  24.9 33.2 %collective-permute-start.2 = (bf16[64,2304]{1,0:T(8,128)(2,1)S(1)}, bf16[64,2304]{1,0:T(8,128)(2,1)S(1)}, u32[]{:S(2)}, u32[]{:S(2)}) collective-permute-start(bf16[64,2304]{1,0:T(8,128)(2,1)S(1)} %get-tuple-element.43.t0), channel_id=1, source_target_pairs={{0,2},{1,3},{2,0},{3,1},{4,6},{5,7},{6,4},{7,5}} | collective-permute-start | bytes 884744 | tf_op jit(solution)/shard_map/ppermute | solution.py:369
  26.7 37.5 %collective-permute-start.7 = (bf16[64,2304]{1,0:T(8,128)(2,1)S(1)}, bf16[64,2304]{1,0:T(8,128)(2,1)S(1)}, u32[]{:S(2)}, u32[]{:S(2)}) collective-permute-start(bf16[64,2304]{1,0:T(8,128)(2,1)S(1)} %get-tuple-element.51.t1), channel_id=1, source_target_pairs={{0,2},{1,3},{2,0},{3,1},{4,6},{5,7},{6,4},{7,5}} | collective-permute-start | bytes 884744 | tf_op jit(solution)/shard_map/ppermute | solution.py:369
  26.9 16.6 %copy-start.5 = (bf16[2304]{0:T(1024)(128)(2,1)S(1)}, bf16[2304]{0:T(1024)(128)(2,1)}, u32[]{:S(2)}) copy-start(bf16[2304]{0:T(1024)(128)(2,1)} %param.8) | copy-start | bytes 13828
  27.0 31.2 %copy-start = (bf16[2,64,2304]{2,1,0:T(8,128)(2,1)S(1)}, bf16[2,64,2304]{2,1,0:T(8,128)(2,1)}, u32[]{:S(2)}) copy-start(bf16[2,64,2304]{2,1,0:T(8,128)(2,1)} %dres_ref.3) | copy-start | bytes 1769476
  27.0 31.2 %copy-start.1 = (bf16[128,2304]{1,0:T(8,128)(2,1)S(1)}, bf16[128,2304]{1,0:T(8,128)(2,1)}, u32[]{:S(2)}) copy-start(bf16[128,2304]{1,0:T(8,128)(2,1)} %get-tuple-element.44.p0) | copy-start | bytes 1769476
  27.0 31.2 %copy-start.4 = (s32[2,256]{1,0:T(2,128)S(1)}, s32[2,256]{1,0:T(2,128)}, u32[]{:S(2)}) copy-start(s32[2,256]{1,0:T(2,128)} %ids_ref.7) | copy-start | bytes 6148
  58.9 23.9 %collective-permute-start.6 = (bf16[128,2304]{1,0:T(8,128)(2,1)S(1)}, bf16[128,2304]{1,0:T(8,128)(2,1)S(1)}, u32[]{:S(2)}, u32[]{:S(2)}) collective-permute-start(bf16[128,2304]{1,0:T(8,128)(2,1)S(1)} %get-tuple-element.49.refs_0_.d0.x0), channel_id=1, source_target_pairs={{0,1},{1,0},{2,3},{3,2},{4,5},{5,4},{6,7},{7,6}} | collective-permute-start | bytes 1769480 | tf_op jit(solution)/shard_map/ppermute | solution.py:369
  66.3 17.6 %collective-permute-start.8 = (bf16[128,2304]{1,0:T(8,128)(2,1)S(1)}, bf16[128,2304]{1,0:T(8,128)(2,1)S(1)}, u32[]{:S(2)}, u32[]{:S(2)}) collective-permute-start(bf16[128,2304]{1,0:T(8,128)(2,1)S(1)} %get-tuple-element.53.d1.x1), channel_id=1, source_target_pairs={{0,1},{1,0},{2,3},{3,2},{4,5},{5,4},{6,7},{7,6}} | collective-permute-start | bytes 1769480 | tf_op jit(solution)/shard_map/ppermute | solution.py:369
  66.3 15.9 %collective-permute-start.9 = (bf16[64,2304]{1,0:T(8,128)(2,1)S(1)}, bf16[64,2304]{1,0:T(8,128)(2,1)S(1)}, u32[]{:S(2)}, u32[]{:S(2)}) collective-permute-start(bf16[64,2304]{1,0:T(8,128)(2,1)S(1)} %get-tuple-element.56), channel_id=1, source_target_pairs={{0,2},{1,3},{2,0},{3,1},{4,6},{5,7},{6,4},{7,5}} | collective-permute-start | bytes 884744 | tf_op jit(solution)/shard_map/ppermute | solution.py:369
  68.1 14.7 %collective-permute-start.11 = (bf16[64,2304]{1,0:T(8,128)(2,1)S(1)}, bf16[64,2304]{1,0:T(8,128)(2,1)S(1)}, u32[]{:S(2)}, u32[]{:S(2)}) collective-permute-start(bf16[64,2304]{1,0:T(8,128)(2,1)S(1)} %get-tuple-element.57), channel_id=1, source_target_pairs={{0,2},{1,3},{2,0},{3,1},{4,6},{5,7},{6,4},{7,5}} | collective-permute-start | bytes 884744 | tf_op jit(solution)/shard_map/ppermute | solution.py:369
  68.3 1.2 %collective-permute-start.15 = (f32[1,2304]{1,0:T(1,128)S(1)}, f32[1,2304]{1,0:T(1,128)S(1)}, u32[]{:S(2)}, u32[]{:S(2)}) collective-permute-start(f32[1,2304]{1,0:T(1,128)S(1)} %get-tuple-element.54.tok_ref), channel_id=1, source_target_pairs={{0,1},{1,0},{2,3},{3,2},{4,5},{5,4},{6,7},{7,6}} | collective-permute-start | bytes 27656 | tf_op jit(solution)/shard_map/ppermute | solution.py:369
  69.5 12.7 %collective-permute-start.16 = (f32[1,2304]{1,0:T(1,128)S(1)}, f32[1,2304]{1,0:T(1,128)S(1)}, u32[]{:S(2)}, u32[]{:S(2)}) collective-permute-start(f32[1,2304]{1,0:T(1,128)S(1)} %add.6), channel_id=1, source_target_pairs={{0,2},{1,3},{2,0},{3,1},{4,6},{5,7},{6,4},{7,5}} | collective-permute-start | bytes 27656 | tf_op jit(solution)/shard_map/ppermute | solution.py:369
  82.2 9.7 %collective-permute-start.13 = (bf16[64,2304]{1,0:T(8,128)(2,1)S(1)}, bf16[64,2304]{1,0:T(8,128)(2,1)S(1)}, u32[]{:S(2)}, u32[]{:S(2)}) collective-permute-start(bf16[64,2304]{1,0:T(8,128)(2,1)S(1)} %get-tuple-element.43.t0), channel_id=1, source_target_pairs={{0,1},{1,0},{2,3},{3,2},{4,5},{5,4},{6,7},{7,6}} | collective-permute-start | bytes 884744 | tf_op jit(solution)/shard_map/ppermute | solution.py:369
  82.3 9.7 %collective-permute-start.14 = (bf16[64,2304]{1,0:T(8,128)(2,1)S(1)}, bf16[64,2304]{1,0:T(8,128)(2,1)S(1)}, u32[]{:S(2)}, u32[]{:S(2)}) collective-permute-start(bf16[64,2304]{1,0:T(8,128)(2,1)S(1)} %get-tuple-element.51.t1), channel_id=1, source_target_pairs={{0,1},{1,0},{2,3},{3,2},{4,5},{5,4},{6,7},{7,6}} | collective-permute-start | bytes 884744 | tf_op jit(solution)/shard_map/ppermute | solution.py:369
  82.8 9.2 %collective-permute-start.10 = (bf16[64,2304]{1,0:T(8,128)(2,1)S(1)}, bf16[64,2304]{1,0:T(8,128)(2,1)S(1)}, u32[]{:S(2)}, u32[]{:S(2)}) collective-permute-start(bf16[64,2304]{1,0:T(8,128)(2,1)S(1)} %collective-permute-done.9.c0), channel_id=1, source_target_pairs={{0,1},{1,0},{2,3},{3,2},{4,5},{5,4},{6,7},{7,6}} | collective-permute-start | bytes 884744 | tf_op jit(solution)/shard_map/ppermute | solution.py:369
  82.8 9.2 %collective-permute-start.12 = (bf16[64,2304]{1,0:T(8,128)(2,1)S(1)}, bf16[64,2304]{1,0:T(8,128)(2,1)S(1)}, u32[]{:S(2)}, u32[]{:S(2)}) collective-permute-start(bf16[64,2304]{1,0:T(8,128)(2,1)S(1)} %collective-permute-done.11.c1), channel_id=1, source_target_pairs={{0,1},{1,0},{2,3},{3,2},{4,5},{5,4},{6,7},{7,6}} | collective-permute-start | bytes 884744 | tf_op jit(solution)/shard_map/ppermute | solution.py:369
  83.3 3.1 %slice-start = ((s8[4718592]{0:T(1024)(128)(4,1)}), s8[4194304]{0:T(1024)(128)(4,1)S(1)}, s32[]{:S(2)}) async-start(s8[4718592]{0:T(1024)(128)(4,1)} %bitcast), calls=%async_computation | async-start | bytes 8388608
  83.9 2.4 %slice-start.1 = ((s8[4718592]{0:T(1024)(128)(4,1)}), s8[524288]{0:T(1024)(128)(4,1)S(1)}, s32[]{:S(2)}) async-start(s8[4718592]{0:T(1024)(128)(4,1)} %bitcast), calls=%async_computation.1 | async-start | bytes 1048576
  83.9 2.4 %copy-start.2 = (bf16[2,256,1024]{2,1,0:T(8,128)(2,1)S(1)}, bf16[2,256,1024]{2,1,0:T(8,128)(2,1)}, u32[]{:S(2)}) copy-start(bf16[2,256,1024]{2,1,0:T(8,128)(2,1)} %du_ref.5) | copy-start | bytes 3145732

commit v13 on v12

--- a/solution.py
+++ b/solution.py
@@ -225,13 +225,9 @@
 
 def umat(n_ref, w_ref, ub, u_ref, q0, q1, sem):
     blk = 256
-
-    def tile(i, c):
-        cols = pl.ds(pl.multiple_of(i * blk, blk), blk)
-        ub[:, cols] = jnp.dot(n_ref[...], w_ref[:, cols], preferred_element_type=F32).astype(BF16)
-        return c
-
-    lax.fori_loop(0, ub.shape[1] // blk, tile, 0)
+    for i in range(ub.shape[1] // blk):
+        ub[:, i * blk:(i + 1) * blk] = jnp.dot(
+            n_ref[...], w_ref[:, i * blk:(i + 1) * blk], preferred_element_type=F32).astype(BF16)
     k = u_ref.shape[0]
     tl = u_ref.shape[1] // 4
     copies = []
@@ -250,7 +246,7 @@
 
 
 def dw_tile(n_ref, du2, i, blk):
-    return lax.dot_general(n_ref[:, pl.ds(pl.multiple_of(i * blk, blk), blk)], du2[...], (((0,), (0,)), ((), ())), preferred_element_type=F32)
+    return lax.dot_general(n_ref[:, i * blk:(i + 1) * blk], du2[...], (((0,), (0,)), ((), ())), preferred_element_type=F32)
 
 
 def u_kernel(x0, y0, x1, y1, g_ref, w_ref, du_ref, tok_ref, u_ref, dwp_ref, n_ref, du2, ub, usem):
@@ -261,12 +257,8 @@
     take_du(du_ref, du2, tl, ((0, r), (0, r ^ 1), (1, r), (1, r ^ 1)))
     copies = umat(n_ref, w_ref, ub, u_ref, r, r ^ 1, usem)
     blk = 256
-
-    def tile(i, c):
-        dwp_ref[pl.ds(pl.multiple_of(i * blk, blk), blk), :] = dw_tile(n_ref, du2, i, blk)
-        return c
-
-    lax.fori_loop(0, dwp_ref.shape[0] // blk, tile, 0)
+    for i in range(dwp_ref.shape[0] // blk):
+        dwp_ref[i * blk:(i + 1) * blk, :] = dw_tile(n_ref, du2, i, blk)
     for c in copies:
         c.wait()
 
@@ -333,14 +325,10 @@
         x = jnp.where(chip_mask(ids_ref, m, q, tl, chip_rows), own[...].astype(F32), got[...].astype(F32))
         n_ref[a * tl:(a + 1) * tl, :] = norm(x, g_ref)
     blk = 256
-
-    def tile(i, c):
-        rows = pl.ds(pl.multiple_of(i * blk, blk), blk)
+    for i in range(d // blk):
+        rows = slice(i * blk, (i + 1) * blk)
         dwb[rows, :] = dwp_ref[rows, :] + dw_tile(n_ref, du2, i, blk)
-        pltpu.make_async_copy(dwb.at[rows, :], dw_ref.at[rows, :], wsem).start()
-        return c
-
-    lax.fori_loop(0, d // blk, tile, 0)
+        pltpu.make_async_copy(dwb.at[pl.ds(i * blk, blk), :], dw_ref.at[pl.ds(i * blk, blk), :], wsem).start()
     copies = umat(n_ref, w_ref, ub, u_ref, r ^ 2, r ^ 3, usem)
     scatter_wait(False, list_ref, xf, de_ref, sem)
     pltpu.make_async_copy(dwb, dw_ref, wsem).wait()

time: 101 us -> 96.5 us (0.955)
  Pallas kernels: 56.4 us -> 52.1 us
    pallas_call x1, Pallas kernels: 5.59 us -> 2.93 us  [local(): call(u_kernel, 32, [S((k, t, fc), BF16), S((d, fc), F32)], [VMEM] * 8, [H...]
    pallas_call x1, Pallas kernels: 8.44 us -> 6.72 us  [local(): call(functools.partial(last_kernel, 2 * vl), 20, [S((k, t, fc), BF16), S(...]
  transfers between devices with their start and end apart: 17 -> 17, of which waited for: 5 -> 5; matrix products, arithmetic and copies ran while one was open for 1% -> 1% of each run, Pallas kernels for 35% -> 34%
where the time goes in v13:
time: 96.5 us; the launch traced here: 96.1 us
  Pallas kernels  52.1 us (54%)
  waiting for transfers between devices  31.9 us (33%)
  starting transfers between devices  9.91 us (10%)
    ppermute x17, waiting for transfers between devices, perm(): return lax.ppermute(v, 'tp', p)  31.9 us
    pallas_call x1, Pallas kernels, local(): call(zero_kernel, 8, [S((4, 2 * h + 16), jnp.int32), S((vl, d), F32)], [S...  16.6 us
    pallas_call x1, Pallas kernels, local(): call(gather_kernel, 36, [S((n, d), BF16)] * 4 + [S((2, 2 * h + 16), jnp.i...  12.7 us
    ppermute x17, starting transfers between devices, perm(): return lax.ppermute(v, 'tp', p)  9.91 us
    pallas_call x1, Pallas kernels, local(): call(pdn_kernel, 60, [S((n, d), BF16)] * 4, [HBM] * 2, [HBM] * 4, [pltpu....  7.68 us
    pallas_call x1, Pallas kernels, local(): call(functools.partial(last_kernel, 2 * vl), 20, [S((k, t, fc), BF16), S(...  6.72 us
    pallas_call x1, Pallas kernels, local(): call(u_kernel, 32, [S((k, t, fc), BF16), S((d, fc), F32)], [VMEM] * 8, [H...  2.93 us
    pallas_call x2, Pallas kernels, dxk(): call(functools.partial(dx_kernel, m, 2 * vl), 16, outs, [VMEM] * 9 + [SME...  2.92 us
  transfers between devices with their start and end apart: 17, of which 5 were waited for; matrix products, arithmetic and copies ran while one was open for 1% of the time, Pallas kernels for 34%

profile of v13, /device:TPU:0, one launch (start us, length us, event | category | flops | bytes accessed | tf_op | source)
XLA Modules:
  0.0 96.1 jit_solution(16412088433817041725)
XLA Ops:
  0.6 0.0 copy-start.3
  0.6 0.7 copy-done.3
  1.3 12.7 %shard_map.101 = (bf16[128,2304]{1,0:T(8,128)(2,1)S(1)}, bf16[128,2304]{1,0:T(8,128)(2,1)S(1)}, bf16[128,2304]{1,0:T(8,128)(2,1)S(1)}, bf16[128,2304]{1,0:T(8,12...) custom-call(s32[2,256]{1,0:T(2,128)S(1)} %copy-done.3, bf16[8192,2304]{1,0:T(8,128)(2,1)} %emb_ref.1), custom_call_target="tpu_custom_call" | custom-call | flops 500000000 | bytes 9437184 | tf_op jit(solution)/shard_map/pallas_call | solution.py:365
  14.1 0.5 collective-permute-start
  14.6 0.0 collective-permute-start.1
  14.6 7.7 %shard_map.104 = (bf16[128,2304]{1,0:T(8,128)(2,1)}, bf16[128,2304]{1,0:T(8,128)(2,1)}, bf16[128,2304]{1,0:T(8,128)(2,1)}, bf16[128,2304]{1,0:T(8,128)(2,1)}) custom-call(bf16[2,256,1024]{2,1,0:T(8,128)(2,1)} %du_ref.5, bf16[2304,1024]{1,0:T(8,128)(2,1)} %w_ref.5), custom_call_target="tpu_custom_call" | custom-call | flops 2415919104 | bytes 8126464 | tf_op jit(solution)/shard_map/pallas_call | solution.py:359
  22.3 0.5 collective-permute-start.3
  22.8 1.9 %collective-permute-start.4 = (bf16[128,2304]{1,0:T(8,128)(2,1)}, bf16[128,2304]{1,0:T(8,128)(2,1)S(1)}, u32[]{:S(2)}, u32[]{:S(2)}) collective-permute-start(bf16[128,2304]{1,0:T(8,128)(2,1)} %get-tuple-element.46), channel_id=1, source_target_pairs={{0,2},{1,3},{2,0},{3,1},{4,6},{5,7},{6,4},{7,5}} | collective-permute-start | bytes 1769480 | tf_op jit(solution)/shard_map/ppermute | solution.py:357
  24.7 0.1 collective-permute-start.5
  24.8 0.0 collective-permute-done.y0
  24.8 0.0 collective-permute-done.1.y1
  24.8 0.1 shard_map.103
  24.9 1.8 %collective-permute-start.2 = (bf16[64,2304]{1,0:T(8,128)(2,1)S(1)}, bf16[64,2304]{1,0:T(8,128)(2,1)S(1)}, u32[]{:S(2)}, u32[]{:S(2)}) collective-permute-start(bf16[64,2304]{1,0:T(8,128)(2,1)S(1)} %get-tuple-element.43.t0), channel_id=1, source_target_pairs={{0,2},{1,3},{2,0},{3,1},{4,6},{5,7},{6,4},{7,5}} | collective-permute-start | bytes 884744 | tf_op jit(solution)/shard_map/ppermute | solution.py:357
  26.7 0.3 collective-permute-start.7
  26.9 0.0 copy-start.5
  27.0 0.0 copy-start
  27.0 0.0 copy-start.1
  27.0 0.0 copy-start.4
  27.0 16.6 %shard_map.102 = (s32[4,528]{1,0:T(4,128)S(1)}, f32[8192,2304]{1,0:T(8,128)}) custom-call(s32[2,528]{1,0:T(2,128)S(1)} %get-tuple-element.35.own_ref, f32[8192,2304]{1,0:T(8,128)} %get-tuple-element.36.de_in), custom_call_target="tpu_custom_call", output_to_operand_aliasing={{1}: (1, {})} | custom-call | flops 6000000000 | bytes 37748736 | tf_op jit(solution)/shard_map/pallas_call | solution.py:381
  43.5 0.0 copy-done.5
  43.5 0.0 collective-permute-done.3.p1
  43.6 0.0 collective-permute-done.4.p2
  43.6 7.8 %collective-permute-done.5.p3 = bf16[128,2304]{1,0:T(8,128)(2,1)S(1)} collective-permute-done((bf16[128,2304]{1,0:T(8,128)(2,1)}, bf16[128,2304]{1,0:T(8,128)(2,1)S(1)}, u32[]{:S(2)}, u32[]{:S(2)}) %collective-permute-start.5) | collective-permute-done | bytes 589856 | tf_op jit(solution)/shard_map/ppermute | solution.py:357
  51.4 6.8 %collective-permute-done.2.z_ref = bf16[64,2304]{1,0:T(8,128)(2,1)S(1)} collective-permute-done((bf16[64,2304]{1,0:T(8,128)(2,1)S(1)}, bf16[64,2304]{1,0:T(8,128)(2,1)S(1)}, u32[]{:S(2)}, u32[]{:S(2)}) %collective-permute-start.2) | collective-permute-done | bytes 294944 | tf_op jit(solution)/shard_map/ppermute | solution.py:357
  58.2 0.0 copy-done
  58.2 0.0 copy-done.1
  58.2 0.0 copy-done.4
  58.2 0.8 shard_map.105
  58.9 0.0 collective-permute-start.6
  59.0 5.2 %collective-permute-done.7.z_ref = bf16[64,2304]{1,0:T(8,128)(2,1)S(1)} collective-permute-done((bf16[64,2304]{1,0:T(8,128)(2,1)S(1)}, bf16[64,2304]{1,0:T(8,128)(2,1)S(1)}, u32[]{:S(2)}, u32[]{:S(2)}) %collective-permute-start.7) | collective-permute-done | bytes 294944 | tf_op jit(solution)/shard_map/ppermute | solution.py:357
  64.1 2.2 %shard_map.106 = (bf16[128,2304]{1,0:T(8,128)(2,1)S(1)}, bf16[64,2304]{1,0:T(8,128)(2,1)S(1)}, f32[1,2304]{1,0:T(1,128)S(1)}, bf16[2,64,2304]{2,1,0:T(8,128)(2,1)}) custom-call(bf16[64,2304]{1,0:T(8,128)(2,1)S(1)} %get-tuple-element.50.xh_ref, bf16[64,2304]{1,0:T(8,128)(2,1)S(1)} %collective-permute-done.7.z_ref, bf16[128,2304]{1,0:T(8,128)(2,1)S(1)} %copy-done.1, ...), custom_call_target="tpu_custom_call" | custom-call | flops 8847360 | bytes 4718592 | tf_op jit(solution)/shard_map/pallas_call | solution.py:388
  66.3 0.0 collective-permute-start.8
  66.3 1.7 %collective-permute-start.9 = (bf16[64,2304]{1,0:T(8,128)(2,1)S(1)}, bf16[64,2304]{1,0:T(8,128)(2,1)S(1)}, u32[]{:S(2)}, u32[]{:S(2)}) collective-permute-start(bf16[64,2304]{1,0:T(8,128)(2,1)S(1)} %get-tuple-element.56), channel_id=1, source_target_pairs={{0,2},{1,3},{2,0},{3,1},{4,6},{5,7},{6,4},{7,5}} | collective-permute-start | bytes 884744 | tf_op jit(solution)/shard_map/ppermute | solution.py:357
  68.1 0.3 collective-permute-start.11
  68.3 0.0 collective-permute-start.15
  68.3 1.2 %collective-permute-done.15 = f32[1,2304]{1,0:T(1,128)S(1)} collective-permute-done((f32[1,2304]{1,0:T(1,128)S(1)}, f32[1,2304]{1,0:T(1,128)S(1)}, u32[]{:S(2)}, u32[]{:S(2)}) %collective-permute-start.15) | collective-permute-done | bytes 9248 | tf_op jit(solution)/shard_map/ppermute | solution.py:357
  69.5 1.8 %collective-permute-start.16 = (f32[1,2304]{1,0:T(1,128)S(1)}, f32[1,2304]{1,0:T(1,128)S(1)}, u32[]{:S(2)}, u32[]{:S(2)}) collective-permute-start(f32[1,2304]{1,0:T(1,128)S(1)} %add.6), channel_id=1, source_target_pairs={{0,2},{1,3},{2,0},{3,1},{4,6},{5,7},{6,4},{7,5}} | collective-permute-start | bytes 27656 | tf_op jit(solution)/shard_map/ppermute | solution.py:357
  71.3 11.0 %collective-permute-done.16 = f32[1,2304]{1,0:T(1,128)S(1)} collective-permute-done((f32[1,2304]{1,0:T(1,128)S(1)}, f32[1,2304]{1,0:T(1,128)S(1)}, u32[]{:S(2)}, u32[]{:S(2)}) %collective-permute-start.16) | collective-permute-done | bytes 9248 | tf_op jit(solution)/shard_map/ppermute | solution.py:357
  82.2 0.0 collective-permute-start.13
  82.3 0.0 collective-permute-done.9.c0
  82.3 0.5 collective-permute-start.14
  82.8 0.0 collective-permute-done.11.c1
  82.8 0.0 collective-permute-start.10
  82.8 0.0 collective-permute-done.6.a0.y0
  82.8 0.5 collective-permute-start.12
  83.3 0.0 slice-start
  83.3 0.6 add_reduce_fusion
  83.9 0.0 slice-start.1
  83.9 0.0 copy-start.2
  83.9 0.0 collective-permute-done.8.a1.y1
  83.9 2.4 %shard_map.107 = (f32[256,2304]{1,0:T(8,128)S(1)}, f32[8192,2304]{1,0:T(8,128)}) custom-call(s32[4,528]{1,0:T(4,128)S(1)} %get-tuple-element.37.tok_ref.list_ref, bf16[128,2304]{1,0:T(8,128)(2,1)S(1)} %get-tuple-element.49.refs_0_.d0.x0, bf16[128,2304]{1,0:T(8,128)(2,1)S(1)} %collective-permute-done.6.a0.y0, ...), custom_call_target="tpu_custom_call", output_to_operand_aliasing={{1}: (6, {})} | custom-call | flops 4718592 | bytes 4718592 | tf_op jit(solution)/shard_map/pallas_call | solution.py:403
  86.3 0.0 slice-done
  86.3 0.0 slice-done.1
  86.4 0.0 copy-done.2
  86.4 2.9 %shard_map.108 = (bf16[2,256,1024]{2,1,0:T(8,128)(2,1)}, f32[2304,1024]{1,0:T(8,128)S(1)}) custom-call(bf16[128,2304]{1,0:T(8,128)(2,1)S(1)} %get-tuple-element.49.refs_0_.d0.x0, bf16[128,2304]{1,0:T(8,128)(2,1)S(1)} %collective-permute-done.6.a0.y0, bf16[128,2304]{1,0:T(8,128)(2,1)S(1)} %get-tuple-element.53.d1.x1, ...), custom_call_target="tpu_custom_call" | custom-call | flops 2415919104 | bytes 4718592 | tf_op jit(solution)/shard_map/pallas_call | solution.py:399
  89.3 0.0 collective-permute-done.13.w0
  89.3 0.0 collective-permute-done.14.w1
  89.3 0.0 collective-permute-done.10.b0
  89.3 0.0 collective-permute-done.12.b1
  89.3 6.7 %shard_map.109 = (bf16[2,256,1024]{2,1,0:T(8,128)(2,1)}, f32[2304,1024]{1,0:T(8,128)}, f32[8192,2304]{1,0:T(8,128)}) custom-call(s32[4,528]{1,0:T(4,128)S(1)} %get-tuple-element.37.tok_ref.list_ref, f32[256,2304]{1,0:T(8,128)S(1)} %get-tuple-element.55.xn_ref, ...), custom_call_target="tpu_custom_call", output_to_operand_aliasing={{0}: (15, {}), {2}: (16, {})} | custom-call | flops 2415919104 | bytes 14155776 | tf_op jit(solution)/shard_map/pallas_call | solution.py:410
  (3 shorter events, 0.0 us)
Async XLA Ops:
  0.6 0.7 copy-start.3
  14.1 10.7 %collective-permute-start = (bf16[128,2304]{1,0:T(8,128)(2,1)S(1)}, bf16[128,2304]{1,0:T(8,128)(2,1)S(1)}, u32[]{:S(2)}, u32[]{:S(2)}) collective-permute-start(bf16[128,2304]{1,0:T(8,128)(2,1)S(1)} %get-tuple-element.39), channel_id=1, source_target_pairs={{0,1},{1,0},{2,3},{3,2},{4,5},{5,4},{6,7},{7,6}} | collective-permute-start | bytes 1769480 | tf_op jit(solution)/shard_map/ppermute | solution.py:357
  14.6 10.2 %collective-permute-start.1 = (bf16[128,2304]{1,0:T(8,128)(2,1)S(1)}, bf16[128,2304]{1,0:T(8,128)(2,1)S(1)}, u32[]{:S(2)}, u32[]{:S(2)}) collective-permute-start(bf16[128,2304]{1,0:T(8,128)(2,1)S(1)} %get-tuple-element.41), channel_id=1, source_target_pairs={{0,1},{1,0},{2,3},{3,2},{4,5},{5,4},{6,7},{7,6}} | collective-permute-start | bytes 1769480 | tf_op jit(solution)/shard_map/ppermute | solution.py:357
  22.3 21.3 %collective-permute-start.3 = (bf16[128,2304]{1,0:T(8,128)(2,1)}, bf16[128,2304]{1,0:T(8,128)(2,1)S(1)}, u32[]{:S(2)}, u32[]{:S(2)}) collective-permute-start(bf16[128,2304]{1,0:T(8,128)(2,1)} %get-tuple-element.45), channel_id=1, source_target_pairs={{0,1},{1,0},{2,3},{3,2},{4,5},{5,4},{6,7},{7,6}} | collective-permute-start | bytes 1769480 | tf_op jit(solution)/shard_map/ppermute | solution.py:357
  22.8 20.8 %collective-permute-start.4 = (bf16[128,2304]{1,0:T(8,128)(2,1)}, bf16[128,2304]{1,0:T(8,128)(2,1)S(1)}, u32[]{:S(2)}, u32[]{:S(2)}) collective-permute-start(bf16[128,2304]{1,0:T(8,128)(2,1)} %get-tuple-element.46), channel_id=1, source_target_pairs={{0,2},{1,3},{2,0},{3,1},{4,6},{5,7},{6,4},{7,5}} | collective-permute-start | bytes 1769480 | tf_op jit(solution)/shard_map/ppermute | solution.py:357
  24.7 26.7 %collective-permute-start.5 = (bf16[128,2304]{1,0:T(8,128)(2,1)}, bf16[128,2304]{1,0:T(8,128)(2,1)S(1)}, u32[]{:S(2)}, u32[]{:S(2)}) collective-permute-start(bf16[128,2304]{1,0:T(8,128)(2,1)} %get-tuple-element.47), channel_id=1, source_target_pairs={{0,3},{1,2},{2,1},{3,0},{4,7},{5,6},{6,5},{7,4}} | collective-permute-start | bytes 1769480 | tf_op jit(solution)/shard_map/ppermute | solution.py:357
  24.9 33.2 %collective-permute-start.2 = (bf16[64,2304]{1,0:T(8,128)(2,1)S(1)}, bf16[64,2304]{1,0:T(8,128)(2,1)S(1)}, u32[]{:S(2)}, u32[]{:S(2)}) collective-permute-start(bf16[64,2304]{1,0:T(8,128)(2,1)S(1)} %get-tuple-element.43.t0), channel_id=1, source_target_pairs={{0,2},{1,3},{2,0},{3,1},{4,6},{5,7},{6,4},{7,5}} | collective-permute-start | bytes 884744 | tf_op jit(solution)/shard_map/ppermute | solution.py:357
  26.7 37.5 %collective-permute-start.7 = (bf16[64,2304]{1,0:T(8,128)(2,1)S(1)}, bf16[64,2304]{1,0:T(8,128)(2,1)S(1)}, u32[]{:S(2)}, u32[]{:S(2)}) collective-permute-start(bf16[64,2304]{1,0:T(8,128)(2,1)S(1)} %get-tuple-element.51.t1), channel_id=1, source_target_pairs={{0,2},{1,3},{2,0},{3,1},{4,6},{5,7},{6,4},{7,5}} | collective-permute-start | bytes 884744 | tf_op jit(solution)/shard_map/ppermute | solution.py:357
  26.9 16.6 %copy-start.5 = (bf16[2304]{0:T(1024)(128)(2,1)S(1)}, bf16[2304]{0:T(1024)(128)(2,1)}, u32[]{:S(2)}) copy-start(bf16[2304]{0:T(1024)(128)(2,1)} %param.8) | copy-start | bytes 13828
  27.0 31.2 %copy-start = (bf16[2,64,2304]{2,1,0:T(8,128)(2,1)S(1)}, bf16[2,64,2304]{2,1,0:T(8,128)(2,1)}, u32[]{:S(2)}) copy-start(bf16[2,64,2304]{2,1,0:T(8,128)(2,1)} %dres_ref.3) | copy-start | bytes 1769476
  27.0 31.2 %copy-start.1 = (bf16[128,2304]{1,0:T(8,128)(2,1)S(1)}, bf16[128,2304]{1,0:T(8,128)(2,1)}, u32[]{:S(2)}) copy-start(bf16[128,2304]{1,0:T(8,128)(2,1)} %get-tuple-element.44.p0) | copy-start | bytes 1769476
  27.0 31.2 %copy-start.4 = (s32[2,256]{1,0:T(2,128)S(1)}, s32[2,256]{1,0:T(2,128)}, u32[]{:S(2)}) copy-start(s32[2,256]{1,0:T(2,128)} %ids_ref.7) | copy-start | bytes 6148
  58.9 23.9 %collective-permute-start.6 = (bf16[128,2304]{1,0:T(8,128)(2,1)S(1)}, bf16[128,2304]{1,0:T(8,128)(2,1)S(1)}, u32[]{:S(2)}, u32[]{:S(2)}) collective-permute-start(bf16[128,2304]{1,0:T(8,128)(2,1)S(1)} %get-tuple-element.49.refs_0_.d0.x0), channel_id=1, source_target_pairs={{0,1},{1,0},{2,3},{3,2},{4,5},{5,4},{6,7},{7,6}} | collective-permute-start | bytes 1769480 | tf_op jit(solution)/shard_map/ppermute | solution.py:357
  66.3 17.6 %collective-permute-start.8 = (bf16[128,2304]{1,0:T(8,128)(2,1)S(1)}, bf16[128,2304]{1,0:T(8,128)(2,1)S(1)}, u32[]{:S(2)}, u32[]{:S(2)}) collective-permute-start(bf16[128,2304]{1,0:T(8,128)(2,1)S(1)} %get-tuple-element.53.d1.x1), channel_id=1, source_target_pairs={{0,1},{1,0},{2,3},{3,2},{4,5},{5,4},{6,7},{7,6}} | collective-permute-start | bytes 1769480 | tf_op jit(solution)/shard_map/ppermute | solution.py:357
  66.3 15.9 %collective-permute-start.9 = (bf16[64,2304]{1,0:T(8,128)(2,1)S(1)}, bf16[64,2304]{1,0:T(8,128)(2,1)S(1)}, u32[]{:S(2)}, u32[]{:S(2)}) collective-permute-start(bf16[64,2304]{1,0:T(8,128)(2,1)S(1)} %get-tuple-element.56), channel_id=1, source_target_pairs={{0,2},{1,3},{2,0},{3,1},{4,6},{5,7},{6,4},{7,5}} | collective-permute-start | bytes 884744 | tf_op jit(solution)/shard_map/ppermute | solution.py:357
  68.1 14.7 %collective-permute-start.11 = (bf16[64,2304]{1,0:T(8,128)(2,1)S(1)}, bf16[64,2304]{1,0:T(8,128)(2,1)S(1)}, u32[]{:S(2)}, u32[]{:S(2)}) collective-permute-start(bf16[64,2304]{1,0:T(8,128)(2,1)S(1)} %get-tuple-element.57), channel_id=1, source_target_pairs={{0,2},{1,3},{2,0},{3,1},{4,6},{5,7},{6,4},{7,5}} | collective-permute-start | bytes 884744 | tf_op jit(solution)/shard_map/ppermute | solution.py:357
  68.3 1.2 %collective-permute-start.15 = (f32[1,2304]{1,0:T(1,128)S(1)}, f32[1,2304]{1,0:T(1,128)S(1)}, u32[]{:S(2)}, u32[]{:S(2)}) collective-permute-start(f32[1,2304]{1,0:T(1,128)S(1)} %get-tuple-element.54.tok_ref), channel_id=1, source_target_pairs={{0,1},{1,0},{2,3},{3,2},{4,5},{5,4},{6,7},{7,6}} | collective-permute-start | bytes 27656 | tf_op jit(solution)/shard_map/ppermute | solution.py:357
  69.5 12.7 %collective-permute-start.16 = (f32[1,2304]{1,0:T(1,128)S(1)}, f32[1,2304]{1,0:T(1,128)S(1)}, u32[]{:S(2)}, u32[]{:S(2)}) collective-permute-start(f32[1,2304]{1,0:T(1,128)S(1)} %add.6), channel_id=1, source_target_pairs={{0,2},{1,3},{2,0},{3,1},{4,6},{5,7},{6,4},{7,5}} | collective-permute-start | bytes 27656 | tf_op jit(solution)/shard_map/ppermute | solution.py:357
  82.2 7.1 %collective-permute-start.13 = (bf16[64,2304]{1,0:T(8,128)(2,1)S(1)}, bf16[64,2304]{1,0:T(8,128)(2,1)S(1)}, u32[]{:S(2)}, u32[]{:S(2)}) collective-permute-start(bf16[64,2304]{1,0:T(8,128)(2,1)S(1)} %get-tuple-element.43.t0), channel_id=1, source_target_pairs={{0,1},{1,0},{2,3},{3,2},{4,5},{5,4},{6,7},{7,6}} | collective-permute-start | bytes 884744 | tf_op jit(solution)/shard_map/ppermute | solution.py:357
  82.3 7.1 %collective-permute-start.14 = (bf16[64,2304]{1,0:T(8,128)(2,1)S(1)}, bf16[64,2304]{1,0:T(8,128)(2,1)S(1)}, u32[]{:S(2)}, u32[]{:S(2)}) collective-permute-start(bf16[64,2304]{1,0:T(8,128)(2,1)S(1)} %get-tuple-element.51.t1), channel_id=1, source_target_pairs={{0,1},{1,0},{2,3},{3,2},{4,5},{5,4},{6,7},{7,6}} | collective-permute-start | bytes 884744 | tf_op jit(solution)/shard_map/ppermute | solution.py:357
  82.8 6.6 %collective-permute-start.10 = (bf16[64,2304]{1,0:T(8,128)(2,1)S(1)}, bf16[64,2304]{1,0:T(8,128)(2,1)S(1)}, u32[]{:S(2)}, u32[]{:S(2)}) collective-permute-start(bf16[64,2304]{1,0:T(8,128)(2,1)S(1)} %collective-permute-done.9.c0), channel_id=1, source_target_pairs={{0,1},{1,0},{2,3},{3,2},{4,5},{5,4},{6,7},{7,6}} | collective-permute-start | bytes 884744 | tf_op jit(solution)/shard_map/ppermute | solution.py:357
  82.8 6.5 %collective-permute-start.12 = (bf16[64,2304]{1,0:T(8,128)(2,1)S(1)}, bf16[64,2304]{1,0:T(8,128)(2,1)S(1)}, u32[]{:S(2)}, u32[]{:S(2)}) collective-permute-start(bf16[64,2304]{1,0:T(8,128)(2,1)S(1)} %collective-permute-done.11.c1), channel_id=1, source_target_pairs={{0,1},{1,0},{2,3},{3,2},{4,5},{5,4},{6,7},{7,6}} | collective-permute-start | bytes 884744 | tf_op jit(solution)/shard_map/ppermute | solution.py:357
  83.3 3.1 %slice-start = ((s8[4718592]{0:T(1024)(128)(4,1)}), s8[4194304]{0:T(1024)(128)(4,1)S(1)}, s32[]{:S(2)}) async-start(s8[4718592]{0:T(1024)(128)(4,1)} %bitcast), calls=%async_computation | async-start | bytes 8388608
  83.9 2.4 %slice-start.1 = ((s8[4718592]{0:T(1024)(128)(4,1)}), s8[524288]{0:T(1024)(128)(4,1)S(1)}, s32[]{:S(2)}) async-start(s8[4718592]{0:T(1024)(128)(4,1)} %bitcast), calls=%async_computation.1 | async-start | bytes 1048576
  83.9 2.4 %copy-start.2 = (bf16[2,256,1024]{2,1,0:T(8,128)(2,1)S(1)}, bf16[2,256,1024]{2,1,0:T(8,128)(2,1)}, u32[]{:S(2)}) copy-start(bf16[2,256,1024]{2,1,0:T(8,128)(2,1)} %du_ref.5) | copy-start | bytes 3145732

commit v14 on v13

--- a/solution.py
+++ b/solution.py
@@ -29,17 +29,25 @@
     )
 
 
-def pdn_kernel(du_ref, w_ref, *refs):
+def pdn_kernel(lo, fill, du_ref, w_ref, *refs):
+    refs = refs[fill:]
     outs = refs[:4]
-    dub, dup, wb, ob, dsem, wsem, osem = refs[4:]
-    n, d = outs[0].shape
+    if fill:
+        de_ref, z, zsem = refs[4], refs[-2], refs[-1]
+    dub, dup, wb, ob, dsem, wsem, osem = refs[5:12]
+    n, width = outs[0].shape
     k, tl = dub.shape[0], dub.shape[1] // 4
     blk = 256
-    nb = d // blk
+    nb = width // blk
     dc = pltpu.make_async_copy(du_ref, dub, dsem)
     dc.start()
     for i in range(nb):
-        pltpu.make_async_copy(w_ref.at[pl.ds(i * blk, blk), :], wb.at[pl.ds(i * blk, blk), :], wsem.at[i]).start()
+        pltpu.make_async_copy(w_ref.at[pl.ds(lo + i * blk, blk), :], wb.at[pl.ds(i * blk, blk), :], wsem.at[i]).start()
+    if fill:
+        z[...] = jnp.zeros_like(z)
+        zero_start(z, de_ref, *FILL[0], zsem)
+    else:
+        refs[4][0] = 0
     r = lax.axis_index("tp")
     dc.wait()
     for a, j in enumerate((2, 3, 1, 0)):
@@ -59,9 +67,11 @@
     lax.fori_loop(0, nb, tile, 0)
     for a in range(4):
         pltpu.make_async_copy(ob.at[pl.ds(a * n, n), :], outs[a], osem).wait()
-
-
-FILL = ((0, 3), (3, 6), (6, 16))
+    if fill:
+        zero_wait(z, de_ref, *FILL[0], zsem)
+
+
+FILL = ((0, 3), (3, 6), (6, 9), (9, 13), (13, 16))
 
 
 def zero_start(z, de_ref, lo, hi, sem):
@@ -79,7 +89,7 @@
 
 def zero_kernel(own_ref, de_in, list_ref, de_ref, z, lnxt, tab, sem):
     z[...] = jnp.zeros_like(z)
-    zero_start(z, de_ref, *FILL[2], sem)
+    zero_start(z, de_ref, *FILL[3], sem)
     n = own_ref[0, own_ref.shape[1] - 1]
     t = lnxt.shape[0] - 8
 
@@ -112,17 +122,23 @@
     nl, nd, nl0, nd0 = lax.fori_loop(0, n, lists, (0, 0, 0, 0))
     for a, v in enumerate((nl, nl0, nd, nd0)):
         list_ref[a, list_ref.shape[1] - 1] = v
-    zero_wait(z, de_ref, *FILL[2], sem)
-
-
-def gather_kernel(ids_ref, emb_ref, k0, s0, k1, s1, own_ref, de_ref, buf, tmp, xf, z, lst, sem, zsem):
+    zero_wait(z, de_ref, *FILL[3], sem)
+
+
+def zero2_kernel(tok_ref, de_in, de_ref, z, sem):
+    z[...] = jnp.zeros_like(z)
+    zero_start(z, de_ref, *FILL[4], sem)
+    zero_wait(z, de_ref, *FILL[4], sem)
+
+
+def gather_kernel(ids_ref, emb_ref, de_in, k0, s0, k1, s1, own_ref, de_ref, buf, tmp, xf, z, lst, sem, zsem):
     k, t = ids_ref.shape
     vl = emb_ref.shape[0]
     h = k0.shape[0]
     tl = t // 4
     r = lax.axis_index("tp")
     z[...] = jnp.zeros_like(z)
-    zero_start(z, de_ref, *FILL[0], zsem)
+    zero_start(z, de_ref, *FILL[1], zsem)
     n = 0
     for c in range(2):
         lo = ((r >> 1) ^ c) * h
@@ -146,7 +162,7 @@
         return c
 
     lax.fori_loop(0, n, start, 0)
-    zero_start(z, de_ref, *FILL[1], zsem)
+    zero_start(z, de_ref, *FILL[2], zsem)
     for a in range(8):
         own_ref[0, n + a] = k * t
         own_ref[1, n + a] = 0
@@ -170,7 +186,7 @@
     for a, ref in enumerate((k0, s0, k1, s1)):
         for c in range(2):
             ref[c * tl:(c + 1) * tl, :] = xf[c * 2 * h + a * tl:c * 2 * h + (a + 1) * tl, :].astype(BF16)
-    zero_wait(z, de_ref, FILL[0][0], FILL[1][1], zsem)
+    zero_wait(z, de_ref, FILL[1][0], FILL[2][1], zsem)
 
 
 def sum_kernel(k0, y0, k1, y1, a0, t0, a1, t1):
@@ -190,7 +206,7 @@
     return jnp.logical_and(col >= lo, col < lo + chip_rows)
 
 
-def dx_kernel(m, chip_rows, xh_ref, z_ref, p0, p1, p2, p3, dres_ref, g_ref, ids_ref, tok_ref, *refs):
+def dx_kernel(m, chip_rows, xh_ref, z_ref, p0, p1, p2, p3, r0, r1, r2, r3, dres_ref, g_ref, ids_ref, tok_ref, *refs):
     if m == 1:
         both0_ref, dg0_ref, both_ref, slot_ref, dg_ref, xs_ref = refs
     else:
@@ -206,7 +222,9 @@
     rs = lax.rsqrt(jnp.mean(x * x, axis=-1, keepdims=True) + EPS)
     nh = x * rs
     s = slice(m * tl, (m + 1) * tl)
-    dn = (p0[s, :].astype(F32) + p1[s, :].astype(F32)) + (p2[s, :].astype(F32) + p3[s, :].astype(F32))
+    dn = jnp.concatenate([
+        (a[s, :].astype(F32) + b[s, :].astype(F32)) + (c[s, :].astype(F32) + e[s, :].astype(F32))
+        for a, b, c, e in ((p0, p1, p2, p3), (r0, r1, r2, r3))], axis=1)
     gdn = g * dn
     mean = jnp.mean(nh * gdn, axis=-1, keepdims=True)
     dxn = rs * (gdn - nh * mean)
@@ -356,22 +374,36 @@
         def perm(v, p):
             return lax.ppermute(v, "tp", p)
 
-        p2, p3, p1, p0 = call(
-            pdn_kernel, 60, [S((n, d), BF16)] * 4, [HBM] * 2, [HBM] * 4,
-            [pltpu.VMEM((k, t, fc), BF16), pltpu.VMEM((4 * n, fc), BF16), pltpu.VMEM((d, fc), BF16), pltpu.VMEM((4 * n, d), BF16),
-             D, D((d // 256,)), D], 8 * n * fc * d, 2 * d * fc + 8 * n * (fc + d))(du, w)
+        d1 = 4 * 256
+        d2 = d - d1
+
+        def pdn(lo, width, fill, *tok):
+            extra = S((vl, d), F32) if fill else S((8,), jnp.int32)
+            return call(
+                functools.partial(pdn_kernel, lo, fill), 60, [S((n, width), BF16)] * 4 + [extra],
+                [HBM] * 2 + [SMEM] * len(tok), [HBM] * 4 + [HBM if fill else SMEM],
+                [pltpu.VMEM((k, t, fc), BF16), pltpu.VMEM((4 * n, fc), BF16), pltpu.VMEM((width, fc), BF16),
+                 pltpu.VMEM((4 * n, width), BF16), D, D((width // 256,)), D]
+                + ([pltpu.VMEM((256, d), F32), D] if fill else []),
+                8 * n * fc * width, 2 * width * fc + 8 * n * (fc + width))(du, w, *tok)
+
+        p2, p3, p1, p0, first = pdn(0, d1, False)
         q2 = perm(p2, cross)
         q3 = perm(p3, diag)
+        r2, r3, r1, r0, de = pdn(d1, d2, True, first)
+        v2 = perm(r2, cross)
+        v3 = perm(r3, diag)
         k0, s0, k1, s1, owned, de = call(
             gather_kernel, 36,
             [S((n, d), BF16)] * 4 + [S((2, 2 * h + 16), jnp.int32), S((vl, d), F32)],
-            [SMEM, HBM], [VMEM] * 4 + [SMEM, HBM],
+            [SMEM, HBM, HBM], [VMEM] * 4 + [SMEM, HBM],
             [pltpu.VMEM((2 * h, 8, d), BF16), pltpu.VMEM((8, 8, d), F32), pltpu.VMEM((2 * h + 8, d), F32), pltpu.VMEM((256, d), F32)]
             + [pltpu.SMEM((2 * h + 8,), jnp.int32), D, D],
-            500_000_000, 16 * h * d)(ids, emb)
+            500_000_000, 16 * h * d, {2: 5})(ids, emb, de)
         y0 = perm(s0, sib)
         y1 = perm(s1, sib)
         q1 = perm(p1, sib)
+        v1 = perm(r1, sib)
         own0, oth0, own1, oth1 = call(sum_kernel, 16, [S((tl, d), BF16)] * 4, [VMEM] * 4, [VMEM] * 4, [],
                                       8 * tl * d, 24 * tl * d)(k0, y0, k1, y1)
         z0 = perm(oth0, cross)
@@ -386,14 +418,16 @@
         def dxk(m, xh, z, tok, more):
             outs = [S((n, d), BF16), S((tl, d), BF16), S((1, d), F32)] + ([S((k, tl, d), BF16)] if m else [])
             return call(functools.partial(dx_kernel, m, 2 * vl), 16, outs,
-                        [VMEM] * 9 + [SMEM if m else HBM] + [VMEM] * len(more),
+                        [VMEM] * 13 + [HBM] + [VMEM] * len(more),
                         [VMEM] * len(outs), [], 30 * n * d, 16 * n * d)(
-                            xh, z, p0, q1, q2, q3, dres, g2, ids, tok, *more)
+                            xh, z, p0, q1, q2, q3, r0, v1, v2, v3, dres, g2, ids, tok, *more)
 
         mine0, slot0, dg0 = dxk(0, own0, z0, de, ())
         c0 = perm(slot0, cross)
         next0 = perm(mine0, sib)
-        mine1, slot1, dg, x = dxk(1, own1, z1, lists, (mine0, dg0))
+        de = call(zero2_kernel, 8, S((vl, d), F32), [VMEM, HBM], HBM, [pltpu.VMEM((256, d), F32), D],
+                  2_000_000_000, vl * d, {1: 0})(dg0, de)
+        mine1, slot1, dg, x = dxk(1, own1, z1, de, (mine0, dg0))
         c1 = perm(slot1, cross)
         next1 = perm(mine1, sib)
         u, dwp = call(

time: 96.5 us -> 101 us (1.047)
  starting transfers between devices: 9.91 us -> 14.1 us
  Pallas kernels: 52.1 us -> 54.1 us
  waiting for transfers between devices: 31.9 us -> 30 us
    pallas_call x3 -> x5, Pallas kernels: 10.6 us -> 20.3 us  [the longest x2 12.8 us: pdn(): call(functools.partial(pdn_kernel, lo, fill), 60, [S((n, width), BF16)] *...]
    pallas_call x1, Pallas kernels: 16.6 us -> 8.96 us  [local(): call(zero_kernel, 8, [S((4, 2 * h + 16), jnp.int32), S((vl, d), F32)], [S...]
    ppermute x17 -> x20, starting transfers between devices: 9.91 us -> 14.1 us  [perm(): return lax.ppermute(v, 'tp', p)]
    ppermute x17 -> x20, waiting for transfers between devices: 31.9 us -> 30 us  [perm(): return lax.ppermute(v, 'tp', p)]
  transfers between devices with their start and end apart: 17 -> 20, of which waited for: 5 -> 6; matrix products, arithmetic and copies ran while one was open for 1% -> 1% of each run, Pallas kernels for 34% -> 22%
where the time goes in v14:
time: 101 us
  Pallas kernels  54.1 us (54%)
  waiting for transfers between devices  30 us (30%)
  starting transfers between devices  14.1 us (14%)
    ppermute x20, waiting for transfers between devices, perm(): return lax.ppermute(v, 'tp', p)  30 us
    ppermute x20, starting transfers between devices, perm(): return lax.ppermute(v, 'tp', p)  14.1 us
    pallas_call x2, Pallas kernels, pdn(): call(functools.partial(pdn_kernel, lo, fill), 60, [S((n, width), BF16)] *...  12.8 us
    pallas_call x1, Pallas kernels, local(): call(gather_kernel, 36, [S((n, d), BF16)] * 4 + [S((2, 2 * h + 16), jnp.i...  12.7 us
    pallas_call x1, Pallas kernels, local(): call(zero_kernel, 8, [S((4, 2 * h + 16), jnp.int32), S((vl, d), F32)], [S...  8.96 us
    pallas_call x1, Pallas kernels, local(): call(functools.partial(last_kernel, 2 * vl), 20, [S((k, t, fc), BF16), S(...  6.68 us
    pallas_call x1, Pallas kernels, local(): call(zero2_kernel, 8, S((vl, d), F32), [VMEM, HBM], HBM, [pltpu.VMEM((256...  5.25 us
    pallas_call x1, Pallas kernels, local(): call(u_kernel, 32, [S((k, t, fc), BF16), S((d, fc), F32)], [VMEM] * 8, [H...  2.93 us
  transfers between devices with their start and end apart: 20, of which 6 were waited for; matrix products, arithmetic and copies ran while one was open for 1% of the time, Pallas kernels for 22%

profile of v14, /device:TPU:0, one launch (start us, length us, event | category | flops | bytes accessed | tf_op | source)
XLA Modules:
  0.0 100.6 jit_solution(14311514692247013520)
XLA Ops:
  0.6 5.0 %shard_map.101 = (bf16[128,1024]{1,0:T(8,128)(2,1)}, bf16[128,1024]{1,0:T(8,128)(2,1)}, bf16[128,1024]{1,0:T(8,128)(2,1)}, bf16[128,1024]{1,0:T(8,128)(2,1)}, s32[8]{0:T(128)}) custom-call(bf16[2,256,1024]{2,1,0:T(8,128)(2,1)} %du_ref.7, bf16[2304,1024]{1,0:T(8,128)(2,1)} %w_ref.7), custom_call_target="tpu_custom_call" | custom-call | flops 1073741824 | bytes 4194304 | tf_op jit(solution)/shard_map/pallas_call | solution.py:382
  5.6 0.0 copy-start.12
  5.6 0.0 copy-start.11
  5.7 0.0 copy-start.10
  5.7 7.8 %shard_map.102 = (bf16[128,1280]{1,0:T(8,128)(2,1)}, bf16[128,1280]{1,0:T(8,128)(2,1)}, bf16[128,1280]{1,0:T(8,128)(2,1)}, bf16[128,1280]{1,0:T(8,128)(2,1)}, f32[8192,2304]{1,0:T(8,128)}) custom-call(bf16[2,256,1024]{2,1,0:T(8,128)(2,1)} %du_ref.7, bf16[2304,1024]{1,0:T(8,128)(2,1)} %w_ref.7, s32[8]{0:T(128)} %get-tuple-element.41.refs_0_), custom_call_target="tpu_custom_call" | custom-call | flops 1342177280 | bytes 4980736 | tf_op jit(solution)/shard_map/pallas_call | solution.py:382
  13.5 0.0 copy-start.4
  13.5 0.7 copy-done.4
  14.2 0.0 copy-start.1
  14.2 0.0 copy-start.2
  14.2 12.7 %shard_map.103 = (bf16[128,2304]{1,0:T(8,128)(2,1)S(1)}, bf16[128,2304]{1,0:T(8,128)(2,1)S(1)}, bf16[128,2304]{1,0:T(8,128)(2,1)S(1)}, bf16[128,2304]{1,0:T(8,12...) custom-call(s32[2,256]{1,0:T(2,128)S(1)} %copy-done.4, ...), custom_call_target="tpu_custom_call", output_to_operand_aliasing={{5}: (2, {})} | custom-call | flops 500000000 | bytes 9437184 | tf_op jit(solution)/shard_map/pallas_call | solution.py:396
  27.0 0.5 collective-permute-start
  27.5 0.0 collective-permute-start.1
  27.5 0.5 collective-permute-start.3
  28.0 1.9 %collective-permute-start.4 = (bf16[128,1024]{1,0:T(8,128)(2,1)S(1)}, bf16[128,1024]{1,0:T(8,128)(2,1)S(1)}, u32[]{:S(2)}, u32[]{:S(2)}) collective-permute-start(bf16[128,1024]{1,0:T(8,128)(2,1)S(1)} %copy-done.11), channel_id=1, source_target_pairs={{0,2},{1,3},{2,0},{3,1},{4,6},{5,7},{6,4},{7,5}} | collective-permute-start | bytes 786440 | tf_op jit(solution)/shard_map/ppermute | solution.py:375
  29.9 0.1 collective-permute-start.5
  30.0 0.0 collective-permute-done.y0
  30.0 0.1 collective-permute-start.6
  30.2 0.0 collective-permute-done.1.y1
  30.2 0.0 copy-done.8
  30.2 2.0 %collective-permute-start.7 = (bf16[128,1280]{1,0:T(8,128)(2,1)S(1)}, bf16[128,1280]{1,0:T(8,128)(2,1)S(1)}, u32[]{:S(2)}, u32[]{:S(2)}) collective-permute-start(bf16[128,1280]{1,0:T(8,128)(2,1)S(1)} %copy-done.8), channel_id=1, source_target_pairs={{0,2},{1,3},{2,0},{3,1},{4,6},{5,7},{6,4},{7,5}} | collective-permute-start | bytes 983048 | tf_op jit(solution)/shard_map/ppermute | solution.py:375
  32.2 0.1 shard_map.105
  32.3 0.0 collective-permute-done.3.p1
  32.4 0.0 collective-permute-start.8
  32.4 4.8 %collective-permute-done.4.p2 = bf16[128,1024]{1,0:T(8,128)(2,1)S(1)} collective-permute-done((bf16[128,1024]{1,0:T(8,128)(2,1)S(1)}, bf16[128,1024]{1,0:T(8,128)(2,1)S(1)}, u32[]{:S(2)}, u32[]{:S(2)}) %collective-permute-start.4) | collective-permute-done | bytes 262176 | tf_op jit(solution)/shard_map/ppermute | solution.py:375
  37.2 1.9 %collective-permute-start.2 = (bf16[64,2304]{1,0:T(8,128)(2,1)S(1)}, bf16[64,2304]{1,0:T(8,128)(2,1)S(1)}, u32[]{:S(2)}, u32[]{:S(2)}) collective-permute-start(bf16[64,2304]{1,0:T(8,128)(2,1)S(1)} %get-tuple-element.51.t0), channel_id=1, source_target_pairs={{0,2},{1,3},{2,0},{3,1},{4,6},{5,7},{6,4},{7,5}} | collective-permute-start | bytes 884744 | tf_op jit(solution)/shard_map/ppermute | solution.py:375
  39.1 3.1 %collective-permute-done.5.p3 = bf16[128,1024]{1,0:T(8,128)(2,1)S(1)} collective-permute-done((bf16[128,1024]{1,0:T(8,128)(2,1)S(1)}, bf16[128,1024]{1,0:T(8,128)(2,1)S(1)}, u32[]{:S(2)}, u32[]{:S(2)}) %collective-permute-start.5) | collective-permute-done | bytes 262176 | tf_op jit(solution)/shard_map/ppermute | solution.py:375
  42.2 1.5 %collective-permute-start.10 = (bf16[64,2304]{1,0:T(8,128)(2,1)S(1)}, bf16[64,2304]{1,0:T(8,128)(2,1)S(1)}, u32[]{:S(2)}, u32[]{:S(2)}) collective-permute-start(bf16[64,2304]{1,0:T(8,128)(2,1)S(1)} %get-tuple-element.63.t1), channel_id=1, source_target_pairs={{0,2},{1,3},{2,0},{3,1},{4,6},{5,7},{6,4},{7,5}} | collective-permute-start | bytes 884744 | tf_op jit(solution)/shard_map/ppermute | solution.py:375
  43.7 9.0 %shard_map.104 = (s32[4,528]{1,0:T(4,128)S(1)}, f32[8192,2304]{1,0:T(8,128)}) custom-call(s32[2,528]{1,0:T(2,128)S(1)} %get-tuple-element.43.own_ref, f32[8192,2304]{1,0:T(8,128)} %get-tuple-element.44.de_in), custom_call_target="tpu_custom_call", output_to_operand_aliasing={{1}: (1, {})} | custom-call | flops 6000000000 | bytes 37748736 | tf_op jit(solution)/shard_map/pallas_call | solution.py:413
  52.7 0.0 collective-permute-done.6.r1
  52.7 0.0 collective-permute-done.7.r2
  52.7 3.5 %collective-permute-done.8.r3 = bf16[128,1280]{1,0:T(8,128)(2,1)S(1)} collective-permute-done((bf16[128,1280]{1,0:T(8,128)(2,1)S(1)}, bf16[128,1280]{1,0:T(8,128)(2,1)S(1)}, u32[]{:S(2)}, u32[]{:S(2)}) %collective-permute-start.8) | collective-permute-done | bytes 327712 | tf_op jit(solution)/shard_map/ppermute | solution.py:375
  56.3 6.9 %collective-permute-done.2.z_ref = bf16[64,2304]{1,0:T(8,128)(2,1)S(1)} collective-permute-done((bf16[64,2304]{1,0:T(8,128)(2,1)S(1)}, bf16[64,2304]{1,0:T(8,128)(2,1)S(1)}, u32[]{:S(2)}, u32[]{:S(2)}) %collective-permute-start.2) | collective-permute-done | bytes 294944 | tf_op jit(solution)/shard_map/ppermute | solution.py:375
  63.2 0.0 copy-done.2
  63.2 0.8 shard_map.106
  63.9 0.0 collective-permute-start.9
  64.0 5.2 %shard_map.107.tok_ref.de_in = f32[8192,2304]{1,0:T(8,128)} custom-call(f32[1,2304]{1,0:T(1,128)S(1)} %get-tuple-element.64.tok_ref.refs_1_, f32[8192,2304]{1,0:T(8,128)} %get-tuple-element.60.tok_ref.de_in), custom_call_target="tpu_custom_call", output_to_operand_aliasing={{}: (1, {})} | custom-call | flops 2000000000 | bytes 18874368 | tf_op jit(solution)/shard_map/pallas_call | solution.py:428
  69.2 0.0 collective-permute-done.10.z_ref
  69.2 0.0 copy-start
  69.3 0.0 copy-start.5
  69.3 1.5 %shard_map.108 = (bf16[128,2304]{1,0:T(8,128)(2,1)S(1)}, bf16[64,2304]{1,0:T(8,128)(2,1)S(1)}, f32[1,2304]{1,0:T(1,128)S(1)}, bf16[2,64,2304]{2,1,0:T(8,128)(2,1)}) custom-call(bf16[64,2304]{1,0:T(8,128)(2,1)S(1)} %get-tuple-element.62.xh_ref, bf16[64,2304]{1,0:T(8,128)(2,1)S(1)} %collective-permute-done.10.z_ref, bf16[128,1024]{1,0:T(8,128)(2,1)S(1)} %copy-done.3, ...), custom_call_target="tpu_custom_call" | custom-call | flops 8847360 | bytes 4718592 | tf_op jit(solution)/shard_map/pallas_call | solution.py:420
  70.7 0.5 collective-permute-start.11
  71.2 1.9 %collective-permute-start.12 = (bf16[64,2304]{1,0:T(8,128)(2,1)S(1)}, bf16[64,2304]{1,0:T(8,128)(2,1)S(1)}, u32[]{:S(2)}, u32[]{:S(2)}) collective-permute-start(bf16[64,2304]{1,0:T(8,128)(2,1)S(1)} %get-tuple-element.68), channel_id=1, source_target_pairs={{0,2},{1,3},{2,0},{3,1},{4,6},{5,7},{6,4},{7,5}} | collective-permute-start | bytes 884744 | tf_op jit(solution)/shard_map/ppermute | solution.py:375
  73.1 0.1 collective-permute-start.14
  73.3 0.0 collective-permute-start.18
  73.3 1.2 %collective-permute-done.18 = f32[1,2304]{1,0:T(1,128)S(1)} collective-permute-done((f32[1,2304]{1,0:T(1,128)S(1)}, f32[1,2304]{1,0:T(1,128)S(1)}, u32[]{:S(2)}, u32[]{:S(2)}) %collective-permute-start.18) | collective-permute-done | bytes 9248 | tf_op jit(solution)/shard_map/ppermute | solution.py:375
  74.4 1.9 %collective-permute-start.19 = (f32[1,2304]{1,0:T(1,128)S(1)}, f32[1,2304]{1,0:T(1,128)S(1)}, u32[]{:S(2)}, u32[]{:S(2)}) collective-permute-start(f32[1,2304]{1,0:T(1,128)S(1)} %add.6), channel_id=1, source_target_pairs={{0,2},{1,3},{2,0},{3,1},{4,6},{5,7},{6,4},{7,5}} | collective-permute-start | bytes 27656 | tf_op jit(solution)/shard_map/ppermute | solution.py:375
  76.4 10.5 %collective-permute-done.19 = f32[1,2304]{1,0:T(1,128)S(1)} collective-permute-done((f32[1,2304]{1,0:T(1,128)S(1)}, f32[1,2304]{1,0:T(1,128)S(1)}, u32[]{:S(2)}, u32[]{:S(2)}) %collective-permute-start.19) | collective-permute-done | bytes 9248 | tf_op jit(solution)/shard_map/ppermute | solution.py:375
  86.8 0.0 collective-permute-start.16
  86.8 0.0 collective-permute-done.12.c0
  86.8 0.5 collective-permute-start.17
  87.4 0.0 collective-permute-done.14.c1
  87.4 0.0 collective-permute-start.13
  87.4 0.0 collective-permute-done.9.a0.y0
  87.4 0.5 collective-permute-start.15
  87.9 0.6 add_reduce_fusion
  88.5 0.0 collective-permute-done.11.a1.y1
  88.5 2.4 %shard_map.109 = (f32[256,2304]{1,0:T(8,128)S(1)}, f32[8192,2304]{1,0:T(8,128)}) custom-call(s32[4,528]{1,0:T(4,128)S(1)} %get-tuple-element.45.list_ref, bf16[128,2304]{1,0:T(8,128)(2,1)S(1)} %get-tuple-element.61.refs_0_.d0.x0, bf16[128,2304]{1,0:T(8,128)(2,1)S(1)} %collective-permute-done.9.a0.y0, ...), custom_call_target="tpu_custom_call", output_to_operand_aliasing={{1}: (6, {})} | custom-call | flops 4718592 | bytes 4718592 | tf_op jit(solution)/shard_map/pallas_call | solution.py:437
  91.0 2.9 %shard_map.110 = (bf16[2,256,1024]{2,1,0:T(8,128)(2,1)}, f32[2304,1024]{1,0:T(8,128)S(1)}) custom-call(bf16[128,2304]{1,0:T(8,128)(2,1)S(1)} %get-tuple-element.61.refs_0_.d0.x0, bf16[128,2304]{1,0:T(8,128)(2,1)S(1)} %collective-permute-done.9.a0.y0, bf16[128,2304]{1,0:T(8,128)(2,1)S(1)} %get-tuple-element.65.d1.x1, ...), custom_call_target="tpu_custom_call" | custom-call | flops 2415919104 | bytes 4718592 | tf_op jit(solution)/shard_map/pallas_call | solution.py:433
  93.9 0.0 collective-permute-done.16.w0
  93.9 0.0 collective-permute-done.17.w1
  93.9 0.0 collective-permute-done.13.b0
  93.9 0.0 collective-permute-done.15.b1
  93.9 0.0 copy-done.5
  93.9 6.7 %shard_map.111 = (bf16[2,256,1024]{2,1,0:T(8,128)(2,1)}, f32[2304,1024]{1,0:T(8,128)}, f32[8192,2304]{1,0:T(8,128)}) custom-call(s32[4,528]{1,0:T(4,128)S(1)} %get-tuple-element.45.list_ref, f32[256,2304]{1,0:T(8,128)S(1)} %get-tuple-element.67.xn_ref, ...), custom_call_target="tpu_custom_call", output_to_operand_aliasing={{0}: (15, {}), {2}: (16, {})} | custom-call | flops 2415919104 | bytes 14155776 | tf_op jit(solution)/shard_map/pallas_call | solution.py:444
  (21 shorter events, 0.1 us)
Async XLA Ops:
  5.6 21.9 %copy-start.12 = (bf16[128,1024]{1,0:T(8,128)(2,1)S(1)}, bf16[128,1024]{1,0:T(8,128)(2,1)}, u32[]{:S(2)}) copy-start(bf16[128,1024]{1,0:T(8,128)(2,1)} %get-tuple-element.53) | copy-start | bytes 786436
  5.6 22.4 %copy-start.11 = (bf16[128,1024]{1,0:T(8,128)(2,1)S(1)}, bf16[128,1024]{1,0:T(8,128)(2,1)}, u32[]{:S(2)}) copy-start(bf16[128,1024]{1,0:T(8,128)(2,1)} %get-tuple-element.54) | copy-start | bytes 786436
  5.7 24.3 %copy-start.10 = (bf16[128,1024]{1,0:T(8,128)(2,1)S(1)}, bf16[128,1024]{1,0:T(8,128)(2,1)}, u32[]{:S(2)}) copy-start(bf16[128,1024]{1,0:T(8,128)(2,1)} %get-tuple-element.55) | copy-start | bytes 786436
  13.5 0.7 copy-start.4
  14.2 15.8 %copy-start.9 = (bf16[128,1280]{1,0:T(8,128)(2,1)S(1)}, bf16[128,1280]{1,0:T(8,128)(2,1)}, u32[]{:S(2)}) copy-start(bf16[128,1280]{1,0:T(8,128)(2,1)} %get-tuple-element.57) | copy-start | bytes 983044
  14.2 16.0 %copy-start.8 = (bf16[128,1280]{1,0:T(8,128)(2,1)S(1)}, bf16[128,1280]{1,0:T(8,128)(2,1)}, u32[]{:S(2)}) copy-start(bf16[128,1280]{1,0:T(8,128)(2,1)} %get-tuple-element.58) | copy-start | bytes 983044
  14.2 18.2 %copy-start.7 = (bf16[128,1280]{1,0:T(8,128)(2,1)S(1)}, bf16[128,1280]{1,0:T(8,128)(2,1)}, u32[]{:S(2)}) copy-start(bf16[128,1280]{1,0:T(8,128)(2,1)} %get-tuple-element.59) | copy-start | bytes 983044
  14.2 38.5 %copy-start.6 = (bf16[2304]{0:T(1024)(128)(2,1)S(1)}, bf16[2304]{0:T(1024)(128)(2,1)}, u32[]{:S(2)}) copy-start(bf16[2304]{0:T(1024)(128)(2,1)} %param.8) | copy-start | bytes 13828
  14.2 49.0 %copy-start.1 = (bf16[2,64,2304]{2,1,0:T(8,128)(2,1)S(1)}, bf16[2,64,2304]{2,1,0:T(8,128)(2,1)}, u32[]{:S(2)}) copy-start(bf16[2,64,2304]{2,1,0:T(8,128)(2,1)} %dres_ref.3) | copy-start | bytes 1769476
  14.2 49.0 %copy-start.2 = (bf16[128,1280]{1,0:T(8,128)(2,1)S(1)}, bf16[128,1280]{1,0:T(8,128)(2,1)}, u32[]{:S(2)}) copy-start(bf16[128,1280]{1,0:T(8,128)(2,1)} %get-tuple-element.56.r0) | copy-start | bytes 983044
  14.2 49.0 %copy-start.3 = (bf16[128,1024]{1,0:T(8,128)(2,1)S(1)}, bf16[128,1024]{1,0:T(8,128)(2,1)}, u32[]{:S(2)}) copy-start(bf16[128,1024]{1,0:T(8,128)(2,1)} %get-tuple-element.52.p0) | copy-start | bytes 786436
  27.0 3.0 %collective-permute-start = (bf16[128,2304]{1,0:T(8,128)(2,1)S(1)}, bf16[128,2304]{1,0:T(8,128)(2,1)S(1)}, u32[]{:S(2)}, u32[]{:S(2)}) collective-permute-start(bf16[128,2304]{1,0:T(8,128)(2,1)S(1)} %get-tuple-element.47), channel_id=1, source_target_pairs={{0,1},{1,0},{2,3},{3,2},{4,5},{5,4},{6,7},{7,6}} | collective-permute-start | bytes 1769480 | tf_op jit(solution)/shard_map/ppermute | solution.py:375
  27.5 2.7 %collective-permute-start.1 = (bf16[128,2304]{1,0:T(8,128)(2,1)S(1)}, bf16[128,2304]{1,0:T(8,128)(2,1)S(1)}, u32[]{:S(2)}, u32[]{:S(2)}) collective-permute-start(bf16[128,2304]{1,0:T(8,128)(2,1)S(1)} %get-tuple-element.49), channel_id=1, source_target_pairs={{0,1},{1,0},{2,3},{3,2},{4,5},{5,4},{6,7},{7,6}} | collective-permute-start | bytes 1769480 | tf_op jit(solution)/shard_map/ppermute | solution.py:375
  27.5 4.8 %collective-permute-start.3 = (bf16[128,1024]{1,0:T(8,128)(2,1)S(1)}, bf16[128,1024]{1,0:T(8,128)(2,1)S(1)}, u32[]{:S(2)}, u32[]{:S(2)}) collective-permute-start(bf16[128,1024]{1,0:T(8,128)(2,1)S(1)} %copy-done.12), channel_id=1, source_target_pairs={{0,1},{1,0},{2,3},{3,2},{4,5},{5,4},{6,7},{7,6}} | collective-permute-start | bytes 786440 | tf_op jit(solution)/shard_map/ppermute | solution.py:375
  28.0 9.2 %collective-permute-start.4 = (bf16[128,1024]{1,0:T(8,128)(2,1)S(1)}, bf16[128,1024]{1,0:T(8,128)(2,1)S(1)}, u32[]{:S(2)}, u32[]{:S(2)}) collective-permute-start(bf16[128,1024]{1,0:T(8,128)(2,1)S(1)} %copy-done.11), channel_id=1, source_target_pairs={{0,2},{1,3},{2,0},{3,1},{4,6},{5,7},{6,4},{7,5}} | collective-permute-start | bytes 786440 | tf_op jit(solution)/shard_map/ppermute | solution.py:375
  29.9 12.3 %collective-permute-start.5 = (bf16[128,1024]{1,0:T(8,128)(2,1)S(1)}, bf16[128,1024]{1,0:T(8,128)(2,1)S(1)}, u32[]{:S(2)}, u32[]{:S(2)}) collective-permute-start(bf16[128,1024]{1,0:T(8,128)(2,1)S(1)} %copy-done.10), channel_id=1, source_target_pairs={{0,3},{1,2},{2,1},{3,0},{4,7},{5,6},{6,5},{7,4}} | collective-permute-start | bytes 786440 | tf_op jit(solution)/shard_map/ppermute | solution.py:375
  30.0 22.7 %collective-permute-start.6 = (bf16[128,1280]{1,0:T(8,128)(2,1)S(1)}, bf16[128,1280]{1,0:T(8,128)(2,1)S(1)}, u32[]{:S(2)}, u32[]{:S(2)}) collective-permute-start(bf16[128,1280]{1,0:T(8,128)(2,1)S(1)} %copy-done.9), channel_id=1, source_target_pairs={{0,1},{1,0},{2,3},{3,2},{4,5},{5,4},{6,7},{7,6}} | collective-permute-start | bytes 983048 | tf_op jit(solution)/shard_map/ppermute | solution.py:375
  30.2 22.6 %collective-permute-start.7 = (bf16[128,1280]{1,0:T(8,128)(2,1)S(1)}, bf16[128,1280]{1,0:T(8,128)(2,1)S(1)}, u32[]{:S(2)}, u32[]{:S(2)}) collective-permute-start(bf16[128,1280]{1,0:T(8,128)(2,1)S(1)} %copy-done.8), channel_id=1, source_target_pairs={{0,2},{1,3},{2,0},{3,1},{4,6},{5,7},{6,4},{7,5}} | collective-permute-start | bytes 983048 | tf_op jit(solution)/shard_map/ppermute | solution.py:375
  32.4 23.9 %collective-permute-start.8 = (bf16[128,1280]{1,0:T(8,128)(2,1)S(1)}, bf16[128,1280]{1,0:T(8,128)(2,1)S(1)}, u32[]{:S(2)}, u32[]{:S(2)}) collective-permute-start(bf16[128,1280]{1,0:T(8,128)(2,1)S(1)} %copy-done.7), channel_id=1, source_target_pairs={{0,3},{1,2},{2,1},{3,0},{4,7},{5,6},{6,5},{7,4}} | collective-permute-start | bytes 983048 | tf_op jit(solution)/shard_map/ppermute | solution.py:375
  37.2 26.0 %collective-permute-start.2 = (bf16[64,2304]{1,0:T(8,128)(2,1)S(1)}, bf16[64,2304]{1,0:T(8,128)(2,1)S(1)}, u32[]{:S(2)}, u32[]{:S(2)}) collective-permute-start(bf16[64,2304]{1,0:T(8,128)(2,1)S(1)} %get-tuple-element.51.t0), channel_id=1, source_target_pairs={{0,2},{1,3},{2,0},{3,1},{4,6},{5,7},{6,4},{7,5}} | collective-permute-start | bytes 884744 | tf_op jit(solution)/shard_map/ppermute | solution.py:375
  42.2 27.0 %collective-permute-start.10 = (bf16[64,2304]{1,0:T(8,128)(2,1)S(1)}, bf16[64,2304]{1,0:T(8,128)(2,1)S(1)}, u32[]{:S(2)}, u32[]{:S(2)}) collective-permute-start(bf16[64,2304]{1,0:T(8,128)(2,1)S(1)} %get-tuple-element.63.t1), channel_id=1, source_target_pairs={{0,2},{1,3},{2,0},{3,1},{4,6},{5,7},{6,4},{7,5}} | collective-permute-start | bytes 884744 | tf_op jit(solution)/shard_map/ppermute | solution.py:375
  63.9 23.4 %collective-permute-start.9 = (bf16[128,2304]{1,0:T(8,128)(2,1)S(1)}, bf16[128,2304]{1,0:T(8,128)(2,1)S(1)}, u32[]{:S(2)}, u32[]{:S(2)}) collective-permute-start(bf16[128,2304]{1,0:T(8,128)(2,1)S(1)} %get-tuple-element.61.refs_0_.d0.x0), channel_id=1, source_target_pairs={{0,1},{1,0},{2,3},{3,2},{4,5},{5,4},{6,7},{7,6}} | collective-permute-start | bytes 1769480 | tf_op jit(solution)/shard_map/ppermute | solution.py:375
  69.2 21.7 %copy-start = (bf16[2,256,1024]{2,1,0:T(8,128)(2,1)S(1)}, bf16[2,256,1024]{2,1,0:T(8,128)(2,1)}, u32[]{:S(2)}) copy-start(bf16[2,256,1024]{2,1,0:T(8,128)(2,1)} %du_ref.7) | copy-start | bytes 3145732
  69.3 24.7 %copy-start.5 = (s32[2,256]{1,0:T(2,128)S(1)}, s32[2,256]{1,0:T(2,128)}, u32[]{:S(2)}) copy-start(s32[2,256]{1,0:T(2,128)} %ids_ref.7) | copy-start | bytes 6148
  70.7 20.2 %slice-start = ((s8[4718592]{0:T(1024)(128)(4,1)}), s8[4194304]{0:T(1024)(128)(4,1)S(1)}, s32[]{:S(2)}) async-start(s8[4718592]{0:T(1024)(128)(4,1)} %bitcast), calls=%async_computation | async-start | bytes 8388608
  70.7 17.8 %collective-permute-start.11 = (bf16[128,2304]{1,0:T(8,128)(2,1)S(1)}, bf16[128,2304]{1,0:T(8,128)(2,1)S(1)}, u32[]{:S(2)}, u32[]{:S(2)}) collective-permute-start(bf16[128,2304]{1,0:T(8,128)(2,1)S(1)} %get-tuple-element.65.d1.x1), channel_id=1, source_target_pairs={{0,1},{1,0},{2,3},{3,2},{4,5},{5,4},{6,7},{7,6}} | collective-permute-start | bytes 1769480 | tf_op jit(solution)/shard_map/ppermute | solution.py:375
  71.2 15.6 %collective-permute-start.12 = (bf16[64,2304]{1,0:T(8,128)(2,1)S(1)}, bf16[64,2304]{1,0:T(8,128)(2,1)S(1)}, u32[]{:S(2)}, u32[]{:S(2)}) collective-permute-start(bf16[64,2304]{1,0:T(8,128)(2,1)S(1)} %get-tuple-element.68), channel_id=1, source_target_pairs={{0,2},{1,3},{2,0},{3,1},{4,6},{5,7},{6,4},{7,5}} | collective-permute-start | bytes 884744 | tf_op jit(solution)/shard_map/ppermute | solution.py:375
  73.1 14.2 %collective-permute-start.14 = (bf16[64,2304]{1,0:T(8,128)(2,1)S(1)}, bf16[64,2304]{1,0:T(8,128)(2,1)S(1)}, u32[]{:S(2)}, u32[]{:S(2)}) collective-permute-start(bf16[64,2304]{1,0:T(8,128)(2,1)S(1)} %get-tuple-element.69), channel_id=1, source_target_pairs={{0,2},{1,3},{2,0},{3,1},{4,6},{5,7},{6,4},{7,5}} | collective-permute-start | bytes 884744 | tf_op jit(solution)/shard_map/ppermute | solution.py:375
  73.3 1.2 %collective-permute-start.18 = (f32[1,2304]{1,0:T(1,128)S(1)}, f32[1,2304]{1,0:T(1,128)S(1)}, u32[]{:S(2)}, u32[]{:S(2)}) collective-permute-start(f32[1,2304]{1,0:T(1,128)S(1)} %get-tuple-element.66.tok_ref), channel_id=1, source_target_pairs={{0,1},{1,0},{2,3},{3,2},{4,5},{5,4},{6,7},{7,6}} | collective-permute-start | bytes 27656 | tf_op jit(solution)/shard_map/ppermute | solution.py:375
  74.4 12.4 %collective-permute-start.19 = (f32[1,2304]{1,0:T(1,128)S(1)}, f32[1,2304]{1,0:T(1,128)S(1)}, u32[]{:S(2)}, u32[]{:S(2)}) collective-permute-start(f32[1,2304]{1,0:T(1,128)S(1)} %add.6), channel_id=1, source_target_pairs={{0,2},{1,3},{2,0},{3,1},{4,6},{5,7},{6,4},{7,5}} | collective-permute-start | bytes 27656 | tf_op jit(solution)/shard_map/ppermute | solution.py:375
  86.8 7.1 %collective-permute-start.16 = (bf16[64,2304]{1,0:T(8,128)(2,1)S(1)}, bf16[64,2304]{1,0:T(8,128)(2,1)S(1)}, u32[]{:S(2)}, u32[]{:S(2)}) collective-permute-start(bf16[64,2304]{1,0:T(8,128)(2,1)S(1)} %get-tuple-element.51.t0), channel_id=1, source_target_pairs={{0,1},{1,0},{2,3},{3,2},{4,5},{5,4},{6,7},{7,6}} | collective-permute-start | bytes 884744 | tf_op jit(solution)/shard_map/ppermute | solution.py:375
  86.8 7.1 %collective-permute-start.17 = (bf16[64,2304]{1,0:T(8,128)(2,1)S(1)}, bf16[64,2304]{1,0:T(8,128)(2,1)S(1)}, u32[]{:S(2)}, u32[]{:S(2)}) collective-permute-start(bf16[64,2304]{1,0:T(8,128)(2,1)S(1)} %get-tuple-element.63.t1), channel_id=1, source_target_pairs={{0,1},{1,0},{2,3},{3,2},{4,5},{5,4},{6,7},{7,6}} | collective-permute-start | bytes 884744 | tf_op jit(solution)/shard_map/ppermute | solution.py:375
  87.4 6.6 %collective-permute-start.13 = (bf16[64,2304]{1,0:T(8,128)(2,1)S(1)}, bf16[64,2304]{1,0:T(8,128)(2,1)S(1)}, u32[]{:S(2)}, u32[]{:S(2)}) collective-permute-start(bf16[64,2304]{1,0:T(8,128)(2,1)S(1)} %collective-permute-done.12.c0), channel_id=1, source_target_pairs={{0,1},{1,0},{2,3},{3,2},{4,5},{5,4},{6,7},{7,6}} | collective-permute-start | bytes 884744 | tf_op jit(solution)/shard_map/ppermute | solution.py:375
  87.4 6.5 %collective-permute-start.15 = (bf16[64,2304]{1,0:T(8,128)(2,1)S(1)}, bf16[64,2304]{1,0:T(8,128)(2,1)S(1)}, u32[]{:S(2)}, u32[]{:S(2)}) collective-permute-start(bf16[64,2304]{1,0:T(8,128)(2,1)S(1)} %collective-permute-done.14.c1), channel_id=1, source_target_pairs={{0,1},{1,0},{2,3},{3,2},{4,5},{5,4},{6,7},{7,6}} | collective-permute-start | bytes 884744 | tf_op jit(solution)/shard_map/ppermute | solution.py:375
  88.5 2.4 %slice-start.1 = ((s8[4718592]{0:T(1024)(128)(4,1)}), s8[524288]{0:T(1024)(128)(4,1)S(1)}, s32[]{:S(2)}) async-start(s8[4718592]{0:T(1024)(128)(4,1)} %bitcast), calls=%async_computation.1 | async-start | bytes 1048576

commit v15 on v13

--- a/solution.py
+++ b/solution.py
@@ -97,7 +97,7 @@
     lax.fori_loop(0, n, link, 0)
 
     def lists(i, c):
-        nl, nd, nl0, nd0 = c
+        nl, nd, nl0, nd0, nl1, nd1 = c
         x = lnxt[i]
         end = (x < 0).astype(jnp.int32)
         pos = own_ref[0, i]
@@ -105,13 +105,17 @@
         list_ref[1, nl] = own_ref[1, i]
         list_ref[2, nd] = pos
         list_ref[3, nd] = own_ref[0, jnp.maximum(x, 0)]
-        near = (pos < t // 2).astype(jnp.int32)
-        near2 = (list_ref[3, nd] < t // 2).astype(jnp.int32)
-        return nl + end, nd + 1 - end, nl0 + end * near, nd0 + (1 - end) * near2
-
-    nl, nd, nl0, nd0 = lax.fori_loop(0, n, lists, (0, 0, 0, 0))
-    for a, v in enumerate((nl, nl0, nd, nd0)):
-        list_ref[a, list_ref.shape[1] - 1] = v
+        to = list_ref[3, nd]
+        dup = 1 - end
+        return (nl + end, nd + dup, nl0 + end * (pos < SEG[1]).astype(jnp.int32), nd0 + dup * (to < SEG[1]).astype(jnp.int32),
+                nl1 + end * (pos < SEG[2]).astype(jnp.int32), nd1 + dup * (to < SEG[2]).astype(jnp.int32))
+
+    nl, nd, nl0, nd0, nl1, nd1 = lax.fori_loop(0, n, lists, (0,) * 6)
+    e = list_ref.shape[1]
+    for a, v in enumerate((0, nl0, nl1, nl)):
+        list_ref[a, e - 1] = v
+    for a, v in enumerate((0, nd0, nd1, nd)):
+        list_ref[a, e - 2] = v
     zero_wait(z, de_ref, *FILL[2], sem)
 
 
@@ -124,15 +128,13 @@
     z[...] = jnp.zeros_like(z)
     zero_start(z, de_ref, *FILL[0], zsem)
     n = 0
-    for c in range(2):
-        lo = ((r >> 1) ^ c) * h
-        for m in range(k):
-            def scan(i, n):
-                j = lo + i
-                lst[n] = m * t + j
-                return n + (lax.shift_right_logical(ids_ref[m, j], vl.bit_length() - 1) == r).astype(jnp.int32)
-
-            n = lax.fori_loop(0, h, scan, n, unroll=16)
+    for m, q in ((0, r), (0, r ^ 1), (1, r), (1, r ^ 1), (0, r ^ 2), (0, r ^ 3), (1, r ^ 2), (1, r ^ 3)):
+        def scan(i, n):
+            j = q * tl + i
+            lst[n] = m * t + j
+            return n + (lax.shift_right_logical(ids_ref[m, j], vl.bit_length() - 1) == r).astype(jnp.int32)
+
+        n = lax.fori_loop(0, tl, scan, n, unroll=16)
     own_ref[0, own_ref.shape[1] - 1] = n
 
     def start(i, c):
@@ -263,74 +265,103 @@
         c.wait()
 
 
-def scatter(near, list_ref, xf, de_ref, sem):
-    e = list_ref.shape[1] - 1
-    split = xf.shape[0] if near else xf.shape[0] // 2
+SEG = (0, 256, 448, 512)
+
+
+def scatter(p, list_ref, xf, de_ref, sem):
+    e = list_ref.shape[1]
 
     def add(i, c):
         a = list_ref[2, i]
         b = list_ref[3, i]
 
-        @pl.when((b < split) if near else (b >= split))
+        @pl.when(jnp.logical_and(b >= SEG[p], b < SEG[p + 1]))
         def _():
             xf[pl.ds(b, 1), :] = xf[pl.ds(b, 1), :] + xf[pl.ds(a, 1), :]
 
         return c
 
-    @pl.when((list_ref[3, e] > 0) if near else (list_ref[2, e] > list_ref[3, e]))
+    @pl.when(repeats(p, list_ref))
     def _():
-        lax.fori_loop(0, list_ref[2, e], add, 0)
+        lax.fori_loop(0, list_ref[3, e - 2], add, 0)
 
     def put(i, c):
         pltpu.make_async_copy(xf.at[pl.ds(list_ref[0, i], 1), :], de_ref.at[pl.ds(list_ref[1, i], 1), :], sem).start()
         return c
 
-    lax.fori_loop(*((0, list_ref[1, e]) if near else (list_ref[1, e], list_ref[0, e])), put, 0)
-
-
-def scatter_wait(near, list_ref, xf, de_ref, sem):
-    e = list_ref.shape[1] - 1
+    lax.fori_loop(list_ref[p, e - 1], list_ref[p + 1, e - 1], put, 0)
+
+
+def repeats(p, list_ref):
+    e = list_ref.shape[1]
+    return list_ref[p + 1, e - 2] > list_ref[p, e - 2]
+
+
+def scatter_wait(p, list_ref, xf, de_ref, sem):
+    e = list_ref.shape[1]
 
     def wait(i, c):
         pltpu.make_async_copy(xf.at[pl.ds(0, 1), :], de_ref.at[pl.ds(0, 1), :], sem).wait()
         return c
 
-    lax.fori_loop(*((0, list_ref[1, e]) if near else (list_ref[1, e], list_ref[0, e])), wait, 0)
+    lax.fori_loop(list_ref[p, e - 1], list_ref[p + 1, e - 1], wait, 0)
 
 
 def near_kernel(list_ref, d0, a0, d1, a1, tok_ref, de_in, xn_ref, de_ref, sem):
     tl = d0.shape[0] // 2
     for a, ref in enumerate((d0, a0, d1, a1)):
         xn_ref[a * tl:(a + 1) * tl, :] = ref[tl:2 * tl, :].astype(F32)
-    scatter(True, list_ref, xn_ref, de_ref, sem)
-    scatter_wait(True, list_ref, xn_ref, de_ref, sem)
-
-
-def last_kernel(chip_rows, list_ref, xn_ref, c0, b0, c1, b1, t0, w0, t1, w1, dwp_ref, ids_ref, g_ref,
+    scatter(0, list_ref, xn_ref, de_ref, sem)
+    scatter_wait(0, list_ref, xn_ref, de_ref, sem)
+
+
+def far_n(ids_ref, m, q, own, got, g_ref, chip_rows):
+    own_x = chip_mask(ids_ref, m, q, got.shape[0], chip_rows)
+    return norm(jnp.where(own_x, own[...].astype(F32), got[...].astype(F32)), g_ref)
+
+
+def mid_kernel(chip_rows, list_ref, xn_ref, c0, b0, c1, t0, w0, t1, ids_ref, g_ref, de_in, n_ref, xm_ref, de_ref, xf, sem):
+    tl = c0.shape[0]
+    h = xn_ref.shape[0]
+    r = lax.axis_index("tp")
+
+    @pl.when(repeats(1, list_ref))
+    def _():
+        xf[0:h, :] = xn_ref[...]
+
+    for a, ref in enumerate((c0, b0, c1)):
+        xf[h + a * tl:h + (a + 1) * tl, :] = ref[...].astype(F32)
+    scatter(1, list_ref, xf, de_ref, sem)
+    for a, (m, q, own, got) in enumerate(((0, r ^ 2, t0, c0), (0, r ^ 3, w0, b0), (1, r ^ 2, t1, c1))):
+        n_ref[a * tl:(a + 1) * tl, :] = far_n(ids_ref, m, q, own, got, g_ref, chip_rows)
+    xm_ref[...] = xf[h:h + 3 * tl, :]
+    scatter_wait(1, list_ref, xf, de_ref, sem)
+
+
+def last_kernel(chip_rows, list_ref, xn_ref, xm_ref, nm_ref, b1, w1, dwp_ref, ids_ref, g_ref,
                 w_ref, du_ref, u_in, de_in, u_ref, dw_ref, de_ref, xf, n_ref, du2, ub, dwb, usem, wsem, sem):
     d = w_ref.shape[0]
-    tl = c0.shape[0]
+    tl = b1.shape[0]
     r = lax.axis_index("tp")
     h = xn_ref.shape[0]
 
-    @pl.when(list_ref[2, list_ref.shape[1] - 1] > list_ref[3, list_ref.shape[1] - 1])
+    @pl.when(repeats(2, list_ref))
     def _():
         xf[0:h, :] = xn_ref[...]
-
-    for a, ref in enumerate((c0, b0, c1, b1)):
-        xf[h + a * tl:h + (a + 1) * tl, :] = ref[...].astype(F32)
-    scatter(False, list_ref, xf, de_ref, sem)
+        xf[h:h + 3 * tl, :] = xm_ref[...]
+
+    xf[h + 3 * tl:h + 4 * tl, :] = b1[...].astype(F32)
+    scatter(2, list_ref, xf, de_ref, sem)
     take_du(du_ref, du2, tl, ((0, r ^ 2), (0, r ^ 3), (1, r ^ 2), (1, r ^ 3)))
-    for a, (m, q, own, got) in enumerate(((0, r ^ 2, t0, c0), (0, r ^ 3, w0, b0), (1, r ^ 2, t1, c1), (1, r ^ 3, w1, b1))):
-        x = jnp.where(chip_mask(ids_ref, m, q, tl, chip_rows), own[...].astype(F32), got[...].astype(F32))
-        n_ref[a * tl:(a + 1) * tl, :] = norm(x, g_ref)
+    n_ref[0:3 * tl, :] = nm_ref[...]
+    n_ref[3 * tl:4 * tl, :] = far_n(ids_ref, 1, r ^ 3, w1, b1, g_ref, chip_rows)
     blk = 256
     for i in range(d // blk):
         rows = slice(i * blk, (i + 1) * blk)
         dwb[rows, :] = dwp_ref[rows, :] + dw_tile(n_ref, du2, i, blk)
         pltpu.make_async_copy(dwb.at[pl.ds(i * blk, blk), :], dw_ref.at[pl.ds(i * blk, blk), :], wsem).start()
     copies = umat(n_ref, w_ref, ub, u_ref, r ^ 2, r ^ 3, usem)
-    scatter_wait(False, list_ref, xf, de_ref, sem)
+    scatter_wait(2, list_ref, xf, de_ref, sem)
     pltpu.make_async_copy(dwb, dw_ref, wsem).wait()
     for c in copies:
         c.wait()
@@ -386,14 +417,14 @@
         def dxk(m, xh, z, tok, more):
             outs = [S((n, d), BF16), S((tl, d), BF16), S((1, d), F32)] + ([S((k, tl, d), BF16)] if m else [])
             return call(functools.partial(dx_kernel, m, 2 * vl), 16, outs,
-                        [VMEM] * 9 + [SMEM if m else HBM] + [VMEM] * len(more),
+                        [VMEM] * 9 + [HBM] + [VMEM] * len(more),
                         [VMEM] * len(outs), [], 30 * n * d, 16 * n * d)(
                             xh, z, p0, q1, q2, q3, dres, g2, ids, tok, *more)
 
         mine0, slot0, dg0 = dxk(0, own0, z0, de, ())
         c0 = perm(slot0, cross)
         next0 = perm(mine0, sib)
-        mine1, slot1, dg, x = dxk(1, own1, z1, lists, (mine0, dg0))
+        mine1, slot1, dg, x = dxk(1, own1, z1, de, (mine0, dg0))
         c1 = perm(slot1, cross)
         next1 = perm(mine1, sib)
         u, dwp = call(
@@ -407,13 +438,17 @@
         dgs = dg + perm(dg, sib)
         dgs = dgs + perm(dgs, cross)
 
+        nm, xm, de = call(
+            functools.partial(mid_kernel, 2 * vl), 16, [S((3 * tl, d), BF16), S((3 * tl, d), F32), S((vl, d), F32)],
+            [SMEM] + [VMEM] * 9 + [HBM], [VMEM, VMEM, HBM], [pltpu.VMEM((t + 3 * tl, d), F32), D],
+            8 * h * d, 8 * h * d, {10: 2})(lists, xn, c0, b0, c1, oth0, w0, oth1, ids, g2, de)
         u, dw, de = call(
             functools.partial(last_kernel, 2 * vl), 20, [S((k, t, fc), BF16), S((d, fc), F32), S((vl, d), F32)],
-            [SMEM] + [VMEM] * 14 + [HBM] * 2, [HBM] * 3,
+            [SMEM] + [VMEM] * 10 + [HBM] * 2, [HBM] * 3,
             [pltpu.VMEM((2 * h, d), F32), pltpu.VMEM((t, d), BF16), pltpu.VMEM((t, fc), BF16), pltpu.VMEM((t, fc), BF16),
              pltpu.VMEM((d, fc), F32), D, D, D],
-            4 * t * d * fc, 6 * d * fc, {15: 0, 16: 2})(
-                lists, xn, c0, b0, c1, b1, oth0, w0, oth1, w1, dwp, ids, g2, w, du, u, de)
+            4 * t * d * fc, 6 * d * fc, {11: 0, 12: 2})(
+                lists, xn, xm, nm, b1, w1, dwp, ids, g2, w, du, u, de)
         return u, x, de, dw, dgs.reshape(d)
 
     return jax.shard_map(

time: 96.5 us -> 97.2 us (level)
    pallas_call x2 -> x3, Pallas kernels: 2.92 us -> 4.98 us  [the longest x1 2.76 us: local(): call(functools.partial(mid_kernel, 2 * vl), 16, [S((3 * tl, d), BF16), S(...]
    pallas_call x1, Pallas kernels: 6.72 us -> 5.32 us  [local(): call(functools.partial(last_kernel, 2 * vl), 20, [S((k, t, fc), BF16), S(...]
  transfers between devices with their start and end apart: 17 -> 17, of which waited for: 5 -> 5; matrix products, arithmetic and copies ran while one was open for 1% -> 1% of each run, Pallas kernels for 34% -> 36%
where the time goes in v15:
time: 97.2 us; the launch traced here: 96.7 us
  Pallas kernels  52.5 us (54%)
  waiting for transfers between devices  31.9 us (33%)
  starting transfers between devices  10 us (10%)
    ppermute x17, waiting for transfers between devices, perm(): return lax.ppermute(v, 'tp', p)  31.9 us
    pallas_call x1, Pallas kernels, local(): call(zero_kernel, 8, [S((4, 2 * h + 16), jnp.int32), S((vl, d), F32)], [S...  16.6 us
    pallas_call x1, Pallas kernels, local(): call(gather_kernel, 36, [S((n, d), BF16)] * 4 + [S((2, 2 * h + 16), jnp.i...  12.7 us
    ppermute x17, starting transfers between devices, perm(): return lax.ppermute(v, 'tp', p)  10 us
    pallas_call x1, Pallas kernels, local(): call(pdn_kernel, 60, [S((n, d), BF16)] * 4, [HBM] * 2, [HBM] * 4, [pltpu....  7.6 us
    pallas_call x1, Pallas kernels, local(): call(functools.partial(last_kernel, 2 * vl), 20, [S((k, t, fc), BF16), S(...  5.32 us
    pallas_call x1, Pallas kernels, local(): call(u_kernel, 32, [S((k, t, fc), BF16), S((d, fc), F32)], [VMEM] * 8, [H...  2.87 us
    pallas_call x1, Pallas kernels, local(): call(functools.partial(mid_kernel, 2 * vl), 16, [S((3 * tl, d), BF16), S(...  2.76 us
  transfers between devices with their start and end apart: 17, of which 5 were waited for; matrix products, arithmetic and copies ran while one was open for 1% of the time, Pallas kernels for 36%

profile of v15, /device:TPU:0, one launch (start us, length us, event | category | flops | bytes accessed | tf_op | source)
XLA Modules:
  0.0 96.7 jit_solution(3967452288694243088)
XLA Ops:
  0.6 0.0 copy-start.3
  0.6 0.7 copy-done.3
  1.3 12.7 %shard_map.101 = (bf16[128,2304]{1,0:T(8,128)(2,1)S(1)}, bf16[128,2304]{1,0:T(8,128)(2,1)S(1)}, bf16[128,2304]{1,0:T(8,128)(2,1)S(1)}, bf16[128,2304]{1,0:T(8,12...) custom-call(s32[2,256]{1,0:T(2,128)S(1)} %copy-done.3, bf16[8192,2304]{1,0:T(8,128)(2,1)} %emb_ref.1), custom_call_target="tpu_custom_call" | custom-call | flops 500000000 | bytes 9437184 | tf_op jit(solution)/shard_map/pallas_call | solution.py:396
  14.0 0.5 collective-permute-start
  14.6 0.0 collective-permute-start.1
  14.6 7.6 %shard_map.104 = (bf16[128,2304]{1,0:T(8,128)(2,1)}, bf16[128,2304]{1,0:T(8,128)(2,1)}, bf16[128,2304]{1,0:T(8,128)(2,1)}, bf16[128,2304]{1,0:T(8,128)(2,1)}) custom-call(bf16[2,256,1024]{2,1,0:T(8,128)(2,1)} %du_ref.5, bf16[2304,1024]{1,0:T(8,128)(2,1)} %w_ref.5), custom_call_target="tpu_custom_call" | custom-call | flops 2415919104 | bytes 8126464 | tf_op jit(solution)/shard_map/pallas_call | solution.py:390
  22.2 0.6 collective-permute-start.3
  22.8 1.9 %collective-permute-start.4 = (bf16[128,2304]{1,0:T(8,128)(2,1)}, bf16[128,2304]{1,0:T(8,128)(2,1)S(1)}, u32[]{:S(2)}, u32[]{:S(2)}) collective-permute-start(bf16[128,2304]{1,0:T(8,128)(2,1)} %get-tuple-element.49), channel_id=1, source_target_pairs={{0,2},{1,3},{2,0},{3,1},{4,6},{5,7},{6,4},{7,5}} | collective-permute-start | bytes 1769480 | tf_op jit(solution)/shard_map/ppermute | solution.py:388
  24.7 0.1 collective-permute-start.5
  24.8 0.0 collective-permute-done.y0
  24.8 0.0 collective-permute-done.1.y1
  24.8 0.1 shard_map.103
  24.9 1.8 %collective-permute-start.2 = (bf16[64,2304]{1,0:T(8,128)(2,1)S(1)}, bf16[64,2304]{1,0:T(8,128)(2,1)S(1)}, u32[]{:S(2)}, u32[]{:S(2)}) collective-permute-start(bf16[64,2304]{1,0:T(8,128)(2,1)S(1)} %get-tuple-element.46.t0), channel_id=1, source_target_pairs={{0,2},{1,3},{2,0},{3,1},{4,6},{5,7},{6,4},{7,5}} | collective-permute-start | bytes 884744 | tf_op jit(solution)/shard_map/ppermute | solution.py:388
  26.7 0.3 collective-permute-start.7
  27.0 0.0 copy-start.5
  27.0 0.0 copy-start
  27.0 0.0 copy-start.1
  27.0 0.0 copy-start.4
  27.0 16.6 %shard_map.102 = (s32[4,528]{1,0:T(4,128)S(1)}, f32[8192,2304]{1,0:T(8,128)}) custom-call(s32[2,528]{1,0:T(2,128)S(1)} %get-tuple-element.38.own_ref, f32[8192,2304]{1,0:T(8,128)} %get-tuple-element.39.de_in), custom_call_target="tpu_custom_call", output_to_operand_aliasing={{1}: (1, {})} | custom-call | flops 6000000000 | bytes 37748736 | tf_op jit(solution)/shard_map/pallas_call | solution.py:412
  43.5 0.0 copy-done.5
  43.6 0.0 collective-permute-done.3.p1
  43.6 0.0 collective-permute-done.4.p2
  43.6 7.8 %collective-permute-done.5.p3 = bf16[128,2304]{1,0:T(8,128)(2,1)S(1)} collective-permute-done((bf16[128,2304]{1,0:T(8,128)(2,1)}, bf16[128,2304]{1,0:T(8,128)(2,1)S(1)}, u32[]{:S(2)}, u32[]{:S(2)}) %collective-permute-start.5) | collective-permute-done | bytes 589856 | tf_op jit(solution)/shard_map/ppermute | solution.py:388
  51.4 6.8 %collective-permute-done.2.z_ref = bf16[64,2304]{1,0:T(8,128)(2,1)S(1)} collective-permute-done((bf16[64,2304]{1,0:T(8,128)(2,1)S(1)}, bf16[64,2304]{1,0:T(8,128)(2,1)S(1)}, u32[]{:S(2)}, u32[]{:S(2)}) %collective-permute-start.2) | collective-permute-done | bytes 294944 | tf_op jit(solution)/shard_map/ppermute | solution.py:388
  58.2 0.0 copy-done
  58.2 0.0 copy-done.1
  58.2 0.0 copy-done.4
  58.2 0.8 shard_map.105
  58.9 0.0 collective-permute-start.6
  59.0 5.2 %collective-permute-done.7.z_ref = bf16[64,2304]{1,0:T(8,128)(2,1)S(1)} collective-permute-done((bf16[64,2304]{1,0:T(8,128)(2,1)S(1)}, bf16[64,2304]{1,0:T(8,128)(2,1)S(1)}, u32[]{:S(2)}, u32[]{:S(2)}) %collective-permute-start.7) | collective-permute-done | bytes 294944 | tf_op jit(solution)/shard_map/ppermute | solution.py:388
  64.2 1.5 %shard_map.106 = (bf16[128,2304]{1,0:T(8,128)(2,1)S(1)}, bf16[64,2304]{1,0:T(8,128)(2,1)S(1)}, f32[1,2304]{1,0:T(1,128)S(1)}, bf16[2,64,2304]{2,1,0:T(8,128)(2,1)}) custom-call(bf16[64,2304]{1,0:T(8,128)(2,1)S(1)} %get-tuple-element.53.xh_ref, bf16[64,2304]{1,0:T(8,128)(2,1)S(1)} %collective-permute-done.7.z_ref, bf16[128,2304]{1,0:T(8,128)(2,1)S(1)} %copy-done.1, ...), custom_call_target="tpu_custom_call" | custom-call | flops 8847360 | bytes 4718592 | tf_op jit(solution)/shard_map/pallas_call | solution.py:419
  65.6 0.0 collective-permute-start.8
  65.6 1.7 %collective-permute-start.9 = (bf16[64,2304]{1,0:T(8,128)(2,1)S(1)}, bf16[64,2304]{1,0:T(8,128)(2,1)S(1)}, u32[]{:S(2)}, u32[]{:S(2)}) collective-permute-start(bf16[64,2304]{1,0:T(8,128)(2,1)S(1)} %get-tuple-element.59), channel_id=1, source_target_pairs={{0,2},{1,3},{2,0},{3,1},{4,6},{5,7},{6,4},{7,5}} | collective-permute-start | bytes 884744 | tf_op jit(solution)/shard_map/ppermute | solution.py:388
  67.4 0.3 collective-permute-start.11
  67.6 0.0 collective-permute-start.15
  67.6 1.2 %collective-permute-done.15 = f32[1,2304]{1,0:T(1,128)S(1)} collective-permute-done((f32[1,2304]{1,0:T(1,128)S(1)}, f32[1,2304]{1,0:T(1,128)S(1)}, u32[]{:S(2)}, u32[]{:S(2)}) %collective-permute-start.15) | collective-permute-done | bytes 9248 | tf_op jit(solution)/shard_map/ppermute | solution.py:388
  68.8 1.8 %collective-permute-start.16 = (f32[1,2304]{1,0:T(1,128)S(1)}, f32[1,2304]{1,0:T(1,128)S(1)}, u32[]{:S(2)}, u32[]{:S(2)}) collective-permute-start(f32[1,2304]{1,0:T(1,128)S(1)} %add.6), channel_id=1, source_target_pairs={{0,2},{1,3},{2,0},{3,1},{4,6},{5,7},{6,4},{7,5}} | collective-permute-start | bytes 27656 | tf_op jit(solution)/shard_map/ppermute | solution.py:388
  70.6 11.0 %collective-permute-done.16 = f32[1,2304]{1,0:T(1,128)S(1)} collective-permute-done((f32[1,2304]{1,0:T(1,128)S(1)}, f32[1,2304]{1,0:T(1,128)S(1)}, u32[]{:S(2)}, u32[]{:S(2)}) %collective-permute-start.16) | collective-permute-done | bytes 9248 | tf_op jit(solution)/shard_map/ppermute | solution.py:388
  81.6 0.0 collective-permute-start.12
  81.6 0.0 collective-permute-done.9.c0
  81.6 0.5 collective-permute-start.10
  82.1 0.0 collective-permute-done.11.c1
  82.1 0.0 collective-permute-start.14
  82.1 0.0 collective-permute-done.6.a0.y0
  82.1 0.5 collective-permute-start.13
  82.6 0.6 add_reduce_fusion
  83.2 0.0 collective-permute-done.8.a1.y1
  83.2 0.0 slice-start
  83.2 2.4 %shard_map.107 = (f32[256,2304]{1,0:T(8,128)S(1)}, f32[8192,2304]{1,0:T(8,128)}) custom-call(s32[4,528]{1,0:T(4,128)S(1)} %get-tuple-element.40.list_ref, bf16[128,2304]{1,0:T(8,128)(2,1)S(1)} %get-tuple-element.52.refs_0_.d0.x0, bf16[128,2304]{1,0:T(8,128)(2,1)S(1)} %collective-permute-done.6.a0.y0, ...), custom_call_target="tpu_custom_call", output_to_operand_aliasing={{1}: (6, {})} | custom-call | flops 4718592 | bytes 4718592 | tf_op jit(solution)/shard_map/pallas_call | solution.py:434
  85.6 0.0 collective-permute-done.12.w0
  85.6 0.0 collective-permute-done.10.b0
  85.7 0.0 slice-start.1
  85.7 0.0 copy-start.2
  85.7 2.8 %shard_map.108 = (bf16[192,2304]{1,0:T(8,128)(2,1)S(1)}, f32[192,2304]{1,0:T(8,128)S(1)}, f32[8192,2304]{1,0:T(8,128)}) custom-call(s32[4,528]{1,0:T(4,128)S(1)} %get-tuple-element.40.list_ref, f32[256,2304]{1,0:T(8,128)S(1)} %get-tuple-element.58.xn_ref, bf16[64,2304]{1,0:T(8,128)(2,1)S(1)} %collective-permute-done.9.c0, ...), custom_call_target="tpu_custom_call", output_to_operand_aliasing={{2}: (10, {})} | custom-call | flops 4718592 | bytes 4718592 | tf_op jit(solution)/shard_map/pallas_call | solution.py:441
  88.4 0.0 slice-done
  88.5 0.0 slice-done.1
  88.5 0.0 copy-done.2
  88.5 2.9 %shard_map.109 = (bf16[2,256,1024]{2,1,0:T(8,128)(2,1)}, f32[2304,1024]{1,0:T(8,128)S(1)}) custom-call(bf16[128,2304]{1,0:T(8,128)(2,1)S(1)} %get-tuple-element.52.refs_0_.d0.x0, bf16[128,2304]{1,0:T(8,128)(2,1)S(1)} %collective-permute-done.6.a0.y0, bf16[128,2304]{1,0:T(8,128)(2,1)S(1)} %get-tuple-element.56.d1.x1, ...), custom_call_target="tpu_custom_call" | custom-call | flops 2415919104 | bytes 4718592 | tf_op jit(solution)/shard_map/pallas_call | solution.py:430
  91.4 0.0 collective-permute-done.14.w1
  91.4 0.0 collective-permute-done.13.b1
  91.4 5.3 %shard_map.110 = (bf16[2,256,1024]{2,1,0:T(8,128)(2,1)}, f32[2304,1024]{1,0:T(8,128)}, f32[8192,2304]{1,0:T(8,128)}) custom-call(s32[4,528]{1,0:T(4,128)S(1)} %get-tuple-element.40.list_ref, f32[256,2304]{1,0:T(8,128)S(1)} %get-tuple-element.58.xn_ref, f32[192,2304]{1,0:T(8,128)S(1)} %get-tuple-element.62.xm_ref, ...), custom_call_target="tpu_custom_call", output_to_operand_aliasing={{0}: (11, {}), {2}: (12, {})} | custom-call | flops 2415919104 | bytes 14155776 | tf_op jit(solution)/shard_map/pallas_call | solution.py:445
  (3 shorter events, 0.0 us)
Async XLA Ops:
  0.6 0.7 copy-start.3
  14.0 10.8 %collective-permute-start = (bf16[128,2304]{1,0:T(8,128)(2,1)S(1)}, bf16[128,2304]{1,0:T(8,128)(2,1)S(1)}, u32[]{:S(2)}, u32[]{:S(2)}) collective-permute-start(bf16[128,2304]{1,0:T(8,128)(2,1)S(1)} %get-tuple-element.42), channel_id=1, source_target_pairs={{0,1},{1,0},{2,3},{3,2},{4,5},{5,4},{6,7},{7,6}} | collective-permute-start | bytes 1769480 | tf_op jit(solution)/shard_map/ppermute | solution.py:388
  14.6 10.2 %collective-permute-start.1 = (bf16[128,2304]{1,0:T(8,128)(2,1)S(1)}, bf16[128,2304]{1,0:T(8,128)(2,1)S(1)}, u32[]{:S(2)}, u32[]{:S(2)}) collective-permute-start(bf16[128,2304]{1,0:T(8,128)(2,1)S(1)} %get-tuple-element.44), channel_id=1, source_target_pairs={{0,1},{1,0},{2,3},{3,2},{4,5},{5,4},{6,7},{7,6}} | collective-permute-start | bytes 1769480 | tf_op jit(solution)/shard_map/ppermute | solution.py:388
  22.2 21.3 %collective-permute-start.3 = (bf16[128,2304]{1,0:T(8,128)(2,1)}, bf16[128,2304]{1,0:T(8,128)(2,1)S(1)}, u32[]{:S(2)}, u32[]{:S(2)}) collective-permute-start(bf16[128,2304]{1,0:T(8,128)(2,1)} %get-tuple-element.48), channel_id=1, source_target_pairs={{0,1},{1,0},{2,3},{3,2},{4,5},{5,4},{6,7},{7,6}} | collective-permute-start | bytes 1769480 | tf_op jit(solution)/shard_map/ppermute | solution.py:388
  22.8 20.8 %collective-permute-start.4 = (bf16[128,2304]{1,0:T(8,128)(2,1)}, bf16[128,2304]{1,0:T(8,128)(2,1)S(1)}, u32[]{:S(2)}, u32[]{:S(2)}) collective-permute-start(bf16[128,2304]{1,0:T(8,128)(2,1)} %get-tuple-element.49), channel_id=1, source_target_pairs={{0,2},{1,3},{2,0},{3,1},{4,6},{5,7},{6,4},{7,5}} | collective-permute-start | bytes 1769480 | tf_op jit(solution)/shard_map/ppermute | solution.py:388
  24.7 26.7 %collective-permute-start.5 = (bf16[128,2304]{1,0:T(8,128)(2,1)}, bf16[128,2304]{1,0:T(8,128)(2,1)S(1)}, u32[]{:S(2)}, u32[]{:S(2)}) collective-permute-start(bf16[128,2304]{1,0:T(8,128)(2,1)} %get-tuple-element.50), channel_id=1, source_target_pairs={{0,3},{1,2},{2,1},{3,0},{4,7},{5,6},{6,5},{7,4}} | collective-permute-start | bytes 1769480 | tf_op jit(solution)/shard_map/ppermute | solution.py:388
  24.9 33.2 %collective-permute-start.2 = (bf16[64,2304]{1,0:T(8,128)(2,1)S(1)}, bf16[64,2304]{1,0:T(8,128)(2,1)S(1)}, u32[]{:S(2)}, u32[]{:S(2)}) collective-permute-start(bf16[64,2304]{1,0:T(8,128)(2,1)S(1)} %get-tuple-element.46.t0), channel_id=1, source_target_pairs={{0,2},{1,3},{2,0},{3,1},{4,6},{5,7},{6,4},{7,5}} | collective-permute-start | bytes 884744 | tf_op jit(solution)/shard_map/ppermute | solution.py:388
  26.7 37.5 %collective-permute-start.7 = (bf16[64,2304]{1,0:T(8,128)(2,1)S(1)}, bf16[64,2304]{1,0:T(8,128)(2,1)S(1)}, u32[]{:S(2)}, u32[]{:S(2)}) collective-permute-start(bf16[64,2304]{1,0:T(8,128)(2,1)S(1)} %get-tuple-element.54.t1), channel_id=1, source_target_pairs={{0,2},{1,3},{2,0},{3,1},{4,6},{5,7},{6,4},{7,5}} | collective-permute-start | bytes 884744 | tf_op jit(solution)/shard_map/ppermute | solution.py:388
  27.0 16.6 %copy-start.5 = (bf16[2304]{0:T(1024)(128)(2,1)S(1)}, bf16[2304]{0:T(1024)(128)(2,1)}, u32[]{:S(2)}) copy-start(bf16[2304]{0:T(1024)(128)(2,1)} %param.8) | copy-start | bytes 13828
  27.0 31.2 %copy-start = (bf16[2,64,2304]{2,1,0:T(8,128)(2,1)S(1)}, bf16[2,64,2304]{2,1,0:T(8,128)(2,1)}, u32[]{:S(2)}) copy-start(bf16[2,64,2304]{2,1,0:T(8,128)(2,1)} %dres_ref.3) | copy-start | bytes 1769476
  27.0 31.2 %copy-start.1 = (bf16[128,2304]{1,0:T(8,128)(2,1)S(1)}, bf16[128,2304]{1,0:T(8,128)(2,1)}, u32[]{:S(2)}) copy-start(bf16[128,2304]{1,0:T(8,128)(2,1)} %get-tuple-element.47.p0) | copy-start | bytes 1769476
  27.0 31.2 %copy-start.4 = (s32[2,256]{1,0:T(2,128)S(1)}, s32[2,256]{1,0:T(2,128)}, u32[]{:S(2)}) copy-start(s32[2,256]{1,0:T(2,128)} %ids_ref.9) | copy-start | bytes 6148
  58.9 23.2 %collective-permute-start.6 = (bf16[128,2304]{1,0:T(8,128)(2,1)S(1)}, bf16[128,2304]{1,0:T(8,128)(2,1)S(1)}, u32[]{:S(2)}, u32[]{:S(2)}) collective-permute-start(bf16[128,2304]{1,0:T(8,128)(2,1)S(1)} %get-tuple-element.52.refs_0_.d0.x0), channel_id=1, source_target_pairs={{0,1},{1,0},{2,3},{3,2},{4,5},{5,4},{6,7},{7,6}} | collective-permute-start | bytes 1769480 | tf_op jit(solution)/shard_map/ppermute | solution.py:388
  65.6 17.6 %collective-permute-start.8 = (bf16[128,2304]{1,0:T(8,128)(2,1)S(1)}, bf16[128,2304]{1,0:T(8,128)(2,1)S(1)}, u32[]{:S(2)}, u32[]{:S(2)}) collective-permute-start(bf16[128,2304]{1,0:T(8,128)(2,1)S(1)} %get-tuple-element.56.d1.x1), channel_id=1, source_target_pairs={{0,1},{1,0},{2,3},{3,2},{4,5},{5,4},{6,7},{7,6}} | collective-permute-start | bytes 1769480 | tf_op jit(solution)/shard_map/ppermute | solution.py:388
  65.6 15.9 %collective-permute-start.9 = (bf16[64,2304]{1,0:T(8,128)(2,1)S(1)}, bf16[64,2304]{1,0:T(8,128)(2,1)S(1)}, u32[]{:S(2)}, u32[]{:S(2)}) collective-permute-start(bf16[64,2304]{1,0:T(8,128)(2,1)S(1)} %get-tuple-element.59), channel_id=1, source_target_pairs={{0,2},{1,3},{2,0},{3,1},{4,6},{5,7},{6,4},{7,5}} | collective-permute-start | bytes 884744 | tf_op jit(solution)/shard_map/ppermute | solution.py:388
  67.4 14.7 %collective-permute-start.11 = (bf16[64,2304]{1,0:T(8,128)(2,1)S(1)}, bf16[64,2304]{1,0:T(8,128)(2,1)S(1)}, u32[]{:S(2)}, u32[]{:S(2)}) collective-permute-start(bf16[64,2304]{1,0:T(8,128)(2,1)S(1)} %get-tuple-element.60), channel_id=1, source_target_pairs={{0,2},{1,3},{2,0},{3,1},{4,6},{5,7},{6,4},{7,5}} | collective-permute-start | bytes 884744 | tf_op jit(solution)/shard_map/ppermute | solution.py:388
  67.6 1.2 %collective-permute-start.15 = (f32[1,2304]{1,0:T(1,128)S(1)}, f32[1,2304]{1,0:T(1,128)S(1)}, u32[]{:S(2)}, u32[]{:S(2)}) collective-permute-start(f32[1,2304]{1,0:T(1,128)S(1)} %get-tuple-element.57.tok_ref), channel_id=1, source_target_pairs={{0,1},{1,0},{2,3},{3,2},{4,5},{5,4},{6,7},{7,6}} | collective-permute-start | bytes 27656 | tf_op jit(solution)/shard_map/ppermute | solution.py:388
  68.8 12.7 %collective-permute-start.16 = (f32[1,2304]{1,0:T(1,128)S(1)}, f32[1,2304]{1,0:T(1,128)S(1)}, u32[]{:S(2)}, u32[]{:S(2)}) collective-permute-start(f32[1,2304]{1,0:T(1,128)S(1)} %add.6), channel_id=1, source_target_pairs={{0,2},{1,3},{2,0},{3,1},{4,6},{5,7},{6,4},{7,5}} | collective-permute-start | bytes 27656 | tf_op jit(solution)/shard_map/ppermute | solution.py:388
  81.6 4.1 %collective-permute-start.12 = (bf16[64,2304]{1,0:T(8,128)(2,1)S(1)}, bf16[64,2304]{1,0:T(8,128)(2,1)S(1)}, u32[]{:S(2)}, u32[]{:S(2)}) collective-permute-start(bf16[64,2304]{1,0:T(8,128)(2,1)S(1)} %get-tuple-element.46.t0), channel_id=1, source_target_pairs={{0,1},{1,0},{2,3},{3,2},{4,5},{5,4},{6,7},{7,6}} | collective-permute-start | bytes 884744 | tf_op jit(solution)/shard_map/ppermute | solution.py:388
  81.6 4.1 %collective-permute-start.10 = (bf16[64,2304]{1,0:T(8,128)(2,1)S(1)}, bf16[64,2304]{1,0:T(8,128)(2,1)S(1)}, u32[]{:S(2)}, u32[]{:S(2)}) collective-permute-start(bf16[64,2304]{1,0:T(8,128)(2,1)S(1)} %collective-permute-done.9.c0), channel_id=1, source_target_pairs={{0,1},{1,0},{2,3},{3,2},{4,5},{5,4},{6,7},{7,6}} | collective-permute-start | bytes 884744 | tf_op jit(solution)/shard_map/ppermute | solution.py:388
  82.1 9.3 %collective-permute-start.14 = (bf16[64,2304]{1,0:T(8,128)(2,1)S(1)}, bf16[64,2304]{1,0:T(8,128)(2,1)S(1)}, u32[]{:S(2)}, u32[]{:S(2)}) collective-permute-start(bf16[64,2304]{1,0:T(8,128)(2,1)S(1)} %get-tuple-element.54.t1), channel_id=1, source_target_pairs={{0,1},{1,0},{2,3},{3,2},{4,5},{5,4},{6,7},{7,6}} | collective-permute-start | bytes 884744 | tf_op jit(solution)/shard_map/ppermute | solution.py:388
  82.1 9.3 %collective-permute-start.13 = (bf16[64,2304]{1,0:T(8,128)(2,1)S(1)}, bf16[64,2304]{1,0:T(8,128)(2,1)S(1)}, u32[]{:S(2)}, u32[]{:S(2)}) collective-permute-start(bf16[64,2304]{1,0:T(8,128)(2,1)S(1)} %collective-permute-done.11.c1), channel_id=1, source_target_pairs={{0,1},{1,0},{2,3},{3,2},{4,5},{5,4},{6,7},{7,6}} | collective-permute-start | bytes 884744 | tf_op jit(solution)/shard_map/ppermute | solution.py:388
  83.2 5.2 %slice-start = ((s8[4718592]{0:T(1024)(128)(4,1)}), s8[4194304]{0:T(1024)(128)(4,1)S(1)}, s32[]{:S(2)}) async-start(s8[4718592]{0:T(1024)(128)(4,1)} %bitcast), calls=%async_computation | async-start | bytes 8388608
  85.7 2.8 %slice-start.1 = ((s8[4718592]{0:T(1024)(128)(4,1)}), s8[524288]{0:T(1024)(128)(4,1)S(1)}, s32[]{:S(2)}) async-start(s8[4718592]{0:T(1024)(128)(4,1)} %bitcast), calls=%async_computation.1 | async-start | bytes 1048576
  85.7 2.8 %copy-start.2 = (bf16[2,256,1024]{2,1,0:T(8,128)(2,1)S(1)}, bf16[2,256,1024]{2,1,0:T(8,128)(2,1)}, u32[]{:S(2)}) copy-start(bf16[2,256,1024]{2,1,0:T(8,128)(2,1)} %du_ref.5) | copy-start | bytes 3145732

commit v16 on v15

--- a/solution.py
+++ b/solution.py
@@ -34,7 +34,7 @@
     dub, dup, wb, ob, dsem, wsem, osem = refs[4:]
     n, d = outs[0].shape
     k, tl = dub.shape[0], dub.shape[1] // 4
-    blk = 256
+    blk = 768
     nb = d // blk
     dc = pltpu.make_async_copy(du_ref, dub, dsem)
     dc.start()
@@ -390,7 +390,7 @@
         p2, p3, p1, p0 = call(
             pdn_kernel, 60, [S((n, d), BF16)] * 4, [HBM] * 2, [HBM] * 4,
             [pltpu.VMEM((k, t, fc), BF16), pltpu.VMEM((4 * n, fc), BF16), pltpu.VMEM((d, fc), BF16), pltpu.VMEM((4 * n, d), BF16),
-             D, D((d // 256,)), D], 8 * n * fc * d, 2 * d * fc + 8 * n * (fc + d))(du, w)
+             D, D((d // 768,)), D], 8 * n * fc * d, 2 * d * fc + 8 * n * (fc + d))(du, w)
         q2 = perm(p2, cross)
         q3 = perm(p3, diag)
         k0, s0, k1, s1, owned, de = call(
@@ -435,8 +435,8 @@
                       [D], 8 * h * d, 8 * h * d, {6: 1})(lists, mine0, next0, mine1, next1, dg, de)
         b0 = perm(c0, sib)
         b1 = perm(c1, sib)
-        dgs = dg + perm(dg, sib)
-        dgs = dgs + perm(dgs, cross)
+        dgs = dg + perm(dg, cross)
+        dgs = dgs + perm(dgs, sib)
 
         nm, xm, de = call(
             functools.partial(mid_kernel, 2 * vl), 16, [S((3 * tl, d), BF16), S((3 * tl, d), F32), S((vl, d), F32)],

time: 97.2 us -> 96.9 us (level)
  Pallas kernels: 52.5 us -> 51.2 us
  waiting for transfers between devices: 31.9 us -> 33.1 us
    pallas_call x1, Pallas kernels: 7.6 us -> 6.24 us  [local(): call(pdn_kernel, 60, [S((n, d), BF16)] * 4, [HBM] * 2, [HBM] * 4, [pltpu....]
    ppermute x17, waiting for transfers between devices: 31.9 us -> 33.1 us  [perm(): return lax.ppermute(v, 'tp', p)]
  transfers between devices with their start and end apart: 17 -> 17, of which waited for: 5 -> 5; matrix products, arithmetic and copies ran while one was open for 1% -> 1% of each run, Pallas kernels for 36% -> 34%
where the time goes in v16:
time: 96.9 us; the launch traced here: 96.5 us
  Pallas kernels  51.2 us (53%)
  waiting for transfers between devices  33.1 us (34%)
  starting transfers between devices  9.95 us (10%)
    ppermute x17, waiting for transfers between devices, perm(): return lax.ppermute(v, 'tp', p)  33.1 us
    pallas_call x1, Pallas kernels, local(): call(zero_kernel, 8, [S((4, 2 * h + 16), jnp.int32), S((vl, d), F32)], [S...  16.6 us
    pallas_call x1, Pallas kernels, local(): call(gather_kernel, 36, [S((n, d), BF16)] * 4 + [S((2, 2 * h + 16), jnp.i...  12.7 us
    ppermute x17, starting transfers between devices, perm(): return lax.ppermute(v, 'tp', p)  9.95 us
    pallas_call x1, Pallas kernels, local(): call(pdn_kernel, 60, [S((n, d), BF16)] * 4, [HBM] * 2, [HBM] * 4, [pltpu....  6.24 us
    pallas_call x1, Pallas kernels, local(): call(functools.partial(last_kernel, 2 * vl), 20, [S((k, t, fc), BF16), S(...  5.32 us
    pallas_call x1, Pallas kernels, local(): call(u_kernel, 32, [S((k, t, fc), BF16), S((d, fc), F32)], [VMEM] * 8, [H...  2.87 us
    pallas_call x1, Pallas kernels, local(): call(functools.partial(mid_kernel, 2 * vl), 16, [S((3 * tl, d), BF16), S(...  2.76 us
  transfers between devices with their start and end apart: 17, of which 5 were waited for; matrix products, arithmetic and copies ran while one was open for 1% of the time, Pallas kernels for 34%

profile of v16, /device:TPU:0, one launch (start us, length us, event | category | flops | bytes accessed | tf_op | source)
XLA Modules:
  0.0 96.5 jit_solution(8736434324685968343)
XLA Ops:
  0.6 0.0 copy-start.3
  0.6 0.7 copy-done.3
  1.3 12.7 %shard_map.101 = (bf16[128,2304]{1,0:T(8,128)(2,1)S(1)}, bf16[128,2304]{1,0:T(8,128)(2,1)S(1)}, bf16[128,2304]{1,0:T(8,128)(2,1)S(1)}, bf16[128,2304]{1,0:T(8,12...) custom-call(s32[2,256]{1,0:T(2,128)S(1)} %copy-done.3, bf16[8192,2304]{1,0:T(8,128)(2,1)} %emb_ref.1), custom_call_target="tpu_custom_call" | custom-call | flops 500000000 | bytes 9437184 | tf_op jit(solution)/shard_map/pallas_call | solution.py:396
  14.0 0.5 collective-permute-start
  14.6 0.0 collective-permute-start.1
  14.6 6.2 %shard_map.104 = (bf16[128,2304]{1,0:T(8,128)(2,1)}, bf16[128,2304]{1,0:T(8,128)(2,1)}, bf16[128,2304]{1,0:T(8,128)(2,1)}, bf16[128,2304]{1,0:T(8,128)(2,1)}) custom-call(bf16[2,256,1024]{2,1,0:T(8,128)(2,1)} %du_ref.5, bf16[2304,1024]{1,0:T(8,128)(2,1)} %w_ref.5), custom_call_target="tpu_custom_call" | custom-call | flops 2415919104 | bytes 8126464 | tf_op jit(solution)/shard_map/pallas_call | solution.py:390
  20.9 0.5 collective-permute-start.3
  21.3 1.9 %collective-permute-start.4 = (bf16[128,2304]{1,0:T(8,128)(2,1)}, bf16[128,2304]{1,0:T(8,128)(2,1)S(1)}, u32[]{:S(2)}, u32[]{:S(2)}) collective-permute-start(bf16[128,2304]{1,0:T(8,128)(2,1)} %get-tuple-element.49), channel_id=1, source_target_pairs={{0,2},{1,3},{2,0},{3,1},{4,6},{5,7},{6,4},{7,5}} | collective-permute-start | bytes 1769480 | tf_op jit(solution)/shard_map/ppermute | solution.py:388
  23.3 0.1 collective-permute-start.5
  23.3 0.0 collective-permute-done.y0
  23.3 0.0 collective-permute-done.1.y1
  23.3 0.1 shard_map.103
  23.5 1.8 %collective-permute-start.2 = (bf16[64,2304]{1,0:T(8,128)(2,1)S(1)}, bf16[64,2304]{1,0:T(8,128)(2,1)S(1)}, u32[]{:S(2)}, u32[]{:S(2)}) collective-permute-start(bf16[64,2304]{1,0:T(8,128)(2,1)S(1)} %get-tuple-element.46.t0), channel_id=1, source_target_pairs={{0,2},{1,3},{2,0},{3,1},{4,6},{5,7},{6,4},{7,5}} | collective-permute-start | bytes 884744 | tf_op jit(solution)/shard_map/ppermute | solution.py:388
  25.2 0.3 collective-permute-start.7
  25.5 0.0 copy-start.5
  25.5 0.0 copy-start
  25.5 0.0 copy-start.1
  25.5 0.0 copy-start.4
  25.5 16.6 %shard_map.102 = (s32[4,528]{1,0:T(4,128)S(1)}, f32[8192,2304]{1,0:T(8,128)}) custom-call(s32[2,528]{1,0:T(2,128)S(1)} %get-tuple-element.38.own_ref, f32[8192,2304]{1,0:T(8,128)} %get-tuple-element.39.de_in), custom_call_target="tpu_custom_call", output_to_operand_aliasing={{1}: (1, {})} | custom-call | flops 6000000000 | bytes 37748736 | tf_op jit(solution)/shard_map/pallas_call | solution.py:412
  42.1 0.0 copy-done.5
  42.1 0.0 collective-permute-done.3.p1
  42.1 0.0 collective-permute-done.4.p2
  42.1 7.8 %collective-permute-done.5.p3 = bf16[128,2304]{1,0:T(8,128)(2,1)S(1)} collective-permute-done((bf16[128,2304]{1,0:T(8,128)(2,1)}, bf16[128,2304]{1,0:T(8,128)(2,1)S(1)}, u32[]{:S(2)}, u32[]{:S(2)}) %collective-permute-start.5) | collective-permute-done | bytes 589856 | tf_op jit(solution)/shard_map/ppermute | solution.py:388
  49.9 6.8 %collective-permute-done.2.z_ref = bf16[64,2304]{1,0:T(8,128)(2,1)S(1)} collective-permute-done((bf16[64,2304]{1,0:T(8,128)(2,1)S(1)}, bf16[64,2304]{1,0:T(8,128)(2,1)S(1)}, u32[]{:S(2)}, u32[]{:S(2)}) %collective-permute-start.2) | collective-permute-done | bytes 294944 | tf_op jit(solution)/shard_map/ppermute | solution.py:388
  56.7 0.0 copy-done
  56.7 0.0 copy-done.1
  56.7 0.0 copy-done.4
  56.7 0.8 shard_map.105
  57.5 0.0 collective-permute-start.6
  57.5 5.2 %collective-permute-done.7.z_ref = bf16[64,2304]{1,0:T(8,128)(2,1)S(1)} collective-permute-done((bf16[64,2304]{1,0:T(8,128)(2,1)S(1)}, bf16[64,2304]{1,0:T(8,128)(2,1)S(1)}, u32[]{:S(2)}, u32[]{:S(2)}) %collective-permute-start.7) | collective-permute-done | bytes 294944 | tf_op jit(solution)/shard_map/ppermute | solution.py:388
  62.7 1.5 %shard_map.106 = (bf16[128,2304]{1,0:T(8,128)(2,1)S(1)}, bf16[64,2304]{1,0:T(8,128)(2,1)S(1)}, f32[1,2304]{1,0:T(1,128)S(1)}, bf16[2,64,2304]{2,1,0:T(8,128)(2,1)}) custom-call(bf16[64,2304]{1,0:T(8,128)(2,1)S(1)} %get-tuple-element.53.xh_ref, bf16[64,2304]{1,0:T(8,128)(2,1)S(1)} %collective-permute-done.7.z_ref, bf16[128,2304]{1,0:T(8,128)(2,1)S(1)} %copy-done.1, ...), custom_call_target="tpu_custom_call" | custom-call | flops 8847360 | bytes 4718592 | tf_op jit(solution)/shard_map/pallas_call | solution.py:419
  64.2 0.0 collective-permute-start.8
  64.2 1.7 %collective-permute-start.9 = (bf16[64,2304]{1,0:T(8,128)(2,1)S(1)}, bf16[64,2304]{1,0:T(8,128)(2,1)S(1)}, u32[]{:S(2)}, u32[]{:S(2)}) collective-permute-start(bf16[64,2304]{1,0:T(8,128)(2,1)S(1)} %get-tuple-element.59), channel_id=1, source_target_pairs={{0,2},{1,3},{2,0},{3,1},{4,6},{5,7},{6,4},{7,5}} | collective-permute-start | bytes 884744 | tf_op jit(solution)/shard_map/ppermute | solution.py:388
  65.9 0.3 collective-permute-start.11
  66.2 1.7 %collective-permute-start.15 = (f32[1,2304]{1,0:T(1,128)S(1)}, f32[1,2304]{1,0:T(1,128)S(1)}, u32[]{:S(2)}, u32[]{:S(2)}) collective-permute-start(f32[1,2304]{1,0:T(1,128)S(1)} %get-tuple-element.57.tok_ref), channel_id=1, source_target_pairs={{0,2},{1,3},{2,0},{3,1},{4,6},{5,7},{6,4},{7,5}} | collective-permute-start | bytes 27656 | tf_op jit(solution)/shard_map/ppermute | solution.py:388
  67.9 12.2 %collective-permute-done.15 = f32[1,2304]{1,0:T(1,128)S(1)} collective-permute-done((f32[1,2304]{1,0:T(1,128)S(1)}, f32[1,2304]{1,0:T(1,128)S(1)}, u32[]{:S(2)}, u32[]{:S(2)}) %collective-permute-start.15) | collective-permute-done | bytes 9248 | tf_op jit(solution)/shard_map/ppermute | solution.py:388
  80.1 0.0 collective-permute-start.16
  80.2 1.2 %collective-permute-done.16 = f32[1,2304]{1,0:T(1,128)S(1)} collective-permute-done((f32[1,2304]{1,0:T(1,128)S(1)}, f32[1,2304]{1,0:T(1,128)S(1)}, u32[]{:S(2)}, u32[]{:S(2)}) %collective-permute-start.16) | collective-permute-done | bytes 9248 | tf_op jit(solution)/shard_map/ppermute | solution.py:388
  81.3 0.2 collective-permute-start.12
  81.5 0.0 collective-permute-done.9.c0
  81.5 0.3 collective-permute-start.10
  81.8 0.0 collective-permute-done.11.c1
  81.8 0.2 collective-permute-start.14
  82.0 0.0 collective-permute-done.6.a0.y0
  82.0 0.3 collective-permute-start.13
  82.4 0.6 add_reduce_fusion
  83.0 0.0 collective-permute-done.8.a1.y1
  83.0 0.0 slice-start
  83.0 2.4 %shard_map.107 = (f32[256,2304]{1,0:T(8,128)S(1)}, f32[8192,2304]{1,0:T(8,128)}) custom-call(s32[4,528]{1,0:T(4,128)S(1)} %get-tuple-element.40.list_ref, bf16[128,2304]{1,0:T(8,128)(2,1)S(1)} %get-tuple-element.52.refs_0_.d0.x0, bf16[128,2304]{1,0:T(8,128)(2,1)S(1)} %collective-permute-done.6.a0.y0, ...), custom_call_target="tpu_custom_call", output_to_operand_aliasing={{1}: (6, {})} | custom-call | flops 4718592 | bytes 4718592 | tf_op jit(solution)/shard_map/pallas_call | solution.py:434
  85.4 0.0 collective-permute-done.12.w0
  85.4 0.0 collective-permute-done.10.b0
  85.4 0.0 slice-start.1
  85.4 0.0 copy-start.2
  85.4 2.8 %shard_map.108 = (bf16[192,2304]{1,0:T(8,128)(2,1)S(1)}, f32[192,2304]{1,0:T(8,128)S(1)}, f32[8192,2304]{1,0:T(8,128)}) custom-call(s32[4,528]{1,0:T(4,128)S(1)} %get-tuple-element.40.list_ref, f32[256,2304]{1,0:T(8,128)S(1)} %get-tuple-element.58.xn_ref, bf16[64,2304]{1,0:T(8,128)(2,1)S(1)} %collective-permute-done.9.c0, ...), custom_call_target="tpu_custom_call", output_to_operand_aliasing={{2}: (10, {})} | custom-call | flops 4718592 | bytes 4718592 | tf_op jit(solution)/shard_map/pallas_call | solution.py:441
  88.2 0.0 slice-done
  88.2 0.0 slice-done.1
  88.2 0.0 copy-done.2
  88.3 2.9 %shard_map.109 = (bf16[2,256,1024]{2,1,0:T(8,128)(2,1)}, f32[2304,1024]{1,0:T(8,128)S(1)}) custom-call(bf16[128,2304]{1,0:T(8,128)(2,1)S(1)} %get-tuple-element.52.refs_0_.d0.x0, bf16[128,2304]{1,0:T(8,128)(2,1)S(1)} %collective-permute-done.6.a0.y0, bf16[128,2304]{1,0:T(8,128)(2,1)S(1)} %get-tuple-element.56.d1.x1, ...), custom_call_target="tpu_custom_call" | custom-call | flops 2415919104 | bytes 4718592 | tf_op jit(solution)/shard_map/pallas_call | solution.py:430
  91.1 0.0 collective-permute-done.14.w1
  91.1 0.0 collective-permute-done.13.b1
  91.2 5.3 %shard_map.110 = (bf16[2,256,1024]{2,1,0:T(8,128)(2,1)}, f32[2304,1024]{1,0:T(8,128)}, f32[8192,2304]{1,0:T(8,128)}) custom-call(s32[4,528]{1,0:T(4,128)S(1)} %get-tuple-element.40.list_ref, f32[256,2304]{1,0:T(8,128)S(1)} %get-tuple-element.58.xn_ref, f32[192,2304]{1,0:T(8,128)S(1)} %get-tuple-element.62.xm_ref, ...), custom_call_target="tpu_custom_call", output_to_operand_aliasing={{0}: (11, {}), {2}: (12, {})} | custom-call | flops 2415919104 | bytes 14155776 | tf_op jit(solution)/shard_map/pallas_call | solution.py:445
  (3 shorter events, 0.0 us)
Async XLA Ops:
  0.6 0.7 copy-start.3
  14.0 9.3 %collective-permute-start = (bf16[128,2304]{1,0:T(8,128)(2,1)S(1)}, bf16[128,2304]{1,0:T(8,128)(2,1)S(1)}, u32[]{:S(2)}, u32[]{:S(2)}) collective-permute-start(bf16[128,2304]{1,0:T(8,128)(2,1)S(1)} %get-tuple-element.42), channel_id=1, source_target_pairs={{0,1},{1,0},{2,3},{3,2},{4,5},{5,4},{6,7},{7,6}} | collective-permute-start | bytes 1769480 | tf_op jit(solution)/shard_map/ppermute | solution.py:388
  14.6 8.8 %collective-permute-start.1 = (bf16[128,2304]{1,0:T(8,128)(2,1)S(1)}, bf16[128,2304]{1,0:T(8,128)(2,1)S(1)}, u32[]{:S(2)}, u32[]{:S(2)}) collective-permute-start(bf16[128,2304]{1,0:T(8,128)(2,1)S(1)} %get-tuple-element.44), channel_id=1, source_target_pairs={{0,1},{1,0},{2,3},{3,2},{4,5},{5,4},{6,7},{7,6}} | collective-permute-start | bytes 1769480 | tf_op jit(solution)/shard_map/ppermute | solution.py:388
  20.9 21.3 %collective-permute-start.3 = (bf16[128,2304]{1,0:T(8,128)(2,1)}, bf16[128,2304]{1,0:T(8,128)(2,1)S(1)}, u32[]{:S(2)}, u32[]{:S(2)}) collective-permute-start(bf16[128,2304]{1,0:T(8,128)(2,1)} %get-tuple-element.48), channel_id=1, source_target_pairs={{0,1},{1,0},{2,3},{3,2},{4,5},{5,4},{6,7},{7,6}} | collective-permute-start | bytes 1769480 | tf_op jit(solution)/shard_map/ppermute | solution.py:388
  21.3 20.8 %collective-permute-start.4 = (bf16[128,2304]{1,0:T(8,128)(2,1)}, bf16[128,2304]{1,0:T(8,128)(2,1)S(1)}, u32[]{:S(2)}, u32[]{:S(2)}) collective-permute-start(bf16[128,2304]{1,0:T(8,128)(2,1)} %get-tuple-element.49), channel_id=1, source_target_pairs={{0,2},{1,3},{2,0},{3,1},{4,6},{5,7},{6,4},{7,5}} | collective-permute-start | bytes 1769480 | tf_op jit(solution)/shard_map/ppermute | solution.py:388
  23.3 26.7 %collective-permute-start.5 = (bf16[128,2304]{1,0:T(8,128)(2,1)}, bf16[128,2304]{1,0:T(8,128)(2,1)S(1)}, u32[]{:S(2)}, u32[]{:S(2)}) collective-permute-start(bf16[128,2304]{1,0:T(8,128)(2,1)} %get-tuple-element.50), channel_id=1, source_target_pairs={{0,3},{1,2},{2,1},{3,0},{4,7},{5,6},{6,5},{7,4}} | collective-permute-start | bytes 1769480 | tf_op jit(solution)/shard_map/ppermute | solution.py:388
  23.5 33.3 %collective-permute-start.2 = (bf16[64,2304]{1,0:T(8,128)(2,1)S(1)}, bf16[64,2304]{1,0:T(8,128)(2,1)S(1)}, u32[]{:S(2)}, u32[]{:S(2)}) collective-permute-start(bf16[64,2304]{1,0:T(8,128)(2,1)S(1)} %get-tuple-element.46.t0), channel_id=1, source_target_pairs={{0,2},{1,3},{2,0},{3,1},{4,6},{5,7},{6,4},{7,5}} | collective-permute-start | bytes 884744 | tf_op jit(solution)/shard_map/ppermute | solution.py:388
  25.2 37.5 %collective-permute-start.7 = (bf16[64,2304]{1,0:T(8,128)(2,1)S(1)}, bf16[64,2304]{1,0:T(8,128)(2,1)S(1)}, u32[]{:S(2)}, u32[]{:S(2)}) collective-permute-start(bf16[64,2304]{1,0:T(8,128)(2,1)S(1)} %get-tuple-element.54.t1), channel_id=1, source_target_pairs={{0,2},{1,3},{2,0},{3,1},{4,6},{5,7},{6,4},{7,5}} | collective-permute-start | bytes 884744 | tf_op jit(solution)/shard_map/ppermute | solution.py:388
  25.5 16.6 %copy-start.5 = (bf16[2304]{0:T(1024)(128)(2,1)S(1)}, bf16[2304]{0:T(1024)(128)(2,1)}, u32[]{:S(2)}) copy-start(bf16[2304]{0:T(1024)(128)(2,1)} %param.8) | copy-start | bytes 13828
  25.5 31.2 %copy-start = (bf16[2,64,2304]{2,1,0:T(8,128)(2,1)S(1)}, bf16[2,64,2304]{2,1,0:T(8,128)(2,1)}, u32[]{:S(2)}) copy-start(bf16[2,64,2304]{2,1,0:T(8,128)(2,1)} %dres_ref.3) | copy-start | bytes 1769476
  25.5 31.2 %copy-start.1 = (bf16[128,2304]{1,0:T(8,128)(2,1)S(1)}, bf16[128,2304]{1,0:T(8,128)(2,1)}, u32[]{:S(2)}) copy-start(bf16[128,2304]{1,0:T(8,128)(2,1)} %get-tuple-element.47.p0) | copy-start | bytes 1769476
  25.5 31.2 %copy-start.4 = (s32[2,256]{1,0:T(2,128)S(1)}, s32[2,256]{1,0:T(2,128)}, u32[]{:S(2)}) copy-start(s32[2,256]{1,0:T(2,128)} %ids_ref.9) | copy-start | bytes 6148
  57.5 24.5 %collective-permute-start.6 = (bf16[128,2304]{1,0:T(8,128)(2,1)S(1)}, bf16[128,2304]{1,0:T(8,128)(2,1)S(1)}, u32[]{:S(2)}, u32[]{:S(2)}) collective-permute-start(bf16[128,2304]{1,0:T(8,128)(2,1)S(1)} %get-tuple-element.52.refs_0_.d0.x0), channel_id=1, source_target_pairs={{0,1},{1,0},{2,3},{3,2},{4,5},{5,4},{6,7},{7,6}} | collective-permute-start | bytes 1769480 | tf_op jit(solution)/shard_map/ppermute | solution.py:388
  64.2 18.8 %collective-permute-start.8 = (bf16[128,2304]{1,0:T(8,128)(2,1)S(1)}, bf16[128,2304]{1,0:T(8,128)(2,1)S(1)}, u32[]{:S(2)}, u32[]{:S(2)}) collective-permute-start(bf16[128,2304]{1,0:T(8,128)(2,1)S(1)} %get-tuple-element.56.d1.x1), channel_id=1, source_target_pairs={{0,1},{1,0},{2,3},{3,2},{4,5},{5,4},{6,7},{7,6}} | collective-permute-start | bytes 1769480 | tf_op jit(solution)/shard_map/ppermute | solution.py:388
  64.2 17.3 %collective-permute-start.9 = (bf16[64,2304]{1,0:T(8,128)(2,1)S(1)}, bf16[64,2304]{1,0:T(8,128)(2,1)S(1)}, u32[]{:S(2)}, u32[]{:S(2)}) collective-permute-start(bf16[64,2304]{1,0:T(8,128)(2,1)S(1)} %get-tuple-element.59), channel_id=1, source_target_pairs={{0,2},{1,3},{2,0},{3,1},{4,6},{5,7},{6,4},{7,5}} | collective-permute-start | bytes 884744 | tf_op jit(solution)/shard_map/ppermute | solution.py:388
  65.9 15.9 %collective-permute-start.11 = (bf16[64,2304]{1,0:T(8,128)(2,1)S(1)}, bf16[64,2304]{1,0:T(8,128)(2,1)S(1)}, u32[]{:S(2)}, u32[]{:S(2)}) collective-permute-start(bf16[64,2304]{1,0:T(8,128)(2,1)S(1)} %get-tuple-element.60), channel_id=1, source_target_pairs={{0,2},{1,3},{2,0},{3,1},{4,6},{5,7},{6,4},{7,5}} | collective-permute-start | bytes 884744 | tf_op jit(solution)/shard_map/ppermute | solution.py:388
  66.2 13.9 %collective-permute-start.15 = (f32[1,2304]{1,0:T(1,128)S(1)}, f32[1,2304]{1,0:T(1,128)S(1)}, u32[]{:S(2)}, u32[]{:S(2)}) collective-permute-start(f32[1,2304]{1,0:T(1,128)S(1)} %get-tuple-element.57.tok_ref), channel_id=1, source_target_pairs={{0,2},{1,3},{2,0},{3,1},{4,6},{5,7},{6,4},{7,5}} | collective-permute-start | bytes 27656 | tf_op jit(solution)/shard_map/ppermute | solution.py:388
  80.1 1.2 %collective-permute-start.16 = (f32[1,2304]{1,0:T(1,128)S(1)}, f32[1,2304]{1,0:T(1,128)S(1)}, u32[]{:S(2)}, u32[]{:S(2)}) collective-permute-start(f32[1,2304]{1,0:T(1,128)S(1)} %add.6), channel_id=1, source_target_pairs={{0,1},{1,0},{2,3},{3,2},{4,5},{5,4},{6,7},{7,6}} | collective-permute-start | bytes 27656 | tf_op jit(solution)/shard_map/ppermute | solution.py:388
  81.3 4.1 %collective-permute-start.12 = (bf16[64,2304]{1,0:T(8,128)(2,1)S(1)}, bf16[64,2304]{1,0:T(8,128)(2,1)S(1)}, u32[]{:S(2)}, u32[]{:S(2)}) collective-permute-start(bf16[64,2304]{1,0:T(8,128)(2,1)S(1)} %get-tuple-element.46.t0), channel_id=1, source_target_pairs={{0,1},{1,0},{2,3},{3,2},{4,5},{5,4},{6,7},{7,6}} | collective-permute-start | bytes 884744 | tf_op jit(solution)/shard_map/ppermute | solution.py:388
  81.5 3.9 %collective-permute-start.10 = (bf16[64,2304]{1,0:T(8,128)(2,1)S(1)}, bf16[64,2304]{1,0:T(8,128)(2,1)S(1)}, u32[]{:S(2)}, u32[]{:S(2)}) collective-permute-start(bf16[64,2304]{1,0:T(8,128)(2,1)S(1)} %collective-permute-done.9.c0), channel_id=1, source_target_pairs={{0,1},{1,0},{2,3},{3,2},{4,5},{5,4},{6,7},{7,6}} | collective-permute-start | bytes 884744 | tf_op jit(solution)/shard_map/ppermute | solution.py:388
  81.8 9.3 %collective-permute-start.14 = (bf16[64,2304]{1,0:T(8,128)(2,1)S(1)}, bf16[64,2304]{1,0:T(8,128)(2,1)S(1)}, u32[]{:S(2)}, u32[]{:S(2)}) collective-permute-start(bf16[64,2304]{1,0:T(8,128)(2,1)S(1)} %get-tuple-element.54.t1), channel_id=1, source_target_pairs={{0,1},{1,0},{2,3},{3,2},{4,5},{5,4},{6,7},{7,6}} | collective-permute-start | bytes 884744 | tf_op jit(solution)/shard_map/ppermute | solution.py:388
  82.0 9.1 %collective-permute-start.13 = (bf16[64,2304]{1,0:T(8,128)(2,1)S(1)}, bf16[64,2304]{1,0:T(8,128)(2,1)S(1)}, u32[]{:S(2)}, u32[]{:S(2)}) collective-permute-start(bf16[64,2304]{1,0:T(8,128)(2,1)S(1)} %collective-permute-done.11.c1), channel_id=1, source_target_pairs={{0,1},{1,0},{2,3},{3,2},{4,5},{5,4},{6,7},{7,6}} | collective-permute-start | bytes 884744 | tf_op jit(solution)/shard_map/ppermute | solution.py:388
  83.0 5.2 %slice-start = ((s8[4718592]{0:T(1024)(128)(4,1)}), s8[4194304]{0:T(1024)(128)(4,1)S(1)}, s32[]{:S(2)}) async-start(s8[4718592]{0:T(1024)(128)(4,1)} %bitcast), calls=%async_computation | async-start | bytes 8388608
  85.4 2.8 %slice-start.1 = ((s8[4718592]{0:T(1024)(128)(4,1)}), s8[524288]{0:T(1024)(128)(4,1)S(1)}, s32[]{:S(2)}) async-start(s8[4718592]{0:T(1024)(128)(4,1)} %bitcast), calls=%async_computation.1 | async-start | bytes 1048576
  85.4 2.8 %copy-start.2 = (bf16[2,256,1024]{2,1,0:T(8,128)(2,1)S(1)}, bf16[2,256,1024]{2,1,0:T(8,128)(2,1)}, u32[]{:S(2)}) copy-start(bf16[2,256,1024]{2,1,0:T(8,128)(2,1)} %du_ref.5) | copy-start | bytes 3145732

commit v17 on v16

--- a/solution.py
+++ b/solution.py
@@ -97,7 +97,7 @@
     lax.fori_loop(0, n, link, 0)
 
     def lists(i, c):
-        nl, nd, nl0, nd0, nl1, nd1 = c
+        nl, nd, nl0, nd0 = c
         x = lnxt[i]
         end = (x < 0).astype(jnp.int32)
         pos = own_ref[0, i]
@@ -107,15 +107,13 @@
         list_ref[3, nd] = own_ref[0, jnp.maximum(x, 0)]
         to = list_ref[3, nd]
         dup = 1 - end
-        return (nl + end, nd + dup, nl0 + end * (pos < SEG[1]).astype(jnp.int32), nd0 + dup * (to < SEG[1]).astype(jnp.int32),
-                nl1 + end * (pos < SEG[2]).astype(jnp.int32), nd1 + dup * (to < SEG[2]).astype(jnp.int32))
-
-    nl, nd, nl0, nd0, nl1, nd1 = lax.fori_loop(0, n, lists, (0,) * 6)
+        return nl + end, nd + dup, nl0 + end * (pos < SEG[1]).astype(jnp.int32), nd0 + dup * (to < SEG[1]).astype(jnp.int32)
+
+    nl, nd, nl0, nd0 = lax.fori_loop(0, n, lists, (0,) * 4)
     e = list_ref.shape[1]
-    for a, v in enumerate((0, nl0, nl1, nl)):
+    for a, (v, x) in enumerate(((0, 0), (nl0, nd0), (nl, nd))):
         list_ref[a, e - 1] = v
-    for a, v in enumerate((0, nd0, nd1, nd)):
-        list_ref[a, e - 2] = v
+        list_ref[a, e - 2] = x
     zero_wait(z, de_ref, *FILL[2], sem)
 
 
@@ -265,7 +263,7 @@
         c.wait()
 
 
-SEG = (0, 256, 448, 512)
+SEG = (0, 256, 512)
 
 
 def scatter(p, list_ref, xf, de_ref, sem):
@@ -283,7 +281,7 @@
 
     @pl.when(repeats(p, list_ref))
     def _():
-        lax.fori_loop(0, list_ref[3, e - 2], add, 0)
+        lax.fori_loop(0, list_ref[2, e - 2], add, 0)
 
     def put(i, c):
         pltpu.make_async_copy(xf.at[pl.ds(list_ref[0, i], 1), :], de_ref.at[pl.ds(list_ref[1, i], 1), :], sem).start()
@@ -320,48 +318,30 @@
     return norm(jnp.where(own_x, own[...].astype(F32), got[...].astype(F32)), g_ref)
 
 
-def mid_kernel(chip_rows, list_ref, xn_ref, c0, b0, c1, t0, w0, t1, ids_ref, g_ref, de_in, n_ref, xm_ref, de_ref, xf, sem):
-    tl = c0.shape[0]
-    h = xn_ref.shape[0]
-    r = lax.axis_index("tp")
-
-    @pl.when(repeats(1, list_ref))
-    def _():
-        xf[0:h, :] = xn_ref[...]
-
-    for a, ref in enumerate((c0, b0, c1)):
-        xf[h + a * tl:h + (a + 1) * tl, :] = ref[...].astype(F32)
-    scatter(1, list_ref, xf, de_ref, sem)
-    for a, (m, q, own, got) in enumerate(((0, r ^ 2, t0, c0), (0, r ^ 3, w0, b0), (1, r ^ 2, t1, c1))):
-        n_ref[a * tl:(a + 1) * tl, :] = far_n(ids_ref, m, q, own, got, g_ref, chip_rows)
-    xm_ref[...] = xf[h:h + 3 * tl, :]
-    scatter_wait(1, list_ref, xf, de_ref, sem)
-
-
-def last_kernel(chip_rows, list_ref, xn_ref, xm_ref, nm_ref, b1, w1, dwp_ref, ids_ref, g_ref,
+def last_kernel(chip_rows, list_ref, xn_ref, c0, b0, c1, b1, t0, w0, t1, w1, dwp_ref, ids_ref, g_ref,
                 w_ref, du_ref, u_in, de_in, u_ref, dw_ref, de_ref, xf, n_ref, du2, ub, dwb, usem, wsem, sem):
     d = w_ref.shape[0]
-    tl = b1.shape[0]
+    tl = c0.shape[0]
     r = lax.axis_index("tp")
     h = xn_ref.shape[0]
-
-    @pl.when(repeats(2, list_ref))
-    def _():
-        xf[0:h, :] = xn_ref[...]
-        xf[h:h + 3 * tl, :] = xm_ref[...]
-
-    xf[h + 3 * tl:h + 4 * tl, :] = b1[...].astype(F32)
-    scatter(2, list_ref, xf, de_ref, sem)
     take_du(du_ref, du2, tl, ((0, r ^ 2), (0, r ^ 3), (1, r ^ 2), (1, r ^ 3)))
-    n_ref[0:3 * tl, :] = nm_ref[...]
-    n_ref[3 * tl:4 * tl, :] = far_n(ids_ref, 1, r ^ 3, w1, b1, g_ref, chip_rows)
+    for a, (m, q, own, got) in enumerate(((0, r ^ 2, t0, c0), (0, r ^ 3, w0, b0), (1, r ^ 2, t1, c1), (1, r ^ 3, w1, b1))):
+        n_ref[a * tl:(a + 1) * tl, :] = far_n(ids_ref, m, q, own, got, g_ref, chip_rows)
     blk = 256
     for i in range(d // blk):
         rows = slice(i * blk, (i + 1) * blk)
         dwb[rows, :] = dwp_ref[rows, :] + dw_tile(n_ref, du2, i, blk)
         pltpu.make_async_copy(dwb.at[pl.ds(i * blk, blk), :], dw_ref.at[pl.ds(i * blk, blk), :], wsem).start()
+
+    @pl.when(repeats(1, list_ref))
+    def _():
+        xf[0:h, :] = xn_ref[...]
+
+    for a, ref in enumerate((c0, b0, c1, b1)):
+        xf[h + a * tl:h + (a + 1) * tl, :] = ref[...].astype(F32)
+    scatter(1, list_ref, xf, de_ref, sem)
     copies = umat(n_ref, w_ref, ub, u_ref, r ^ 2, r ^ 3, usem)
-    scatter_wait(2, list_ref, xf, de_ref, sem)
+    scatter_wait(1, list_ref, xf, de_ref, sem)
     pltpu.make_async_copy(dwb, dw_ref, wsem).wait()
     for c in copies:
         c.wait()
@@ -438,17 +418,13 @@
         dgs = dg + perm(dg, cross)
         dgs = dgs + perm(dgs, sib)
 
-        nm, xm, de = call(
-            functools.partial(mid_kernel, 2 * vl), 16, [S((3 * tl, d), BF16), S((3 * tl, d), F32), S((vl, d), F32)],
-            [SMEM] + [VMEM] * 9 + [HBM], [VMEM, VMEM, HBM], [pltpu.VMEM((t + 3 * tl, d), F32), D],
-            8 * h * d, 8 * h * d, {10: 2})(lists, xn, c0, b0, c1, oth0, w0, oth1, ids, g2, de)
         u, dw, de = call(
             functools.partial(last_kernel, 2 * vl), 20, [S((k, t, fc), BF16), S((d, fc), F32), S((vl, d), F32)],
-            [SMEM] + [VMEM] * 10 + [HBM] * 2, [HBM] * 3,
+            [SMEM] + [VMEM] * 14 + [HBM] * 2, [HBM] * 3,
             [pltpu.VMEM((2 * h, d), F32), pltpu.VMEM((t, d), BF16), pltpu.VMEM((t, fc), BF16), pltpu.VMEM((t, fc), BF16),
              pltpu.VMEM((d, fc), F32), D, D, D],
-            4 * t * d * fc, 6 * d * fc, {11: 0, 12: 2})(
-                lists, xn, xm, nm, b1, w1, dwp, ids, g2, w, du, u, de)
+            4 * t * d * fc, 6 * d * fc, {15: 0, 16: 2})(
+                lists, xn, c0, b0, c1, b1, oth0, w0, oth1, w1, dwp, ids, g2, w, du, u, de)
         return u, x, de, dw, dgs.reshape(d)
 
     return jax.shard_map(

time: 96.9 us -> 95.2 us (0.982)
  Pallas kernels: 51.2 us -> 49.5 us
    pallas_call x1 -> x0, Pallas kernels: 2.76 us -> none  [local(): call(functools.partial(mid_kernel, 2 * vl), 16, [S((3 * tl, d), BF16), S(...]
    pallas_call x1, Pallas kernels: 5.32 us -> 6.39 us  [local(): call(functools.partial(last_kernel, 2 * vl), 20, [S((k, t, fc), BF16), S(...]
  transfers between devices with their start and end apart: 17 -> 17, of which waited for: 5 -> 5; matrix products, arithmetic and copies ran while one was open for 1% -> 1% of each run, Pallas kernels for 34% -> 32%
where the time goes in v17:
time: 95.2 us; the launch traced here: 94.8 us
  Pallas kernels  49.5 us (52%)
  waiting for transfers between devices  33.1 us (35%)
  starting transfers between devices  9.95 us (10%)
    ppermute x17, waiting for transfers between devices, perm(): return lax.ppermute(v, 'tp', p)  33.1 us
    pallas_call x1, Pallas kernels, local(): call(zero_kernel, 8, [S((4, 2 * h + 16), jnp.int32), S((vl, d), F32)], [S...  16.6 us
    pallas_call x1, Pallas kernels, local(): call(gather_kernel, 36, [S((n, d), BF16)] * 4 + [S((2, 2 * h + 16), jnp.i...  12.7 us
    ppermute x17, starting transfers between devices, perm(): return lax.ppermute(v, 'tp', p)  9.95 us
    pallas_call x1, Pallas kernels, local(): call(functools.partial(last_kernel, 2 * vl), 20, [S((k, t, fc), BF16), S(...  6.39 us
    pallas_call x1, Pallas kernels, local(): call(pdn_kernel, 60, [S((n, d), BF16)] * 4, [HBM] * 2, [HBM] * 4, [pltpu....  6.22 us
    pallas_call x1, Pallas kernels, local(): call(u_kernel, 32, [S((k, t, fc), BF16), S((d, fc), F32)], [VMEM] * 8, [H...  2.93 us
    pallas_call x1, Pallas kernels, local(): call(near_kernel, 8, [S((t, d), F32), S((vl, d), F32)], [SMEM] + [VMEM] *...  2.41 us
  transfers between devices with their start and end apart: 17, of which 5 were waited for; matrix products, arithmetic and copies ran while one was open for 1% of the time, Pallas kernels for 32%

profile of v17, /device:TPU:0, one launch (start us, length us, event | category | flops | bytes accessed | tf_op | source)
XLA Modules:
  0.0 94.8 jit_solution(14640057876780005664)
XLA Ops:
  0.6 0.0 copy-start.3
  0.6 0.7 copy-done.3
  1.3 12.7 %shard_map.101 = (bf16[128,2304]{1,0:T(8,128)(2,1)S(1)}, bf16[128,2304]{1,0:T(8,128)(2,1)S(1)}, bf16[128,2304]{1,0:T(8,128)(2,1)S(1)}, bf16[128,2304]{1,0:T(8,12...) custom-call(s32[2,256]{1,0:T(2,128)S(1)} %copy-done.3, bf16[8192,2304]{1,0:T(8,128)(2,1)} %emb_ref.1), custom_call_target="tpu_custom_call" | custom-call | flops 500000000 | bytes 9437184 | tf_op jit(solution)/shard_map/pallas_call | solution.py:376
  14.0 0.5 collective-permute-start
  14.6 0.0 collective-permute-start.1
  14.6 6.2 %shard_map.104 = (bf16[128,2304]{1,0:T(8,128)(2,1)}, bf16[128,2304]{1,0:T(8,128)(2,1)}, bf16[128,2304]{1,0:T(8,128)(2,1)}, bf16[128,2304]{1,0:T(8,128)(2,1)}) custom-call(bf16[2,256,1024]{2,1,0:T(8,128)(2,1)} %du_ref.5, bf16[2304,1024]{1,0:T(8,128)(2,1)} %w_ref.5), custom_call_target="tpu_custom_call" | custom-call | flops 2415919104 | bytes 8126464 | tf_op jit(solution)/shard_map/pallas_call | solution.py:370
  20.8 0.5 collective-permute-start.3
  21.3 1.9 %collective-permute-start.4 = (bf16[128,2304]{1,0:T(8,128)(2,1)}, bf16[128,2304]{1,0:T(8,128)(2,1)S(1)}, u32[]{:S(2)}, u32[]{:S(2)}) collective-permute-start(bf16[128,2304]{1,0:T(8,128)(2,1)} %get-tuple-element.46), channel_id=1, source_target_pairs={{0,2},{1,3},{2,0},{3,1},{4,6},{5,7},{6,4},{7,5}} | collective-permute-start | bytes 1769480 | tf_op jit(solution)/shard_map/ppermute | solution.py:368
  23.2 0.1 collective-permute-start.5
  23.3 0.0 collective-permute-done.y0
  23.3 0.0 collective-permute-done.1.y1
  23.3 0.1 shard_map.103
  23.4 1.8 %collective-permute-start.2 = (bf16[64,2304]{1,0:T(8,128)(2,1)S(1)}, bf16[64,2304]{1,0:T(8,128)(2,1)S(1)}, u32[]{:S(2)}, u32[]{:S(2)}) collective-permute-start(bf16[64,2304]{1,0:T(8,128)(2,1)S(1)} %get-tuple-element.43.t0), channel_id=1, source_target_pairs={{0,2},{1,3},{2,0},{3,1},{4,6},{5,7},{6,4},{7,5}} | collective-permute-start | bytes 884744 | tf_op jit(solution)/shard_map/ppermute | solution.py:368
  25.2 0.3 collective-permute-start.7
  25.5 0.0 copy-start.5
  25.5 0.0 copy-start
  25.5 0.0 copy-start.1
  25.5 0.0 copy-start.4
  25.5 16.6 %shard_map.102 = (s32[4,528]{1,0:T(4,128)S(1)}, f32[8192,2304]{1,0:T(8,128)}) custom-call(s32[2,528]{1,0:T(2,128)S(1)} %get-tuple-element.35.own_ref, f32[8192,2304]{1,0:T(8,128)} %get-tuple-element.36.de_in), custom_call_target="tpu_custom_call", output_to_operand_aliasing={{1}: (1, {})} | custom-call | flops 6000000000 | bytes 37748736 | tf_op jit(solution)/shard_map/pallas_call | solution.py:392
  42.1 0.0 copy-done.5
  42.1 0.0 collective-permute-done.3.p1
  42.1 0.0 collective-permute-done.4.p2
  42.1 7.8 %collective-permute-done.5.p3 = bf16[128,2304]{1,0:T(8,128)(2,1)S(1)} collective-permute-done((bf16[128,2304]{1,0:T(8,128)(2,1)}, bf16[128,2304]{1,0:T(8,128)(2,1)S(1)}, u32[]{:S(2)}, u32[]{:S(2)}) %collective-permute-start.5) | collective-permute-done | bytes 589856 | tf_op jit(solution)/shard_map/ppermute | solution.py:368
  49.9 6.8 %collective-permute-done.2.z_ref = bf16[64,2304]{1,0:T(8,128)(2,1)S(1)} collective-permute-done((bf16[64,2304]{1,0:T(8,128)(2,1)S(1)}, bf16[64,2304]{1,0:T(8,128)(2,1)S(1)}, u32[]{:S(2)}, u32[]{:S(2)}) %collective-permute-start.2) | collective-permute-done | bytes 294944 | tf_op jit(solution)/shard_map/ppermute | solution.py:368
  56.7 0.0 copy-done
  56.7 0.0 copy-done.1
  56.7 0.0 copy-done.4
  56.7 0.0 slice-start
  56.7 0.8 shard_map.105
  57.5 0.0 collective-permute-start.6
  57.5 5.2 %collective-permute-done.7.z_ref = bf16[64,2304]{1,0:T(8,128)(2,1)S(1)} collective-permute-done((bf16[64,2304]{1,0:T(8,128)(2,1)S(1)}, bf16[64,2304]{1,0:T(8,128)(2,1)S(1)}, u32[]{:S(2)}, u32[]{:S(2)}) %collective-permute-start.7) | collective-permute-done | bytes 294944 | tf_op jit(solution)/shard_map/ppermute | solution.py:368
  62.7 0.0 slice-start.1
  62.7 1.5 %shard_map.106 = (bf16[128,2304]{1,0:T(8,128)(2,1)S(1)}, bf16[64,2304]{1,0:T(8,128)(2,1)S(1)}, f32[1,2304]{1,0:T(1,128)S(1)}, bf16[2,64,2304]{2,1,0:T(8,128)(2,1)}) custom-call(bf16[64,2304]{1,0:T(8,128)(2,1)S(1)} %get-tuple-element.50.xh_ref, bf16[64,2304]{1,0:T(8,128)(2,1)S(1)} %collective-permute-done.7.z_ref, bf16[128,2304]{1,0:T(8,128)(2,1)S(1)} %copy-done.1, ...), custom_call_target="tpu_custom_call" | custom-call | flops 8847360 | bytes 4718592 | tf_op jit(solution)/shard_map/pallas_call | solution.py:399
  64.1 0.0 collective-permute-start.8
  64.1 1.7 %collective-permute-start.9 = (bf16[64,2304]{1,0:T(8,128)(2,1)S(1)}, bf16[64,2304]{1,0:T(8,128)(2,1)S(1)}, u32[]{:S(2)}, u32[]{:S(2)}) collective-permute-start(bf16[64,2304]{1,0:T(8,128)(2,1)S(1)} %get-tuple-element.56), channel_id=1, source_target_pairs={{0,2},{1,3},{2,0},{3,1},{4,6},{5,7},{6,4},{7,5}} | collective-permute-start | bytes 884744 | tf_op jit(solution)/shard_map/ppermute | solution.py:368
  65.9 0.3 collective-permute-start.11
  66.2 1.7 %collective-permute-start.15 = (f32[1,2304]{1,0:T(1,128)S(1)}, f32[1,2304]{1,0:T(1,128)S(1)}, u32[]{:S(2)}, u32[]{:S(2)}) collective-permute-start(f32[1,2304]{1,0:T(1,128)S(1)} %get-tuple-element.54.tok_ref), channel_id=1, source_target_pairs={{0,2},{1,3},{2,0},{3,1},{4,6},{5,7},{6,4},{7,5}} | collective-permute-start | bytes 27656 | tf_op jit(solution)/shard_map/ppermute | solution.py:368
  67.9 12.2 %collective-permute-done.15 = f32[1,2304]{1,0:T(1,128)S(1)} collective-permute-done((f32[1,2304]{1,0:T(1,128)S(1)}, f32[1,2304]{1,0:T(1,128)S(1)}, u32[]{:S(2)}, u32[]{:S(2)}) %collective-permute-start.15) | collective-permute-done | bytes 9248 | tf_op jit(solution)/shard_map/ppermute | solution.py:368
  80.1 0.0 collective-permute-start.16
  80.1 1.2 %collective-permute-done.16 = f32[1,2304]{1,0:T(1,128)S(1)} collective-permute-done((f32[1,2304]{1,0:T(1,128)S(1)}, f32[1,2304]{1,0:T(1,128)S(1)}, u32[]{:S(2)}, u32[]{:S(2)}) %collective-permute-start.16) | collective-permute-done | bytes 9248 | tf_op jit(solution)/shard_map/ppermute | solution.py:368
  81.3 0.2 collective-permute-start.13
  81.5 0.0 collective-permute-done.9.c0
  81.5 0.3 collective-permute-start.14
  81.8 0.0 collective-permute-done.11.c1
  81.8 0.2 collective-permute-start.10
  82.0 0.0 collective-permute-done.6.a0.y0
  82.0 0.3 collective-permute-start.12
  82.3 0.6 add_reduce_fusion
  82.9 0.0 collective-permute-done.8.a1.y1
  83.0 0.0 copy-start.2
  83.0 2.4 %shard_map.107 = (f32[256,2304]{1,0:T(8,128)S(1)}, f32[8192,2304]{1,0:T(8,128)}) custom-call(s32[4,528]{1,0:T(4,128)S(1)} %get-tuple-element.37.list_ref, bf16[128,2304]{1,0:T(8,128)(2,1)S(1)} %get-tuple-element.49.refs_0_.d0.x0, bf16[128,2304]{1,0:T(8,128)(2,1)S(1)} %collective-permute-done.6.a0.y0, ...), custom_call_target="tpu_custom_call", output_to_operand_aliasing={{1}: (6, {})} | custom-call | flops 4718592 | bytes 4718592 | tf_op jit(solution)/shard_map/pallas_call | solution.py:414
  85.4 0.0 slice-done
  85.4 0.0 slice-done.1
  85.4 0.0 copy-done.2
  85.4 2.9 %shard_map.108 = (bf16[2,256,1024]{2,1,0:T(8,128)(2,1)}, f32[2304,1024]{1,0:T(8,128)S(1)}) custom-call(bf16[128,2304]{1,0:T(8,128)(2,1)S(1)} %get-tuple-element.49.refs_0_.d0.x0, bf16[128,2304]{1,0:T(8,128)(2,1)S(1)} %collective-permute-done.6.a0.y0, bf16[128,2304]{1,0:T(8,128)(2,1)S(1)} %get-tuple-element.53.d1.x1, ...), custom_call_target="tpu_custom_call" | custom-call | flops 2415919104 | bytes 4718592 | tf_op jit(solution)/shard_map/pallas_call | solution.py:410
  88.3 0.0 collective-permute-done.13.w0
  88.4 0.0 collective-permute-done.14.w1
  88.4 0.0 collective-permute-done.10.b0
  88.4 0.0 collective-permute-done.12.b1
  88.4 6.4 %shard_map.109 = (bf16[2,256,1024]{2,1,0:T(8,128)(2,1)}, f32[2304,1024]{1,0:T(8,128)}, f32[8192,2304]{1,0:T(8,128)}) custom-call(s32[4,528]{1,0:T(4,128)S(1)} %get-tuple-element.37.list_ref, f32[256,2304]{1,0:T(8,128)S(1)} %get-tuple-element.55.xn_ref, ...), custom_call_target="tpu_custom_call", output_to_operand_aliasing={{0}: (15, {}), {2}: (16, {})} | custom-call | flops 2415919104 | bytes 14155776 | tf_op jit(solution)/shard_map/pallas_call | solution.py:421
  (3 shorter events, 0.0 us)
Async XLA Ops:
  0.6 0.7 copy-start.3
  14.0 9.3 %collective-permute-start = (bf16[128,2304]{1,0:T(8,128)(2,1)S(1)}, bf16[128,2304]{1,0:T(8,128)(2,1)S(1)}, u32[]{:S(2)}, u32[]{:S(2)}) collective-permute-start(bf16[128,2304]{1,0:T(8,128)(2,1)S(1)} %get-tuple-element.39), channel_id=1, source_target_pairs={{0,1},{1,0},{2,3},{3,2},{4,5},{5,4},{6,7},{7,6}} | collective-permute-start | bytes 1769480 | tf_op jit(solution)/shard_map/ppermute | solution.py:368
  14.6 8.7 %collective-permute-start.1 = (bf16[128,2304]{1,0:T(8,128)(2,1)S(1)}, bf16[128,2304]{1,0:T(8,128)(2,1)S(1)}, u32[]{:S(2)}, u32[]{:S(2)}) collective-permute-start(bf16[128,2304]{1,0:T(8,128)(2,1)S(1)} %get-tuple-element.41), channel_id=1, source_target_pairs={{0,1},{1,0},{2,3},{3,2},{4,5},{5,4},{6,7},{7,6}} | collective-permute-start | bytes 1769480 | tf_op jit(solution)/shard_map/ppermute | solution.py:368
  20.8 21.3 %collective-permute-start.3 = (bf16[128,2304]{1,0:T(8,128)(2,1)}, bf16[128,2304]{1,0:T(8,128)(2,1)S(1)}, u32[]{:S(2)}, u32[]{:S(2)}) collective-permute-start(bf16[128,2304]{1,0:T(8,128)(2,1)} %get-tuple-element.45), channel_id=1, source_target_pairs={{0,1},{1,0},{2,3},{3,2},{4,5},{5,4},{6,7},{7,6}} | collective-permute-start | bytes 1769480 | tf_op jit(solution)/shard_map/ppermute | solution.py:368
  21.3 20.8 %collective-permute-start.4 = (bf16[128,2304]{1,0:T(8,128)(2,1)}, bf16[128,2304]{1,0:T(8,128)(2,1)S(1)}, u32[]{:S(2)}, u32[]{:S(2)}) collective-permute-start(bf16[128,2304]{1,0:T(8,128)(2,1)} %get-tuple-element.46), channel_id=1, source_target_pairs={{0,2},{1,3},{2,0},{3,1},{4,6},{5,7},{6,4},{7,5}} | collective-permute-start | bytes 1769480 | tf_op jit(solution)/shard_map/ppermute | solution.py:368
  23.2 26.7 %collective-permute-start.5 = (bf16[128,2304]{1,0:T(8,128)(2,1)}, bf16[128,2304]{1,0:T(8,128)(2,1)S(1)}, u32[]{:S(2)}, u32[]{:S(2)}) collective-permute-start(bf16[128,2304]{1,0:T(8,128)(2,1)} %get-tuple-element.47), channel_id=1, source_target_pairs={{0,3},{1,2},{2,1},{3,0},{4,7},{5,6},{6,5},{7,4}} | collective-permute-start | bytes 1769480 | tf_op jit(solution)/shard_map/ppermute | solution.py:368
  23.4 33.3 %collective-permute-start.2 = (bf16[64,2304]{1,0:T(8,128)(2,1)S(1)}, bf16[64,2304]{1,0:T(8,128)(2,1)S(1)}, u32[]{:S(2)}, u32[]{:S(2)}) collective-permute-start(bf16[64,2304]{1,0:T(8,128)(2,1)S(1)} %get-tuple-element.43.t0), channel_id=1, source_target_pairs={{0,2},{1,3},{2,0},{3,1},{4,6},{5,7},{6,4},{7,5}} | collective-permute-start | bytes 884744 | tf_op jit(solution)/shard_map/ppermute | solution.py:368
  25.2 37.5 %collective-permute-start.7 = (bf16[64,2304]{1,0:T(8,128)(2,1)S(1)}, bf16[64,2304]{1,0:T(8,128)(2,1)S(1)}, u32[]{:S(2)}, u32[]{:S(2)}) collective-permute-start(bf16[64,2304]{1,0:T(8,128)(2,1)S(1)} %get-tuple-element.51.t1), channel_id=1, source_target_pairs={{0,2},{1,3},{2,0},{3,1},{4,6},{5,7},{6,4},{7,5}} | collective-permute-start | bytes 884744 | tf_op jit(solution)/shard_map/ppermute | solution.py:368
  25.5 16.6 %copy-start.5 = (bf16[2304]{0:T(1024)(128)(2,1)S(1)}, bf16[2304]{0:T(1024)(128)(2,1)}, u32[]{:S(2)}) copy-start(bf16[2304]{0:T(1024)(128)(2,1)} %param.8) | copy-start | bytes 13828
  25.5 31.2 %copy-start = (bf16[2,64,2304]{2,1,0:T(8,128)(2,1)S(1)}, bf16[2,64,2304]{2,1,0:T(8,128)(2,1)}, u32[]{:S(2)}) copy-start(bf16[2,64,2304]{2,1,0:T(8,128)(2,1)} %dres_ref.3) | copy-start | bytes 1769476
  25.5 31.2 %copy-start.1 = (bf16[128,2304]{1,0:T(8,128)(2,1)S(1)}, bf16[128,2304]{1,0:T(8,128)(2,1)}, u32[]{:S(2)}) copy-start(bf16[128,2304]{1,0:T(8,128)(2,1)} %get-tuple-element.44.p0) | copy-start | bytes 1769476
  25.5 31.2 %copy-start.4 = (s32[2,256]{1,0:T(2,128)S(1)}, s32[2,256]{1,0:T(2,128)}, u32[]{:S(2)}) copy-start(s32[2,256]{1,0:T(2,128)} %ids_ref.7) | copy-start | bytes 6148
  56.7 28.7 %slice-start = ((s8[4718592]{0:T(1024)(128)(4,1)}), s8[4194304]{0:T(1024)(128)(4,1)S(1)}, s32[]{:S(2)}) async-start(s8[4718592]{0:T(1024)(128)(4,1)} %bitcast), calls=%async_computation | async-start | bytes 8388608
  57.5 24.5 %collective-permute-start.6 = (bf16[128,2304]{1,0:T(8,128)(2,1)S(1)}, bf16[128,2304]{1,0:T(8,128)(2,1)S(1)}, u32[]{:S(2)}, u32[]{:S(2)}) collective-permute-start(bf16[128,2304]{1,0:T(8,128)(2,1)S(1)} %get-tuple-element.49.refs_0_.d0.x0), channel_id=1, source_target_pairs={{0,1},{1,0},{2,3},{3,2},{4,5},{5,4},{6,7},{7,6}} | collective-permute-start | bytes 1769480 | tf_op jit(solution)/shard_map/ppermute | solution.py:368
  62.7 22.7 %slice-start.1 = ((s8[4718592]{0:T(1024)(128)(4,1)}), s8[524288]{0:T(1024)(128)(4,1)S(1)}, s32[]{:S(2)}) async-start(s8[4718592]{0:T(1024)(128)(4,1)} %bitcast), calls=%async_computation.1 | async-start | bytes 1048576
  64.1 18.8 %collective-permute-start.8 = (bf16[128,2304]{1,0:T(8,128)(2,1)S(1)}, bf16[128,2304]{1,0:T(8,128)(2,1)S(1)}, u32[]{:S(2)}, u32[]{:S(2)}) collective-permute-start(bf16[128,2304]{1,0:T(8,128)(2,1)S(1)} %get-tuple-element.53.d1.x1), channel_id=1, source_target_pairs={{0,1},{1,0},{2,3},{3,2},{4,5},{5,4},{6,7},{7,6}} | collective-permute-start | bytes 1769480 | tf_op jit(solution)/shard_map/ppermute | solution.py:368
  64.1 17.3 %collective-permute-start.9 = (bf16[64,2304]{1,0:T(8,128)(2,1)S(1)}, bf16[64,2304]{1,0:T(8,128)(2,1)S(1)}, u32[]{:S(2)}, u32[]{:S(2)}) collective-permute-start(bf16[64,2304]{1,0:T(8,128)(2,1)S(1)} %get-tuple-element.56), channel_id=1, source_target_pairs={{0,2},{1,3},{2,0},{3,1},{4,6},{5,7},{6,4},{7,5}} | collective-permute-start | bytes 884744 | tf_op jit(solution)/shard_map/ppermute | solution.py:368
  65.9 15.9 %collective-permute-start.11 = (bf16[64,2304]{1,0:T(8,128)(2,1)S(1)}, bf16[64,2304]{1,0:T(8,128)(2,1)S(1)}, u32[]{:S(2)}, u32[]{:S(2)}) collective-permute-start(bf16[64,2304]{1,0:T(8,128)(2,1)S(1)} %get-tuple-element.57), channel_id=1, source_target_pairs={{0,2},{1,3},{2,0},{3,1},{4,6},{5,7},{6,4},{7,5}} | collective-permute-start | bytes 884744 | tf_op jit(solution)/shard_map/ppermute | solution.py:368
  66.2 13.9 %collective-permute-start.15 = (f32[1,2304]{1,0:T(1,128)S(1)}, f32[1,2304]{1,0:T(1,128)S(1)}, u32[]{:S(2)}, u32[]{:S(2)}) collective-permute-start(f32[1,2304]{1,0:T(1,128)S(1)} %get-tuple-element.54.tok_ref), channel_id=1, source_target_pairs={{0,2},{1,3},{2,0},{3,1},{4,6},{5,7},{6,4},{7,5}} | collective-permute-start | bytes 27656 | tf_op jit(solution)/shard_map/ppermute | solution.py:368
  80.1 1.2 %collective-permute-start.16 = (f32[1,2304]{1,0:T(1,128)S(1)}, f32[1,2304]{1,0:T(1,128)S(1)}, u32[]{:S(2)}, u32[]{:S(2)}) collective-permute-start(f32[1,2304]{1,0:T(1,128)S(1)} %add.6), channel_id=1, source_target_pairs={{0,1},{1,0},{2,3},{3,2},{4,5},{5,4},{6,7},{7,6}} | collective-permute-start | bytes 27656 | tf_op jit(solution)/shard_map/ppermute | solution.py:368
  81.3 7.1 %collective-permute-start.13 = (bf16[64,2304]{1,0:T(8,128)(2,1)S(1)}, bf16[64,2304]{1,0:T(8,128)(2,1)S(1)}, u32[]{:S(2)}, u32[]{:S(2)}) collective-permute-start(bf16[64,2304]{1,0:T(8,128)(2,1)S(1)} %get-tuple-element.43.t0), channel_id=1, source_target_pairs={{0,1},{1,0},{2,3},{3,2},{4,5},{5,4},{6,7},{7,6}} | collective-permute-start | bytes 884744 | tf_op jit(solution)/shard_map/ppermute | solution.py:368
  81.5 6.9 %collective-permute-start.14 = (bf16[64,2304]{1,0:T(8,128)(2,1)S(1)}, bf16[64,2304]{1,0:T(8,128)(2,1)S(1)}, u32[]{:S(2)}, u32[]{:S(2)}) collective-permute-start(bf16[64,2304]{1,0:T(8,128)(2,1)S(1)} %get-tuple-element.51.t1), channel_id=1, source_target_pairs={{0,1},{1,0},{2,3},{3,2},{4,5},{5,4},{6,7},{7,6}} | collective-permute-start | bytes 884744 | tf_op jit(solution)/shard_map/ppermute | solution.py:368
  81.8 6.6 %collective-permute-start.10 = (bf16[64,2304]{1,0:T(8,128)(2,1)S(1)}, bf16[64,2304]{1,0:T(8,128)(2,1)S(1)}, u32[]{:S(2)}, u32[]{:S(2)}) collective-permute-start(bf16[64,2304]{1,0:T(8,128)(2,1)S(1)} %collective-permute-done.9.c0), channel_id=1, source_target_pairs={{0,1},{1,0},{2,3},{3,2},{4,5},{5,4},{6,7},{7,6}} | collective-permute-start | bytes 884744 | tf_op jit(solution)/shard_map/ppermute | solution.py:368
  82.0 6.4 %collective-permute-start.12 = (bf16[64,2304]{1,0:T(8,128)(2,1)S(1)}, bf16[64,2304]{1,0:T(8,128)(2,1)S(1)}, u32[]{:S(2)}, u32[]{:S(2)}) collective-permute-start(bf16[64,2304]{1,0:T(8,128)(2,1)S(1)} %collective-permute-done.11.c1), channel_id=1, source_target_pairs={{0,1},{1,0},{2,3},{3,2},{4,5},{5,4},{6,7},{7,6}} | collective-permute-start | bytes 884744 | tf_op jit(solution)/shard_map/ppermute | solution.py:368
  83.0 2.4 %copy-start.2 = (bf16[2,256,1024]{2,1,0:T(8,128)(2,1)S(1)}, bf16[2,256,1024]{2,1,0:T(8,128)(2,1)}, u32[]{:S(2)}) copy-start(bf16[2,256,1024]{2,1,0:T(8,128)(2,1)} %du_ref.5) | copy-start | bytes 3145732

commit v18 on v17

--- a/solution.py
+++ b/solution.py
@@ -223,20 +223,18 @@
     return ((x * rs) * g_ref[...].astype(F32)).astype(BF16)
 
 
-def umat(n_ref, w_ref, ub, u_ref, q0, q1, sem):
+def umat(n_ref, row, w_ref, ub, u_ref, order, sem):
     blk = 256
+    tl = u_ref.shape[1] // 4
+    rows = len(order) * tl
     for i in range(ub.shape[1] // blk):
         ub[:, i * blk:(i + 1) * blk] = jnp.dot(
-            n_ref[...], w_ref[:, i * blk:(i + 1) * blk], preferred_element_type=F32).astype(BF16)
-    k = u_ref.shape[0]
-    tl = u_ref.shape[1] // 4
+            n_ref[row:row + rows, :], w_ref[:, i * blk:(i + 1) * blk], preferred_element_type=F32).astype(BF16)
     copies = []
-    for m in range(k):
-        for a, q in enumerate((q0, q1)):
-            c = pltpu.make_async_copy(ub.at[pl.ds((m * 2 + a) * tl, tl), :],
-                                      u_ref.at[m, pl.ds(pl.multiple_of(q * tl, tl), tl), :], sem)
-            c.start()
-            copies.append(c)
+    for a, (m, q) in enumerate(order):
+        c = pltpu.make_async_copy(ub.at[pl.ds(a * tl, tl), :], u_ref.at[m, pl.ds(pl.multiple_of(q * tl, tl), tl), :], sem)
+        c.start()
+        copies.append(c)
     return copies
 
 
@@ -254,8 +252,9 @@
     tl = x0.shape[0] // 2
     for a, x in enumerate((x0, y0, x1, y1)):
         n_ref[a * tl:(a + 1) * tl, :] = norm(x[0:tl, :].astype(F32), g_ref)
-    take_du(du_ref, du2, tl, ((0, r), (0, r ^ 1), (1, r), (1, r ^ 1)))
-    copies = umat(n_ref, w_ref, ub, u_ref, r, r ^ 1, usem)
+    order = ((0, r), (0, r ^ 1), (1, r), (1, r ^ 1))
+    take_du(du_ref, du2, tl, order)
+    copies = umat(n_ref, 0, w_ref, ub, u_ref, order, usem)
     blk = 256
     for i in range(dwp_ref.shape[0] // blk):
         dwp_ref[i * blk:(i + 1) * blk, :] = dw_tile(n_ref, du2, i, blk)
@@ -318,15 +317,25 @@
     return norm(jnp.where(own_x, own[...].astype(F32), got[...].astype(F32)), g_ref)
 
 
-def last_kernel(chip_rows, list_ref, xn_ref, c0, b0, c1, b1, t0, w0, t1, w1, dwp_ref, ids_ref, g_ref,
+def mid_kernel(chip_rows, c0, b0, c1, t0, w0, t1, ids_ref, g_ref, w_ref, u_in, n_ref, u_ref, ub, usem):
+    tl = c0.shape[0]
+    r = lax.axis_index("tp")
+    for a, (m, q, own, got) in enumerate(((0, r ^ 2, t0, c0), (0, r ^ 3, w0, b0), (1, r ^ 2, t1, c1))):
+        n_ref[a * tl:(a + 1) * tl, :] = far_n(ids_ref, m, q, own, got, g_ref, chip_rows)
+    for c in umat(n_ref, 0, w_ref, ub, u_ref, ((0, r ^ 2), (0, r ^ 3)), usem):
+        c.wait()
+
+
+def last_kernel(chip_rows, list_ref, xn_ref, nm_ref, c0, b0, c1, b1, w1, dwp_ref, ids_ref, g_ref,
                 w_ref, du_ref, u_in, de_in, u_ref, dw_ref, de_ref, xf, n_ref, du2, ub, dwb, usem, wsem, sem):
     d = w_ref.shape[0]
     tl = c0.shape[0]
     r = lax.axis_index("tp")
     h = xn_ref.shape[0]
-    take_du(du_ref, du2, tl, ((0, r ^ 2), (0, r ^ 3), (1, r ^ 2), (1, r ^ 3)))
-    for a, (m, q, own, got) in enumerate(((0, r ^ 2, t0, c0), (0, r ^ 3, w0, b0), (1, r ^ 2, t1, c1), (1, r ^ 3, w1, b1))):
-        n_ref[a * tl:(a + 1) * tl, :] = far_n(ids_ref, m, q, own, got, g_ref, chip_rows)
+    order = ((0, r ^ 2), (0, r ^ 3), (1, r ^ 2), (1, r ^ 3))
+    take_du(du_ref, du2, tl, order)
+    n_ref[0:3 * tl, :] = nm_ref[...]
+    n_ref[3 * tl:4 * tl, :] = far_n(ids_ref, 1, r ^ 3, w1, b1, g_ref, chip_rows)
     blk = 256
     for i in range(d // blk):
         rows = slice(i * blk, (i + 1) * blk)
@@ -340,7 +349,7 @@
     for a, ref in enumerate((c0, b0, c1, b1)):
         xf[h + a * tl:h + (a + 1) * tl, :] = ref[...].astype(F32)
     scatter(1, list_ref, xf, de_ref, sem)
-    copies = umat(n_ref, w_ref, ub, u_ref, r ^ 2, r ^ 3, usem)
+    copies = umat(n_ref, 2 * tl, w_ref, ub, u_ref, order[2:], usem)
     scatter_wait(1, list_ref, xf, de_ref, sem)
     pltpu.make_async_copy(dwb, dw_ref, wsem).wait()
     for c in copies:
@@ -411,21 +420,26 @@
             u_kernel, 32, [S((k, t, fc), BF16), S((d, fc), F32)], [VMEM] * 8, [HBM, VMEM],
             [pltpu.VMEM((t, d), BF16), pltpu.VMEM((t, fc), BF16), pltpu.VMEM((t, fc), BF16), D],
             4 * t * d * fc, 2 * d * fc)(mine0, next0, mine1, next1, g2, w, du, dg)
+        dgs = dg + perm(dg, cross)
+        dgs = dgs + perm(dgs, sib)
+        dgs = dgs.reshape(d)
         xn, de = call(near_kernel, 8, [S((t, d), F32), S((vl, d), F32)], [SMEM] + [VMEM] * 5 + [HBM], [VMEM, HBM],
-                      [D], 8 * h * d, 8 * h * d, {6: 1})(lists, mine0, next0, mine1, next1, dg, de)
+                      [D], 8 * h * d, 8 * h * d, {6: 1})(lists, mine0, next0, mine1, next1, dgs, de)
         b0 = perm(c0, sib)
         b1 = perm(c1, sib)
-        dgs = dg + perm(dg, cross)
-        dgs = dgs + perm(dgs, sib)
-
+
+        nm, u = call(
+            functools.partial(mid_kernel, 2 * vl), 12, [S((3 * tl, d), BF16), S((k, t, fc), BF16)],
+            [VMEM] * 9 + [HBM], [VMEM, HBM], [pltpu.VMEM((2 * tl, fc), BF16), D],
+            4 * tl * d * fc, 2 * d * fc, {9: 1})(c0, b0, c1, oth0, w0, oth1, ids, g2, w, u)
         u, dw, de = call(
             functools.partial(last_kernel, 2 * vl), 20, [S((k, t, fc), BF16), S((d, fc), F32), S((vl, d), F32)],
-            [SMEM] + [VMEM] * 14 + [HBM] * 2, [HBM] * 3,
-            [pltpu.VMEM((2 * h, d), F32), pltpu.VMEM((t, d), BF16), pltpu.VMEM((t, fc), BF16), pltpu.VMEM((t, fc), BF16),
+            [SMEM] + [VMEM] * 12 + [HBM] * 2, [HBM] * 3,
+            [pltpu.VMEM((2 * h, d), F32), pltpu.VMEM((t, d), BF16), pltpu.VMEM((t, fc), BF16), pltpu.VMEM((2 * tl, fc), BF16),
              pltpu.VMEM((d, fc), F32), D, D, D],
-            4 * t * d * fc, 6 * d * fc, {15: 0, 16: 2})(
-                lists, xn, c0, b0, c1, b1, oth0, w0, oth1, w1, dwp, ids, g2, w, du, u, de)
-        return u, x, de, dw, dgs.reshape(d)
+            4 * t * d * fc, 6 * d * fc, {13: 0, 14: 2})(
+                lists, xn, nm, c0, b0, c1, b1, w1, dwp, ids, g2, w, du, u, de)
+        return u, x, de, dw, dgs
 
     return jax.shard_map(
         local,

time: 95.2 us -> 95.6 us (level)
  Pallas kernels: 49.5 us -> 50.5 us
    pallas_call x0 -> x1, Pallas kernels: none -> 1.96 us  [local(): call(functools.partial(mid_kernel, 2 * vl), 12, [S((3 * tl, d), BF16), S(...]
    pallas_call x1, Pallas kernels: 6.39 us -> 5.38 us  [local(): call(functools.partial(last_kernel, 2 * vl), 20, [S((k, t, fc), BF16), S(...]
  transfers between devices with their start and end apart: 17 -> 17, of which waited for: 5 -> 5; matrix products, arithmetic and copies ran while one was open for 1% -> 0% of each run, Pallas kernels for 32% -> 32%
where the time goes in v18:
time: 95.6 us; the launch traced here: 95.2 us
  Pallas kernels  50.5 us (53%)
  waiting for transfers between devices  32.7 us (34%)
  starting transfers between devices  10.4 us (11%)
    ppermute x17, waiting for transfers between devices, perm(): return lax.ppermute(v, 'tp', p)  32.7 us
    pallas_call x1, Pallas kernels, local(): call(zero_kernel, 8, [S((4, 2 * h + 16), jnp.int32), S((vl, d), F32)], [S...  16.5 us
    pallas_call x1, Pallas kernels, local(): call(gather_kernel, 36, [S((n, d), BF16)] * 4 + [S((2, 2 * h + 16), jnp.i...  12.7 us
    ppermute x17, starting transfers between devices, perm(): return lax.ppermute(v, 'tp', p)  10.4 us
    pallas_call x1, Pallas kernels, local(): call(pdn_kernel, 60, [S((n, d), BF16)] * 4, [HBM] * 2, [HBM] * 4, [pltpu....  6.21 us
    pallas_call x1, Pallas kernels, local(): call(functools.partial(last_kernel, 2 * vl), 20, [S((k, t, fc), BF16), S(...  5.38 us
    pallas_call x1, Pallas kernels, local(): call(u_kernel, 32, [S((k, t, fc), BF16), S((d, fc), F32)], [VMEM] * 8, [H...  2.92 us
    pallas_call x1, Pallas kernels, local(): call(near_kernel, 8, [S((t, d), F32), S((vl, d), F32)], [SMEM] + [VMEM] *...  2.41 us
  transfers between devices with their start and end apart: 17, of which 5 were waited for; matrix products, arithmetic and copies ran while one was open for 0% of the time, Pallas kernels for 32%

profile of v18, /device:TPU:0, one launch (start us, length us, event | category | flops | bytes accessed | tf_op | source)
XLA Modules:
  0.0 95.2 jit_solution(8334788130037977252)
XLA Ops:
  0.6 0.0 copy-start.3
  0.6 0.7 copy-done.3
  1.3 0.0 copy-start.6
  1.3 12.7 %shard_map.101 = (bf16[128,2304]{1,0:T(8,128)(2,1)S(1)}, bf16[128,2304]{1,0:T(8,128)(2,1)S(1)}, bf16[128,2304]{1,0:T(8,128)(2,1)S(1)}, bf16[128,2304]{1,0:T(8,12...) custom-call(s32[2,256]{1,0:T(2,128)S(1)} %copy-done.3, bf16[8192,2304]{1,0:T(8,128)(2,1)} %emb_ref.1), custom_call_target="tpu_custom_call" | custom-call | flops 500000000 | bytes 9437184 | tf_op jit(solution)/shard_map/pallas_call | solution.py:385
  14.0 0.5 collective-permute-start
  14.6 0.0 collective-permute-start.1
  14.6 6.2 %shard_map.104 = (bf16[128,2304]{1,0:T(8,128)(2,1)}, bf16[128,2304]{1,0:T(8,128)(2,1)}, bf16[128,2304]{1,0:T(8,128)(2,1)}, bf16[128,2304]{1,0:T(8,128)(2,1)}) custom-call(bf16[2,256,1024]{2,1,0:T(8,128)(2,1)} %du_ref.5, bf16[2304,1024]{1,0:T(8,128)(2,1)} %w_ref.7), custom_call_target="tpu_custom_call" | custom-call | flops 2415919104 | bytes 8126464 | tf_op jit(solution)/shard_map/pallas_call | solution.py:379
  20.8 0.5 collective-permute-start.3
  21.3 1.9 %collective-permute-start.4 = (bf16[128,2304]{1,0:T(8,128)(2,1)}, bf16[128,2304]{1,0:T(8,128)(2,1)S(1)}, u32[]{:S(2)}, u32[]{:S(2)}) collective-permute-start(bf16[128,2304]{1,0:T(8,128)(2,1)} %get-tuple-element.48), channel_id=1, source_target_pairs={{0,2},{1,3},{2,0},{3,1},{4,6},{5,7},{6,4},{7,5}} | collective-permute-start | bytes 1769480 | tf_op jit(solution)/shard_map/ppermute | solution.py:377
  23.2 0.1 collective-permute-start.5
  23.3 0.0 copy-done.6
  23.3 0.0 collective-permute-done.y0
  23.3 0.0 collective-permute-done.1.y1
  23.3 0.1 shard_map.103
  23.5 1.8 %collective-permute-start.2 = (bf16[64,2304]{1,0:T(8,128)(2,1)S(1)}, bf16[64,2304]{1,0:T(8,128)(2,1)S(1)}, u32[]{:S(2)}, u32[]{:S(2)}) collective-permute-start(bf16[64,2304]{1,0:T(8,128)(2,1)S(1)} %get-tuple-element.45.t0), channel_id=1, source_target_pairs={{0,2},{1,3},{2,0},{3,1},{4,6},{5,7},{6,4},{7,5}} | collective-permute-start | bytes 884744 | tf_op jit(solution)/shard_map/ppermute | solution.py:377
  25.2 0.3 collective-permute-start.7
  25.5 0.0 copy-start
  25.5 0.0 copy-start.1
  25.5 0.0 copy-start.4
  25.5 16.5 %shard_map.102 = (s32[4,528]{1,0:T(4,128)S(1)}, f32[8192,2304]{1,0:T(8,128)}) custom-call(s32[2,528]{1,0:T(2,128)S(1)} %get-tuple-element.37.own_ref, f32[8192,2304]{1,0:T(8,128)} %get-tuple-element.38.de_in), custom_call_target="tpu_custom_call", output_to_operand_aliasing={{1}: (1, {})} | custom-call | flops 6000000000 | bytes 37748736 | tf_op jit(solution)/shard_map/pallas_call | solution.py:401
  42.1 0.0 collective-permute-done.3.p1
  42.1 0.0 collective-permute-done.4.p2
  42.1 7.8 %collective-permute-done.5.p3 = bf16[128,2304]{1,0:T(8,128)(2,1)S(1)} collective-permute-done((bf16[128,2304]{1,0:T(8,128)(2,1)}, bf16[128,2304]{1,0:T(8,128)(2,1)S(1)}, u32[]{:S(2)}, u32[]{:S(2)}) %collective-permute-start.5) | collective-permute-done | bytes 589856 | tf_op jit(solution)/shard_map/ppermute | solution.py:377
  49.9 6.8 %collective-permute-done.2.z_ref = bf16[64,2304]{1,0:T(8,128)(2,1)S(1)} collective-permute-done((bf16[64,2304]{1,0:T(8,128)(2,1)S(1)}, bf16[64,2304]{1,0:T(8,128)(2,1)S(1)}, u32[]{:S(2)}, u32[]{:S(2)}) %collective-permute-start.2) | collective-permute-done | bytes 294944 | tf_op jit(solution)/shard_map/ppermute | solution.py:377
  56.7 0.0 copy-done
  56.7 0.0 copy-done.1
  56.7 0.0 copy-done.4
  56.7 0.0 slice-start
  56.7 0.8 shard_map.105
  57.5 5.2 %collective-permute-done.7.z_ref = bf16[64,2304]{1,0:T(8,128)(2,1)S(1)} collective-permute-done((bf16[64,2304]{1,0:T(8,128)(2,1)S(1)}, bf16[64,2304]{1,0:T(8,128)(2,1)S(1)}, u32[]{:S(2)}, u32[]{:S(2)}) %collective-permute-start.7) | collective-permute-done | bytes 294944 | tf_op jit(solution)/shard_map/ppermute | solution.py:377
  62.7 0.0 slice-start.1
  62.7 1.5 %shard_map.106 = (bf16[128,2304]{1,0:T(8,128)(2,1)S(1)}, bf16[64,2304]{1,0:T(8,128)(2,1)S(1)}, f32[1,2304]{1,0:T(1,128)S(1)}, bf16[2,64,2304]{2,1,0:T(8,128)(2,1)}) custom-call(bf16[64,2304]{1,0:T(8,128)(2,1)S(1)} %get-tuple-element.52.xh_ref, bf16[64,2304]{1,0:T(8,128)(2,1)S(1)} %collective-permute-done.7.z_ref, bf16[128,2304]{1,0:T(8,128)(2,1)S(1)} %copy-done.1, ...), custom_call_target="tpu_custom_call" | custom-call | flops 8847360 | bytes 4718592 | tf_op jit(solution)/shard_map/pallas_call | solution.py:408
  64.1 0.0 collective-permute-start.8
  64.1 0.5 collective-permute-start.6
  64.6 1.7 %collective-permute-start.13 = (bf16[64,2304]{1,0:T(8,128)(2,1)S(1)}, bf16[64,2304]{1,0:T(8,128)(2,1)S(1)}, u32[]{:S(2)}, u32[]{:S(2)}) collective-permute-start(bf16[64,2304]{1,0:T(8,128)(2,1)S(1)} %get-tuple-element.59), channel_id=1, source_target_pairs={{0,2},{1,3},{2,0},{3,1},{4,6},{5,7},{6,4},{7,5}} | collective-permute-start | bytes 884744 | tf_op jit(solution)/shard_map/ppermute | solution.py:377
  66.4 0.3 collective-permute-start.11
  66.7 1.7 %collective-permute-start.9 = (f32[1,2304]{1,0:T(1,128)S(1)}, f32[1,2304]{1,0:T(1,128)S(1)}, u32[]{:S(2)}, u32[]{:S(2)}) collective-permute-start(f32[1,2304]{1,0:T(1,128)S(1)} %get-tuple-element.56.tok_ref), channel_id=1, source_target_pairs={{0,2},{1,3},{2,0},{3,1},{4,6},{5,7},{6,4},{7,5}} | collective-permute-start | bytes 27656 | tf_op jit(solution)/shard_map/ppermute | solution.py:377
  68.4 11.7 %collective-permute-done.9 = f32[1,2304]{1,0:T(1,128)S(1)} collective-permute-done((f32[1,2304]{1,0:T(1,128)S(1)}, f32[1,2304]{1,0:T(1,128)S(1)}, u32[]{:S(2)}, u32[]{:S(2)}) %collective-permute-start.9) | collective-permute-done | bytes 9248 | tf_op jit(solution)/shard_map/ppermute | solution.py:377
  80.1 0.0 collective-permute-start.10
  80.1 1.2 %collective-permute-done.10 = f32[1,2304]{1,0:T(1,128)S(1)} collective-permute-done((f32[1,2304]{1,0:T(1,128)S(1)}, f32[1,2304]{1,0:T(1,128)S(1)}, u32[]{:S(2)}, u32[]{:S(2)}) %collective-permute-start.10) | collective-permute-done | bytes 9248 | tf_op jit(solution)/shard_map/ppermute | solution.py:377
  81.3 0.2 collective-permute-start.14
  81.5 0.0 collective-permute-done.13.c1
  81.5 0.3 collective-permute-start.16
  81.8 0.0 collective-permute-done.11.c0
  81.8 0.2 collective-permute-start.15
  82.0 0.0 collective-permute-done.8.a1.y1
  82.0 0.3 collective-permute-start.12
  82.4 0.0 copy-start.5
  82.4 0.0 collective-permute-done.6.a0.y0
  82.4 0.0 copy-start.2
  82.4 2.4 %shard_map.107 = (f32[256,2304]{1,0:T(8,128)S(1)}, f32[8192,2304]{1,0:T(8,128)}) custom-call(s32[4,528]{1,0:T(4,128)S(1)} %get-tuple-element.39.list_ref, bf16[128,2304]{1,0:T(8,128)(2,1)S(1)} %get-tuple-element.51.refs_0_.d0.x0, bf16[128,2304]{1,0:T(8,128)(2,1)S(1)} %collective-permute-done.6.a0.y0, ...), custom_call_target="tpu_custom_call", output_to_operand_aliasing={{1}: (6, {})} | custom-call | flops 4718592 | bytes 4718592 | tf_op jit(solution)/shard_map/pallas_call | solution.py:426
  84.8 0.0 copy-done.5
  84.8 0.0 slice-done
  84.8 0.0 slice-done.1
  84.8 0.0 copy-done.2
  84.9 2.9 %shard_map.108 = (bf16[2,256,1024]{2,1,0:T(8,128)(2,1)}, f32[2304,1024]{1,0:T(8,128)S(1)}) custom-call(bf16[128,2304]{1,0:T(8,128)(2,1)S(1)} %get-tuple-element.51.refs_0_.d0.x0, bf16[128,2304]{1,0:T(8,128)(2,1)S(1)} %collective-permute-done.6.a0.y0, bf16[128,2304]{1,0:T(8,128)(2,1)S(1)} %get-tuple-element.55.d1.x1, ...), custom_call_target="tpu_custom_call" | custom-call | flops 2415919104 | bytes 4718592 | tf_op jit(solution)/shard_map/pallas_call | solution.py:419
  87.8 0.0 collective-permute-done.14.w0
  87.8 0.0 collective-permute-done.12.b0
  87.8 2.0 %shard_map.109 = (bf16[192,2304]{1,0:T(8,128)(2,1)S(1)}, bf16[2,256,1024]{2,1,0:T(8,128)(2,1)}) custom-call(bf16[64,2304]{1,0:T(8,128)(2,1)S(1)} %collective-permute-done.11.c0, bf16[64,2304]{1,0:T(8,128)(2,1)S(1)} %collective-permute-done.12.b0, bf16[64,2304]{1,0:T(8,128)(2,1)S(1)} %collective-permute-done.13.c1, ...), custom_call_target="tpu_custom_call", output_to_operand_aliasing={{1}: (9, {})} | custom-call | flops 603979776 | bytes 4718592 | tf_op jit(solution)/shard_map/pallas_call | solution.py:431
  89.8 0.0 collective-permute-done.16.w1
  89.8 0.0 collective-permute-done.15.b1
  89.8 5.4 %shard_map.110 = (bf16[2,256,1024]{2,1,0:T(8,128)(2,1)}, f32[2304,1024]{1,0:T(8,128)}, f32[8192,2304]{1,0:T(8,128)}) custom-call(s32[4,528]{1,0:T(4,128)S(1)} %get-tuple-element.39.list_ref, f32[256,2304]{1,0:T(8,128)S(1)} %get-tuple-element.57.xn_ref, ...), custom_call_target="tpu_custom_call", output_to_operand_aliasing={{0}: (13, {}), {2}: (14, {})} | custom-call | flops 2415919104 | bytes 14155776 | tf_op jit(solution)/shard_map/pallas_call | solution.py:435
  (4 shorter events, 0.0 us)
Async XLA Ops:
  0.6 0.7 copy-start.3
  1.3 22.0 %copy-start.6 = (bf16[2304]{0:T(1024)(128)(2,1)S(1)}, bf16[2304]{0:T(1024)(128)(2,1)}, u32[]{:S(2)}) copy-start(bf16[2304]{0:T(1024)(128)(2,1)} %param.8) | copy-start | bytes 13828
  14.0 9.3 %collective-permute-start = (bf16[128,2304]{1,0:T(8,128)(2,1)S(1)}, bf16[128,2304]{1,0:T(8,128)(2,1)S(1)}, u32[]{:S(2)}, u32[]{:S(2)}) collective-permute-start(bf16[128,2304]{1,0:T(8,128)(2,1)S(1)} %get-tuple-element.41), channel_id=1, source_target_pairs={{0,1},{1,0},{2,3},{3,2},{4,5},{5,4},{6,7},{7,6}} | collective-permute-start | bytes 1769480 | tf_op jit(solution)/shard_map/ppermute | solution.py:377
  14.6 8.8 %collective-permute-start.1 = (bf16[128,2304]{1,0:T(8,128)(2,1)S(1)}, bf16[128,2304]{1,0:T(8,128)(2,1)S(1)}, u32[]{:S(2)}, u32[]{:S(2)}) collective-permute-start(bf16[128,2304]{1,0:T(8,128)(2,1)S(1)} %get-tuple-element.43), channel_id=1, source_target_pairs={{0,1},{1,0},{2,3},{3,2},{4,5},{5,4},{6,7},{7,6}} | collective-permute-start | bytes 1769480 | tf_op jit(solution)/shard_map/ppermute | solution.py:377
  20.8 21.3 %collective-permute-start.3 = (bf16[128,2304]{1,0:T(8,128)(2,1)}, bf16[128,2304]{1,0:T(8,128)(2,1)S(1)}, u32[]{:S(2)}, u32[]{:S(2)}) collective-permute-start(bf16[128,2304]{1,0:T(8,128)(2,1)} %get-tuple-element.47), channel_id=1, source_target_pairs={{0,1},{1,0},{2,3},{3,2},{4,5},{5,4},{6,7},{7,6}} | collective-permute-start | bytes 1769480 | tf_op jit(solution)/shard_map/ppermute | solution.py:377
  21.3 20.8 %collective-permute-start.4 = (bf16[128,2304]{1,0:T(8,128)(2,1)}, bf16[128,2304]{1,0:T(8,128)(2,1)S(1)}, u32[]{:S(2)}, u32[]{:S(2)}) collective-permute-start(bf16[128,2304]{1,0:T(8,128)(2,1)} %get-tuple-element.48), channel_id=1, source_target_pairs={{0,2},{1,3},{2,0},{3,1},{4,6},{5,7},{6,4},{7,5}} | collective-permute-start | bytes 1769480 | tf_op jit(solution)/shard_map/ppermute | solution.py:377
  23.2 26.7 %collective-permute-start.5 = (bf16[128,2304]{1,0:T(8,128)(2,1)}, bf16[128,2304]{1,0:T(8,128)(2,1)S(1)}, u32[]{:S(2)}, u32[]{:S(2)}) collective-permute-start(bf16[128,2304]{1,0:T(8,128)(2,1)} %get-tuple-element.49), channel_id=1, source_target_pairs={{0,3},{1,2},{2,1},{3,0},{4,7},{5,6},{6,5},{7,4}} | collective-permute-start | bytes 1769480 | tf_op jit(solution)/shard_map/ppermute | solution.py:377
  23.5 33.2 %collective-permute-start.2 = (bf16[64,2304]{1,0:T(8,128)(2,1)S(1)}, bf16[64,2304]{1,0:T(8,128)(2,1)S(1)}, u32[]{:S(2)}, u32[]{:S(2)}) collective-permute-start(bf16[64,2304]{1,0:T(8,128)(2,1)S(1)} %get-tuple-element.45.t0), channel_id=1, source_target_pairs={{0,2},{1,3},{2,0},{3,1},{4,6},{5,7},{6,4},{7,5}} | collective-permute-start | bytes 884744 | tf_op jit(solution)/shard_map/ppermute | solution.py:377
  25.2 37.4 %collective-permute-start.7 = (bf16[64,2304]{1,0:T(8,128)(2,1)S(1)}, bf16[64,2304]{1,0:T(8,128)(2,1)S(1)}, u32[]{:S(2)}, u32[]{:S(2)}) collective-permute-start(bf16[64,2304]{1,0:T(8,128)(2,1)S(1)} %get-tuple-element.53.t1), channel_id=1, source_target_pairs={{0,2},{1,3},{2,0},{3,1},{4,6},{5,7},{6,4},{7,5}} | collective-permute-start | bytes 884744 | tf_op jit(solution)/shard_map/ppermute | solution.py:377
  25.5 31.2 %copy-start = (bf16[2,64,2304]{2,1,0:T(8,128)(2,1)S(1)}, bf16[2,64,2304]{2,1,0:T(8,128)(2,1)}, u32[]{:S(2)}) copy-start(bf16[2,64,2304]{2,1,0:T(8,128)(2,1)} %dres_ref.3) | copy-start | bytes 1769476
  25.5 31.2 %copy-start.1 = (bf16[128,2304]{1,0:T(8,128)(2,1)S(1)}, bf16[128,2304]{1,0:T(8,128)(2,1)}, u32[]{:S(2)}) copy-start(bf16[128,2304]{1,0:T(8,128)(2,1)} %get-tuple-element.46.p0) | copy-start | bytes 1769476
  25.5 31.2 %copy-start.4 = (s32[2,256]{1,0:T(2,128)S(1)}, s32[2,256]{1,0:T(2,128)}, u32[]{:S(2)}) copy-start(s32[2,256]{1,0:T(2,128)} %ids_ref.9) | copy-start | bytes 6148
  56.7 28.1 %slice-start = ((s8[4718592]{0:T(1024)(128)(4,1)}), s8[4194304]{0:T(1024)(128)(4,1)S(1)}, s32[]{:S(2)}) async-start(s8[4718592]{0:T(1024)(128)(4,1)} %bitcast), calls=%async_computation | async-start | bytes 8388608
  62.7 22.2 %slice-start.1 = ((s8[4718592]{0:T(1024)(128)(4,1)}), s8[524288]{0:T(1024)(128)(4,1)S(1)}, s32[]{:S(2)}) async-start(s8[4718592]{0:T(1024)(128)(4,1)} %bitcast), calls=%async_computation.1 | async-start | bytes 1048576
  64.1 17.8 %collective-permute-start.8 = (bf16[128,2304]{1,0:T(8,128)(2,1)S(1)}, bf16[128,2304]{1,0:T(8,128)(2,1)S(1)}, u32[]{:S(2)}, u32[]{:S(2)}) collective-permute-start(bf16[128,2304]{1,0:T(8,128)(2,1)S(1)} %get-tuple-element.55.d1.x1), channel_id=1, source_target_pairs={{0,1},{1,0},{2,3},{3,2},{4,5},{5,4},{6,7},{7,6}} | collective-permute-start | bytes 1769480 | tf_op jit(solution)/shard_map/ppermute | solution.py:377
  64.1 18.2 %collective-permute-start.6 = (bf16[128,2304]{1,0:T(8,128)(2,1)S(1)}, bf16[128,2304]{1,0:T(8,128)(2,1)S(1)}, u32[]{:S(2)}, u32[]{:S(2)}) collective-permute-start(bf16[128,2304]{1,0:T(8,128)(2,1)S(1)} %get-tuple-element.51.refs_0_.d0.x0), channel_id=1, source_target_pairs={{0,1},{1,0},{2,3},{3,2},{4,5},{5,4},{6,7},{7,6}} | collective-permute-start | bytes 1769480 | tf_op jit(solution)/shard_map/ppermute | solution.py:377
  64.6 16.8 %collective-permute-start.13 = (bf16[64,2304]{1,0:T(8,128)(2,1)S(1)}, bf16[64,2304]{1,0:T(8,128)(2,1)S(1)}, u32[]{:S(2)}, u32[]{:S(2)}) collective-permute-start(bf16[64,2304]{1,0:T(8,128)(2,1)S(1)} %get-tuple-element.59), channel_id=1, source_target_pairs={{0,2},{1,3},{2,0},{3,1},{4,6},{5,7},{6,4},{7,5}} | collective-permute-start | bytes 884744 | tf_op jit(solution)/shard_map/ppermute | solution.py:377
  66.4 15.4 %collective-permute-start.11 = (bf16[64,2304]{1,0:T(8,128)(2,1)S(1)}, bf16[64,2304]{1,0:T(8,128)(2,1)S(1)}, u32[]{:S(2)}, u32[]{:S(2)}) collective-permute-start(bf16[64,2304]{1,0:T(8,128)(2,1)S(1)} %get-tuple-element.58), channel_id=1, source_target_pairs={{0,2},{1,3},{2,0},{3,1},{4,6},{5,7},{6,4},{7,5}} | collective-permute-start | bytes 884744 | tf_op jit(solution)/shard_map/ppermute | solution.py:377
  66.7 13.4 %collective-permute-start.9 = (f32[1,2304]{1,0:T(1,128)S(1)}, f32[1,2304]{1,0:T(1,128)S(1)}, u32[]{:S(2)}, u32[]{:S(2)}) collective-permute-start(f32[1,2304]{1,0:T(1,128)S(1)} %get-tuple-element.56.tok_ref), channel_id=1, source_target_pairs={{0,2},{1,3},{2,0},{3,1},{4,6},{5,7},{6,4},{7,5}} | collective-permute-start | bytes 27656 | tf_op jit(solution)/shard_map/ppermute | solution.py:377
  80.1 1.2 %collective-permute-start.10 = (f32[1,2304]{1,0:T(1,128)S(1)}, f32[1,2304]{1,0:T(1,128)S(1)}, u32[]{:S(2)}, u32[]{:S(2)}) collective-permute-start(f32[1,2304]{1,0:T(1,128)S(1)} %add.6), channel_id=1, source_target_pairs={{0,1},{1,0},{2,3},{3,2},{4,5},{5,4},{6,7},{7,6}} | collective-permute-start | bytes 27656 | tf_op jit(solution)/shard_map/ppermute | solution.py:377
  81.3 6.5 %collective-permute-start.14 = (bf16[64,2304]{1,0:T(8,128)(2,1)S(1)}, bf16[64,2304]{1,0:T(8,128)(2,1)S(1)}, u32[]{:S(2)}, u32[]{:S(2)}) collective-permute-start(bf16[64,2304]{1,0:T(8,128)(2,1)S(1)} %get-tuple-element.45.t0), channel_id=1, source_target_pairs={{0,1},{1,0},{2,3},{3,2},{4,5},{5,4},{6,7},{7,6}} | collective-permute-start | bytes 884744 | tf_op jit(solution)/shard_map/ppermute | solution.py:377
  81.5 8.3 %collective-permute-start.16 = (bf16[64,2304]{1,0:T(8,128)(2,1)S(1)}, bf16[64,2304]{1,0:T(8,128)(2,1)S(1)}, u32[]{:S(2)}, u32[]{:S(2)}) collective-permute-start(bf16[64,2304]{1,0:T(8,128)(2,1)S(1)} %get-tuple-element.53.t1), channel_id=1, source_target_pairs={{0,1},{1,0},{2,3},{3,2},{4,5},{5,4},{6,7},{7,6}} | collective-permute-start | bytes 884744 | tf_op jit(solution)/shard_map/ppermute | solution.py:377
  81.8 8.0 %collective-permute-start.15 = (bf16[64,2304]{1,0:T(8,128)(2,1)S(1)}, bf16[64,2304]{1,0:T(8,128)(2,1)S(1)}, u32[]{:S(2)}, u32[]{:S(2)}) collective-permute-start(bf16[64,2304]{1,0:T(8,128)(2,1)S(1)} %collective-permute-done.13.c1), channel_id=1, source_target_pairs={{0,1},{1,0},{2,3},{3,2},{4,5},{5,4},{6,7},{7,6}} | collective-permute-start | bytes 884744 | tf_op jit(solution)/shard_map/ppermute | solution.py:377
  82.0 5.8 %collective-permute-start.12 = (bf16[64,2304]{1,0:T(8,128)(2,1)S(1)}, bf16[64,2304]{1,0:T(8,128)(2,1)S(1)}, u32[]{:S(2)}, u32[]{:S(2)}) collective-permute-start(bf16[64,2304]{1,0:T(8,128)(2,1)S(1)} %collective-permute-done.11.c0), channel_id=1, source_target_pairs={{0,1},{1,0},{2,3},{3,2},{4,5},{5,4},{6,7},{7,6}} | collective-permute-start | bytes 884744 | tf_op jit(solution)/shard_map/ppermute | solution.py:377
  82.4 2.5 %copy-start.5 = (f32[2304]{0:T(1024)}, f32[2304]{0:T(1024)S(1)}, u32[]{:S(2)}) copy-start(f32[2304]{0:T(1024)S(1)} %add_reduce_fusion.tok_ref) | copy-start | bytes 27652
  82.4 2.5 %copy-start.2 = (bf16[2,256,1024]{2,1,0:T(8,128)(2,1)S(1)}, bf16[2,256,1024]{2,1,0:T(8,128)(2,1)}, u32[]{:S(2)}) copy-start(bf16[2,256,1024]{2,1,0:T(8,128)(2,1)} %du_ref.5) | copy-start | bytes 3145732

commit v19 on v18

--- a/solution.py
+++ b/solution.py
@@ -341,6 +341,7 @@
         rows = slice(i * blk, (i + 1) * blk)
         dwb[rows, :] = dwp_ref[rows, :] + dw_tile(n_ref, du2, i, blk)
         pltpu.make_async_copy(dwb.at[pl.ds(i * blk, blk), :], dw_ref.at[pl.ds(i * blk, blk), :], wsem).start()
+    copies = umat(n_ref, 2 * tl, w_ref, ub, u_ref, order[2:], usem)
 
     @pl.when(repeats(1, list_ref))
     def _():
@@ -349,7 +350,6 @@
     for a, ref in enumerate((c0, b0, c1, b1)):
         xf[h + a * tl:h + (a + 1) * tl, :] = ref[...].astype(F32)
     scatter(1, list_ref, xf, de_ref, sem)
-    copies = umat(n_ref, 2 * tl, w_ref, ub, u_ref, order[2:], usem)
     scatter_wait(1, list_ref, xf, de_ref, sem)
     pltpu.make_async_copy(dwb, dw_ref, wsem).wait()
     for c in copies:
@@ -420,13 +420,12 @@
             u_kernel, 32, [S((k, t, fc), BF16), S((d, fc), F32)], [VMEM] * 8, [HBM, VMEM],
             [pltpu.VMEM((t, d), BF16), pltpu.VMEM((t, fc), BF16), pltpu.VMEM((t, fc), BF16), D],
             4 * t * d * fc, 2 * d * fc)(mine0, next0, mine1, next1, g2, w, du, dg)
+        xn, de = call(near_kernel, 8, [S((t, d), F32), S((vl, d), F32)], [SMEM] + [VMEM] * 5 + [HBM], [VMEM, HBM],
+                      [D], 8 * h * d, 8 * h * d, {6: 1})(lists, mine0, next0, mine1, next1, dg, de)
+        b0 = perm(c0, sib)
+        b1 = perm(c1, sib)
         dgs = dg + perm(dg, cross)
         dgs = dgs + perm(dgs, sib)
-        dgs = dgs.reshape(d)
-        xn, de = call(near_kernel, 8, [S((t, d), F32), S((vl, d), F32)], [SMEM] + [VMEM] * 5 + [HBM], [VMEM, HBM],
-                      [D], 8 * h * d, 8 * h * d, {6: 1})(lists, mine0, next0, mine1, next1, dgs, de)
-        b0 = perm(c0, sib)
-        b1 = perm(c1, sib)
 
         nm, u = call(
             functools.partial(mid_kernel, 2 * vl), 12, [S((3 * tl, d), BF16), S((k, t, fc), BF16)],
@@ -439,7 +438,7 @@
              pltpu.VMEM((d, fc), F32), D, D, D],
             4 * t * d * fc, 6 * d * fc, {13: 0, 14: 2})(
                 lists, xn, nm, c0, b0, c1, b1, w1, dwp, ids, g2, w, du, u, de)
-        return u, x, de, dw, dgs
+        return u, x, de, dw, dgs.reshape(d)
 
     return jax.shard_map(
         local,

time: 95.6 us -> 96.3 us (level)
  transfers between devices with their start and end apart: 17 -> 17, of which waited for: 5 -> 5; matrix products, arithmetic and copies ran while one was open for 0% -> 1% of each run, Pallas kernels for 32% -> 34%
where the time goes in v19:
time: 96.3 us; the launch traced here: 95.8 us
  Pallas kernels  50.5 us (52%)
  waiting for transfers between devices  33.1 us (34%)
  starting transfers between devices  9.95 us (10%)
    ppermute x17, waiting for transfers between devices, perm(): return lax.ppermute(v, 'tp', p)  33.1 us
    pallas_call x1, Pallas kernels, local(): call(zero_kernel, 8, [S((4, 2 * h + 16), jnp.int32), S((vl, d), F32)], [S...  16.6 us
    pallas_call x1, Pallas kernels, local(): call(gather_kernel, 36, [S((n, d), BF16)] * 4 + [S((2, 2 * h + 16), jnp.i...  12.7 us
    ppermute x17, starting transfers between devices, perm(): return lax.ppermute(v, 'tp', p)  9.95 us
    pallas_call x1, Pallas kernels, local(): call(pdn_kernel, 60, [S((n, d), BF16)] * 4, [HBM] * 2, [HBM] * 4, [pltpu....  6.24 us
    pallas_call x1, Pallas kernels, local(): call(functools.partial(last_kernel, 2 * vl), 20, [S((k, t, fc), BF16), S(...  5.43 us
    pallas_call x1, Pallas kernels, local(): call(u_kernel, 32, [S((k, t, fc), BF16), S((d, fc), F32)], [VMEM] * 8, [H...  2.93 us
    pallas_call x1, Pallas kernels, local(): call(near_kernel, 8, [S((t, d), F32), S((vl, d), F32)], [SMEM] + [VMEM] *...  2.41 us
  transfers between devices with their start and end apart: 17, of which 5 were waited for; matrix products, arithmetic and copies ran while one was open for 1% of the time, Pallas kernels for 34%

profile of v19, /device:TPU:0, one launch (start us, length us, event | category | flops | bytes accessed | tf_op | source)
XLA Modules:
  0.0 95.8 jit_solution(6639003174925904929)
XLA Ops:
  0.6 0.0 copy-start.3
  0.6 0.7 copy-done.3
  1.3 12.7 %shard_map.101 = (bf16[128,2304]{1,0:T(8,128)(2,1)S(1)}, bf16[128,2304]{1,0:T(8,128)(2,1)S(1)}, bf16[128,2304]{1,0:T(8,128)(2,1)S(1)}, bf16[128,2304]{1,0:T(8,12...) custom-call(s32[2,256]{1,0:T(2,128)S(1)} %copy-done.3, bf16[8192,2304]{1,0:T(8,128)(2,1)} %emb_ref.1), custom_call_target="tpu_custom_call" | custom-call | flops 500000000 | bytes 9437184 | tf_op jit(solution)/shard_map/pallas_call | solution.py:385
  14.0 0.5 collective-permute-start
  14.6 0.0 collective-permute-start.1
  14.6 6.2 %shard_map.104 = (bf16[128,2304]{1,0:T(8,128)(2,1)}, bf16[128,2304]{1,0:T(8,128)(2,1)}, bf16[128,2304]{1,0:T(8,128)(2,1)}, bf16[128,2304]{1,0:T(8,128)(2,1)}) custom-call(bf16[2,256,1024]{2,1,0:T(8,128)(2,1)} %du_ref.5, bf16[2304,1024]{1,0:T(8,128)(2,1)} %w_ref.7), custom_call_target="tpu_custom_call" | custom-call | flops 2415919104 | bytes 8126464 | tf_op jit(solution)/shard_map/pallas_call | solution.py:379
  20.9 0.5 collective-permute-start.3
  21.3 1.9 %collective-permute-start.4 = (bf16[128,2304]{1,0:T(8,128)(2,1)}, bf16[128,2304]{1,0:T(8,128)(2,1)S(1)}, u32[]{:S(2)}, u32[]{:S(2)}) collective-permute-start(bf16[128,2304]{1,0:T(8,128)(2,1)} %get-tuple-element.48), channel_id=1, source_target_pairs={{0,2},{1,3},{2,0},{3,1},{4,6},{5,7},{6,4},{7,5}} | collective-permute-start | bytes 1769480 | tf_op jit(solution)/shard_map/ppermute | solution.py:377
  23.3 0.1 collective-permute-start.5
  23.3 0.0 collective-permute-done.y0
  23.3 0.0 collective-permute-done.1.y1
  23.3 0.1 shard_map.103
  23.5 1.8 %collective-permute-start.2 = (bf16[64,2304]{1,0:T(8,128)(2,1)S(1)}, bf16[64,2304]{1,0:T(8,128)(2,1)S(1)}, u32[]{:S(2)}, u32[]{:S(2)}) collective-permute-start(bf16[64,2304]{1,0:T(8,128)(2,1)S(1)} %get-tuple-element.45.t0), channel_id=1, source_target_pairs={{0,2},{1,3},{2,0},{3,1},{4,6},{5,7},{6,4},{7,5}} | collective-permute-start | bytes 884744 | tf_op jit(solution)/shard_map/ppermute | solution.py:377
  25.2 0.3 collective-permute-start.7
  25.5 0.0 copy-start.5
  25.5 0.0 copy-start
  25.5 0.0 copy-start.1
  25.5 0.0 copy-start.4
  25.5 16.6 %shard_map.102 = (s32[4,528]{1,0:T(4,128)S(1)}, f32[8192,2304]{1,0:T(8,128)}) custom-call(s32[2,528]{1,0:T(2,128)S(1)} %get-tuple-element.37.own_ref, f32[8192,2304]{1,0:T(8,128)} %get-tuple-element.38.de_in), custom_call_target="tpu_custom_call", output_to_operand_aliasing={{1}: (1, {})} | custom-call | flops 6000000000 | bytes 37748736 | tf_op jit(solution)/shard_map/pallas_call | solution.py:401
  42.1 0.0 copy-done.5
  42.1 0.0 collective-permute-done.3.p1
  42.1 0.0 collective-permute-done.4.p2
  42.1 7.8 %collective-permute-done.5.p3 = bf16[128,2304]{1,0:T(8,128)(2,1)S(1)} collective-permute-done((bf16[128,2304]{1,0:T(8,128)(2,1)}, bf16[128,2304]{1,0:T(8,128)(2,1)S(1)}, u32[]{:S(2)}, u32[]{:S(2)}) %collective-permute-start.5) | collective-permute-done | bytes 589856 | tf_op jit(solution)/shard_map/ppermute | solution.py:377
  49.9 6.8 %collective-permute-done.2.z_ref = bf16[64,2304]{1,0:T(8,128)(2,1)S(1)} collective-permute-done((bf16[64,2304]{1,0:T(8,128)(2,1)S(1)}, bf16[64,2304]{1,0:T(8,128)(2,1)S(1)}, u32[]{:S(2)}, u32[]{:S(2)}) %collective-permute-start.2) | collective-permute-done | bytes 294944 | tf_op jit(solution)/shard_map/ppermute | solution.py:377
  56.7 0.0 copy-done
  56.7 0.0 copy-done.1
  56.7 0.0 copy-done.4
  56.7 0.0 slice-start
  56.7 0.8 shard_map.105
  57.5 0.0 collective-permute-start.6
  57.5 5.2 %collective-permute-done.7.z_ref = bf16[64,2304]{1,0:T(8,128)(2,1)S(1)} collective-permute-done((bf16[64,2304]{1,0:T(8,128)(2,1)S(1)}, bf16[64,2304]{1,0:T(8,128)(2,1)S(1)}, u32[]{:S(2)}, u32[]{:S(2)}) %collective-permute-start.7) | collective-permute-done | bytes 294944 | tf_op jit(solution)/shard_map/ppermute | solution.py:377
  62.7 0.0 slice-start.1
  62.7 1.5 %shard_map.106 = (bf16[128,2304]{1,0:T(8,128)(2,1)S(1)}, bf16[64,2304]{1,0:T(8,128)(2,1)S(1)}, f32[1,2304]{1,0:T(1,128)S(1)}, bf16[2,64,2304]{2,1,0:T(8,128)(2,1)}) custom-call(bf16[64,2304]{1,0:T(8,128)(2,1)S(1)} %get-tuple-element.52.xh_ref, bf16[64,2304]{1,0:T(8,128)(2,1)S(1)} %collective-permute-done.7.z_ref, bf16[128,2304]{1,0:T(8,128)(2,1)S(1)} %copy-done.1, ...), custom_call_target="tpu_custom_call" | custom-call | flops 8847360 | bytes 4718592 | tf_op jit(solution)/shard_map/pallas_call | solution.py:408
  64.2 0.0 collective-permute-start.8
  64.2 1.7 %collective-permute-start.9 = (bf16[64,2304]{1,0:T(8,128)(2,1)S(1)}, bf16[64,2304]{1,0:T(8,128)(2,1)S(1)}, u32[]{:S(2)}, u32[]{:S(2)}) collective-permute-start(bf16[64,2304]{1,0:T(8,128)(2,1)S(1)} %get-tuple-element.58), channel_id=1, source_target_pairs={{0,2},{1,3},{2,0},{3,1},{4,6},{5,7},{6,4},{7,5}} | collective-permute-start | bytes 884744 | tf_op jit(solution)/shard_map/ppermute | solution.py:377
  65.9 0.3 collective-permute-start.11
  66.2 1.7 %collective-permute-start.15 = (f32[1,2304]{1,0:T(1,128)S(1)}, f32[1,2304]{1,0:T(1,128)S(1)}, u32[]{:S(2)}, u32[]{:S(2)}) collective-permute-start(f32[1,2304]{1,0:T(1,128)S(1)} %get-tuple-element.56.tok_ref), channel_id=1, source_target_pairs={{0,2},{1,3},{2,0},{3,1},{4,6},{5,7},{6,4},{7,5}} | collective-permute-start | bytes 27656 | tf_op jit(solution)/shard_map/ppermute | solution.py:377
  67.9 12.2 %collective-permute-done.15 = f32[1,2304]{1,0:T(1,128)S(1)} collective-permute-done((f32[1,2304]{1,0:T(1,128)S(1)}, f32[1,2304]{1,0:T(1,128)S(1)}, u32[]{:S(2)}, u32[]{:S(2)}) %collective-permute-start.15) | collective-permute-done | bytes 9248 | tf_op jit(solution)/shard_map/ppermute | solution.py:377
  80.1 0.0 collective-permute-start.16
  80.2 1.2 %collective-permute-done.16 = f32[1,2304]{1,0:T(1,128)S(1)} collective-permute-done((f32[1,2304]{1,0:T(1,128)S(1)}, f32[1,2304]{1,0:T(1,128)S(1)}, u32[]{:S(2)}, u32[]{:S(2)}) %collective-permute-start.16) | collective-permute-done | bytes 9248 | tf_op jit(solution)/shard_map/ppermute | solution.py:377
  81.3 0.2 collective-permute-start.12
  81.5 0.0 collective-permute-done.9.c0
  81.5 0.3 collective-permute-start.14
  81.8 0.0 collective-permute-done.11.c1
  81.8 0.2 collective-permute-start.10
  82.0 0.0 collective-permute-done.6.a0.y0
  82.0 0.3 collective-permute-start.13
  82.3 0.6 add_reduce_fusion
  83.0 0.0 collective-permute-done.8.a1.y1
  83.0 0.0 copy-start.2
  83.0 2.4 %shard_map.107 = (f32[256,2304]{1,0:T(8,128)S(1)}, f32[8192,2304]{1,0:T(8,128)}) custom-call(s32[4,528]{1,0:T(4,128)S(1)} %get-tuple-element.39.list_ref, bf16[128,2304]{1,0:T(8,128)(2,1)S(1)} %get-tuple-element.51.refs_0_.d0.x0, bf16[128,2304]{1,0:T(8,128)(2,1)S(1)} %collective-permute-done.6.a0.y0, ...), custom_call_target="tpu_custom_call", output_to_operand_aliasing={{1}: (6, {})} | custom-call | flops 4718592 | bytes 4718592 | tf_op jit(solution)/shard_map/pallas_call | solution.py:423
  85.4 0.0 slice-done
  85.4 0.0 slice-done.1
  85.4 0.0 copy-done.2
  85.4 2.9 %shard_map.108 = (bf16[2,256,1024]{2,1,0:T(8,128)(2,1)}, f32[2304,1024]{1,0:T(8,128)S(1)}) custom-call(bf16[128,2304]{1,0:T(8,128)(2,1)S(1)} %get-tuple-element.51.refs_0_.d0.x0, bf16[128,2304]{1,0:T(8,128)(2,1)S(1)} %collective-permute-done.6.a0.y0, bf16[128,2304]{1,0:T(8,128)(2,1)S(1)} %get-tuple-element.55.d1.x1, ...), custom_call_target="tpu_custom_call" | custom-call | flops 2415919104 | bytes 4718592 | tf_op jit(solution)/shard_map/pallas_call | solution.py:419
  88.4 0.0 collective-permute-done.12.w0
  88.4 0.0 collective-permute-done.10.b0
  88.4 2.0 %shard_map.109 = (bf16[192,2304]{1,0:T(8,128)(2,1)S(1)}, bf16[2,256,1024]{2,1,0:T(8,128)(2,1)}) custom-call(bf16[64,2304]{1,0:T(8,128)(2,1)S(1)} %collective-permute-done.9.c0, bf16[64,2304]{1,0:T(8,128)(2,1)S(1)} %collective-permute-done.10.b0, bf16[64,2304]{1,0:T(8,128)(2,1)S(1)} %collective-permute-done.11.c1, ...), custom_call_target="tpu_custom_call", output_to_operand_aliasing={{1}: (9, {})} | custom-call | flops 603979776 | bytes 4718592 | tf_op jit(solution)/shard_map/pallas_call | solution.py:430
  90.4 0.0 collective-permute-done.14.w1
  90.4 0.0 collective-permute-done.13.b1
  90.4 5.4 %shard_map.110 = (bf16[2,256,1024]{2,1,0:T(8,128)(2,1)}, f32[2304,1024]{1,0:T(8,128)}, f32[8192,2304]{1,0:T(8,128)}) custom-call(s32[4,528]{1,0:T(4,128)S(1)} %get-tuple-element.39.list_ref, f32[256,2304]{1,0:T(8,128)S(1)} %get-tuple-element.57.xn_ref, ...), custom_call_target="tpu_custom_call", output_to_operand_aliasing={{0}: (13, {}), {2}: (14, {})} | custom-call | flops 2415919104 | bytes 14155776 | tf_op jit(solution)/shard_map/pallas_call | solution.py:434
  (3 shorter events, 0.0 us)
Async XLA Ops:
  0.6 0.7 copy-start.3
  14.0 9.3 %collective-permute-start = (bf16[128,2304]{1,0:T(8,128)(2,1)S(1)}, bf16[128,2304]{1,0:T(8,128)(2,1)S(1)}, u32[]{:S(2)}, u32[]{:S(2)}) collective-permute-start(bf16[128,2304]{1,0:T(8,128)(2,1)S(1)} %get-tuple-element.41), channel_id=1, source_target_pairs={{0,1},{1,0},{2,3},{3,2},{4,5},{5,4},{6,7},{7,6}} | collective-permute-start | bytes 1769480 | tf_op jit(solution)/shard_map/ppermute | solution.py:377
  14.6 8.8 %collective-permute-start.1 = (bf16[128,2304]{1,0:T(8,128)(2,1)S(1)}, bf16[128,2304]{1,0:T(8,128)(2,1)S(1)}, u32[]{:S(2)}, u32[]{:S(2)}) collective-permute-start(bf16[128,2304]{1,0:T(8,128)(2,1)S(1)} %get-tuple-element.43), channel_id=1, source_target_pairs={{0,1},{1,0},{2,3},{3,2},{4,5},{5,4},{6,7},{7,6}} | collective-permute-start | bytes 1769480 | tf_op jit(solution)/shard_map/ppermute | solution.py:377
  20.9 21.3 %collective-permute-start.3 = (bf16[128,2304]{1,0:T(8,128)(2,1)}, bf16[128,2304]{1,0:T(8,128)(2,1)S(1)}, u32[]{:S(2)}, u32[]{:S(2)}) collective-permute-start(bf16[128,2304]{1,0:T(8,128)(2,1)} %get-tuple-element.47), channel_id=1, source_target_pairs={{0,1},{1,0},{2,3},{3,2},{4,5},{5,4},{6,7},{7,6}} | collective-permute-start | bytes 1769480 | tf_op jit(solution)/shard_map/ppermute | solution.py:377
  21.3 20.8 %collective-permute-start.4 = (bf16[128,2304]{1,0:T(8,128)(2,1)}, bf16[128,2304]{1,0:T(8,128)(2,1)S(1)}, u32[]{:S(2)}, u32[]{:S(2)}) collective-permute-start(bf16[128,2304]{1,0:T(8,128)(2,1)} %get-tuple-element.48), channel_id=1, source_target_pairs={{0,2},{1,3},{2,0},{3,1},{4,6},{5,7},{6,4},{7,5}} | collective-permute-start | bytes 1769480 | tf_op jit(solution)/shard_map/ppermute | solution.py:377
  23.3 26.7 %collective-permute-start.5 = (bf16[128,2304]{1,0:T(8,128)(2,1)}, bf16[128,2304]{1,0:T(8,128)(2,1)S(1)}, u32[]{:S(2)}, u32[]{:S(2)}) collective-permute-start(bf16[128,2304]{1,0:T(8,128)(2,1)} %get-tuple-element.49), channel_id=1, source_target_pairs={{0,3},{1,2},{2,1},{3,0},{4,7},{5,6},{6,5},{7,4}} | collective-permute-start | bytes 1769480 | tf_op jit(solution)/shard_map/ppermute | solution.py:377
  23.5 33.3 %collective-permute-start.2 = (bf16[64,2304]{1,0:T(8,128)(2,1)S(1)}, bf16[64,2304]{1,0:T(8,128)(2,1)S(1)}, u32[]{:S(2)}, u32[]{:S(2)}) collective-permute-start(bf16[64,2304]{1,0:T(8,128)(2,1)S(1)} %get-tuple-element.45.t0), channel_id=1, source_target_pairs={{0,2},{1,3},{2,0},{3,1},{4,6},{5,7},{6,4},{7,5}} | collective-permute-start | bytes 884744 | tf_op jit(solution)/shard_map/ppermute | solution.py:377
  25.2 37.5 %collective-permute-start.7 = (bf16[64,2304]{1,0:T(8,128)(2,1)S(1)}, bf16[64,2304]{1,0:T(8,128)(2,1)S(1)}, u32[]{:S(2)}, u32[]{:S(2)}) collective-permute-start(bf16[64,2304]{1,0:T(8,128)(2,1)S(1)} %get-tuple-element.53.t1), channel_id=1, source_target_pairs={{0,2},{1,3},{2,0},{3,1},{4,6},{5,7},{6,4},{7,5}} | collective-permute-start | bytes 884744 | tf_op jit(solution)/shard_map/ppermute | solution.py:377
  25.5 16.6 %copy-start.5 = (bf16[2304]{0:T(1024)(128)(2,1)S(1)}, bf16[2304]{0:T(1024)(128)(2,1)}, u32[]{:S(2)}) copy-start(bf16[2304]{0:T(1024)(128)(2,1)} %param.8) | copy-start | bytes 13828
  25.5 31.2 %copy-start = (bf16[2,64,2304]{2,1,0:T(8,128)(2,1)S(1)}, bf16[2,64,2304]{2,1,0:T(8,128)(2,1)}, u32[]{:S(2)}) copy-start(bf16[2,64,2304]{2,1,0:T(8,128)(2,1)} %dres_ref.3) | copy-start | bytes 1769476
  25.5 31.2 %copy-start.1 = (bf16[128,2304]{1,0:T(8,128)(2,1)S(1)}, bf16[128,2304]{1,0:T(8,128)(2,1)}, u32[]{:S(2)}) copy-start(bf16[128,2304]{1,0:T(8,128)(2,1)} %get-tuple-element.46.p0) | copy-start | bytes 1769476
  25.5 31.2 %copy-start.4 = (s32[2,256]{1,0:T(2,128)S(1)}, s32[2,256]{1,0:T(2,128)}, u32[]{:S(2)}) copy-start(s32[2,256]{1,0:T(2,128)} %ids_ref.9) | copy-start | bytes 6148
  56.7 28.7 %slice-start = ((s8[4718592]{0:T(1024)(128)(4,1)}), s8[4194304]{0:T(1024)(128)(4,1)S(1)}, s32[]{:S(2)}) async-start(s8[4718592]{0:T(1024)(128)(4,1)} %bitcast), calls=%async_computation | async-start | bytes 8388608
  57.5 24.5 %collective-permute-start.6 = (bf16[128,2304]{1,0:T(8,128)(2,1)S(1)}, bf16[128,2304]{1,0:T(8,128)(2,1)S(1)}, u32[]{:S(2)}, u32[]{:S(2)}) collective-permute-start(bf16[128,2304]{1,0:T(8,128)(2,1)S(1)} %get-tuple-element.51.refs_0_.d0.x0), channel_id=1, source_target_pairs={{0,1},{1,0},{2,3},{3,2},{4,5},{5,4},{6,7},{7,6}} | collective-permute-start | bytes 1769480 | tf_op jit(solution)/shard_map/ppermute | solution.py:377
  62.7 22.7 %slice-start.1 = ((s8[4718592]{0:T(1024)(128)(4,1)}), s8[524288]{0:T(1024)(128)(4,1)S(1)}, s32[]{:S(2)}) async-start(s8[4718592]{0:T(1024)(128)(4,1)} %bitcast), calls=%async_computation.1 | async-start | bytes 1048576
  64.2 18.8 %collective-permute-start.8 = (bf16[128,2304]{1,0:T(8,128)(2,1)S(1)}, bf16[128,2304]{1,0:T(8,128)(2,1)S(1)}, u32[]{:S(2)}, u32[]{:S(2)}) collective-permute-start(bf16[128,2304]{1,0:T(8,128)(2,1)S(1)} %get-tuple-element.55.d1.x1), channel_id=1, source_target_pairs={{0,1},{1,0},{2,3},{3,2},{4,5},{5,4},{6,7},{7,6}} | collective-permute-start | bytes 1769480 | tf_op jit(solution)/shard_map/ppermute | solution.py:377
  64.2 17.3 %collective-permute-start.9 = (bf16[64,2304]{1,0:T(8,128)(2,1)S(1)}, bf16[64,2304]{1,0:T(8,128)(2,1)S(1)}, u32[]{:S(2)}, u32[]{:S(2)}) collective-permute-start(bf16[64,2304]{1,0:T(8,128)(2,1)S(1)} %get-tuple-element.58), channel_id=1, source_target_pairs={{0,2},{1,3},{2,0},{3,1},{4,6},{5,7},{6,4},{7,5}} | collective-permute-start | bytes 884744 | tf_op jit(solution)/shard_map/ppermute | solution.py:377
  65.9 15.9 %collective-permute-start.11 = (bf16[64,2304]{1,0:T(8,128)(2,1)S(1)}, bf16[64,2304]{1,0:T(8,128)(2,1)S(1)}, u32[]{:S(2)}, u32[]{:S(2)}) collective-permute-start(bf16[64,2304]{1,0:T(8,128)(2,1)S(1)} %get-tuple-element.59), channel_id=1, source_target_pairs={{0,2},{1,3},{2,0},{3,1},{4,6},{5,7},{6,4},{7,5}} | collective-permute-start | bytes 884744 | tf_op jit(solution)/shard_map/ppermute | solution.py:377
  66.2 13.9 %collective-permute-start.15 = (f32[1,2304]{1,0:T(1,128)S(1)}, f32[1,2304]{1,0:T(1,128)S(1)}, u32[]{:S(2)}, u32[]{:S(2)}) collective-permute-start(f32[1,2304]{1,0:T(1,128)S(1)} %get-tuple-element.56.tok_ref), channel_id=1, source_target_pairs={{0,2},{1,3},{2,0},{3,1},{4,6},{5,7},{6,4},{7,5}} | collective-permute-start | bytes 27656 | tf_op jit(solution)/shard_map/ppermute | solution.py:377
  80.1 1.2 %collective-permute-start.16 = (f32[1,2304]{1,0:T(1,128)S(1)}, f32[1,2304]{1,0:T(1,128)S(1)}, u32[]{:S(2)}, u32[]{:S(2)}) collective-permute-start(f32[1,2304]{1,0:T(1,128)S(1)} %add.6), channel_id=1, source_target_pairs={{0,1},{1,0},{2,3},{3,2},{4,5},{5,4},{6,7},{7,6}} | collective-permute-start | bytes 27656 | tf_op jit(solution)/shard_map/ppermute | solution.py:377
  81.3 7.1 %collective-permute-start.12 = (bf16[64,2304]{1,0:T(8,128)(2,1)S(1)}, bf16[64,2304]{1,0:T(8,128)(2,1)S(1)}, u32[]{:S(2)}, u32[]{:S(2)}) collective-permute-start(bf16[64,2304]{1,0:T(8,128)(2,1)S(1)} %get-tuple-element.45.t0), channel_id=1, source_target_pairs={{0,1},{1,0},{2,3},{3,2},{4,5},{5,4},{6,7},{7,6}} | collective-permute-start | bytes 884744 | tf_op jit(solution)/shard_map/ppermute | solution.py:377
  81.5 8.9 %collective-permute-start.14 = (bf16[64,2304]{1,0:T(8,128)(2,1)S(1)}, bf16[64,2304]{1,0:T(8,128)(2,1)S(1)}, u32[]{:S(2)}, u32[]{:S(2)}) collective-permute-start(bf16[64,2304]{1,0:T(8,128)(2,1)S(1)} %get-tuple-element.53.t1), channel_id=1, source_target_pairs={{0,1},{1,0},{2,3},{3,2},{4,5},{5,4},{6,7},{7,6}} | collective-permute-start | bytes 884744 | tf_op jit(solution)/shard_map/ppermute | solution.py:377
  81.8 6.5 %collective-permute-start.10 = (bf16[64,2304]{1,0:T(8,128)(2,1)S(1)}, bf16[64,2304]{1,0:T(8,128)(2,1)S(1)}, u32[]{:S(2)}, u32[]{:S(2)}) collective-permute-start(bf16[64,2304]{1,0:T(8,128)(2,1)S(1)} %collective-permute-done.9.c0), channel_id=1, source_target_pairs={{0,1},{1,0},{2,3},{3,2},{4,5},{5,4},{6,7},{7,6}} | collective-permute-start | bytes 884744 | tf_op jit(solution)/shard_map/ppermute | solution.py:377
  82.0 8.4 %collective-permute-start.13 = (bf16[64,2304]{1,0:T(8,128)(2,1)S(1)}, bf16[64,2304]{1,0:T(8,128)(2,1)S(1)}, u32[]{:S(2)}, u32[]{:S(2)}) collective-permute-start(bf16[64,2304]{1,0:T(8,128)(2,1)S(1)} %collective-permute-done.11.c1), channel_id=1, source_target_pairs={{0,1},{1,0},{2,3},{3,2},{4,5},{5,4},{6,7},{7,6}} | collective-permute-start | bytes 884744 | tf_op jit(solution)/shard_map/ppermute | solution.py:377
  83.0 2.4 %copy-start.2 = (bf16[2,256,1024]{2,1,0:T(8,128)(2,1)S(1)}, bf16[2,256,1024]{2,1,0:T(8,128)(2,1)}, u32[]{:S(2)}) copy-start(bf16[2,256,1024]{2,1,0:T(8,128)(2,1)} %du_ref.5) | copy-start | bytes 3145732
